TPU v7x, 32 devices: a whole 2x2x4 slice. The times are simulated.
32 devices in a mesh: dp: 8 (over y, x, core), tensor: 4 (over z).
Axes of the slice: x: 2, y: 2, z: 4, core: 2. Of those that a mesh axis runs over, the one named last changes fastest.
Arguments:
- layer_in: bfloat16 [8, 1024, 1024], P(None, ('dp', 'tensor')), may hold values from -6 to 6
- text_mask: int32 [1024], P(('dp', 'tensor')), may hold values 0 or 1
- w_qkv: float32 [8, 3, 1024, 1024], P(None, None, 'dp', 'tensor'), may hold values from -0.1875 to 0.1875
- w_out: float32 [8, 1024, 1024], P(None, 'tensor', 'dp'), may hold values from -0.375 to 0.375
- w_gate_up: float32 [8, 2, 1024, 4096], P(None, None, 'dp', 'tensor'), may hold values from -0.1875 to 0.1875
- w_down: float32 [8, 4096, 1024], P(None, 'tensor', 'dp'), may hold values from -0.1875 to 0.1875
- norm_gains: float32 [2, 1024], P(None, 'dp'), may hold values from 0.1 to 1.9
- pad_row: float32 [1024], P('dp'), may hold values from -6 to 6
- out_grad: bfloat16 [8, 1024, 1024], P(None, ('dp', 'tensor')), may hold values from -6 to 6
Outputs:
- layer_out: bfloat16 [8, 1024, 1024], P(None, ('dp', 'tensor'))
- input_grad: bfloat16 [8, 1024, 1024], P(None, ('dp', 'tensor'))
- grad_qkv: float32 [8, 3, 1024, 1024], P(None, None, 'dp', 'tensor')
- grad_out: float32 [8, 1024, 1024], P(None, 'tensor', 'dp')
- grad_gate_up: float32 [8, 2, 1024, 4096], P(None, None, 'dp', 'tensor')
- grad_down: float32 [8, 4096, 1024], P(None, 'tensor', 'dp')
- grad_gains: float32 [2, 1024], P(None, 'dp')
- grad_pad: float32 [1024], P('dp')
All inputs are finite; a program needn't handle non-finite values. No bound on the sum of `text_mask` on one device may be relied on, other than what follows from the above.
Results may differ from a plain program's by a relative error of at most 0.014.
The roundings to bfloat16 on the way count: a program that leaves them out, or rounds other values in their place, can miss the bound.
Values may be sent and summed in bfloat16 or wider, within the bound.
No kernel may reach another device: no remote copies, remote signals or barrier semaphores. Data moves between devices by JAX's collectives and lax.ppermute only.
A program may use at most 320 MiB of HBM per device.

v0:
```python
import math

import jax
import jax.numpy as jnp
from jax import lax
from jax.sharding import PartitionSpec as P

HEAD = 64


EPS = 1e-05
HIGH = lax.Precision.HIGHEST


def fetch_parts(w_qkv, w_out, w_gate_up, w_down, norm_gains, pad_row):
    local_width = pad_row.shape[0]
    small = jnp.concatenate(
        [norm_gains.reshape(2, 1, local_width), pad_row.reshape(1, 1, local_width)], axis=0
    )
    return (
        w_qkv.astype(jnp.bfloat16),
        w_out.astype(jnp.bfloat16),
        w_gate_up.astype(jnp.bfloat16),
        w_down.astype(jnp.bfloat16),
        small.astype(jnp.bfloat16),
    )


def norm_back(upstream, hval, rstat, gain):
    scaled = upstream * gain
    dgain = jnp.sum(upstream * hval * rstat, axis=(0, 1))
    dhval = rstat * scaled - hval * rstat**3 * jnp.mean(scaled * hval, axis=-1, keepdims=True)
    return (dhval, dgain)


def shards(layer_in, text_mask, w_qkv, w_out, w_gate_up, w_down, norm_gains, pad_row, out_grad):
    parts = fetch_parts(w_qkv, w_out, w_gate_up, w_down, norm_gains, pad_row)
    wqkv_all, wout_all, wgu_all, wdown_all, small = (
        lax.all_gather(parts[0], "dp", axis=2, tiled=True),
        lax.all_gather(parts[1], "dp", axis=2, tiled=True),
        lax.all_gather(parts[2], "dp", axis=2, tiled=True),
        lax.all_gather(parts[3], "dp", axis=2, tiled=True),
        lax.all_gather(parts[4], "dp", axis=2, tiled=True),
    )
    steps, local_frames, width = layer_in.shape
    gain_one = small[0, 0].astype(jnp.float32)
    gain_two = small[1, 0].astype(jnp.float32)
    pad_vec = small[2, 0].astype(jnp.float32)
    maskf = text_mask.astype(jnp.float32)
    first = (jnp.arange(steps) == 0).astype(jnp.float32)
    h0 = (
        layer_in.astype(jnp.float32)
        + first[:, None, None] * (1.0 - maskf)[None, :, None] * pad_vec[None, None, :]
    )
    r1 = lax.rsqrt(jnp.mean(h0 * h0, axis=-1, keepdims=True) + EPS)
    n1 = (h0 * r1 * gain_one).astype(jnp.bfloat16)
    n1_all = lax.all_gather(n1, "tensor", axis=1, tiled=True)
    frames = n1_all.shape[1]
    qkv = jnp.einsum("sfd,sjde->sjfe", n1_all, wqkv_all, preferred_element_type=jnp.float32).astype(
        jnp.bfloat16
    )
    col_width = qkv.shape[-1]
    heads = col_width // HEAD
    scale = 1.0 / math.sqrt(HEAD)
    query = qkv[:, 0].reshape(steps, frames, heads, HEAD)
    keyv = qkv[:, 1].reshape(steps, frames, heads, HEAD)
    value = qkv[:, 2].reshape(steps, frames, heads, HEAD)
    causal = jnp.arange(steps)[:, None] >= jnp.arange(steps)[None, :]

    def score_of(qv, kv):
        raw = jnp.einsum("sfhe,tfhe->fhst", qv, kv, preferred_element_type=jnp.float32) * scale
        return jnp.where(causal, raw, -1e30)

    scores = score_of(query, keyv)
    top = jnp.max(scores, axis=-1, keepdims=True)
    expo = jnp.exp(scores - top)
    total = jnp.sum(expo, axis=-1, keepdims=True)
    lse = top + jnp.log(total)
    probs_low = (expo / total).astype(jnp.bfloat16)
    mixed = jnp.einsum("fhst,tfhe->sfhe", probs_low, value, preferred_element_type=jnp.float32)
    mixed = mixed.reshape(steps, frames, col_width).astype(jnp.bfloat16)
    attn_part = jnp.einsum("sfd,sde->sfe", mixed, wout_all, preferred_element_type=jnp.float32)
    attn = lax.psum_scatter(attn_part, "tensor", scatter_dimension=1, tiled=True)
    h1 = h0 + attn
    r2 = lax.rsqrt(jnp.mean(h1 * h1, axis=-1, keepdims=True) + EPS)
    n2 = (h1 * r2 * gain_two).astype(jnp.bfloat16)
    n2_all = lax.all_gather(n2, "tensor", axis=1, tiled=True)
    gate_up = jnp.einsum("sfd,sjde->sjfe", n2_all, wgu_all, preferred_element_type=jnp.float32)
    gate = gate_up[:, 0]
    upval = gate_up[:, 1]
    sigma = jax.nn.sigmoid(gate)
    silu_val = gate * sigma
    hidden = (silu_val * upval).astype(jnp.bfloat16)
    ff_part = jnp.einsum("sfk,skd->sfd", hidden, wdown_all, preferred_element_type=jnp.float32)
    ffout = lax.psum_scatter(
        ff_part.astype(jnp.bfloat16), "tensor", scatter_dimension=1, tiled=True
    ).astype(jnp.float32)
    layer_out = (h1 + ffout).astype(jnp.bfloat16)
    parts = fetch_parts(w_qkv, w_out, w_gate_up, w_down, norm_gains, pad_row)
    wqkv_all, wout_all, wgu_all, wdown_all, small = (
        lax.all_gather(parts[0], "dp", axis=2, tiled=True),
        lax.all_gather(parts[1], "dp", axis=2, tiled=True),
        lax.all_gather(parts[2], "dp", axis=2, tiled=True),
        lax.all_gather(parts[3], "dp", axis=2, tiled=True),
        lax.all_gather(parts[4], "dp", axis=2, tiled=True),
    )
    grad_all = lax.all_gather(out_grad, "tensor", axis=1, tiled=True)
    d_down = jnp.einsum("sfk,sfd->skd", hidden, grad_all, preferred_element_type=jnp.float32)
    d_hidden = jnp.einsum("sfd,skd->sfk", grad_all, wdown_all, preferred_element_type=jnp.float32)
    d_gate = d_hidden * upval * (sigma * (1.0 + gate * (1.0 - sigma)))
    d_up = d_hidden * silu_val
    d_gu = jnp.stack([d_gate, d_up], axis=1).astype(jnp.bfloat16)
    d_gate_up = jnp.einsum("sfd,sjfe->sjde", n2_all, d_gu, preferred_element_type=jnp.float32)
    dn2_part = jnp.einsum("sjfe,sjde->sfd", d_gu, wgu_all, preferred_element_type=jnp.float32)
    dn2 = lax.psum_scatter(dn2_part, "tensor", scatter_dimension=1, tiled=True)
    dh_norm2, dgain_two = norm_back(dn2, h1, r2, gain_two)
    dh1 = out_grad.astype(jnp.float32) + dh_norm2
    dh1_all = lax.all_gather(dh1.astype(jnp.bfloat16), "tensor", axis=1, tiled=True)
    d_out = jnp.einsum("sfd,sfe->sde", mixed, dh1_all, preferred_element_type=jnp.float32)
    d_mixed = jnp.einsum("sfe,sde->sfd", dh1_all, wout_all, preferred_element_type=jnp.float32)
    d_mixed = d_mixed.astype(jnp.bfloat16).reshape(steps, frames, heads, HEAD)
    probs = jnp.exp(score_of(query, keyv) - lse)
    d_probs = jnp.einsum("sfhe,tfhe->fhst", d_mixed, value, preferred_element_type=jnp.float32)
    d_value = jnp.einsum("fhst,sfhe->tfhe", probs_low, d_mixed, preferred_element_type=jnp.float32)
    d_scores = probs * (d_probs - jnp.sum(probs * d_probs, axis=-1, keepdims=True))
    d_query = (
        jnp.einsum("fhst,tfhe->sfhe", d_scores, keyv.astype(jnp.float32), precision=HIGH) * scale
    )
    d_key = (
        jnp.einsum("fhst,sfhe->tfhe", d_scores, query.astype(jnp.float32), precision=HIGH) * scale
    )
    d_qkv = jnp.stack(
        [
            d_query.reshape(steps, frames, col_width),
            d_key.reshape(steps, frames, col_width),
            d_value.reshape(steps, frames, col_width),
        ],
        axis=1,
    ).astype(jnp.bfloat16)
    d_wqkv = jnp.einsum("sfd,sjfe->sjde", n1_all, d_qkv, preferred_element_type=jnp.float32)
    dn1_part = jnp.einsum("sjfe,sjde->sfd", d_qkv, wqkv_all, preferred_element_type=jnp.float32)
    dn1 = lax.psum_scatter(
        dn1_part.astype(jnp.bfloat16), "tensor", scatter_dimension=1, tiled=True
    ).astype(jnp.float32)
    dh_norm1, dgain_one = norm_back(dn1, h0, r1, gain_one)
    dh0 = dh1 + dh_norm1
    input_grad = dh0.astype(jnp.bfloat16)
    d_pad = jnp.sum(dh0[0] * (1.0 - maskf)[:, None], axis=0)
    small_grad = jnp.stack([dgain_one, dgain_two, d_pad], axis=0).reshape(3, 1, width)
    g_qkv, g_out, g_gate_up, g_down, g_small = (
        lax.psum_scatter(d_wqkv, "dp", scatter_dimension=2, tiled=True),
        lax.psum_scatter(d_out, "dp", scatter_dimension=2, tiled=True),
        lax.psum_scatter(d_gate_up, "dp", scatter_dimension=2, tiled=True),
        lax.psum_scatter(d_down, "dp", scatter_dimension=2, tiled=True),
        lax.psum_scatter(small_grad, "dp", scatter_dimension=2, tiled=True),
    )
    local_width = g_small.shape[2]
    g_small = lax.psum(g_small.reshape(3, local_width), "tensor")
    return (layer_out, input_grad, g_qkv, g_out, g_gate_up, g_down, g_small[0:2], g_small[2])


def solution(mesh):
    placed = (
        P(None, ("dp", "tensor"), None),
        P(("dp", "tensor")),
        P(None, None, "dp", "tensor"),
        P(None, "tensor", "dp"),
        P(None, None, "dp", "tensor"),
        P(None, "tensor", "dp"),
        P(None, "dp"),
        P("dp"),
        P(None, ("dp", "tensor"), None),
    )
    return jax.shard_map(
        shards,
        mesh=mesh,
        in_specs=placed,
        out_specs=(
            P(None, ("dp", "tensor"), None),
            P(None, ("dp", "tensor"), None),
            P(None, None, "dp", "tensor"),
            P(None, "tensor", "dp"),
            P(None, None, "dp", "tensor"),
            P(None, "tensor", "dp"),
            P(None, "dp"),
            P("dp"),
        ),
        check_vma=False,
    )
```

profile of v0, /device:TPU:0, one launch (start us, length us, event | category | flops | bytes accessed | tf_op | source)
XLA Modules:
  0.0 1783.5 jit_solution(14408283715642600926)
XLA Ops:
  8.6 10.4 all_gather.31
  27.7 41.7 %all-gather.9.cloned.1.call-done = bf16[8,128,1024]{2,1,0:T(8,128)(2,1)} async-done(((bf16[8,32,1024]{2,1,0:T(8,128)(2,1)}), bf16[8,128,1024]{2,1,0:T(8,128)(2,1)}) %all-gather.9.cloned.1.call-update) | async-done | bytes 2097168 | tf_op jit(solution)/shard_map/all_gather | solution.py:57
  69.3 73.3 %all-gather.11.cloned.1.call-done = bf16[8,3,1024,256]{3,2,1,0:T(8,128)(2,1)} async-done(((bf16[8,3,128,256]{3,2,1,0:T(8,128)(2,1)}), bf16[8,3,1024,256]{3,2,1,0:T(8,128)(2,1)}) %all-gather.11.cloned.1.call-update) | async-done | bytes 12582928 | tf_op jit(solution)/shard_map/all_gather | solution.py:39
  142.6 7.1 fusion.18
  165.2 17.3 all-gather.13.cloned.1.call-done
  182.5 5.0 fusion.43
  187.5 76.9 %reduce-scatter.12.cloned.1.call-done = f32[8,32,1024]{2,1,0:T(8,128)} async-done(((f32[8,128,1024]{2,1,0:T(8,128)}), f32[8,32,1024]{2,1,0:T(8,128)}) %reduce-scatter.12.cloned.1.call-update) | async-done | bytes 1048592 | tf_op jit(solution)/shard_map/reduce_scatter | solution.py:83
  267.7 6.1 convert_element_type.115
  278.7 34.7 %all-gather.15.cloned.1.call-done = bf16[8,128,1024]{2,1,0:T(8,128)(2,1)} async-done(((bf16[8,32,1024]{2,1,0:T(8,128)(2,1)}), bf16[8,128,1024]{2,1,0:T(8,128)(2,1)}) %all-gather.15.cloned.1.call-update) | async-done | bytes 2097168 | tf_op jit(solution)/shard_map/all_gather | solution.py:87
  313.4 161.8 %all-gather.17.cloned.1.call-done = bf16[8,2,1024,1024]{3,2,1,0:T(8,128)(2,1)} async-done(((bf16[8,2,128,1024]{3,2,1,0:T(8,128)(2,1)}), bf16[8,2,1024,1024]{3,2,1,0:T(8,128)(2,1)}) %all-gather.17.cloned.1.call-update) | async-done | bytes 33554448 | tf_op jit(solution)/shard_map/all_gather | solution.py:41
  475.3 19.7 %convolution_bitcast_fusion.2 = f32[8,2,128,1024]{3,2,1,0:T(8,128)} fusion(bf16[8,2,1024,1024]{3,2,1,0:T(8,128)(2,1)} %all-gather.17.cloned.1.call-done, bf16[8,128,1024]{2,1,0:T(8,128)(2,1)} %all-gather.15.cloned.1.call-done), kind=kOutput, calls=%fused_computation.14 | convolution fusion | flops 4294967296 | bytes 44040192 | tf_op jit(solution)/shard_map/sfd,sjde->sjfe/dot_general | solution.py:88
  494.9 27.6 %all-gather.21.cloned.1.call-done = bf16[8,128,1024]{2,1,0:T(8,128)(2,1)} async-done(((bf16[8,32,1024]{2,1,0:T(8,128)(2,1)}), bf16[8,128,1024]{2,1,0:T(8,128)(2,1)}) %all-gather.21.cloned.1.call-update) | async-done | bytes 2097168 | tf_op jit(solution)/shard_map/all_gather | solution.py:107
  522.5 94.3 %all-gather.19.cloned.1.call-done = bf16[8,1024,1024]{2,1,0:T(8,128)(2,1)} async-done(((bf16[8,1024,128]{2,1,0:T(8,128)(2,1)}), bf16[8,1024,1024]{2,1,0:T(8,128)(2,1)}) %all-gather.19.cloned.1.call-update) | async-done | bytes 16777232 | tf_op jit(solution)/shard_map/all_gather | solution.py:42
  616.8 13.6 fusion.13
  630.5 18.4 %fusion.4 = f32[8,128,1024]{2,1,0:T(8,128)} fusion(bf16[8,2,1024,1024]{3,2,1,0:T(8,128)(2,1)} %all-gather.17.cloned.1.call-done, bf16[8,1,128,1024]{3,2,0,1:T(8,128)(2,1)} %get-tuple-element.41, bf16[8,1,128,1024]{3,2,0,1:T(8,128)(2,1)} %get-tuple-element.40), kind=kOutput, calls=%fused_computation.15 | convolution fusion | flops 4297064448 | bytes 41943040 | tf_op jit(solution)/shard_map/sjfe,sjde->sfd/dot_general | solution.py:114
  648.9 76.9 %reduce-scatter.16.cloned.1.call-done = f32[8,32,1024]{2,1,0:T(8,128)} async-done(((f32[8,128,1024]{2,1,0:T(8,128)}), f32[8,32,1024]{2,1,0:T(8,128)}) %reduce-scatter.16.cloned.1.call-update) | async-done | bytes 1048592 | tf_op jit(solution)/shard_map/reduce_scatter | solution.py:115
  729.9 45.0 %all-gather.23.cloned.1.call-done = bf16[8,128,1024]{2,1,0:T(8,128)(2,1)} async-done(((bf16[8,32,1024]{2,1,0:T(8,128)(2,1)}), bf16[8,128,1024]{2,1,0:T(8,128)(2,1)}) %all-gather.23.cloned.1.call-update) | async-done | bytes 2097168 | tf_op jit(solution)/shard_map/all_gather | solution.py:118
  775.0 5.1 convolution_convert_fusion.3
  808.9 10.1 bitcast_convert_fusion
  820.6 9.9 convolution_convert_fusion
  830.5 31.2 %reduce-scatter.18.cloned.1.call-done = bf16[8,32,1024]{2,1,0:T(8,128)(2,1)} async-done(((bf16[8,128,1024]{2,1,0:T(8,128)(2,1)}), bf16[8,32,1024]{2,1,0:T(8,128)(2,1)}) %reduce-scatter.18.cloned.1.call-update) | async-done | bytes 524304 | tf_op jit(solution)/shard_map/reduce_scatter | solution.py:142
  863.4 43.8 %reduce-scatter.14.cloned.1.call-done = bf16[8,32,1024]{2,1,0:T(8,128)(2,1)} async-done(((bf16[8,128,1024]{2,1,0:T(8,128)(2,1)}), bf16[8,32,1024]{2,1,0:T(8,128)(2,1)}) %reduce-scatter.14.cloned.1.call-update) | async-done | bytes 524304 | tf_op jit(solution)/shard_map/reduce_scatter | solution.py:95
  911.9 14.1 convolution_bitcast_fusion.1
  926.4 26.0 %convolution_bitcast_fusion = f32[8,2,1024,1024]{2,3,1,0:T(8,128)} fusion(bf16[8,128,1024]{2,1,0:T(8,128)(2,1)} %all-gather.15.cloned.1.call-done, bf16[8,1,128,1024]{3,2,0,1:T(8,128)(2,1)} %get-tuple-element.41, bf16[8,1,128,1024]{3,2,0,1:T(8,128)(2,1)} %get-tuple-element.40), kind=kOutput, calls=%fused_computation.2 | convolution fusion | flops 4297064448 | bytes 73400320 | tf_op jit(solution)/shard_map/sfd,sjfe->sjde/dot_general | solution.py:113
  953.4 8.8 fusion.44
  962.2 21.7 %fusion.45 = f32[8,1024,1024]{2,1,0:T(8,128)} fusion(bf16[8,128,1024]{2,1,0:T(8,128)(2,1)S(1)} %copy-done, bf16[8,128,1024]{2,1,0:T(8,128)(2,1)} %all-gather.21.cloned.1.call-done), kind=kOutput, calls=%fused_computation.92 | convolution fusion | flops 2147483648 | bytes 37748736 | tf_op jit(solution)/shard_map/sfk,sfd->skd/dot_general | solution.py:108
  984.9 9.9 psum.7
  995.9 108.9 %reduce-scatter.20.cloned.1.call-done = f32[8,3,128,256]{2,3,1,0:T(8,128)} async-done(((f32[8,3,1024,256]{2,3,1,0:T(8,128)}), f32[8,3,128,256]{2,3,1,0:T(8,128)}) %reduce-scatter.20.cloned.1.call-update) | async-done | bytes 3145744 | tf_op jit(solution)/shard_map/reduce_scatter | solution.py:151
  1108.4 383.6 %reduce-scatter.24.cloned.1.call-done = f32[8,2,128,1024]{2,3,1,0:T(8,128)} async-done(((f32[8,2,1024,1024]{2,3,1,0:T(8,128)}), f32[8,2,128,1024]{2,3,1,0:T(8,128)}) %reduce-scatter.24.cloned.1.call-update) | async-done | bytes 8388624 | tf_op jit(solution)/shard_map/reduce_scatter | solution.py:153
  1492.0 9.1 copy.95
  1501.2 66.1 %reduce-scatter.22.cloned.1.call-done = f32[8,256,128]{2,1,0:T(8,128)} async-done(((f32[8,256,1024]{2,1,0:T(8,128)}), f32[8,256,128]{2,1,0:T(8,128)}) %reduce-scatter.22.cloned.1.call-update) | async-done | bytes 1048592 | tf_op jit(solution)/shard_map/reduce_scatter | solution.py:152
  1567.2 209.3 %reduce-scatter.26.cloned.1.call-done = f32[8,1024,128]{2,1,0:T(8,128)} async-done(((f32[8,1024,1024]{2,1,0:T(8,128)}), f32[8,1024,128]{2,1,0:T(8,128)}) %reduce-scatter.26.cloned.1.call-update) | async-done | bytes 4194320 | tf_op jit(solution)/shard_map/reduce_scatter | solution.py:154
  (127 shorter events, 81.5 us)
Async XLA Ops:
  7.2 62.2 %all-gather.9.cloned.1.call-start = ((), (), s32[]{:S(2)}) async-start(), calls=%async_computation.9 | async-start | bytes 2621440 | tf_op jit(solution)/shard_map/all_gather | solution.py:57
  23.2 3.5 copy-start.18
  23.2 119.4 %all-gather.11.cloned.1.call-start = ((), (), s32[]{:S(2)}) async-start(), calls=%async_computation.10 | async-start | bytes 14155776 | tf_op jit(solution)/shard_map/all_gather | solution.py:39
  26.7 155.8 %all-gather.13.cloned.1.call-start = ((), (), s32[]{:S(2)}) async-start(), calls=%async_computation.11 | async-start | bytes 4718592 | tf_op jit(solution)/shard_map/all_gather | solution.py:40
  27.6 236.8 %reduce-scatter.12.cloned.1.call-start = ((), (), s32[]{:S(2)}) async-start(), calls=%async_computation.12 | async-start | bytes 5242880 | tf_op jit(solution)/shard_map/reduce_scatter | solution.py:83
  154.5 5.0 copy-start.1
  159.6 3.4 copy-start.13
  159.6 1.6 copy-start.8
  165.2 22.3 %copy-start.6 = (bf16[8,128,4,64]{1,3,2,0:T(8,128)(2,1)}, bf16[8,128,4,64]{1,3,2,0:T(8,128)(2,1)S(1)}, u32[]{:S(2)}) copy-start(bf16[8,128,4,64]{1,3,2,0:T(8,128)(2,1)S(1)} %copy.74) | copy-start | bytes 1572868
  187.5 126.0 %all-gather.15.cloned.1.call-start = ((), (), s32[]{:S(2)}) async-start(), calls=%async_computation.13 | async-start | bytes 2621440 | tf_op jit(solution)/shard_map/all_gather | solution.py:87
  267.1 208.1 %all-gather.17.cloned.1.call-start = ((), (), s32[]{:S(2)}) async-start(), calls=%async_computation.14 | async-start | bytes 37748736 | tf_op jit(solution)/shard_map/all_gather | solution.py:41
  273.7 248.8 %all-gather.21.cloned.1.call-start = ((), (), s32[]{:S(2)}) async-start(), calls=%async_computation.17 | async-start | bytes 2621440 | tf_op jit(solution)/shard_map/all_gather | solution.py:107
  274.5 342.3 %all-gather.19.cloned.1.call-start = ((), (), s32[]{:S(2)}) async-start(), calls=%async_computation.15 | async-start | bytes 18874368 | tf_op jit(solution)/shard_map/all_gather | solution.py:42
  278.7 447.1 %reduce-scatter.16.cloned.1.call-start = ((), (), s32[]{:S(2)}) async-start(), calls=%async_computation.18 | async-start | bytes 5242880 | tf_op jit(solution)/shard_map/reduce_scatter | solution.py:115
  648.9 126.1 %all-gather.23.cloned.1.call-start = ((), (), s32[]{:S(2)}) async-start(), calls=%async_computation.19 | async-start | bytes 2621440 | tf_op jit(solution)/shard_map/all_gather | solution.py:118
  725.8 1.6 copy-start.4
  725.8 1.7 copy-start.5
  728.6 133.0 %reduce-scatter.18.cloned.1.call-start = ((), (), s32[]{:S(2)}) async-start(), calls=%async_computation.20 | async-start | bytes 2621440 | tf_op jit(solution)/shard_map/reduce_scatter | solution.py:142
  785.5 3.2 copy-start.9
  785.5 3.2 copy-start.12
  789.9 3.2 copy-start.3
  796.4 5.2 copy-start.11
  799.4 5.3 copy-start.10
  803.4 5.5 copy-start.14
  804.8 3.3 copy-start.15
  819.0 1.6 copy-start
  819.0 88.2 %reduce-scatter.14.cloned.1.call-start = ((), (), s32[]{:S(2)}) async-start(), calls=%async_computation.16 | async-start | bytes 2621440 | tf_op jit(solution)/shard_map/reduce_scatter | solution.py:95
  830.4 153.6 %reduce-scatter.28.cloned.1.call-start = ((), (), s32[]{:S(2)}) async-start(), calls=%async_computation.25 | async-start | bytes 589824
  911.9 192.9 %reduce-scatter.20.cloned.1.call-start = ((), (), s32[]{:S(2)}) async-start(), calls=%async_computation.21 | async-start | bytes 28311552 | tf_op jit(solution)/shard_map/reduce_scatter | solution.py:151
  926.1 565.9 %reduce-scatter.24.cloned.1.call-start = ((), (), s32[]{:S(2)}) async-start(), calls=%async_computation.23 | async-start | bytes 75497472 | tf_op jit(solution)/shard_map/reduce_scatter | solution.py:153
  952.4 614.9 %reduce-scatter.22.cloned.1.call-start = ((), (), s32[]{:S(2)}) async-start(), calls=%async_computation.22 | async-start | bytes 9437184 | tf_op jit(solution)/shard_map/reduce_scatter | solution.py:152
  962.2 814.3 %reduce-scatter.26.cloned.1.call-start = ((), (), s32[]{:S(2)}) async-start(), calls=%async_computation.24 | async-start | bytes 37748736 | tf_op jit(solution)/shard_map/reduce_scatter | solution.py:154
  (4 other events, 3.8 us)
Sparse Core Ops, SparseCore 0:
  23.4 45.9 all-gather.8
  71.8 70.7 all-gather.10
  145.1 37.3 all-gather.12
  187.6 76.7 reduce-scatter.11
  267.3 46.1 all-gather.14
  315.8 159.4 all-gather.16
  476.8 45.6 all-gather.20
  525.0 91.8 all-gather.18
  649.0 76.7 reduce-scatter.15
  728.7 46.1 all-gather.22
  819.1 42.5 reduce-scatter.17
  864.4 42.8 reduce-scatter.13
  912.0 33.3 reduce-scatter.27
  948.8 155.9 reduce-scatter.19
  1108.2 383.7 reduce-scatter.23
  1495.9 71.2 reduce-scatter.21
  1571.2 205.2 reduce-scatter.25
where the time goes:
time: 1790 us; the launch traced here: 1780 us
  waiting for transfers between devices  1490 us (83%)
  matrix products  174 us (10%)
  local copies, waits for them, and re-layouts  46.5 us (3%)
  other arithmetic  32.6 us (2%)
  blocking collectives  20.3 us (1%)
    reduce_scatter x1, waiting for transfers between devices, shards(): lax.psum_scatter(d_gate_up, 'dp', scatter_dimension=2, tiled=True)  384 us
    reduce_scatter x1, waiting for transfers between devices, shards(): lax.psum_scatter(d_down, 'dp', scatter_dimension=2, tiled=True)  209 us
    all_gather x1, waiting for transfers between devices, shards(): lax.all_gather(parts[2], 'dp', axis=2, tiled=True)  162 us
    reduce_scatter x1, waiting for transfers between devices, shards(): lax.psum_scatter(d_wqkv, 'dp', scatter_dimension=2, tiled=True)  109 us
    all_gather x1, waiting for transfers between devices, shards(): lax.all_gather(parts[3], 'dp', axis=2, tiled=True)  94.3 us
    reduce_scatter x1, waiting for transfers between devices, shards(): lax.psum_scatter(attn_part, 'tensor', scatter_dimension=1, tiled=True)  76.9 us
    reduce_scatter x1, waiting for transfers between devices, shards(): dn2 = lax.psum_scatter(dn2_part, 'tensor', scatter_dimension=1, tiled=True)  76.9 us
    all_gather x1, waiting for transfers between devices, shards(): lax.all_gather(parts[0], 'dp', axis=2, tiled=True)  73.3 us
  transfers between devices with their start and end apart: 17, of which 16 were waited for; matrix products, arithmetic and copies ran while one was open for 9% of the time, Pallas kernels for 0%

commit v1 on v0

v1 whole, which is shorter than its diff:
```python
import math

import jax
import jax.numpy as jnp
import numpy as np
from jax import lax
from jax.sharding import Mesh
from jax.sharding import PartitionSpec as P

HEAD = 64
EPS = 1e-05
HIGH = lax.Precision.HIGHEST
BF = jnp.bfloat16
F32 = jnp.float32
SWAP = ((0, 1), (1, 0))


def norm_back(upstream, hval, rstat, gain):
    scaled = upstream * gain
    dgain = jnp.sum(upstream * hval * rstat, axis=(0, 1))
    dhval = rstat * scaled - hval * rstat**3 * jnp.mean(scaled * hval, axis=-1, keepdims=True)
    return (dhval, dgain)


def half(array, axis, which):
    size = array.shape[axis] // 2
    return lax.dynamic_slice_in_dim(array, which * size, size, axis)


def ordered(core, own, other, axis):
    is_first = core == 0
    return jnp.concatenate(
        [jnp.where(is_first, own, other), jnp.where(is_first, other, own)], axis=axis
    )


def make_shards(tensor_size):
    def around(shift):
        return [(i, (i + shift) % tensor_size) for i in range(tensor_size)]

    def trade(core, weight, split_axis, join_axis):
        mine = half(weight, split_axis, core)
        theirs = half(weight, split_axis, 1 - core)
        got = lax.ppermute(theirs, "core", SWAP)
        return ordered(core, mine, got, join_axis)

    def collect(rows):
        parts = [rows] + [
            lax.ppermute(rows, "tensor", around(k)) for k in range(1, tensor_size)
        ]
        near = jnp.stack(parts, axis=1)
        far = lax.ppermute(near, "core", SWAP)
        whole = jnp.concatenate([near, far], axis=1)
        return whole.reshape(rows.shape[0], -1, rows.shape[2])

    def deal(partial):
        steps, frames, width = partial.shape
        split = partial.reshape(steps, 2, tensor_size, frames // (2 * tensor_size), width)
        got = lax.ppermute(split[:, 1].astype(BF), "core", SWAP)
        chip = split[:, 0].astype(F32) + got.astype(F32)
        total = chip[:, 0]
        for k in range(1, tensor_size):
            total = total + lax.ppermute(chip[:, k].astype(BF), "tensor", around(-k)).astype(F32)
        return total

    def shards(
        layer_in, text_mask, w_qkv, w_out, w_gate_up, w_down, norm_gains, pad_row, out_grad
    ):
        core = lax.axis_index("core")
        steps, local_frames, width = layer_in.shape

        w_attn = jnp.concatenate(
            [w_qkv.astype(BF), jnp.swapaxes(w_out, 1, 2)[:, None].astype(BF)], axis=1
        )
        w_attn = lax.all_gather(trade(core, w_attn, 3, 2), "xy", axis=2, tiled=True)
        small = jnp.concatenate([norm_gains, pad_row[None]], axis=0).astype(BF)
        small = lax.all_gather(small, ("xy", "core"), axis=1, tiled=True).astype(F32)
        wgu = lax.all_gather(trade(core, w_gate_up.astype(BF), 3, 2), "xy", axis=2, tiled=True)
        wdown = lax.all_gather(trade(core, w_down.astype(BF), 1, 2), "xy", axis=2, tiled=True)

        gain_one, gain_two, pad_vec = small[0], small[1], small[2]
        maskf = text_mask.astype(F32)
        first = (jnp.arange(steps) == 0).astype(F32)
        h0 = (
            layer_in.astype(F32)
            + first[:, None, None] * (1.0 - maskf)[None, :, None] * pad_vec[None, None, :]
        )
        r1 = lax.rsqrt(jnp.mean(h0 * h0, axis=-1, keepdims=True) + EPS)
        n1 = (h0 * r1 * gain_one).astype(BF)
        n1_all = collect(n1)
        grad_all = collect(out_grad)
        frames = n1_all.shape[1]
        wqkv, wout_t = w_attn[:, :3], w_attn[:, 3]
        qkv = jnp.einsum("sfd,sjde->sjfe", n1_all, wqkv, preferred_element_type=F32).astype(BF)
        col_width = qkv.shape[-1]
        heads = col_width // HEAD
        scale = 1.0 / math.sqrt(HEAD)
        query = qkv[:, 0].reshape(steps, frames, heads, HEAD)
        keyv = qkv[:, 1].reshape(steps, frames, heads, HEAD)
        value = qkv[:, 2].reshape(steps, frames, heads, HEAD)
        causal = jnp.arange(steps)[:, None] >= jnp.arange(steps)[None, :]

        def score_of(qv, kv):
            raw = jnp.einsum("sfhe,tfhe->fhst", qv, kv, preferred_element_type=F32) * scale
            return jnp.where(causal, raw, -1e30)

        scores = score_of(query, keyv)
        top = jnp.max(scores, axis=-1, keepdims=True)
        expo = jnp.exp(scores - top)
        total = jnp.sum(expo, axis=-1, keepdims=True)
        lse = top + jnp.log(total)
        probs_low = (expo / total).astype(BF)
        mixed = jnp.einsum("fhst,tfhe->sfhe", probs_low, value, preferred_element_type=F32)
        mixed = mixed.reshape(steps, frames, col_width).astype(BF)
        attn = deal(jnp.einsum("sfd,sed->sfe", mixed, wout_t, preferred_element_type=F32))
        h1 = h0 + attn
        r2 = lax.rsqrt(jnp.mean(h1 * h1, axis=-1, keepdims=True) + EPS)
        n2 = (h1 * r2 * gain_two).astype(BF)
        n2_all = collect(n2)
        gate_up = jnp.einsum("sfd,sjde->sjfe", n2_all, wgu, preferred_element_type=F32)
        gate = gate_up[:, 0]
        upval = gate_up[:, 1]
        sigma = jax.nn.sigmoid(gate)
        silu_val = gate * sigma
        hidden = (silu_val * upval).astype(BF)
        d_down = jnp.einsum("sfk,sfd->skd", hidden, grad_all, preferred_element_type=F32)
        r_down = lax.psum_scatter(d_down.astype(BF), "xy", scatter_dimension=2, tiled=True)
        d_hidden = jnp.einsum("sfd,skd->sfk", grad_all, wdown, preferred_element_type=F32)
        d_gate = d_hidden * upval * (sigma * (1.0 + gate * (1.0 - sigma)))
        d_up = d_hidden * silu_val
        d_gu = jnp.stack([d_gate, d_up], axis=1).astype(BF)
        d_gate_up = jnp.einsum("sfd,sjfe->sjde", n2_all, d_gu, preferred_element_type=F32)
        r_gate_up = lax.psum_scatter(d_gate_up.astype(BF), "xy", scatter_dimension=2, tiled=True)
        dn2 = deal(jnp.einsum("sjfe,sjde->sfd", d_gu, wgu, preferred_element_type=F32))
        dh_norm2, dgain_two = norm_back(dn2, h1, r2, gain_two)
        dh1 = out_grad.astype(F32) + dh_norm2
        dh1_all = collect(dh1.astype(BF))
        ffout = deal(jnp.einsum("sfk,skd->sfd", hidden, wdown, preferred_element_type=F32))
        layer_out = (h1 + ffout).astype(BF)
        d_out_t = jnp.einsum("sfe,sfd->sed", dh1_all, mixed, preferred_element_type=F32)
        d_mixed = jnp.einsum("sfe,sed->sfd", dh1_all, wout_t, preferred_element_type=F32)
        d_mixed = d_mixed.astype(BF).reshape(steps, frames, heads, HEAD)
        probs = jnp.exp(score_of(query, keyv) - lse)
        d_probs = jnp.einsum("sfhe,tfhe->fhst", d_mixed, value, preferred_element_type=F32)
        d_value = jnp.einsum("fhst,sfhe->tfhe", probs_low, d_mixed, preferred_element_type=F32)
        d_scores = probs * (d_probs - jnp.sum(probs * d_probs, axis=-1, keepdims=True))
        d_query = (
            jnp.einsum("fhst,tfhe->sfhe", d_scores, keyv.astype(F32), precision=HIGH) * scale
        )
        d_key = (
            jnp.einsum("fhst,sfhe->tfhe", d_scores, query.astype(F32), precision=HIGH) * scale
        )
        d_qkv = jnp.stack(
            [
                d_query.reshape(steps, frames, col_width),
                d_key.reshape(steps, frames, col_width),
                d_value.reshape(steps, frames, col_width),
            ],
            axis=1,
        ).astype(BF)
        d_wqkv = jnp.einsum("sfd,sjfe->sjde", n1_all, d_qkv, preferred_element_type=F32)
        d_attn = jnp.concatenate([d_wqkv.astype(BF), d_out_t[:, None].astype(BF)], axis=1)
        r_attn = lax.psum_scatter(d_attn, "xy", scatter_dimension=2, tiled=True)
        dn1 = deal(jnp.einsum("sjfe,sjde->sfd", d_qkv, wqkv, preferred_element_type=F32))
        dh_norm1, dgain_one = norm_back(dn1, h0, r1, gain_one)
        dh0 = dh1 + dh_norm1
        input_grad = dh0.astype(BF)
        d_pad = jnp.sum(dh0[0] * (1.0 - maskf)[:, None], axis=0)
        small_grad = jnp.stack([dgain_one, dgain_two, d_pad], axis=0)
        small_grad = lax.psum(small_grad, ("xy", "core", "tensor"))
        place = lax.axis_index("xy") * 2 + core
        g_small = lax.dynamic_slice_in_dim(
            small_grad, place * pad_row.shape[0], pad_row.shape[0], 1
        )

        def settle(reduced, split_axis, join_axis):
            return trade(core, reduced, split_axis, join_axis).astype(F32)

        g_down = settle(r_down, 2, 1)
        g_gate_up = settle(r_gate_up, 2, 3)
        g_attn = settle(r_attn, 2, 3)
        g_qkv = g_attn[:, :3]
        g_out = jnp.swapaxes(g_attn[:, 3], 1, 2)
        return (layer_out, input_grad, g_qkv, g_out, g_gate_up, g_down, g_small[0:2], g_small[2])

    return shards


def solution(mesh):
    dp_size, tensor_size = mesh.shape["dp"], mesh.shape["tensor"]
    inner = Mesh(
        np.asarray(mesh.devices).reshape(dp_size // 2, 2, tensor_size), ("xy", "core", "tensor")
    )
    dp = ("xy", "core")
    rows = ("xy", "core", "tensor")
    return jax.shard_map(
        make_shards(tensor_size),
        mesh=inner,
        in_specs=(
            P(None, rows, None),
            P(rows),
            P(None, None, dp, "tensor"),
            P(None, "tensor", dp),
            P(None, None, dp, "tensor"),
            P(None, "tensor", dp),
            P(None, dp),
            P(dp),
            P(None, rows, None),
        ),
        out_specs=(
            P(None, rows, None),
            P(None, rows, None),
            P(None, None, dp, "tensor"),
            P(None, "tensor", dp),
            P(None, None, dp, "tensor"),
            P(None, "tensor", dp),
            P(None, dp),
            P(dp),
        ),
        check_vma=False,
    )
```

time: 1790 us -> 793 us (0.44)
  waiting for transfers between devices: 1490 us -> 371 us
  starting transfers between devices: 1.59 us -> 82 us
  matrix products: 174 us -> 114 us
  local copies, waits for them, and re-layouts: 46.5 us -> 95.4 us
  blocking collectives: 20.3 us -> 50.4 us
  other arithmetic: 32.6 us -> 59.5 us
    reduce_scatter x8 -> x3, waiting for transfers between devices: 997 us -> 30.8 us  [the longest x1 30.7 us: shards(): r_attn = lax.psum_scatter(d_attn, 'xy', scatter_dimension=2, tiled=True)]
    all_gather x8 -> x3, waiting for transfers between devices: 496 us -> 64.5 us  [the longest x1 61.9 us: shards(): lax.all_gather(trade(core, w_down.astype(BF), 1, 2), 'xy', axis=2, tiled=...]
    ppermute x0 -> x38, waiting for transfers between devices: none -> 275 us  [the longest x12 137 us: deal(): lax.ppermute(chip[:, k].astype(BF), 'tensor', around(-k)).astype(F32)]
    ppermute x0 -> x38, starting transfers between devices: none -> 81.6 us  [the longest x12 47.3 us: collect(): lax.ppermute(rows, 'tensor', around(k))]
    dot_general x17, matrix products: 171 us -> 111 us  [the longest x1 15.5 us: shards(): jnp.einsum('sjfe,sjde->sfd', d_gu, wgu, preferred_element_type=F32)]
    psum x1, blocking collectives: 9.91 us -> 39.4 us  [shards(): small_grad = lax.psum(small_grad, ('xy', 'core', 'tensor'))]
    unnamed x42 -> x111, local copies, waits for them, and re-layouts: 18.7 us -> 40.5 us
  transfers between devices with their start and end apart: 17 -> 44, of which waited for: 16 -> 24; matrix products, arithmetic and copies ran while one was open for 9% -> 27% of each run, Pallas kernels for 0% -> 0%
where the time goes in v1:
time: 793 us; the launch traced here: 787 us
  waiting for transfers between devices  371 us (47%)
  matrix products  114 us (14%)
  local copies, waits for them, and re-layouts  95.4 us (12%)
  starting transfers between devices  82 us (10%)
  other arithmetic  59.5 us (8%)
  blocking collectives  50.4 us (6%)
  between operations  15.3 us (2%)
    ppermute x12, waiting for transfers between devices, deal(): lax.ppermute(chip[:, k].astype(BF), 'tensor', around(-k)).astype(F32)  137 us
    ppermute x12, waiting for transfers between devices, collect(): lax.ppermute(rows, 'tensor', around(k))  123 us
    all_gather x1, waiting for transfers between devices, shards(): lax.all_gather(trade(core, w_down.astype(BF), 1, 2), 'xy', axis=2, tiled=...  61.9 us
    ppermute x12, starting transfers between devices, collect(): lax.ppermute(rows, 'tensor', around(k))  47.3 us
    unnamed x111, local copies, waits for them, and re-layouts  40.5 us
    psum x1, blocking collectives, shards(): small_grad = lax.psum(small_grad, ('xy', 'core', 'tensor'))  39.4 us
    ppermute x12, starting transfers between devices, deal(): lax.ppermute(chip[:, k].astype(BF), 'tensor', around(-k)).astype(F32)  31.5 us
    reduce_scatter x1, waiting for transfers between devices, shards(): r_attn = lax.psum_scatter(d_attn, 'xy', scatter_dimension=2, tiled=True)  30.7 us
  transfers between devices with their start and end apart: 44, of which 24 were waited for; matrix products, arithmetic and copies ran while one was open for 27% of the time, Pallas kernels for 0%

profile of v1, /device:TPU:0, one launch (start us, length us, event | category | flops | bytes accessed | tf_op | source)
XLA Modules:
  0.0 787.1 jit_solution(1994732268361771725)
XLA Ops:
  16.3 7.3 copy.66
  37.0 11.0 %all_gather.12 = bf16[3,1024]{1,0:T(4,128)(2,1)S(1)} all-gather(bf16[3,128]{1,0:T(4,128)(2,1)S(1)} %pad_maximum_fusion.13), channel_id=1, replica_groups=mesh['xy'=4,'core'=2,'tensor'=4] {'xy','core'}, dimensions={1}, use_global_device_ids=true | all-gather | bytes 6912 | tf_op jit(solution)/shard_map/all_gather | solution.py:77
  58.8 8.5 %collective-permute-done.1 = bf16[8,32,1024]{2,1,0:T(8,128)(2,1)S(1)} collective-permute-done((bf16[8,32,1024]{2,1,0:T(8,128)(2,1)S(1)}, bf16[8,32,1024]{2,1,0:T(8,128)(2,1)S(1)}, u32[]{:S(2)}, u32[]{:S(2)}) %collective-permute-start.1) | collective-permute-done | bytes 524320 | tf_op jit(solution)/shard_map/ppermute | solution.py:49
  67.4 21.9 %collective-permute-done.2 = bf16[8,32,1024]{2,1,0:T(8,128)(2,1)S(1)} collective-permute-done((bf16[8,32,1024]{2,1,0:T(8,128)(2,1)S(1)}, bf16[8,32,1024]{2,1,0:T(8,128)(2,1)S(1)}, u32[]{:S(2)}, u32[]{:S(2)}) %collective-permute-start.2) | collective-permute-done | bytes 524320 | tf_op jit(solution)/shard_map/ppermute | solution.py:49
  106.3 5.8 fusion.19
  130.6 10.8 %collective-permute-start.19 = (bf16[8,32,1024]{2,1,0:T(8,128)(2,1)S(1)}, bf16[8,32,1024]{2,1,0:T(8,128)(2,1)S(1)}, u32[]{:S(2)}, u32[]{:S(2)}) collective-permute-start(bf16[8,32,1024]{2,1,0:T(8,128)(2,1)S(1)} %copy-done.19), channel_id=1, source_target_pairs={{0,1},{1,2},{2,3},{3,0},{4,5},{5,6},{6,7},{7,4},{8,9},{9,10},{10,1... | collective-permute-start | bytes 1572872 | tf_op jit(solution)/shard_map/ppermute | solution.py:49
  147.8 6.9 collective-permute-done.19
  157.5 19.7 %collective-permute-done.20 = bf16[8,32,1024]{2,1,0:T(8,128)(2,1)S(1)} collective-permute-done((bf16[8,32,1024]{2,1,0:T(8,128)(2,1)S(1)}, bf16[8,32,1024]{2,1,0:T(8,128)(2,1)S(1)}, u32[]{:S(2)}, u32[]{:S(2)}) %collective-permute-start.20) | collective-permute-done | bytes 524320 | tf_op jit(solution)/shard_map/ppermute | solution.py:49
  177.6 10.9 %collective-permute-done.8 = bf16[8,32,1024]{2,1,0:T(8,128)(2,1)S(1)} collective-permute-done((bf16[8,32,1024]{2,1,0:T(8,128)(2,1)S(1)}, bf16[8,32,1024]{2,1,0:T(8,128)(2,1)S(1)}, u32[]{:S(2)}, u32[]{:S(2)}) %collective-permute-start.8) | collective-permute-done | bytes 524320 | tf_op jit(solution)/shard_map/ppermute | solution.py:63
  188.5 33.6 %collective-permute-done.7 = bf16[8,32,1024]{2,1,0:T(8,128)(2,1)S(1)} collective-permute-done((bf16[8,32,1024]{2,1,0:T(8,128)(2,1)S(1)}, bf16[8,32,1024]{2,1,0:T(8,128)(2,1)S(1)}, u32[]{:S(2)}, u32[]{:S(2)}) %collective-permute-start.7) | collective-permute-done | bytes 524320 | tf_op jit(solution)/shard_map/ppermute | solution.py:63
  222.8 11.8 %collective-permute-start.10 = (bf16[8,32,1024]{2,1,0:T(8,128)(2,1)S(1)}, bf16[8,32,1024]{2,1,0:T(8,128)(2,1)S(1)}, u32[]{:S(2)}, u32[]{:S(2)}) collective-permute-start(bf16[8,32,1024]{2,1,0:T(8,128)(2,1)S(1)} %get-tuple-element.41), channel_id=1, source_target_pairs={{0,1},{1,2},{2,3},{3,0},{4,5},{5,6},{6,7},{7,4},{8,9},{9,10},{10,1... | collective-permute-start | bytes 1572872 | tf_op jit(solution)/shard_map/ppermute | solution.py:49
  237.2 11.5 %collective-permute-done.10 = bf16[8,32,1024]{2,1,0:T(8,128)(2,1)S(1)} collective-permute-done((bf16[8,32,1024]{2,1,0:T(8,128)(2,1)S(1)}, bf16[8,32,1024]{2,1,0:T(8,128)(2,1)S(1)}, u32[]{:S(2)}, u32[]{:S(2)}) %collective-permute-start.10) | collective-permute-done | bytes 524320 | tf_op jit(solution)/shard_map/ppermute | solution.py:49
  248.7 21.7 %collective-permute-done.11 = bf16[8,32,1024]{2,1,0:T(8,128)(2,1)S(1)} collective-permute-done((bf16[8,32,1024]{2,1,0:T(8,128)(2,1)S(1)}, bf16[8,32,1024]{2,1,0:T(8,128)(2,1)S(1)}, u32[]{:S(2)}, u32[]{:S(2)}) %collective-permute-start.11) | collective-permute-done | bytes 524320 | tf_op jit(solution)/shard_map/ppermute | solution.py:49
  277.7 15.5 %convolution_bitcast_fusion = f32[8,2,256,512]{2,3,1,0:T(8,128)} fusion(bf16[8,2,1024,512]{2,3,1,0:T(8,128)(2,1)} %all-gather.6.cloned.1.call-done, bf16[8,256,1024,1]{2,1,3,0:T(8,128)(2,1)} %bitcast.263), kind=kOutput, calls=%fused_computation.31 | convolution fusion | flops 4294967296 | bytes 29360128 | tf_op jit(solution)/shard_map/sfd,sjde->sjfe/dot_general | solution.py:120
  293.2 61.9 %all-gather.8.cloned.1.call-done = bf16[8,512,1024]{2,1,0:T(8,128)(2,1)} async-done(((bf16[8,512,256]{2,1,0:T(8,128)(2,1)}), bf16[8,512,1024]{2,1,0:T(8,128)(2,1)}) %all-gather.8.cloned.1.call-update) | async-done | bytes 8388624 | tf_op jit(solution)/shard_map/all_gather | solution.py:79
  355.1 13.8 %fusion.15 = (bf16[8,1,256,512]{2,3,0,1:T(8,128)(2,1)}, bf16[8,1,256,512]{2,3,0,1:T(8,128)(2,1)}, bf16[8,256,512]{1,2,0:T(8,128)(2,1)}) fusion(f32[8,2,256,512]{2,3,1,0:T(8,128)} %convolution_bitcast_fusion, bf16[8,256,1024]{2,1,0:T(8,128)(2,1)} %bitcast.265, bf16[8,512,1024]{2,1,0:T(8,128)(2,1)} %all-gather.8.cloned.1.call-done), kind=kOutput, calls=%fused_computation.63 | convolution fusion | flops 2163212288 | bytes 27262976 | tf_op jit(solution)/shard_map/sfd,skd->sfk/dot_general | solution.py:128
  368.9 7.7 convolution_convert_fusion
  376.7 11.2 %convert_bitcast_fusion = bf16[8,2,1024,512]{2,3,1,0:T(8,128)(2,1)} fusion(bf16[8,256,1024,1]{2,1,3,0:T(8,128)(2,1)} %bitcast.264, bf16[8,1,256,512]{2,3,0,1:T(8,128)(2,1)} %get-tuple-element.49, bf16[8,1,256,512]{2,3,0,1:T(8,128)(2,1)} %get-tuple-element.48), kind=kOutput, calls=%fused_computation.2 | convolution fusion | flops 4305453056 | bytes 25165824 | tf_op jit(solution)/shard_map/sfd,sjfe->sjde/dot_general | solution.py:132
  388.0 15.5 %fusion = f32[8,256,1024,1]{2,1,0,3:T(8,128)} fusion(bf16[8,2,1024,512]{2,3,1,0:T(8,128)(2,1)} %all-gather.6.cloned.1.call-done, bf16[8,1,256,512]{2,3,0,1:T(8,128)(2,1)} %get-tuple-element.49, bf16[8,1,256,512]{2,3,0,1:T(8,128)(2,1)} %get-tuple-element.48), kind=kOutput, calls=%fused_computation | convolution fusion | flops 4297064448 | bytes 29360128 | tf_op jit(solution)/shard_map/sjfe,sjde->sfd/dot_general | solution.py:134
  419.1 11.4 %collective-permute-done.26 = bf16[8,32,1024]{2,1,0:T(8,128)(2,1)S(1)} collective-permute-done((bf16[8,32,1024]{2,1,0:T(8,128)(2,1)S(1)}, bf16[8,32,1024]{2,1,0:T(8,128)(2,1)S(1)}, u32[]{:S(2)}, u32[]{:S(2)}) %collective-permute-start.26) | collective-permute-done | bytes 524320 | tf_op jit(solution)/shard_map/ppermute | solution.py:63
  430.5 21.9 %collective-permute-done.25 = bf16[8,32,1024]{2,1,0:T(8,128)(2,1)S(1)} collective-permute-done((bf16[8,32,1024]{2,1,0:T(8,128)(2,1)S(1)}, bf16[8,32,1024]{2,1,0:T(8,128)(2,1)S(1)}, u32[]{:S(2)}, u32[]{:S(2)}) %collective-permute-start.25) | collective-permute-done | bytes 524320 | tf_op jit(solution)/shard_map/ppermute | solution.py:63
  453.9 11.7 %collective-permute-start.27 = (bf16[8,32,1024]{2,1,0:T(8,128)(2,1)S(1)}, bf16[8,32,1024]{2,1,0:T(8,128)(2,1)S(1)}, u32[]{:S(2)}, u32[]{:S(2)}) collective-permute-start(bf16[8,32,1024]{2,1,0:T(8,128)(2,1)S(1)} %get-tuple-element.34), channel_id=1, source_target_pairs={{0,1},{1,2},{2,3},{3,0},{4,5},{5,6},{6,7},{7,4},{8,9},{9,10},{10,1... | collective-permute-start | bytes 1572872 | tf_op jit(solution)/shard_map/ppermute | solution.py:49
  468.1 11.3 %collective-permute-done.27 = bf16[8,32,1024]{2,1,0:T(8,128)(2,1)S(1)} collective-permute-done((bf16[8,32,1024]{2,1,0:T(8,128)(2,1)S(1)}, bf16[8,32,1024]{2,1,0:T(8,128)(2,1)S(1)}, u32[]{:S(2)}, u32[]{:S(2)}) %collective-permute-start.27) | collective-permute-done | bytes 524320 | tf_op jit(solution)/shard_map/ppermute | solution.py:49
  479.4 21.3 %collective-permute-done.28 = bf16[8,32,1024]{2,1,0:T(8,128)(2,1)S(1)} collective-permute-done((bf16[8,32,1024]{2,1,0:T(8,128)(2,1)S(1)}, bf16[8,32,1024]{2,1,0:T(8,128)(2,1)S(1)}, u32[]{:S(2)}, u32[]{:S(2)}) %collective-permute-start.28) | collective-permute-done | bytes 524320 | tf_op jit(solution)/shard_map/ppermute | solution.py:49
  550.2 5.7 pad_maximum_fusion
  565.5 5.8 fusion.63
  580.9 12.1 %collective-permute-start.34 = (bf16[8,32,1024]{2,1,0:T(8,128)(2,1)S(1)}, bf16[8,32,1024]{2,1,0:T(8,128)(2,1)S(1)}, u32[]{:S(2)}, u32[]{:S(2)}) collective-permute-start(bf16[8,32,1024]{2,1,0:T(8,128)(2,1)S(1)} %get-tuple-element.64), channel_id=1, source_target_pairs={{0,1},{1,2},{2,3},{3,0},{4,5},{5,6},{6,7},{7,4},{8,9},{9,10},{10,1... | collective-permute-start | bytes 1572872 | tf_op jit(solution)/shard_map/ppermute | solution.py:63
  610.6 19.1 %collective-permute-done.33 = bf16[8,32,1024]{2,1,0:T(8,128)(2,1)S(1)} collective-permute-done((bf16[8,32,1024]{2,1,0:T(8,128)(2,1)S(1)}, bf16[8,32,1024]{2,1,0:T(8,128)(2,1)S(1)}, u32[]{:S(2)}, u32[]{:S(2)}) %collective-permute-start.33) | collective-permute-done | bytes 524320 | tf_op jit(solution)/shard_map/ppermute | solution.py:63
  641.0 33.2 %collective-permute-done.17 = bf16[8,32,1024]{2,1,0:T(8,128)(2,1)} collective-permute-done((bf16[8,32,1024]{2,1,0:T(8,128)(2,1)}, bf16[8,32,1024]{2,1,0:T(8,128)(2,1)}, u32[]{:S(2)}, u32[]{:S(2)}) %collective-permute-start.17) | collective-permute-done | bytes 524320 | tf_op jit(solution)/shard_map/ppermute | solution.py:63
  678.4 30.7 %reduce-scatter.4.cloned.1.call-done = bf16[8,4,256,128]{2,3,1,0:T(8,128)(2,1)} async-done(((bf16[8,4,1024,128]{2,3,1,0:T(8,128)(2,1)}), bf16[8,4,256,128]{2,3,1,0:T(8,128)(2,1)}) %reduce-scatter.4.cloned.1.call-update) | async-done | bytes 2097168 | tf_op jit(solution)/shard_map/reduce_scatter | solution.py:163
  711.5 39.4 %psum.7 = f32[3,1024]{1,0:T(4,128)S(1)} all-reduce(f32[3,1024]{1,0:T(4,128)S(1)} %pad_maximum_fusion.12), channel_id=1, replica_groups=mesh['xy'=4,'core'=2,'tensor'=4] {'xy','core','tensor'}, use_global_device_ids=true, to_apply=%region_13.14 | all-reduce | flops 3072 | bytes 24576 | tf_op jit(solution)/shard_map/psum | solution.py:170
  770.8 9.1 %copy.101 = f32[8,2,128,1024]{3,2,1,0:T(8,128)} copy(f32[8,2,128,1024]{2,3,1,0:T(8,128)} %maximum_convert_fusion) | data formatting | bytes 16777216
  (279 shorter events, 231.8 us)
Async XLA Ops:
  7.2 99.2 %all-gather.4.cloned.1.call-start = ((), (), s32[]{:S(2)}) async-start(), calls=%async_computation.3 | async-start | bytes 10485760 | tf_op jit(solution)/shard_map/all_gather | solution.py:75
  16.2 261.5 %all-gather.6.cloned.1.call-start = ((), (), s32[]{:S(2)}) async-start(), calls=%async_computation.4 | async-start | bytes 20971520 | tf_op jit(solution)/shard_map/all_gather | solution.py:78
  36.4 318.8 %all-gather.8.cloned.1.call-start = ((), (), s32[]{:S(2)}) async-start(), calls=%async_computation.5 | async-start | bytes 10485760 | tf_op jit(solution)/shard_map/all_gather | solution.py:79
  52.2 37.1 %collective-permute-start.2 = (bf16[8,32,1024]{2,1,0:T(8,128)(2,1)S(1)}, bf16[8,32,1024]{2,1,0:T(8,128)(2,1)S(1)}, u32[]{:S(2)}, u32[]{:S(2)}) collective-permute-start(bf16[8,32,1024]{2,1,0:T(8,128)(2,1)S(1)} %get-tuple-element.47), channel_id=1, source_target_pairs={{0,2},{1,3},{2,0},{3,1},{4,6},{5,7},{6,4},{7,5},{8,10},{9,11},{10,... | collective-permute-start | bytes 1572872 | tf_op jit(solution)/shard_map/ppermute | solution.py:49
  54.8 34.5 %collective-permute-start.3 = (bf16[8,32,1024]{2,1,0:T(8,128)(2,1)S(1)}, bf16[8,32,1024]{2,1,0:T(8,128)(2,1)S(1)}, u32[]{:S(2)}, u32[]{:S(2)}) collective-permute-start(bf16[8,32,1024]{2,1,0:T(8,128)(2,1)S(1)} %get-tuple-element.47), channel_id=1, source_target_pairs={{0,3},{1,0},{2,1},{3,2},{4,7},{5,4},{6,5},{7,6},{8,11},{9,8},{10,9... | collective-permute-start | bytes 1572872 | tf_op jit(solution)/shard_map/ppermute | solution.py:49
  58.8 30.9 %collective-permute-start.14 = (bf16[8,512,128]{2,1,0:T(8,128)(2,1)S(1)}, bf16[8,512,128]{2,1,0:T(8,128)(2,1)S(1)}, u32[]{:S(2)}, u32[]{:S(2)}) collective-permute-start(bf16[8,512,128]{2,1,0:T(8,128)(2,1)S(1)} %constant_dynamic-slice_fusion.4), channel_id=1, source_target_pairs={{0,4},{4,0},{1,5},{5,1},{2,6},{6,2},{3,7},{7,3},{8,12},{12,8},{9,1... | collective-permute-start | bytes 3145736 | tf_op jit(solution)/shard_map/ppermute | solution.py:44
  91.8 539.6 %reduce-scatter.8.cloned.1.call-start = ((), (), s32[]{:S(2)}) async-start(), calls=%async_computation.8 | async-start | bytes 10485760 | tf_op jit(solution)/shard_map/reduce_scatter | solution.py:127
  141.4 35.8 %collective-permute-start.20 = (bf16[8,32,1024]{2,1,0:T(8,128)(2,1)S(1)}, bf16[8,32,1024]{2,1,0:T(8,128)(2,1)S(1)}, u32[]{:S(2)}, u32[]{:S(2)}) collective-permute-start(bf16[8,32,1024]{2,1,0:T(8,128)(2,1)S(1)} %copy-done.19), channel_id=1, source_target_pairs={{0,2},{1,3},{2,0},{3,1},{4,6},{5,7},{6,4},{7,5},{8,10},{9,11},{10,... | collective-permute-start | bytes 1572872 | tf_op jit(solution)/shard_map/ppermute | solution.py:49
  142.4 34.8 %collective-permute-start.21 = (bf16[8,32,1024]{2,1,0:T(8,128)(2,1)S(1)}, bf16[8,32,1024]{2,1,0:T(8,128)(2,1)S(1)}, u32[]{:S(2)}, u32[]{:S(2)}) collective-permute-start(bf16[8,32,1024]{2,1,0:T(8,128)(2,1)S(1)} %copy-done.19), channel_id=1, source_target_pairs={{0,3},{1,0},{2,1},{3,2},{4,7},{5,4},{6,5},{7,6},{8,11},{9,8},{10,9... | collective-permute-start | bytes 1572872 | tf_op jit(solution)/shard_map/ppermute | solution.py:49
  145.2 43.3 %collective-permute-start.8 = (bf16[8,32,1024]{2,1,0:T(8,128)(2,1)S(1)}, bf16[8,32,1024]{2,1,0:T(8,128)(2,1)S(1)}, u32[]{:S(2)}, u32[]{:S(2)}) collective-permute-start(bf16[8,32,1024]{2,1,0:T(8,128)(2,1)S(1)} %get-tuple-element.73), channel_id=1, source_target_pairs={{0,1},{1,2},{2,3},{3,0},{4,5},{5,6},{6,7},{7,4},{8,9},{9,10},{10,1... | collective-permute-start | bytes 1572872 | tf_op jit(solution)/shard_map/ppermute | solution.py:63
  146.5 75.6 %collective-permute-start.7 = (bf16[8,32,1024]{2,1,0:T(8,128)(2,1)S(1)}, bf16[8,32,1024]{2,1,0:T(8,128)(2,1)S(1)}, u32[]{:S(2)}, u32[]{:S(2)}) collective-permute-start(bf16[8,32,1024]{2,1,0:T(8,128)(2,1)S(1)} %get-tuple-element.74), channel_id=1, source_target_pairs={{0,2},{1,3},{2,0},{3,1},{4,6},{5,7},{6,4},{7,5},{8,10},{9,11},{10,... | collective-permute-start | bytes 1572872 | tf_op jit(solution)/shard_map/ppermute | solution.py:63
  154.7 67.4 %collective-permute-start.6 = (bf16[8,32,1024]{2,1,0:T(8,128)(2,1)S(1)}, bf16[8,32,1024]{2,1,0:T(8,128)(2,1)S(1)}, u32[]{:S(2)}, u32[]{:S(2)}) collective-permute-start(bf16[8,32,1024]{2,1,0:T(8,128)(2,1)S(1)} %get-tuple-element.72), channel_id=1, source_target_pairs={{0,3},{1,0},{2,1},{3,2},{4,7},{5,4},{6,5},{7,6},{8,11},{9,8},{10,9... | collective-permute-start | bytes 1572872 | tf_op jit(solution)/shard_map/ppermute | solution.py:63
  177.5 93.5 %collective-permute-start.22 = (bf16[8,4,32,1024]{3,2,0,1:T(8,128)(2,1)S(1)}, bf16[8,4,32,1024]{3,2,0,1:T(8,128)(2,1)S(1)}, u32[]{:S(2)}, u32[]{:S(2)}) collective-permute-start(bf16[8,4,32,1024]{3,2,0,1:T(8,128)(2,1)S(1)} %pad_maximum_fusion.7), channel_id=1, source_target_pairs={{0,4},{4,0},{1,5},{5,1},{2,6},{6,2},{3,7},{7,3},{8,12},{12,8},{9,1... | collective-permute-start | bytes 6291464 | tf_op jit(solution)/shard_map/ppermute | solution.py:52
  222.8 25.9 %collective-permute-start.10 = (bf16[8,32,1024]{2,1,0:T(8,128)(2,1)S(1)}, bf16[8,32,1024]{2,1,0:T(8,128)(2,1)S(1)}, u32[]{:S(2)}, u32[]{:S(2)}) collective-permute-start(bf16[8,32,1024]{2,1,0:T(8,128)(2,1)S(1)} %get-tuple-element.41), channel_id=1, source_target_pairs={{0,1},{1,2},{2,3},{3,0},{4,5},{5,6},{6,7},{7,4},{8,9},{9,10},{10,1... | collective-permute-start | bytes 1572872 | tf_op jit(solution)/shard_map/ppermute | solution.py:49
  234.6 35.9 %collective-permute-start.11 = (bf16[8,32,1024]{2,1,0:T(8,128)(2,1)S(1)}, bf16[8,32,1024]{2,1,0:T(8,128)(2,1)S(1)}, u32[]{:S(2)}, u32[]{:S(2)}) collective-permute-start(bf16[8,32,1024]{2,1,0:T(8,128)(2,1)S(1)} %get-tuple-element.41), channel_id=1, source_target_pairs={{0,2},{1,3},{2,0},{3,1},{4,6},{5,7},{6,4},{7,5},{8,10},{9,11},{10,... | collective-permute-start | bytes 1572872 | tf_op jit(solution)/shard_map/ppermute | solution.py:49
  236.4 34.1 %collective-permute-start.12 = (bf16[8,32,1024]{2,1,0:T(8,128)(2,1)S(1)}, bf16[8,32,1024]{2,1,0:T(8,128)(2,1)S(1)}, u32[]{:S(2)}, u32[]{:S(2)}) collective-permute-start(bf16[8,32,1024]{2,1,0:T(8,128)(2,1)S(1)} %get-tuple-element.41), channel_id=1, source_target_pairs={{0,3},{1,0},{2,1},{3,2},{4,7},{5,4},{6,5},{7,6},{8,11},{9,8},{10,9... | collective-permute-start | bytes 1572872 | tf_op jit(solution)/shard_map/ppermute | solution.py:49
  376.7 257.1 %reduce-scatter.6.cloned.1.call-start = ((), (), s32[]{:S(2)}) async-start(), calls=%async_computation.7 | async-start | bytes 20971520 | tf_op jit(solution)/shard_map/reduce_scatter | solution.py:133
  388.0 321.1 %reduce-scatter.4.cloned.1.call-start = ((), (), s32[]{:S(2)}) async-start(), calls=%async_computation.6 | async-start | bytes 10485760 | tf_op jit(solution)/shard_map/reduce_scatter | solution.py:163
  415.3 37.1 %collective-permute-start.25 = (bf16[8,32,1024]{2,1,0:T(8,128)(2,1)S(1)}, bf16[8,32,1024]{2,1,0:T(8,128)(2,1)S(1)}, u32[]{:S(2)}, u32[]{:S(2)}) collective-permute-start(bf16[8,32,1024]{2,1,0:T(8,128)(2,1)S(1)} %get-tuple-element.68), channel_id=1, source_target_pairs={{0,2},{1,3},{2,0},{3,1},{4,6},{5,7},{6,4},{7,5},{8,10},{9,11},{10,... | collective-permute-start | bytes 1572872 | tf_op jit(solution)/shard_map/ppermute | solution.py:63
  417.7 34.7 %collective-permute-start.24 = (bf16[8,32,1024]{2,1,0:T(8,128)(2,1)S(1)}, bf16[8,32,1024]{2,1,0:T(8,128)(2,1)S(1)}, u32[]{:S(2)}, u32[]{:S(2)}) collective-permute-start(bf16[8,32,1024]{2,1,0:T(8,128)(2,1)S(1)} %get-tuple-element.66), channel_id=1, source_target_pairs={{0,3},{1,0},{2,1},{3,2},{4,7},{5,4},{6,5},{7,6},{8,11},{9,8},{10,9... | collective-permute-start | bytes 1572872 | tf_op jit(solution)/shard_map/ppermute | solution.py:63
  453.9 25.5 %collective-permute-start.27 = (bf16[8,32,1024]{2,1,0:T(8,128)(2,1)S(1)}, bf16[8,32,1024]{2,1,0:T(8,128)(2,1)S(1)}, u32[]{:S(2)}, u32[]{:S(2)}) collective-permute-start(bf16[8,32,1024]{2,1,0:T(8,128)(2,1)S(1)} %get-tuple-element.34), channel_id=1, source_target_pairs={{0,1},{1,2},{2,3},{3,0},{4,5},{5,6},{6,7},{7,4},{8,9},{9,10},{10,1... | collective-permute-start | bytes 1572872 | tf_op jit(solution)/shard_map/ppermute | solution.py:49
  465.6 35.1 %collective-permute-start.28 = (bf16[8,32,1024]{2,1,0:T(8,128)(2,1)S(1)}, bf16[8,32,1024]{2,1,0:T(8,128)(2,1)S(1)}, u32[]{:S(2)}, u32[]{:S(2)}) collective-permute-start(bf16[8,32,1024]{2,1,0:T(8,128)(2,1)S(1)} %get-tuple-element.34), channel_id=1, source_target_pairs={{0,2},{1,3},{2,0},{3,1},{4,6},{5,7},{6,4},{7,5},{8,10},{9,11},{10,... | collective-permute-start | bytes 1572872 | tf_op jit(solution)/shard_map/ppermute | solution.py:49
  467.1 33.6 %collective-permute-start.29 = (bf16[8,32,1024]{2,1,0:T(8,128)(2,1)S(1)}, bf16[8,32,1024]{2,1,0:T(8,128)(2,1)S(1)}, u32[]{:S(2)}, u32[]{:S(2)}) collective-permute-start(bf16[8,32,1024]{2,1,0:T(8,128)(2,1)S(1)} %get-tuple-element.34), channel_id=1, source_target_pairs={{0,3},{1,0},{2,1},{3,2},{4,7},{5,4},{6,5},{7,6},{8,11},{9,8},{10,9... | collective-permute-start | bytes 1572872 | tf_op jit(solution)/shard_map/ppermute | solution.py:49
  580.9 26.3 %collective-permute-start.34 = (bf16[8,32,1024]{2,1,0:T(8,128)(2,1)S(1)}, bf16[8,32,1024]{2,1,0:T(8,128)(2,1)S(1)}, u32[]{:S(2)}, u32[]{:S(2)}) collective-permute-start(bf16[8,32,1024]{2,1,0:T(8,128)(2,1)S(1)} %get-tuple-element.64), channel_id=1, source_target_pairs={{0,1},{1,2},{2,3},{3,0},{4,5},{5,6},{6,7},{7,4},{8,9},{9,10},{10,1... | collective-permute-start | bytes 1572872 | tf_op jit(solution)/shard_map/ppermute | solution.py:63
  593.0 36.7 %collective-permute-start.33 = (bf16[8,32,1024]{2,1,0:T(8,128)(2,1)S(1)}, bf16[8,32,1024]{2,1,0:T(8,128)(2,1)S(1)}, u32[]{:S(2)}, u32[]{:S(2)}) collective-permute-start(bf16[8,32,1024]{2,1,0:T(8,128)(2,1)S(1)} %get-tuple-element.65), channel_id=1, source_target_pairs={{0,2},{1,3},{2,0},{3,1},{4,6},{5,7},{6,4},{7,5},{8,10},{9,11},{10,... | collective-permute-start | bytes 1572872 | tf_op jit(solution)/shard_map/ppermute | solution.py:63
  594.8 34.9 %collective-permute-start.32 = (bf16[8,32,1024]{2,1,0:T(8,128)(2,1)S(1)}, bf16[8,32,1024]{2,1,0:T(8,128)(2,1)S(1)}, u32[]{:S(2)}, u32[]{:S(2)}) collective-permute-start(bf16[8,32,1024]{2,1,0:T(8,128)(2,1)S(1)} %get-tuple-element.63), channel_id=1, source_target_pairs={{0,3},{1,0},{2,1},{3,2},{4,7},{5,4},{6,5},{7,6},{8,11},{9,8},{10,9... | collective-permute-start | bytes 1572872 | tf_op jit(solution)/shard_map/ppermute | solution.py:63
  601.1 39.9 %collective-permute-start.18 = (bf16[8,32,1024]{2,1,0:T(8,128)(2,1)}, bf16[8,32,1024]{2,1,0:T(8,128)(2,1)}, u32[]{:S(2)}, u32[]{:S(2)}) collective-permute-start(bf16[8,32,1024]{2,1,0:T(8,128)(2,1)} %get-tuple-element.70), channel_id=1, source_target_pairs={{0,1},{1,2},{2,3},{3,0},{4,5},{5,6},{6,7},{7,4},{8,9},{9,10},{10,1... | collective-permute-start | bytes 1572872 | tf_op jit(solution)/shard_map/ppermute | solution.py:63
  602.5 71.7 %collective-permute-start.17 = (bf16[8,32,1024]{2,1,0:T(8,128)(2,1)}, bf16[8,32,1024]{2,1,0:T(8,128)(2,1)}, u32[]{:S(2)}, u32[]{:S(2)}) collective-permute-start(bf16[8,32,1024]{2,1,0:T(8,128)(2,1)} %get-tuple-element.71), channel_id=1, source_target_pairs={{0,2},{1,3},{2,0},{3,1},{4,6},{5,7},{6,4},{7,5},{8,10},{9,11},{10,... | collective-permute-start | bytes 1572872 | tf_op jit(solution)/shard_map/ppermute | solution.py:63
  607.2 67.1 %collective-permute-start.16 = (bf16[8,32,1024]{2,1,0:T(8,128)(2,1)}, bf16[8,32,1024]{2,1,0:T(8,128)(2,1)}, u32[]{:S(2)}, u32[]{:S(2)}) collective-permute-start(bf16[8,32,1024]{2,1,0:T(8,128)(2,1)} %get-tuple-element.69), channel_id=1, source_target_pairs={{0,3},{1,0},{2,1},{3,2},{4,7},{5,4},{6,5},{7,6},{8,11},{9,8},{10,9... | collective-permute-start | bytes 1572872 | tf_op jit(solution)/shard_map/ppermute | solution.py:63
  633.8 118.2 %collective-permute-start.37 = (bf16[8,512,128]{2,1,0:T(8,128)(2,1)}, bf16[8,512,128]{2,1,0:T(8,128)(2,1)}, u32[]{:S(2)}, u32[]{:S(2)}) collective-permute-start(bf16[8,512,128]{2,1,0:T(8,128)(2,1)} %constant_dynamic-slice_fusion.1), channel_id=1, source_target_pairs={{0,4},{4,0},{1,5},{5,1},{2,6},{6,2},{3,7},{7,3},{8,12},{12,8},{9,1... | collective-permute-start | bytes 3145736 | tf_op jit(solution)/shard_map/ppermute | solution.py:44
  637.0 126.3 %collective-permute-start.36 = (bf16[8,2,128,512]{2,3,1,0:T(8,128)(2,1)}, bf16[8,2,128,512]{2,3,1,0:T(8,128)(2,1)}, u32[]{:S(2)}, u32[]{:S(2)}) collective-permute-start(bf16[8,2,128,512]{2,3,1,0:T(8,128)(2,1)} %constant_dynamic-slice_fusion.2), channel_id=1, source_target_pairs={{0,4},{4,0},{1,5},{5,1},{2,6},{6,2},{3,7},{7,3},{8,12},{12,8},{9,1... | collective-permute-start | bytes 6291464 | tf_op jit(solution)/shard_map/ppermute | solution.py:44
  710.4 46.0 %collective-permute-start.35 = (bf16[8,4,128,128]{2,3,1,0:T(8,128)(2,1)S(1)}, bf16[8,4,128,128]{2,3,1,0:T(8,128)(2,1)S(1)}, u32[]{:S(2)}, u32[]{:S(2)}) collective-permute-start(bf16[8,4,128,128]{2,3,1,0:T(8,128)(2,1)S(1)} %constant_dynamic-slice_fusion.3), channel_id=1, source_target_pairs={{0,4},{4,0},{1,5},{5,1},{2,6},{6,2},{3,7},{7,3},{8,12},{12,8},{9,1... | collective-permute-start | bytes 3145736 | tf_op jit(solution)/shard_map/ppermute | solution.py:44
  (59 other events, 1073.8 us)
Sparse Core Ops, SparseCore 0:
  16.3 89.9 all-gather.3
  108.7 157.1 all-gather.5
  267.8 87.3 all-gather.7
  376.8 86.3 reduce-scatter.7
  466.1 153.7 reduce-scatter.5
  622.7 86.3 reduce-scatter.3

commit v2 on v1

--- a/solution.py
+++ b/solution.py
@@ -34,9 +34,63 @@
     )
 
 
-def make_shards(tensor_size):
+def make_shards(plane_size, tensor_size):
+    paired = plane_size == 4
+
     def around(shift):
         return [(i, (i + shift) % tensor_size) for i in range(tensor_size)]
+
+    def across(array, bits):
+        return lax.ppermute(array, "xy", [(i, i ^ bits) for i in range(plane_size)])
+
+    def relative(array):
+        if not paired:
+            return array
+        size = array.shape[-1] // plane_size
+        chip = lax.axis_index("xy")
+        blocks = [
+            lax.dynamic_slice_in_dim(array, (chip ^ r) * size, size, array.ndim - 1)
+            for r in range(plane_size)
+        ]
+        return jnp.concatenate(blocks, axis=-1)
+
+    def plane_gather(weight):
+        if not paired:
+            return lax.all_gather(weight, "xy", axis=2, tiled=True), weight
+        from_x, from_y = across(weight, 1), across(weight, 2)
+        far_a = across(from_y[:, :2], 1)
+        far_b = across(from_x[:, 2:], 2)
+        far = jnp.concatenate([far_a, far_b], axis=1)
+        return jnp.concatenate([weight, from_x, from_y, far], axis=2), (from_x, from_y)
+
+    def plane_reduce(first, second):
+        if not paired:
+            both = jnp.concatenate([first, second], axis=1)
+            return lax.psum_scatter(both, "xy", scatter_dimension=2, tiled=True).astype(F32)
+        size = first.shape[2] // plane_size
+        results = []
+        for part, near, other in ((first, 1, 2), (second, 2, 1)):
+            block = [part[:, :, r * size : (r + 1) * size] for r in range(plane_size)]
+            got = across(jnp.concatenate([block[near], block[3]], axis=2), near)
+            own = block[0].astype(F32) + got[:, :, :size].astype(F32)
+            passed = block[other].astype(F32) + got[:, :, size:].astype(F32)
+            results.append(own + across(passed.astype(BF), other).astype(F32))
+        return jnp.concatenate(results, axis=1)
+
+    def small_sum(vectors, core, local):
+        if not paired:
+            vectors = lax.psum(vectors, ("xy", "core", "tensor"))
+            place = lax.axis_index("xy") * 2 + core
+            return lax.dynamic_slice_in_dim(vectors, place * local, local, 1)
+        total = vectors
+        for k in range(1, tensor_size):
+            total = total + lax.ppermute(vectors, "tensor", around(k))
+        total = relative(total + lax.ppermute(total, "core", SWAP))
+        size = total.shape[1] // plane_size
+        mine = total[:, :size]
+        for r in range(1, plane_size):
+            mine = mine + across(total[:, r * size : (r + 1) * size], r)
+        return half(mine, 1, core)
 
     def trade(core, weight, split_axis, join_axis):
         mine = half(weight, split_axis, core)
@@ -72,10 +126,11 @@
         w_attn = jnp.concatenate(
             [w_qkv.astype(BF), jnp.swapaxes(w_out, 1, 2)[:, None].astype(BF)], axis=1
         )
-        w_attn = lax.all_gather(trade(core, w_attn, 3, 2), "xy", axis=2, tiled=True)
+        w_attn, arrived = plane_gather(trade(core, w_attn, 3, 2))
         small = jnp.concatenate([norm_gains, pad_row[None]], axis=0).astype(BF)
         small = lax.all_gather(small, ("xy", "core"), axis=1, tiled=True).astype(F32)
-        wgu = lax.all_gather(trade(core, w_gate_up.astype(BF), 3, 2), "xy", axis=2, tiled=True)
+        wgu, arrived = lax.optimization_barrier((trade(core, w_gate_up.astype(BF), 3, 2), arrived))
+        wgu = lax.all_gather(wgu, "xy", axis=2, tiled=True)
         wdown = lax.all_gather(trade(core, w_down.astype(BF), 1, 2), "xy", axis=2, tiled=True)
 
         gain_one, gain_two, pad_vec = small[0], small[1], small[2]
@@ -87,7 +142,7 @@
         )
         r1 = lax.rsqrt(jnp.mean(h0 * h0, axis=-1, keepdims=True) + EPS)
         n1 = (h0 * r1 * gain_one).astype(BF)
-        n1_all = collect(n1)
+        n1_all = collect(relative(n1))
         grad_all = collect(out_grad)
         frames = n1_all.shape[1]
         wqkv, wout_t = w_attn[:, :3], w_attn[:, 3]
@@ -112,7 +167,7 @@
         probs_low = (expo / total).astype(BF)
         mixed = jnp.einsum("fhst,tfhe->sfhe", probs_low, value, preferred_element_type=F32)
         mixed = mixed.reshape(steps, frames, col_width).astype(BF)
-        attn = deal(jnp.einsum("sfd,sed->sfe", mixed, wout_t, preferred_element_type=F32))
+        attn = relative(deal(jnp.einsum("sfd,sed->sfe", mixed, wout_t, preferred_element_type=F32)))
         h1 = h0 + attn
         r2 = lax.rsqrt(jnp.mean(h1 * h1, axis=-1, keepdims=True) + EPS)
         n2 = (h1 * r2 * gain_two).astype(BF)
@@ -124,7 +179,8 @@
         silu_val = gate * sigma
         hidden = (silu_val * upval).astype(BF)
         d_down = jnp.einsum("sfk,sfd->skd", hidden, grad_all, preferred_element_type=F32)
-        r_down = lax.psum_scatter(d_down.astype(BF), "xy", scatter_dimension=2, tiled=True)
+        d_down, wdown = lax.optimization_barrier((d_down.astype(BF), wdown))
+        r_down = lax.psum_scatter(d_down, "xy", scatter_dimension=2, tiled=True)
         d_hidden = jnp.einsum("sfd,skd->sfk", grad_all, wdown, preferred_element_type=F32)
         d_gate = d_hidden * upval * (sigma * (1.0 + gate * (1.0 - sigma)))
         d_up = d_hidden * silu_val
@@ -134,7 +190,7 @@
         dn2 = deal(jnp.einsum("sjfe,sjde->sfd", d_gu, wgu, preferred_element_type=F32))
         dh_norm2, dgain_two = norm_back(dn2, h1, r2, gain_two)
         dh1 = out_grad.astype(F32) + dh_norm2
-        dh1_all = collect(dh1.astype(BF))
+        dh1_all = collect(relative(dh1.astype(BF)))
         ffout = deal(jnp.einsum("sfk,skd->sfd", hidden, wdown, preferred_element_type=F32))
         layer_out = (h1 + ffout).astype(BF)
         d_out_t = jnp.einsum("sfe,sfd->sed", dh1_all, mixed, preferred_element_type=F32)
@@ -150,31 +206,31 @@
         d_key = (
             jnp.einsum("fhst,sfhe->tfhe", d_scores, query.astype(F32), precision=HIGH) * scale
         )
-        d_qkv = jnp.stack(
+        d_qk = jnp.stack(
             [
                 d_query.reshape(steps, frames, col_width),
                 d_key.reshape(steps, frames, col_width),
-                d_value.reshape(steps, frames, col_width),
             ],
             axis=1,
         ).astype(BF)
-        d_wqkv = jnp.einsum("sfd,sjfe->sjde", n1_all, d_qkv, preferred_element_type=F32)
-        d_attn = jnp.concatenate([d_wqkv.astype(BF), d_out_t[:, None].astype(BF)], axis=1)
-        r_attn = lax.psum_scatter(d_attn, "xy", scatter_dimension=2, tiled=True)
-        dn1 = deal(jnp.einsum("sjfe,sjde->sfd", d_qkv, wqkv, preferred_element_type=F32))
+        d_v = d_value.reshape(steps, frames, col_width).astype(BF)
+        d_wqk = jnp.einsum("sfd,sjfe->sjde", n1_all, d_qk, preferred_element_type=F32)
+        d_wv = jnp.einsum("sfd,sfe->sde", n1_all, d_v, preferred_element_type=F32)
+        d_vo = jnp.stack([d_wv, d_out_t], axis=1).astype(BF)
+        r_attn = plane_reduce(d_wqk.astype(BF), d_vo)
+        d_qkv = jnp.concatenate([d_qk, d_v[:, None]], axis=1)
+        dn1 = relative(
+            deal(jnp.einsum("sjfe,sjde->sfd", d_qkv, wqkv, preferred_element_type=F32))
+        )
         dh_norm1, dgain_one = norm_back(dn1, h0, r1, gain_one)
         dh0 = dh1 + dh_norm1
         input_grad = dh0.astype(BF)
         d_pad = jnp.sum(dh0[0] * (1.0 - maskf)[:, None], axis=0)
         small_grad = jnp.stack([dgain_one, dgain_two, d_pad], axis=0)
-        small_grad = lax.psum(small_grad, ("xy", "core", "tensor"))
-        place = lax.axis_index("xy") * 2 + core
-        g_small = lax.dynamic_slice_in_dim(
-            small_grad, place * pad_row.shape[0], pad_row.shape[0], 1
-        )
+        g_small = small_sum(small_grad, core, pad_row.shape[0])
 
         def settle(reduced, split_axis, join_axis):
-            return trade(core, reduced, split_axis, join_axis).astype(F32)
+            return trade(core, reduced.astype(BF), split_axis, join_axis).astype(F32)
 
         g_down = settle(r_down, 2, 1)
         g_gate_up = settle(r_gate_up, 2, 3)
@@ -194,7 +250,7 @@
     dp = ("xy", "core")
     rows = ("xy", "core", "tensor")
     return jax.shard_map(
-        make_shards(tensor_size),
+        make_shards(dp_size // 2, tensor_size),
         mesh=inner,
         in_specs=(
             P(None, rows, None),

time: 793 us -> 802 us (1.011)
  blocking collectives: 50.4 us -> 8.94 us
  starting transfers between devices: 82 us -> 115 us
  waiting for transfers between devices: 371 us -> 388 us
  matrix products: 114 us -> 103 us
    ppermute x0 -> x15, waiting for transfers between devices: none -> 148 us  [the longest x11 142 us: across(): return lax.ppermute(array, 'xy', [(i, i ^ bits) for i in range(plane_size)])]
    all_gather x1, waiting for transfers between devices: 61.9 us -> 0.01 us  [shards(): lax.all_gather(trade(core, w_down.astype(BF), 1, 2), 'xy', axis=2, tiled=...]
    psum x1 -> x0, blocking collectives: 39.4 us -> none  [shards(): small_grad = lax.psum(small_grad, ('xy', 'core', 'tensor'))]
    reduce_scatter x2 -> x1, waiting for transfers between devices: 30.8 us -> 0.01 us  [shards(): r_down = lax.psum_scatter(d_down, 'xy', scatter_dimension=2, tiled=True)]
    ppermute x12, waiting for transfers between devices: 137 us -> 112 us  [deal(): lax.ppermute(chip[:, k].astype(BF), 'tensor', around(-k)).astype(F32)]
    ppermute x0 -> x15, starting transfers between devices: none -> 18.1 us  [the longest x11 13.5 us: across(): return lax.ppermute(array, 'xy', [(i, i ^ bits) for i in range(plane_size)])]
    ppermute x12, starting transfers between devices: 31.5 us -> 40.3 us  [deal(): lax.ppermute(chip[:, k].astype(BF), 'tensor', around(-k)).astype(F32)]
    unnamed x111 -> x117, local copies, waits for them, and re-layouts: 40.5 us -> 46 us
  transfers between devices with their start and end apart: 44 -> 57, of which waited for: 24 -> 28; matrix products, arithmetic and copies ran while one was open for 27% -> 26% of each run, Pallas kernels for 0% -> 0%
where the time goes in v2:
time: 802 us; the launch traced here: 794 us
  waiting for transfers between devices  388 us (48%)
  starting transfers between devices  115 us (14%)
  matrix products  103 us (13%)
  local copies, waits for them, and re-layouts  102 us (13%)
  other arithmetic  63.5 us (8%)
  between operations  15.1 us (2%)
  blocking collectives  8.94 us (1%)
    ppermute x11, waiting for transfers between devices, across(): return lax.ppermute(array, 'xy', [(i, i ^ bits) for i in range(plane_size)])  142 us
    ppermute x12, waiting for transfers between devices, collect(): lax.ppermute(rows, 'tensor', around(k))  123 us
    ppermute x12, waiting for transfers between devices, deal(): lax.ppermute(chip[:, k].astype(BF), 'tensor', around(-k)).astype(F32)  112 us
    ppermute x12, starting transfers between devices, collect(): lax.ppermute(rows, 'tensor', around(k))  53.2 us
    unnamed x117, local copies, waits for them, and re-layouts  46 us
    ppermute x12, starting transfers between devices, deal(): lax.ppermute(chip[:, k].astype(BF), 'tensor', around(-k)).astype(F32)  40.3 us
  transfers between devices with their start and end apart: 57, of which 28 were waited for; matrix products, arithmetic and copies ran while one was open for 26% of the time, Pallas kernels for 0%

profile of v2, /device:TPU:0, one launch (start us, length us, event | category | flops | bytes accessed | tf_op | source)
XLA Modules:
  0.0 794.4 jit_solution(17936964474859646375)
XLA Ops:
  11.2 7.2 copy.65
  36.2 38.7 %collective-permute-done.1 = bf16[8,4,256,128]{2,3,1,0:T(8,128)(2,1)S(1)} collective-permute-done((bf16[8,4,256,128]{2,3,1,0:T(8,128)(2,1)}, bf16[8,4,256,128]{2,3,1,0:T(8,128)(2,1)S(1)}, u32[]{:S(2)}, u32[]{:S(2)}) %collective-permute-start.1) | collective-permute-done | bytes 2097184 | tf_op jit(solution)/shard_map/ppermute | solution.py:44
  76.6 8.9 %all_gather.9 = bf16[3,1024]{1,0:T(4,128)(2,1)S(1)} all-gather(bf16[3,128]{1,0:T(4,128)(2,1)S(1)} %pad_maximum_fusion.14), channel_id=1, replica_groups=mesh['xy'=4,'core'=2,'tensor'=4] {'xy','core'}, dimensions={1}, use_global_device_ids=true | all-gather | bytes 6912 | tf_op jit(solution)/shard_map/all_gather | solution.py:131
  93.1 11.2 %collective-permute-done.5 = bf16[8,32,1024]{2,1,0:T(8,128)(2,1)S(1)} collective-permute-done((bf16[8,32,1024]{2,1,0:T(8,128)(2,1)S(1)}, bf16[8,32,1024]{2,1,0:T(8,128)(2,1)S(1)}, u32[]{:S(2)}, u32[]{:S(2)}) %collective-permute-start.5) | collective-permute-done | bytes 524320 | tf_op jit(solution)/shard_map/ppermute | solution.py:103
  104.3 21.9 %collective-permute-done.6 = bf16[8,32,1024]{2,1,0:T(8,128)(2,1)S(1)} collective-permute-done((bf16[8,32,1024]{2,1,0:T(8,128)(2,1)S(1)}, bf16[8,32,1024]{2,1,0:T(8,128)(2,1)S(1)}, u32[]{:S(2)}, u32[]{:S(2)}) %collective-permute-start.6) | collective-permute-done | bytes 524320 | tf_op jit(solution)/shard_map/ppermute | solution.py:103
  152.4 22.3 %collective-permute-done.4 = bf16[8,2,256,128]{2,3,1,0:T(8,128)(2,1)} collective-permute-done((bf16[8,2,256,128]{2,3,1,0:T(8,128)(2,1)}, bf16[8,2,256,128]{2,3,1,0:T(8,128)(2,1)}, u32[]{:S(2)}, u32[]{:S(2)}) %collective-permute-start.4) | collective-permute-done | bytes 1048608 | tf_op jit(solution)/shard_map/ppermute | solution.py:44
  174.7 5.5 collective-permute-done.3
  205.1 16.3 %collective-permute-start.18 = (bf16[8,32,1024]{2,1,0:T(8,128)(2,1)S(1)}, bf16[8,32,1024]{2,1,0:T(8,128)(2,1)S(1)}, u32[]{:S(2)}, u32[]{:S(2)}) collective-permute-start(bf16[8,32,1024]{2,1,0:T(8,128)(2,1)S(1)} %copy-done.19), channel_id=1, source_target_pairs={{0,1},{1,2},{2,3},{3,0},{4,5},{5,6},{6,7},{7,4},{8,9},{9,10},{10,1... | collective-permute-start | bytes 1572872 | tf_op jit(solution)/shard_map/ppermute | solution.py:103
  227.8 7.4 collective-permute-done.18
  238.4 19.4 %collective-permute-done.19 = bf16[8,32,1024]{2,1,0:T(8,128)(2,1)S(1)} collective-permute-done((bf16[8,32,1024]{2,1,0:T(8,128)(2,1)S(1)}, bf16[8,32,1024]{2,1,0:T(8,128)(2,1)S(1)}, u32[]{:S(2)}, u32[]{:S(2)}) %collective-permute-start.19) | collective-permute-done | bytes 524320 | tf_op jit(solution)/shard_map/ppermute | solution.py:103
  258.1 10.9 %collective-permute-done.12 = bf16[8,32,1024]{2,1,0:T(8,128)(2,1)S(1)} collective-permute-done((bf16[8,32,1024]{2,1,0:T(8,128)(2,1)S(1)}, bf16[8,32,1024]{2,1,0:T(8,128)(2,1)S(1)}, u32[]{:S(2)}, u32[]{:S(2)}) %collective-permute-start.12) | collective-permute-done | bytes 524320 | tf_op jit(solution)/shard_map/ppermute | solution.py:117
  269.0 32.9 %collective-permute-done.11 = bf16[8,32,1024]{2,1,0:T(8,128)(2,1)S(1)} collective-permute-done((bf16[8,32,1024]{2,1,0:T(8,128)(2,1)S(1)}, bf16[8,32,1024]{2,1,0:T(8,128)(2,1)S(1)}, u32[]{:S(2)}, u32[]{:S(2)}) %collective-permute-start.11) | collective-permute-done | bytes 524320 | tf_op jit(solution)/shard_map/ppermute | solution.py:117
  303.5 11.7 %collective-permute-start.14 = (bf16[8,32,1024]{2,1,0:T(8,128)(2,1)S(1)}, bf16[8,32,1024]{2,1,0:T(8,128)(2,1)S(1)}, u32[]{:S(2)}, u32[]{:S(2)}) collective-permute-start(bf16[8,32,1024]{2,1,0:T(8,128)(2,1)S(1)} %get-tuple-element.44), channel_id=1, source_target_pairs={{0,1},{1,2},{2,3},{3,0},{4,5},{5,6},{6,7},{7,4},{8,9},{9,10},{10,1... | collective-permute-start | bytes 1572872 | tf_op jit(solution)/shard_map/ppermute | solution.py:103
  318.1 10.9 %collective-permute-done.14 = bf16[8,32,1024]{2,1,0:T(8,128)(2,1)S(1)} collective-permute-done((bf16[8,32,1024]{2,1,0:T(8,128)(2,1)S(1)}, bf16[8,32,1024]{2,1,0:T(8,128)(2,1)S(1)}, u32[]{:S(2)}, u32[]{:S(2)}) %collective-permute-start.14) | collective-permute-done | bytes 524320 | tf_op jit(solution)/shard_map/ppermute | solution.py:103
  328.9 21.1 %collective-permute-done.15 = bf16[8,32,1024]{2,1,0:T(8,128)(2,1)S(1)} collective-permute-done((bf16[8,32,1024]{2,1,0:T(8,128)(2,1)S(1)}, bf16[8,32,1024]{2,1,0:T(8,128)(2,1)S(1)}, u32[]{:S(2)}, u32[]{:S(2)}) %collective-permute-start.15) | collective-permute-done | bytes 524320 | tf_op jit(solution)/shard_map/ppermute | solution.py:103
  357.2 14.9 %convolution_bitcast_fusion = f32[8,2,256,512]{2,3,1,0:T(8,128)} fusion(bf16[8,2,1024,512]{2,3,1,0:T(8,128)(2,1)} %all-gather.3.cloned.1.call-done, bf16[8,256,1024,1]{2,1,3,0:T(8,128)(2,1)} %bitcast.271), kind=kOutput, calls=%fused_computation.32 | convolution fusion | flops 4294967296 | bytes 29360128 | tf_op jit(solution)/shard_map/sfd,sjde->sjfe/dot_general | solution.py:175
  378.2 5.7 convolution_convert_fusion
  383.9 12.4 %fusion.16 = (bf16[8,1,256,512]{2,3,0,1:T(8,128)(2,1)S(1)}, bf16[8,1,256,512]{2,3,0,1:T(8,128)(2,1)}) fusion(f32[8,2,256,512]{2,3,1,0:T(8,128)} %convolution_bitcast_fusion, bf16[8,256,1024]{2,1,0:T(8,128)(2,1)} %bitcast.273, bf16[8,512,1024]{2,1,0:T(8,128)(2,1)} %all-gather.5.cloned.1.call-done), kind=kOutput, calls=%fused_computation.76 | convolution fusion | flops 2161115136 | bytes 25165824 | tf_op jit(solution)/shard_map/sfd,skd->sfk/dot_general | solution.py:184
  397.7 9.8 %convert_bitcast_fusion = bf16[8,2,1024,512]{2,3,1,0:T(8,128)(2,1)} fusion(bf16[8,256,1024,1]{2,1,3,0:T(8,128)(2,1)S(1)} %bitcast.272, bf16[8,1,256,512]{2,3,0,1:T(8,128)(2,1)} %get-tuple-element.54, bf16[8,1,256,512]{2,3,0,1:T(8,128)(2,1)S(1)} %get-tuple-element.53), kind=kOutput, calls=%fused_computation.2 | convolution fusion | flops 4305453056 | bytes 25165824 | tf_op jit(solution)/shard_map/sfd,sjfe->sjde/dot_general | solution.py:188
  407.6 14.9 %fusion = f32[8,256,1024,1]{2,1,0,3:T(8,128)} fusion(bf16[8,2,1024,512]{2,3,1,0:T(8,128)(2,1)} %all-gather.3.cloned.1.call-done, bf16[8,1,256,512]{2,3,0,1:T(8,128)(2,1)} %get-tuple-element.54, bf16[8,1,256,512]{2,3,0,1:T(8,128)(2,1)} %copy-done.35), kind=kOutput, calls=%fused_computation | convolution fusion | flops 4297064448 | bytes 29360128 | tf_op jit(solution)/shard_map/sjfe,sjde->sfd/dot_general | solution.py:190
  427.0 5.8 fusion.76
  442.6 11.7 %collective-permute-start.30 = (bf16[8,32,1024]{2,1,0:T(8,128)(2,1)S(1)}, bf16[8,32,1024]{2,1,0:T(8,128)(2,1)S(1)}, u32[]{:S(2)}, u32[]{:S(2)}) collective-permute-start(bf16[8,32,1024]{2,1,0:T(8,128)(2,1)S(1)} %get-tuple-element.71), channel_id=1, source_target_pairs={{0,1},{1,2},{2,3},{3,0},{4,5},{5,6},{6,7},{7,4},{8,9},{9,10},{10,1... | collective-permute-start | bytes 1572872 | tf_op jit(solution)/shard_map/ppermute | solution.py:117
  472.1 19.4 %collective-permute-done.29 = bf16[8,32,1024]{2,1,0:T(8,128)(2,1)S(1)} collective-permute-done((bf16[8,32,1024]{2,1,0:T(8,128)(2,1)S(1)}, bf16[8,32,1024]{2,1,0:T(8,128)(2,1)S(1)}, u32[]{:S(2)}, u32[]{:S(2)}) %collective-permute-start.29) | collective-permute-done | bytes 524320 | tf_op jit(solution)/shard_map/ppermute | solution.py:117
  492.0 10.7 %collective-permute-done.26 = bf16[8,32,1024]{2,1,0:T(8,128)(2,1)S(1)} collective-permute-done((bf16[8,32,1024]{2,1,0:T(8,128)(2,1)S(1)}, bf16[8,32,1024]{2,1,0:T(8,128)(2,1)S(1)}, u32[]{:S(2)}, u32[]{:S(2)}) %collective-permute-start.26) | collective-permute-done | bytes 524320 | tf_op jit(solution)/shard_map/ppermute | solution.py:117
  502.7 33.1 %collective-permute-done.25 = bf16[8,32,1024]{2,1,0:T(8,128)(2,1)S(1)} collective-permute-done((bf16[8,32,1024]{2,1,0:T(8,128)(2,1)S(1)}, bf16[8,32,1024]{2,1,0:T(8,128)(2,1)S(1)}, u32[]{:S(2)}, u32[]{:S(2)}) %collective-permute-start.25) | collective-permute-done | bytes 524320 | tf_op jit(solution)/shard_map/ppermute | solution.py:117
  537.3 11.8 %collective-permute-start.31 = (bf16[8,32,1024]{2,1,0:T(8,128)(2,1)S(1)}, bf16[8,32,1024]{2,1,0:T(8,128)(2,1)S(1)}, u32[]{:S(2)}, u32[]{:S(2)}) collective-permute-start(bf16[8,32,1024]{2,1,0:T(8,128)(2,1)S(1)} %get-tuple-element.93), channel_id=1, source_target_pairs={{0,1},{1,2},{2,3},{3,0},{4,5},{5,6},{6,7},{7,4},{8,9},{9,10},{10,1... | collective-permute-start | bytes 1572872 | tf_op jit(solution)/shard_map/ppermute | solution.py:103
  551.7 10.3 %collective-permute-done.31 = bf16[8,32,1024]{2,1,0:T(8,128)(2,1)S(1)} collective-permute-done((bf16[8,32,1024]{2,1,0:T(8,128)(2,1)S(1)}, bf16[8,32,1024]{2,1,0:T(8,128)(2,1)S(1)}, u32[]{:S(2)}, u32[]{:S(2)}) %collective-permute-start.31) | collective-permute-done | bytes 524320 | tf_op jit(solution)/shard_map/ppermute | solution.py:103
  562.0 21.2 %collective-permute-done.32 = bf16[8,32,1024]{2,1,0:T(8,128)(2,1)S(1)} collective-permute-done((bf16[8,32,1024]{2,1,0:T(8,128)(2,1)S(1)}, bf16[8,32,1024]{2,1,0:T(8,128)(2,1)S(1)}, u32[]{:S(2)}, u32[]{:S(2)}) %collective-permute-start.32) | collective-permute-done | bytes 524320 | tf_op jit(solution)/shard_map/ppermute | solution.py:103
  643.1 11.4 %collective-permute-start.38 = (bf16[8,32,1024]{2,1,0:T(8,128)(2,1)S(1)}, bf16[8,32,1024]{2,1,0:T(8,128)(2,1)S(1)}, u32[]{:S(2)}, u32[]{:S(2)}) collective-permute-start(bf16[8,32,1024]{2,1,0:T(8,128)(2,1)S(1)} %get-tuple-element.68), channel_id=1, source_target_pairs={{0,1},{1,2},{2,3},{3,0},{4,5},{5,6},{6,7},{7,4},{8,9},{9,10},{10,1... | collective-permute-start | bytes 1572872 | tf_op jit(solution)/shard_map/ppermute | solution.py:117
  657.5 46.9 %collective-permute-done.39 = bf16[8,2,512,128]{2,3,1,0:T(8,128)(2,1)S(1)} collective-permute-done((bf16[8,2,512,128]{2,3,1,0:T(8,128)(2,1)}, bf16[8,2,512,128]{2,3,1,0:T(8,128)(2,1)S(1)}, u32[]{:S(2)}, u32[]{:S(2)}) %collective-permute-start.39) | collective-permute-done | bytes 2097184 | tf_op jit(solution)/shard_map/ppermute | solution.py:44
  710.6 20.8 %collective-permute-done.42 = bf16[8,2,256,128]{2,3,1,0:T(8,128)(2,1)S(1)} collective-permute-done((bf16[8,2,256,128]{2,3,1,0:T(8,128)(2,1)S(1)}, bf16[8,2,256,128]{2,3,1,0:T(8,128)(2,1)S(1)}, u32[]{:S(2)}, u32[]{:S(2)}) %collective-permute-start.42) | collective-permute-done | bytes 1048608 | tf_op jit(solution)/shard_map/ppermute | solution.py:44
  778.6 9.1 %copy.99 = f32[8,2,128,1024]{3,2,1,0:T(8,128)} copy(f32[8,2,128,1024]{2,3,1,0:T(8,128)} %maximum_convert_fusion) | data formatting | bytes 16777216
  (333 shorter events, 263.3 us)
Async XLA Ops:
  7.2 350.1 %all-gather.3.cloned.1.call-start = ((), (), s32[]{:S(2)}) async-start(), calls=%async_computation.2 | async-start | bytes 20971520 | tf_op jit(solution)/shard_map/all_gather | solution.py:133
  25.9 49.0 %collective-permute-start.1 = (bf16[8,4,256,128]{2,3,1,0:T(8,128)(2,1)}, bf16[8,4,256,128]{2,3,1,0:T(8,128)(2,1)S(1)}, u32[]{:S(2)}, u32[]{:S(2)}) collective-permute-start(bf16[8,4,256,128]{2,3,1,0:T(8,128)(2,1)} %pad_maximum_fusion.2), channel_id=1, source_target_pairs={{0,8},{8,0},{16,24},{24,16},{1,9},{9,1},{17,25},{25,17},{2,10},{10... | collective-permute-start | bytes 6291464 | tf_op jit(solution)/shard_map/ppermute | solution.py:44
  28.9 47.6 %collective-permute-start.2 = (bf16[8,4,256,128]{2,3,1,0:T(8,128)(2,1)}, bf16[8,4,256,128]{2,3,1,0:T(8,128)(2,1)}, u32[]{:S(2)}, u32[]{:S(2)}) collective-permute-start(bf16[8,4,256,128]{2,3,1,0:T(8,128)(2,1)} %pad_maximum_fusion.2), channel_id=1, source_target_pairs={{0,16},{8,24},{16,0},{24,8},{1,17},{9,25},{17,1},{25,9},{2,18},{10... | collective-permute-start | bytes 6291464 | tf_op jit(solution)/shard_map/ppermute | solution.py:44
  76.5 307.5 %all-gather.5.cloned.1.call-start = ((), (), s32[]{:S(2)}) async-start(), calls=%async_computation.3 | async-start | bytes 10485760 | tf_op jit(solution)/shard_map/all_gather | solution.py:134
  89.2 37.1 %collective-permute-start.6 = (bf16[8,32,1024]{2,1,0:T(8,128)(2,1)S(1)}, bf16[8,32,1024]{2,1,0:T(8,128)(2,1)S(1)}, u32[]{:S(2)}, u32[]{:S(2)}) collective-permute-start(bf16[8,32,1024]{2,1,0:T(8,128)(2,1)S(1)} %get-tuple-element.99), channel_id=1, source_target_pairs={{0,2},{1,3},{2,0},{3,1},{4,6},{5,7},{6,4},{7,5},{8,10},{9,11},{10,... | collective-permute-start | bytes 1572872 | tf_op jit(solution)/shard_map/ppermute | solution.py:103
  91.8 34.5 %collective-permute-start.7 = (bf16[8,32,1024]{2,1,0:T(8,128)(2,1)S(1)}, bf16[8,32,1024]{2,1,0:T(8,128)(2,1)S(1)}, u32[]{:S(2)}, u32[]{:S(2)}) collective-permute-start(bf16[8,32,1024]{2,1,0:T(8,128)(2,1)S(1)} %get-tuple-element.99), channel_id=1, source_target_pairs={{0,3},{1,0},{2,1},{3,2},{4,7},{5,4},{6,5},{7,6},{8,11},{9,8},{10,9... | collective-permute-start | bytes 1572872 | tf_op jit(solution)/shard_map/ppermute | solution.py:103
  133.3 41.4 %collective-permute-start.4 = (bf16[8,2,256,128]{2,3,1,0:T(8,128)(2,1)}, bf16[8,2,256,128]{2,3,1,0:T(8,128)(2,1)}, u32[]{:S(2)}, u32[]{:S(2)}) collective-permute-start(bf16[8,2,256,128]{2,3,1,0:T(8,128)(2,1)} %slice.225), channel_id=1, source_target_pairs={{0,16},{8,24},{16,0},{24,8},{1,17},{9,25},{17,1},{25,9},{2,18},{10... | collective-permute-start | bytes 3145736 | tf_op jit(solution)/shard_map/ppermute | solution.py:44
  136.1 44.1 %collective-permute-start.3 = (bf16[8,2,256,128]{2,3,1,0:T(8,128)(2,1)}, bf16[8,2,256,128]{2,3,1,0:T(8,128)(2,1)}, u32[]{:S(2)}, u32[]{:S(2)}) collective-permute-start(bf16[8,2,256,128]{2,3,1,0:T(8,128)(2,1)} %slice.224), channel_id=1, source_target_pairs={{0,8},{8,0},{16,24},{24,16},{1,9},{9,1},{17,25},{25,17},{2,10},{10... | collective-permute-start | bytes 3145736 | tf_op jit(solution)/shard_map/ppermute | solution.py:44
  140.6 592.2 %reduce-scatter.3.cloned.1.call-start = ((), (), s32[]{:S(2)}) async-start(), calls=%async_computation.4 | async-start | bytes 20971520 | tf_op jit(solution)/shard_map/reduce_scatter | solution.py:189
  205.1 30.2 %collective-permute-start.18 = (bf16[8,32,1024]{2,1,0:T(8,128)(2,1)S(1)}, bf16[8,32,1024]{2,1,0:T(8,128)(2,1)S(1)}, u32[]{:S(2)}, u32[]{:S(2)}) collective-permute-start(bf16[8,32,1024]{2,1,0:T(8,128)(2,1)S(1)} %copy-done.19), channel_id=1, source_target_pairs={{0,1},{1,2},{2,3},{3,0},{4,5},{5,6},{6,7},{7,4},{8,9},{9,10},{10,1... | collective-permute-start | bytes 1572872 | tf_op jit(solution)/shard_map/ppermute | solution.py:103
  221.4 36.4 %collective-permute-start.19 = (bf16[8,32,1024]{2,1,0:T(8,128)(2,1)S(1)}, bf16[8,32,1024]{2,1,0:T(8,128)(2,1)S(1)}, u32[]{:S(2)}, u32[]{:S(2)}) collective-permute-start(bf16[8,32,1024]{2,1,0:T(8,128)(2,1)S(1)} %copy-done.19), channel_id=1, source_target_pairs={{0,2},{1,3},{2,0},{3,1},{4,6},{5,7},{6,4},{7,5},{8,10},{9,11},{10,... | collective-permute-start | bytes 1572872 | tf_op jit(solution)/shard_map/ppermute | solution.py:103
  222.9 34.9 %collective-permute-start.20 = (bf16[8,32,1024]{2,1,0:T(8,128)(2,1)S(1)}, bf16[8,32,1024]{2,1,0:T(8,128)(2,1)S(1)}, u32[]{:S(2)}, u32[]{:S(2)}) collective-permute-start(bf16[8,32,1024]{2,1,0:T(8,128)(2,1)S(1)} %copy-done.19), channel_id=1, source_target_pairs={{0,3},{1,0},{2,1},{3,2},{4,7},{5,4},{6,5},{7,6},{8,11},{9,8},{10,9... | collective-permute-start | bytes 1572872 | tf_op jit(solution)/shard_map/ppermute | solution.py:103
  225.1 43.9 %collective-permute-start.12 = (bf16[8,32,1024]{2,1,0:T(8,128)(2,1)S(1)}, bf16[8,32,1024]{2,1,0:T(8,128)(2,1)S(1)}, u32[]{:S(2)}, u32[]{:S(2)}) collective-permute-start(bf16[8,32,1024]{2,1,0:T(8,128)(2,1)S(1)} %get-tuple-element.77), channel_id=1, source_target_pairs={{0,1},{1,2},{2,3},{3,0},{4,5},{5,6},{6,7},{7,4},{8,9},{9,10},{10,1... | collective-permute-start | bytes 1572872 | tf_op jit(solution)/shard_map/ppermute | solution.py:117
  226.3 75.6 %collective-permute-start.11 = (bf16[8,32,1024]{2,1,0:T(8,128)(2,1)S(1)}, bf16[8,32,1024]{2,1,0:T(8,128)(2,1)S(1)}, u32[]{:S(2)}, u32[]{:S(2)}) collective-permute-start(bf16[8,32,1024]{2,1,0:T(8,128)(2,1)S(1)} %get-tuple-element.78), channel_id=1, source_target_pairs={{0,2},{1,3},{2,0},{3,1},{4,6},{5,7},{6,4},{7,5},{8,10},{9,11},{10,... | collective-permute-start | bytes 1572872 | tf_op jit(solution)/shard_map/ppermute | solution.py:117
  235.3 66.6 %collective-permute-start.10 = (bf16[8,32,1024]{2,1,0:T(8,128)(2,1)S(1)}, bf16[8,32,1024]{2,1,0:T(8,128)(2,1)S(1)}, u32[]{:S(2)}, u32[]{:S(2)}) collective-permute-start(bf16[8,32,1024]{2,1,0:T(8,128)(2,1)S(1)} %get-tuple-element.76), channel_id=1, source_target_pairs={{0,3},{1,0},{2,1},{3,2},{4,7},{5,4},{6,5},{7,6},{8,11},{9,8},{10,9... | collective-permute-start | bytes 1572872 | tf_op jit(solution)/shard_map/ppermute | solution.py:117
  258.0 92.5 %collective-permute-start.21 = (bf16[8,4,32,1024]{3,2,0,1:T(8,128)(2,1)S(1)}, bf16[8,4,32,1024]{3,2,0,1:T(8,128)(2,1)S(1)}, u32[]{:S(2)}, u32[]{:S(2)}) collective-permute-start(bf16[8,4,32,1024]{3,2,0,1:T(8,128)(2,1)S(1)} %pad_maximum_fusion.5), channel_id=1, source_target_pairs={{0,4},{4,0},{1,5},{5,1},{2,6},{6,2},{3,7},{7,3},{8,12},{12,8},{9,1... | collective-permute-start | bytes 6291464 | tf_op jit(solution)/shard_map/ppermute | solution.py:106
  315.2 34.8 %collective-permute-start.15 = (bf16[8,32,1024]{2,1,0:T(8,128)(2,1)S(1)}, bf16[8,32,1024]{2,1,0:T(8,128)(2,1)S(1)}, u32[]{:S(2)}, u32[]{:S(2)}) collective-permute-start(bf16[8,32,1024]{2,1,0:T(8,128)(2,1)S(1)} %get-tuple-element.44), channel_id=1, source_target_pairs={{0,2},{1,3},{2,0},{3,1},{4,6},{5,7},{6,4},{7,5},{8,10},{9,11},{10,... | collective-permute-start | bytes 1572872 | tf_op jit(solution)/shard_map/ppermute | solution.py:103
  316.6 33.4 %collective-permute-start.16 = (bf16[8,32,1024]{2,1,0:T(8,128)(2,1)S(1)}, bf16[8,32,1024]{2,1,0:T(8,128)(2,1)S(1)}, u32[]{:S(2)}, u32[]{:S(2)}) collective-permute-start(bf16[8,32,1024]{2,1,0:T(8,128)(2,1)S(1)} %get-tuple-element.44), channel_id=1, source_target_pairs={{0,3},{1,0},{2,1},{3,2},{4,7},{5,4},{6,5},{7,6},{8,11},{9,8},{10,9... | collective-permute-start | bytes 1572872 | tf_op jit(solution)/shard_map/ppermute | solution.py:103
  407.6 339.0 %reduce-scatter.5.cloned.1.call-start = ((), (), s32[]{:S(2)}) async-start(), calls=%async_computation.5 | async-start | bytes 10485760 | tf_op jit(solution)/shard_map/reduce_scatter | solution.py:183
  454.3 37.2 %collective-permute-start.29 = (bf16[8,32,1024]{2,1,0:T(8,128)(2,1)S(1)}, bf16[8,32,1024]{2,1,0:T(8,128)(2,1)S(1)}, u32[]{:S(2)}, u32[]{:S(2)}) collective-permute-start(bf16[8,32,1024]{2,1,0:T(8,128)(2,1)S(1)} %get-tuple-element.72), channel_id=1, source_target_pairs={{0,2},{1,3},{2,0},{3,1},{4,6},{5,7},{6,4},{7,5},{8,10},{9,11},{10,... | collective-permute-start | bytes 1572872 | tf_op jit(solution)/shard_map/ppermute | solution.py:117
  456.6 34.9 %collective-permute-start.28 = (bf16[8,32,1024]{2,1,0:T(8,128)(2,1)S(1)}, bf16[8,32,1024]{2,1,0:T(8,128)(2,1)S(1)}, u32[]{:S(2)}, u32[]{:S(2)}) collective-permute-start(bf16[8,32,1024]{2,1,0:T(8,128)(2,1)S(1)} %get-tuple-element.70), channel_id=1, source_target_pairs={{0,3},{1,0},{2,1},{3,2},{4,7},{5,4},{6,5},{7,6},{8,11},{9,8},{10,9... | collective-permute-start | bytes 1572872 | tf_op jit(solution)/shard_map/ppermute | solution.py:117
  460.7 42.0 %collective-permute-start.26 = (bf16[8,32,1024]{2,1,0:T(8,128)(2,1)S(1)}, bf16[8,32,1024]{2,1,0:T(8,128)(2,1)S(1)}, u32[]{:S(2)}, u32[]{:S(2)}) collective-permute-start(bf16[8,32,1024]{2,1,0:T(8,128)(2,1)S(1)} %get-tuple-element.74), channel_id=1, source_target_pairs={{0,1},{1,2},{2,3},{3,0},{4,5},{5,6},{6,7},{7,4},{8,9},{9,10},{10,1... | collective-permute-start | bytes 1572872 | tf_op jit(solution)/shard_map/ppermute | solution.py:117
  462.8 72.9 %collective-permute-start.25 = (bf16[8,32,1024]{2,1,0:T(8,128)(2,1)S(1)}, bf16[8,32,1024]{2,1,0:T(8,128)(2,1)S(1)}, u32[]{:S(2)}, u32[]{:S(2)}) collective-permute-start(bf16[8,32,1024]{2,1,0:T(8,128)(2,1)S(1)} %get-tuple-element.75), channel_id=1, source_target_pairs={{0,2},{1,3},{2,0},{3,1},{4,6},{5,7},{6,4},{7,5},{8,10},{9,11},{10,... | collective-permute-start | bytes 1572872 | tf_op jit(solution)/shard_map/ppermute | solution.py:117
  468.9 66.8 %collective-permute-start.24 = (bf16[8,32,1024]{2,1,0:T(8,128)(2,1)S(1)}, bf16[8,32,1024]{2,1,0:T(8,128)(2,1)S(1)}, u32[]{:S(2)}, u32[]{:S(2)}) collective-permute-start(bf16[8,32,1024]{2,1,0:T(8,128)(2,1)S(1)} %get-tuple-element.73), channel_id=1, source_target_pairs={{0,3},{1,0},{2,1},{3,2},{4,7},{5,4},{6,5},{7,6},{8,11},{9,8},{10,9... | collective-permute-start | bytes 1572872 | tf_op jit(solution)/shard_map/ppermute | solution.py:117
  549.1 34.1 %collective-permute-start.32 = (bf16[8,32,1024]{2,1,0:T(8,128)(2,1)S(1)}, bf16[8,32,1024]{2,1,0:T(8,128)(2,1)S(1)}, u32[]{:S(2)}, u32[]{:S(2)}) collective-permute-start(bf16[8,32,1024]{2,1,0:T(8,128)(2,1)S(1)} %get-tuple-element.93), channel_id=1, source_target_pairs={{0,2},{1,3},{2,0},{3,1},{4,6},{5,7},{6,4},{7,5},{8,10},{9,11},{10,... | collective-permute-start | bytes 1572872 | tf_op jit(solution)/shard_map/ppermute | solution.py:103
  549.6 33.6 %collective-permute-start.33 = (bf16[8,32,1024]{2,1,0:T(8,128)(2,1)S(1)}, bf16[8,32,1024]{2,1,0:T(8,128)(2,1)S(1)}, u32[]{:S(2)}, u32[]{:S(2)}) collective-permute-start(bf16[8,32,1024]{2,1,0:T(8,128)(2,1)S(1)} %get-tuple-element.93), channel_id=1, source_target_pairs={{0,3},{1,0},{2,1},{3,2},{4,7},{5,4},{6,5},{7,6},{8,11},{9,8},{10,9... | collective-permute-start | bytes 1572872 | tf_op jit(solution)/shard_map/ppermute | solution.py:103
  634.9 69.4 %collective-permute-start.39 = (bf16[8,2,512,128]{2,3,1,0:T(8,128)(2,1)}, bf16[8,2,512,128]{2,3,1,0:T(8,128)(2,1)S(1)}, u32[]{:S(2)}, u32[]{:S(2)}) collective-permute-start(bf16[8,2,512,128]{2,3,1,0:T(8,128)(2,1)} %pad_maximum_fusion.8), channel_id=1, source_target_pairs={{0,8},{8,0},{16,24},{24,16},{1,9},{9,1},{17,25},{25,17},{2,10},{10... | collective-permute-start | bytes 6291464 | tf_op jit(solution)/shard_map/ppermute | solution.py:44
  638.4 67.7 %collective-permute-start.41 = (bf16[8,2,512,128]{2,3,1,0:T(8,128)(2,1)S(1)}, bf16[8,2,512,128]{2,3,1,0:T(8,128)(2,1)S(1)}, u32[]{:S(2)}, u32[]{:S(2)}) collective-permute-start(bf16[8,2,512,128]{2,3,1,0:T(8,128)(2,1)S(1)} %fusion.11), channel_id=1, source_target_pairs={{0,16},{8,24},{16,0},{24,8},{1,17},{9,25},{17,1},{25,9},{2,18},{10... | collective-permute-start | bytes 6291464 | tf_op jit(solution)/shard_map/ppermute | solution.py:44
  643.1 64.2 %collective-permute-start.38 = (bf16[8,32,1024]{2,1,0:T(8,128)(2,1)S(1)}, bf16[8,32,1024]{2,1,0:T(8,128)(2,1)S(1)}, u32[]{:S(2)}, u32[]{:S(2)}) collective-permute-start(bf16[8,32,1024]{2,1,0:T(8,128)(2,1)S(1)} %get-tuple-element.68), channel_id=1, source_target_pairs={{0,1},{1,2},{2,3},{3,0},{4,5},{5,6},{6,7},{7,4},{8,9},{9,10},{10,1... | collective-permute-start | bytes 1572872 | tf_op jit(solution)/shard_map/ppermute | solution.py:117
  654.4 52.9 %collective-permute-start.37 = (bf16[8,32,1024]{2,1,0:T(8,128)(2,1)S(1)}, bf16[8,32,1024]{2,1,0:T(8,128)(2,1)S(1)}, u32[]{:S(2)}, u32[]{:S(2)}) collective-permute-start(bf16[8,32,1024]{2,1,0:T(8,128)(2,1)S(1)} %get-tuple-element.69), channel_id=1, source_target_pairs={{0,2},{1,3},{2,0},{3,1},{4,6},{5,7},{6,4},{7,5},{8,10},{9,11},{10,... | collective-permute-start | bytes 1572872 | tf_op jit(solution)/shard_map/ppermute | solution.py:117
  657.3 50.0 %collective-permute-start.36 = (bf16[8,32,1024]{2,1,0:T(8,128)(2,1)S(1)}, bf16[8,32,1024]{2,1,0:T(8,128)(2,1)S(1)}, u32[]{:S(2)}, u32[]{:S(2)}) collective-permute-start(bf16[8,32,1024]{2,1,0:T(8,128)(2,1)S(1)} %get-tuple-element.67), channel_id=1, source_target_pairs={{0,3},{1,0},{2,1},{3,2},{4,7},{5,4},{6,5},{7,6},{8,11},{9,8},{10,9... | collective-permute-start | bytes 1572872 | tf_op jit(solution)/shard_map/ppermute | solution.py:117
  735.9 34.5 %collective-permute-start.44 = (bf16[8,2,128,512]{2,3,1,0:T(8,128)(2,1)}, bf16[8,2,128,512]{2,3,1,0:T(8,128)(2,1)}, u32[]{:S(2)}, u32[]{:S(2)}) collective-permute-start(bf16[8,2,128,512]{2,3,1,0:T(8,128)(2,1)} %constant_dynamic-slice_fusion.6), channel_id=1, source_target_pairs={{0,4},{4,0},{1,5},{5,1},{2,6},{6,2},{3,7},{7,3},{8,12},{12,8},{9,1... | collective-permute-start | bytes 6291464 | tf_op jit(solution)/shard_map/ppermute | solution.py:98
  (74 other events, 776.8 us)
Sparse Core Ops, SparseCore 0:
  76.6 175.0 all-gather.2
  253.5 92.1 all-gather.4
  407.7 163.9 reduce-scatter.2
  574.6 107.7 reduce-scatter.4

commit v3 on v1

--- a/solution.py
+++ b/solution.py
@@ -13,6 +13,7 @@
 BF = jnp.bfloat16
 F32 = jnp.float32
 SWAP = ((0, 1), (1, 0))
+TILE = 16
 
 
 def norm_back(upstream, hval, rstat, gain):
@@ -186,36 +187,267 @@
     return shards
 
 
+def make_step_shards(count, lanes):
+
+    def swap(block, k):
+        return lax.ppermute(block, "dp", [(i, i ^ k) for i in range(count)])
+
+    def exchange(blocks):
+        return [blocks[0]] + [swap(blocks[k], k) for k in range(1, count)]
+
+    def up(block, senders):
+        return lax.ppermute(block, "tensor", [(i, i + 1) for i in range(senders)])
+
+    def down(block, senders):
+        return lax.ppermute(block, "tensor", [(i, i - 1) for i in range(lanes - senders, lanes)])
+
+    def collect(rows):
+        below, above = [rows], [rows]
+        for k in range(1, lanes):
+            below.append(lax.ppermute(
+                below[-1], "tensor", [(i, i + 1) for i in range(k - 1, lanes - 1)]))
+            above.append(lax.ppermute(
+                above[-1], "tensor", [(i, i - 1) for i in range(1, lanes - k + 1)]))
+        parts = [rows] + [above[k] + below[lanes - k] for k in range(1, lanes)]
+        return jnp.stack(parts, axis=1).reshape(-1, rows.shape[-1])
+
+    def deal(partial):
+        slots = partial.reshape(count, lanes, -1, partial.shape[-1])
+        rising, falling = 0.0, 0.0
+        for r in range(1, lanes):
+            rising = up((slots[:, lanes - r] + rising).astype(BF), r).astype(F32)
+            falling = down((slots[:, r] + falling).astype(BF), r).astype(F32)
+        return slots[:, 0] + rising + falling
+
+    def shards(
+        layer_in, text_mask, w_qkv, w_out, w_gate_up, w_down, norm_gains, pad_row, out_grad
+    ):
+        me = lax.axis_index("dp")
+        steps, local, width = layer_in.shape
+        block = width // count
+
+        def pick(array, k):
+            return lax.dynamic_index_in_dim(array, me ^ k, 0, keepdims=False)
+
+        def relative(array):
+            return jnp.concatenate(
+                [
+                    lax.dynamic_slice_in_dim(array, (me ^ r) * block, block, array.ndim - 1)
+                    for r in range(count)
+                ],
+                axis=-1,
+            )
+
+        def place(blocks):
+            whole = jnp.zeros((count,) + blocks[0].shape, blocks[0].dtype)
+            for k in range(count):
+                whole = lax.dynamic_update_index_in_dim(whole, blocks[k], me ^ k, 0)
+            return whole
+
+        def tag(rows, *vectors):
+            line = jnp.concatenate([v.astype(rows.dtype) for v in vectors])
+            return jnp.concatenate(
+                [rows, jnp.pad(line[None], ((0, TILE - 1), (0, width - line.shape[0])))]
+            )
+
+        small = jnp.concatenate([norm_gains, pad_row[None]], axis=0).astype(BF).reshape(-1)
+        hello = exchange([tag(pick(layer_in, k), small, text_mask) for k in range(count)])
+        rows_in = relative(jnp.stack([h[:local] for h in hello])).astype(F32)
+        notes = jnp.stack([h[local] for h in hello]).astype(F32)
+        small = jnp.swapaxes(notes[:, : 3 * block].reshape(count, 3, block), 0, 1)
+        gain_one, gain_two, pad_vec = small.reshape(3, width)
+        padded = jnp.where(me == 0, 1.0 - notes[:, 3 * block : 3 * block + local], 0.0)[..., None]
+        h0 = rows_in + padded * pad_vec
+        r1 = lax.rsqrt(jnp.mean(h0 * h0, axis=-1, keepdims=True) + EPS)
+        n1 = (h0 * r1 * gain_one).astype(BF)
+        n1_all = collect(n1)
+
+        def attn_block(k):
+            parts = [pick(w_qkv, k)[j] for j in range(3)] + [pick(w_out, k).T]
+            return jnp.concatenate(parts, axis=1).astype(BF)
+
+        w_attn = jnp.concatenate(exchange([attn_block(k) for k in range(count)]), axis=0)
+        cols = w_attn.shape[1] // 4
+        w_in, wout_t = w_attn[:, : 3 * cols], w_attn[:, 3 * cols :]
+        qkv = jnp.dot(n1_all, w_in, preferred_element_type=F32).astype(BF)
+
+        def frame_split(array):
+            return jnp.stack(exchange(list(array.reshape(count, -1, array.shape[-1]))))
+
+        def frame_join(array):
+            return jnp.concatenate(exchange(list(array)), axis=0)
+
+        qkv = frame_split(qkv)
+        frames = qkv.shape[1]
+        heads = cols // HEAD
+        scale = 1.0 / math.sqrt(HEAD)
+        query = qkv[..., :cols].reshape(steps, frames, heads, HEAD)
+        keyv = qkv[..., cols : 2 * cols].reshape(steps, frames, heads, HEAD)
+        value = qkv[..., 2 * cols :].reshape(steps, frames, heads, HEAD)
+        order = jnp.arange(steps) ^ me
+        causal = order[:, None] >= order[None, :]
+
+        def score_of(qv, kv):
+            raw = jnp.einsum("sfhe,tfhe->fhst", qv, kv, preferred_element_type=F32) * scale
+            return jnp.where(causal, raw, -1e30)
+
+        scores = score_of(query, keyv)
+        top = jnp.max(scores, axis=-1, keepdims=True)
+        expo = jnp.exp(scores - top)
+        total = jnp.sum(expo, axis=-1, keepdims=True)
+        lse = top + jnp.log(total)
+        probs_low = (expo / total).astype(BF)
+        mixed = jnp.einsum("fhst,tfhe->sfhe", probs_low, value, preferred_element_type=F32)
+        mixed_all = frame_join(mixed.reshape(steps, frames, cols).astype(BF))
+
+        w_gate_up, w_down, mixed_all = lax.optimization_barrier((w_gate_up, w_down, mixed_all))
+
+        def gu_block(k):
+            pair = pick(w_gate_up, k)
+            return jnp.concatenate([pair[0], pair[1]], axis=1).astype(BF)
+
+        wgu = jnp.concatenate(exchange([gu_block(k) for k in range(count)]), axis=0)
+        wdown = jnp.concatenate(
+            exchange([pick(w_down, k).astype(BF) for k in range(count)]), axis=1
+        )
+        out_grad, _ = lax.optimization_barrier((out_grad, n1_all))
+        grad = relative(jnp.stack(exchange([pick(out_grad, k) for k in range(count)])))
+        grad_all = collect(grad)
+
+        attn = deal(jnp.einsum("fe,de->fd", mixed_all, wout_t, preferred_element_type=F32))
+        h1 = h0 + attn
+        r2 = lax.rsqrt(jnp.mean(h1 * h1, axis=-1, keepdims=True) + EPS)
+        n2 = (h1 * r2 * gain_two).astype(BF)
+        n2_all = collect(n2)
+        gate_up = jnp.dot(n2_all, wgu, preferred_element_type=F32)
+        hid_width = gate_up.shape[1] // 2
+        gate, upval = gate_up[:, :hid_width], gate_up[:, hid_width:]
+        sigma = jax.nn.sigmoid(gate)
+        silu_val = gate * sigma
+        hidden = (silu_val * upval).astype(BF)
+        d_hidden = jnp.einsum("fd,kd->fk", grad_all, wdown, preferred_element_type=F32)
+        d_gate = d_hidden * upval * (sigma * (1.0 + gate * (1.0 - sigma)))
+        d_up = d_hidden * silu_val
+        d_gu = jnp.concatenate([d_gate, d_up], axis=1).astype(BF)
+        dn2 = deal(jnp.einsum("fk,dk->fd", d_gu, wgu, preferred_element_type=F32))
+
+        d_down = jnp.einsum("fk,fd->kd", hidden, grad_all, preferred_element_type=F32).astype(BF)
+        g_down = exchange([d_down[:, r * block : (r + 1) * block] for r in range(count)])
+        d_gate_up = jnp.einsum("fd,fk->dk", n2_all, d_gu, preferred_element_type=F32).astype(BF)
+        g_gate_up = exchange(list(d_gate_up.reshape(count, block, -1)))
+
+        dh_norm2, dgain_two = norm_back(dn2, h1, r2, gain_two)
+        dh1 = grad.astype(F32) + dh_norm2
+        dh1_all = collect(dh1.astype(BF))
+        d_mixed = jnp.dot(dh1_all, wout_t, preferred_element_type=F32).astype(BF)
+        d_mixed = frame_split(d_mixed).reshape(steps, frames, heads, HEAD)
+
+        hidden, _ = lax.optimization_barrier((hidden, dh1_all))
+        ffout = deal(jnp.dot(hidden, wdown, preferred_element_type=F32))
+        layer_out = relative((h1 + ffout).astype(BF))
+        layer_out = place(exchange(list(layer_out)))
+
+        probs = jnp.exp(score_of(query, keyv) - lse)
+        d_probs = jnp.einsum("sfhe,tfhe->fhst", d_mixed, value, preferred_element_type=F32)
+        d_value = jnp.einsum("fhst,sfhe->tfhe", probs_low, d_mixed, preferred_element_type=F32)
+        d_scores = probs * (d_probs - jnp.sum(probs * d_probs, axis=-1, keepdims=True))
+        d_query = (
+            jnp.einsum("fhst,tfhe->sfhe", d_scores, keyv.astype(F32), precision=HIGH) * scale
+        )
+        d_key = (
+            jnp.einsum("fhst,sfhe->tfhe", d_scores, query.astype(F32), precision=HIGH) * scale
+        )
+        d_qkv = jnp.concatenate(
+            [a.reshape(steps, frames, cols).astype(BF) for a in (d_query, d_key, d_value)],
+            axis=-1,
+        )
+        d_qkv = frame_join(d_qkv)
+        dn1 = deal(jnp.einsum("fe,de->fd", d_qkv, w_in, preferred_element_type=F32))
+        d_attn = jnp.concatenate(
+            [
+                jnp.einsum("fd,fe->de", n1_all, d_qkv, preferred_element_type=F32).astype(BF),
+                jnp.einsum("fd,fe->de", dh1_all, mixed_all, preferred_element_type=F32).astype(BF),
+            ],
+            axis=1,
+        )
+        g_attn = exchange(list(d_attn.reshape(count, block, -1)))
+
+        dh_norm1, dgain_one = norm_back(dn1, h0, r1, gain_one)
+        dh0 = dh1 + dh_norm1
+        d_pad = jnp.sum(dh0 * padded, axis=(0, 1))
+        sums = jnp.stack([dgain_one, dgain_two, d_pad]).reshape(3, count, block)
+        high = sums.astype(BF)
+        rest = (sums - high.astype(F32)).astype(BF)
+        input_grad = relative(dh0.astype(BF))
+        last = exchange(
+            [
+                tag(input_grad[k], high[:, k].reshape(-1), rest[:, k].reshape(-1))
+                for k in range(count)
+            ]
+        )
+        input_grad = place([h[:local] for h in last])
+        sums = jnp.stack([h[local] for h in last]).astype(F32)
+        sums = jnp.sum(sums, axis=0)[: 6 * block].reshape(2, 3, block)
+        sums = sums[0] + sums[1]
+        g_small = sums
+        for k in range(1, lanes):
+            around = [(i, (i + k) % lanes) for i in range(lanes)]
+            g_small = g_small + lax.ppermute(sums, "tensor", around)
+
+        g_down = place([g.astype(F32) for g in g_down])
+        g_gate_up = place(
+            [
+                jnp.stack([g[:, :hid_width], g[:, hid_width:]]).astype(F32)
+                for g in g_gate_up
+            ]
+        )
+        g_qkv = place(
+            [
+                jnp.stack([g[:, j * cols : (j + 1) * cols] for j in range(3)]).astype(F32)
+                for g in g_attn
+            ]
+        )
+        g_out = place([g[:, 3 * cols :].T.astype(F32) for g in g_attn])
+        return (layer_out, input_grad, g_qkv, g_out, g_gate_up, g_down, g_small[0:2], g_small[2])
+
+    return shards
+
+
+def spread(body, mesh, dp):
+    rows = dp + ("tensor",)
+    weights = (
+        P(None, None, dp, "tensor"),
+        P(None, "tensor", dp),
+        P(None, None, dp, "tensor"),
+        P(None, "tensor", dp),
+        P(None, dp),
+        P(dp),
+    )
+    return jax.shard_map(
+        body,
+        mesh=mesh,
+        in_specs=(P(None, rows, None), P(rows)) + weights + (P(None, rows, None),),
+        out_specs=(P(None, rows, None), P(None, rows, None)) + weights,
+        check_vma=False,
+    )
+
+
 def solution(mesh):
     dp_size, tensor_size = mesh.shape["dp"], mesh.shape["tensor"]
-    inner = Mesh(
-        np.asarray(mesh.devices).reshape(dp_size // 2, 2, tensor_size), ("xy", "core", "tensor")
-    )
-    dp = ("xy", "core")
-    rows = ("xy", "core", "tensor")
-    return jax.shard_map(
-        make_shards(tensor_size),
-        mesh=inner,
-        in_specs=(
-            P(None, rows, None),
-            P(rows),
-            P(None, None, dp, "tensor"),
-            P(None, "tensor", dp),
-            P(None, None, dp, "tensor"),
-            P(None, "tensor", dp),
-            P(None, dp),
-            P(dp),
-            P(None, rows, None),
-        ),
-        out_specs=(
-            P(None, rows, None),
-            P(None, rows, None),
-            P(None, None, dp, "tensor"),
-            P(None, "tensor", dp),
-            P(None, None, dp, "tensor"),
-            P(None, "tensor", dp),
-            P(None, dp),
-            P(dp),
-        ),
-        check_vma=False,
-    )
+
+    def layer(layer_in, *others):
+        steps, frames, width = layer_in.shape
+        local = frames // (dp_size * tensor_size)
+        block = width // dp_size
+        fits = 6 * block <= width and 3 * block + local <= width
+        if steps == dp_size and dp_size & (dp_size - 1) == 0 and fits:
+            body, over, dp = make_step_shards(dp_size, tensor_size), mesh, ("dp",)
+        else:
+            over = Mesh(
+                np.asarray(mesh.devices).reshape(dp_size // 2, 2, tensor_size),
+                ("xy", "core", "tensor"),
+            )
+            body, dp = make_shards(tensor_size), ("xy", "core")
+        return spread(body, over, dp)(layer_in, *others)
+
+    return layer

time: 793 us -> 743 us (0.937)
  starting transfers between devices: 82 us -> 184 us
  matrix products: 114 us -> 49.3 us
  blocking collectives: 50.4 us -> 0 us
  other arithmetic: 59.5 us -> 40.3 us
  waiting for transfers between devices: 371 us -> 353 us
  between operations: 15.3 us -> 4.21 us
  local copies, waits for them, and re-layouts: 95.4 us -> 104 us
    ppermute x38 -> x149, starting transfers between devices: 81.6 us -> 184 us  [the longest x98 89 us: swap(): return lax.ppermute(block, 'dp', [(i, i ^ k) for i in range(count)])]
    ppermute x38 -> x149, waiting for transfers between devices: 275 us -> 353 us  [the longest x98 210 us: swap(): return lax.ppermute(block, 'dp', [(i, i ^ k) for i in range(count)])]
    all_gather x3 -> x0, waiting for transfers between devices: 64.5 us -> none  [the longest x1 61.9 us: shards(): lax.all_gather(trade(core, w_down.astype(BF), 1, 2), 'xy', axis=2, tiled=...]
    dot_general x12, matrix products: 94 us -> 35.3 us  [the longest x1 6.46 us: shards(): jnp.einsum('fd,fk->dk', n2_all, d_gu, preferred_element_type=F32).astype(BF)]
    psum x1 -> x0, blocking collectives: 39.4 us -> none  [shards(): small_grad = lax.psum(small_grad, ('xy', 'core', 'tensor'))]
    another operation x6 -> x52, local copies, waits for them, and re-layouts: 9.82 us -> 41.9 us  [the longest x12 20.9 us: frame_split(): return jnp.stack(exchange(list(array.reshape(count, -1, array.shape[-1]))))]
    reduce_scatter x3 -> x0, waiting for transfers between devices: 30.8 us -> none  [the longest x1 30.7 us: shards(): r_attn = lax.psum_scatter(d_attn, 'xy', scatter_dimension=2, tiled=True)]
    unnamed x111 -> x218, local copies, waits for them, and re-layouts: 40.5 us -> 21.6 us
  transfers between devices with their start and end apart: 44 -> 149, of which waited for: 24 -> 66; matrix products, arithmetic and copies ran while one was open for 27% -> 18% of each run, Pallas kernels for 0% -> 0%
where the time goes in v3:
time: 743 us; the launch traced here: 734 us
  waiting for transfers between devices  353 us (48%)
  starting transfers between devices  184 us (25%)
  local copies, waits for them, and re-layouts  104 us (14%)
  matrix products  49.3 us (7%)
  other arithmetic  40.3 us (5%)
    ppermute x98, waiting for transfers between devices, swap(): return lax.ppermute(block, 'dp', [(i, i ^ k) for i in range(count)])  210 us
    ppermute x12, waiting for transfers between devices, collect(): lax.ppermute(above[-1], 'tensor', [(i, i - 1) for i in range(1, lanes - k...  105 us
    ppermute x98, starting transfers between devices, swap(): return lax.ppermute(block, 'dp', [(i, i ^ k) for i in range(count)])  89 us
    ppermute x12, starting transfers between devices, up(): return lax.ppermute(block, 'tensor', [(i, i + 1) for i in range(senders)])  41.7 us
    unnamed x218, local copies, waits for them, and re-layouts  21.6 us
    another operation x12, local copies, waits for them, and re-layouts, frame_split(): return jnp.stack(exchange(list(array.reshape(count, -1, array.shape[-1]))))  20.9 us
    ppermute x12, starting transfers between devices, collect(): lax.ppermute(below[-1], 'tensor', [(i, i + 1) for i in range(k - 1, lanes...  17.3 us
    ppermute x12, waiting for transfers between devices, up(): return lax.ppermute(block, 'tensor', [(i, i + 1) for i in range(senders)])  16.9 us
  transfers between devices with their start and end apart: 149, of which 66 were waited for; matrix products, arithmetic and copies ran while one was open for 18% of the time, Pallas kernels for 0%

profile of v3, /device:TPU:0, one launch (start us, length us, event | category | flops | bytes accessed | tf_op | source)
XLA Modules:
  0.0 734.3 jit_solution(718349863254350745)
XLA Ops:
  16.0 7.0 collective-permute-done.1
  44.8 8.3 %collective-permute-done.8 = bf16[8,32,1024]{2,1,0:T(8,128)(2,1)S(1)} collective-permute-done((bf16[8,32,1024]{2,1,0:T(8,128)(2,1)S(1)}, bf16[8,32,1024]{2,1,0:T(8,128)(2,1)S(1)}, u32[]{:S(2)}, u32[]{:S(2)}) %collective-permute-start.8) | collective-permute-done | bytes 524320 | tf_op jit(solution)/shard_map/ppermute | solution.py:207
  61.0 8.5 %collective-permute-done.16 = bf16[128,1024]{0,1:T(8,128)(2,1)S(1)} collective-permute-done((bf16[128,1024]{0,1:T(8,128)(2,1)S(1)}, bf16[128,1024]{0,1:T(8,128)(2,1)S(1)}, u32[]{:S(2)}, u32[]{:S(2)}) %collective-permute-start.16) | collective-permute-done | bytes 262176 | tf_op jit(solution)/shard_map/ppermute | solution.py:193
  71.6 8.3 %collective-permute-done.17 = bf16[128,1024]{0,1:T(8,128)(2,1)S(1)} collective-permute-done((bf16[128,1024]{0,1:T(8,128)(2,1)S(1)}, bf16[128,1024]{0,1:T(8,128)(2,1)S(1)}, u32[]{:S(2)}, u32[]{:S(2)}) %collective-permute-start.17) | collective-permute-done | bytes 262176 | tf_op jit(solution)/shard_map/ppermute | solution.py:193
  82.1 16.6 %collective-permute-done.12 = bf16[8,32,1024]{2,1,0:T(8,128)(2,1)S(1)} collective-permute-done((bf16[8,32,1024]{2,1,0:T(8,128)(2,1)S(1)}, bf16[8,32,1024]{2,1,0:T(8,128)(2,1)S(1)}, u32[]{:S(2)}, u32[]{:S(2)}) %collective-permute-start.12) | collective-permute-done | bytes 524320 | tf_op jit(solution)/shard_map/ppermute | solution.py:209
  107.1 8.1 %collective-permute-done.54 = bf16[32,1024]{1,0:T(8,128)(2,1)S(1)} collective-permute-done((bf16[32,1024]{1,0:T(8,128)(2,1)S(1)}, bf16[32,1024]{1,0:T(8,128)(2,1)S(1)}, u32[]{:S(2)}, u32[]{:S(2)}) %collective-permute-start.54) | collective-permute-done | bytes 65568 | tf_op jit(solution)/shard_map/ppermute | solution.py:193
  146.6 5.2 collective-permute-done.25
  213.2 5.2 collective-permute-done.71
  227.2 7.9 %collective-permute-done.47 = bf16[128,2048]{1,0:T(8,128)(2,1)S(1)} collective-permute-done((bf16[128,2048]{1,0:T(8,128)(2,1)S(1)}, bf16[128,2048]{1,0:T(8,128)(2,1)S(1)}, u32[]{:S(2)}, u32[]{:S(2)}) %collective-permute-start.47) | collective-permute-done | bytes 524320 | tf_op jit(solution)/shard_map/ppermute | solution.py:193
  242.8 5.2 collective-permute-start.36
  260.8 5.1 collective-permute-done.39
  266.6 5.3 collective-permute-start.41
  271.9 9.8 %collective-permute-done.51 = bf16[128,2048]{1,0:T(8,128)(2,1)S(1)} collective-permute-done((bf16[128,2048]{1,0:T(8,128)(2,1)S(1)}, bf16[128,2048]{1,0:T(8,128)(2,1)S(1)}, u32[]{:S(2)}, u32[]{:S(2)}) %collective-permute-start.51) | collective-permute-done | bytes 524320 | tf_op jit(solution)/shard_map/ppermute | solution.py:193
  285.2 23.6 %collective-permute-done.40 = bf16[8,32,1024]{2,1,0:T(8,128)(2,1)S(1)} collective-permute-done((bf16[8,32,1024]{2,1,0:T(8,128)(2,1)S(1)}, bf16[8,32,1024]{2,1,0:T(8,128)(2,1)S(1)}, u32[]{:S(2)}, u32[]{:S(2)}) %collective-permute-start.40) | collective-permute-done | bytes 524320 | tf_op jit(solution)/shard_map/ppermute | solution.py:209
  312.6 11.2 %collective-permute-done.44 = bf16[8,32,1024]{2,1,0:T(8,128)(2,1)S(1)} collective-permute-done((bf16[8,32,1024]{2,1,0:T(8,128)(2,1)S(1)}, bf16[8,32,1024]{2,1,0:T(8,128)(2,1)S(1)}, u32[]{:S(2)}, u32[]{:S(2)}) %collective-permute-start.44) | collective-permute-done | bytes 524320 | tf_op jit(solution)/shard_map/ppermute | solution.py:209
  325.6 12.2 %collective-permute-done.45 = bf16[8,32,1024]{2,1,0:T(8,128)(2,1)S(1)} collective-permute-done((bf16[8,32,1024]{2,1,0:T(8,128)(2,1)S(1)}, bf16[8,32,1024]{2,1,0:T(8,128)(2,1)S(1)}, u32[]{:S(2)}, u32[]{:S(2)}) %collective-permute-start.45) | collective-permute-done | bytes 524320 | tf_op jit(solution)/shard_map/ppermute | solution.py:209
  342.9 5.5 multiply_convert_fusion.1
  348.4 6.1 fusion.1
  354.5 6.5 convolution_convert_fusion
  400.4 7.4 %collective-permute-start.75 = (bf16[8,32,1024]{2,1,0:T(8,128)(2,1)S(1)}, bf16[8,32,1024]{2,1,0:T(8,128)(2,1)S(1)}, u32[]{:S(2)}, u32[]{:S(2)}) collective-permute-start(bf16[8,32,1024]{2,1,0:T(8,128)(2,1)S(1)} %get-tuple-element.59), channel_id=1, source_target_pairs={{0,1},{1,2},{2,3},{4,5},{5,6},{6,7},{8,9},{9,10},{10,11},{12,13},{... | collective-permute-start | bytes 1572872 | tf_op jit(solution)/shard_map/ppermute | solution.py:199
  409.2 9.2 %collective-permute-done.134 = bf16[128,2048]{1,0:T(8,128)(2,1)S(1)} collective-permute-done((bf16[128,2048]{1,0:T(8,128)(2,1)S(1)}, bf16[128,2048]{1,0:T(8,128)(2,1)S(1)}, u32[]{:S(2)}, u32[]{:S(2)}) %collective-permute-start.134) | collective-permute-done | bytes 524320 | tf_op jit(solution)/shard_map/ppermute | solution.py:193
  427.2 16.3 %collective-permute-done.136 = bf16[128,2048]{1,0:T(8,128)(2,1)S(1)} collective-permute-done((bf16[128,2048]{1,0:T(8,128)(2,1)S(1)}, bf16[128,2048]{1,0:T(8,128)(2,1)S(1)}, u32[]{:S(2)}, u32[]{:S(2)}) %collective-permute-start.136) | collective-permute-done | bytes 524320 | tf_op jit(solution)/shard_map/ppermute | solution.py:193
  446.1 13.5 %collective-permute-done.79 = bf16[8,32,1024]{2,1,0:T(8,128)(2,1)S(1)} collective-permute-done((bf16[8,32,1024]{2,1,0:T(8,128)(2,1)S(1)}, bf16[8,32,1024]{2,1,0:T(8,128)(2,1)S(1)}, u32[]{:S(2)}, u32[]{:S(2)}) %collective-permute-start.79) | collective-permute-done | bytes 524320 | tf_op jit(solution)/shard_map/ppermute | solution.py:209
  462.0 13.8 %collective-permute-done.83 = bf16[8,32,1024]{2,1,0:T(8,128)(2,1)S(1)} collective-permute-done((bf16[8,32,1024]{2,1,0:T(8,128)(2,1)S(1)}, bf16[8,32,1024]{2,1,0:T(8,128)(2,1)S(1)}, u32[]{:S(2)}, u32[]{:S(2)}) %collective-permute-start.83) | collective-permute-done | bytes 524320 | tf_op jit(solution)/shard_map/ppermute | solution.py:209
  477.3 13.9 %collective-permute-done.84 = bf16[8,32,1024]{2,1,0:T(8,128)(2,1)S(1)} collective-permute-done((bf16[8,32,1024]{2,1,0:T(8,128)(2,1)S(1)}, bf16[8,32,1024]{2,1,0:T(8,128)(2,1)S(1)}, u32[]{:S(2)}, u32[]{:S(2)}) %collective-permute-start.84) | collective-permute-done | bytes 524320 | tf_op jit(solution)/shard_map/ppermute | solution.py:209
  524.4 6.8 stack.396
  562.7 5.0 collective-permute-done.110
  588.0 5.1 collective-permute-done.130
  600.1 6.9 collective-permute-done.128
  612.1 8.7 %collective-permute-done.127 = bf16[128,1024]{0,1:T(8,128)(2,1)S(1)} collective-permute-done((bf16[128,1024]{0,1:T(8,128)(2,1)}, bf16[128,1024]{0,1:T(8,128)(2,1)S(1)}, u32[]{:S(2)}, u32[]{:S(2)}) %collective-permute-start.127) | collective-permute-done | bytes 262176 | tf_op jit(solution)/shard_map/ppermute | solution.py:193
  658.6 8.4 %collective-permute-start.114 = (bf16[8,32,1024]{2,1,0:T(8,128)(2,1)S(1)}, bf16[8,32,1024]{2,1,0:T(8,128)(2,1)S(1)}, u32[]{:S(2)}, u32[]{:S(2)}) collective-permute-start(bf16[8,32,1024]{2,1,0:T(8,128)(2,1)S(1)} %get-tuple-element.47), channel_id=1, source_target_pairs={{0,1},{1,2},{2,3},{4,5},{5,6},{6,7},{8,9},{9,10},{10,11},{12,13},{... | collective-permute-start | bytes 1572872 | tf_op jit(solution)/shard_map/ppermute | solution.py:199
  673.7 7.0 collective-permute-done.114
  (779 shorter events, 442.4 us)
Async XLA Ops:
  3.8 50.3 %collective-permute-start.13 = (bf16[128,1024]{0,1:T(8,128)(2,1)S(1)}, bf16[128,1024]{0,1:T(8,128)(2,1)S(1)}, u32[]{:S(2)}, u32[]{:S(2)}) collective-permute-start(bf16[128,1024]{0,1:T(8,128)(2,1)S(1)} %pad_maximum_fusion.22), channel_id=1, source_target_pairs={{0,4},{4,0},{8,12},{12,8},{16,20},{20,16},{24,28},{28,24},{1,5},{5... | collective-permute-start | bytes 786440 | tf_op jit(solution)/shard_map/ppermute | solution.py:193
  5.3 51.5 %collective-permute-start.14 = (bf16[128,1024]{0,1:T(8,128)(2,1)}, bf16[128,1024]{0,1:T(8,128)(2,1)S(1)}, u32[]{:S(2)}, u32[]{:S(2)}) collective-permute-start(bf16[128,1024]{0,1:T(8,128)(2,1)} %pad_maximum_fusion.23), channel_id=1, source_target_pairs={{0,8},{4,12},{8,0},{12,4},{16,24},{20,28},{24,16},{28,20},{1,9},{5... | collective-permute-start | bytes 786440 | tf_op jit(solution)/shard_map/ppermute | solution.py:193
  8.7 48.3 %collective-permute-start.15 = (bf16[128,1024]{0,1:T(8,128)(2,1)}, bf16[128,1024]{0,1:T(8,128)(2,1)S(1)}, u32[]{:S(2)}, u32[]{:S(2)}) collective-permute-start(bf16[128,1024]{0,1:T(8,128)(2,1)} %pad_maximum_fusion.24), channel_id=1, source_target_pairs={{0,12},{4,8},{8,4},{12,0},{16,28},{20,24},{24,20},{28,16},{1,13},{... | collective-permute-start | bytes 786440 | tf_op jit(solution)/shard_map/ppermute | solution.py:193
  56.8 23.1 %collective-permute-start.17 = (bf16[128,1024]{0,1:T(8,128)(2,1)S(1)}, bf16[128,1024]{0,1:T(8,128)(2,1)S(1)}, u32[]{:S(2)}, u32[]{:S(2)}) collective-permute-start(bf16[128,1024]{0,1:T(8,128)(2,1)S(1)} %pad_maximum_fusion.26), channel_id=1, source_target_pairs={{0,20},{4,16},{8,28},{12,24},{16,4},{20,0},{24,12},{28,8},{1,21},{... | collective-permute-start | bytes 786440 | tf_op jit(solution)/shard_map/ppermute | solution.py:193
  57.0 23.0 %collective-permute-start.18 = (bf16[128,1024]{0,1:T(8,128)(2,1)S(1)}, bf16[128,1024]{0,1:T(8,128)(2,1)S(1)}, u32[]{:S(2)}, u32[]{:S(2)}) collective-permute-start(bf16[128,1024]{0,1:T(8,128)(2,1)S(1)} %pad_maximum_fusion.27), channel_id=1, source_target_pairs={{0,24},{4,28},{8,16},{12,20},{16,8},{20,12},{24,0},{28,4},{1,25},{... | collective-permute-start | bytes 786440 | tf_op jit(solution)/shard_map/ppermute | solution.py:193
  102.2 41.0 %collective-permute-start.20 = (bf16[128,768]{0,1:T(8,128)(2,1)S(1)}, bf16[128,768]{0,1:T(8,128)(2,1)S(1)}, u32[]{:S(2)}, u32[]{:S(2)}) collective-permute-start(bf16[128,768]{0,1:T(8,128)(2,1)S(1)} %get-tuple-element.119), channel_id=1, source_target_pairs={{0,4},{4,0},{8,12},{12,8},{16,20},{20,16},{24,28},{28,24},{1,5},{5... | collective-permute-start | bytes 589832 | tf_op jit(solution)/shard_map/ppermute | solution.py:193
  102.7 41.7 %collective-permute-start.21 = (bf16[128,768]{0,1:T(8,128)(2,1)S(1)}, bf16[128,768]{0,1:T(8,128)(2,1)S(1)}, u32[]{:S(2)}, u32[]{:S(2)}) collective-permute-start(bf16[128,768]{0,1:T(8,128)(2,1)S(1)} %get-tuple-element.118), channel_id=1, source_target_pairs={{0,8},{4,12},{8,0},{12,4},{16,24},{20,28},{24,16},{28,20},{1,9},{5... | collective-permute-start | bytes 589832 | tf_op jit(solution)/shard_map/ppermute | solution.py:193
  104.2 42.2 %collective-permute-start.22 = (bf16[128,768]{0,1:T(8,128)(2,1)S(1)}, bf16[128,768]{0,1:T(8,128)(2,1)S(1)}, u32[]{:S(2)}, u32[]{:S(2)}) collective-permute-start(bf16[128,768]{0,1:T(8,128)(2,1)S(1)} %get-tuple-element.117), channel_id=1, source_target_pairs={{0,12},{4,8},{8,4},{12,0},{16,28},{20,24},{24,20},{28,16},{1,13},{... | collective-permute-start | bytes 589832 | tf_op jit(solution)/shard_map/ppermute | solution.py:193
  104.2 42.3 %collective-permute-start.23 = (bf16[128,768]{0,1:T(8,128)(2,1)S(1)}, bf16[128,768]{0,1:T(8,128)(2,1)S(1)}, u32[]{:S(2)}, u32[]{:S(2)}) collective-permute-start(bf16[128,768]{0,1:T(8,128)(2,1)S(1)} %get-tuple-element.116), channel_id=1, source_target_pairs={{0,16},{4,20},{8,24},{12,28},{16,0},{20,4},{24,8},{28,12},{1,17},{... | collective-permute-start | bytes 589832 | tf_op jit(solution)/shard_map/ppermute | solution.py:193
  210.4 25.1 %collective-permute-start.61 = (bf16[8,32,1024]{2,1,0:T(8,128)(2,1)}, bf16[8,32,1024]{2,1,0:T(8,128)(2,1)S(1)}, u32[]{:S(2)}, u32[]{:S(2)}) collective-permute-start(bf16[8,32,1024]{2,1,0:T(8,128)(2,1)} %constant_dynamic-update-slice_fusion.62), channel_id=1, source_target_pairs={{0,1},{1,2},{2,3},{4,5},{5,6},{6,7},{8,9},{9,10},{10,11},{12,13},{... | collective-permute-start | bytes 1572872 | tf_op jit(solution)/shard_map/ppermute | solution.py:207
  255.3 26.4 %collective-permute-start.52 = (bf16[128,2048]{1,0:T(8,128)(2,1)S(1)}, bf16[128,2048]{1,0:T(8,128)(2,1)S(1)}, u32[]{:S(2)}, u32[]{:S(2)}) collective-permute-start(bf16[128,2048]{1,0:T(8,128)(2,1)S(1)} %pad_maximum_fusion.14), channel_id=1, source_target_pairs={{0,28},{4,24},{8,20},{12,16},{16,12},{20,8},{24,4},{28,0},{1,29},{... | collective-permute-start | bytes 1572872 | tf_op jit(solution)/shard_map/ppermute | solution.py:193
  256.7 25.0 %collective-permute-start.51 = (bf16[128,2048]{1,0:T(8,128)(2,1)S(1)}, bf16[128,2048]{1,0:T(8,128)(2,1)S(1)}, u32[]{:S(2)}, u32[]{:S(2)}) collective-permute-start(bf16[128,2048]{1,0:T(8,128)(2,1)S(1)} %pad_maximum_fusion.13), channel_id=1, source_target_pairs={{0,24},{4,28},{8,16},{12,20},{16,8},{20,12},{24,0},{28,4},{1,25},{... | collective-permute-start | bytes 1572872 | tf_op jit(solution)/shard_map/ppermute | solution.py:193
  257.9 23.8 %collective-permute-start.64 = (bf16[8,32,1024]{2,1,0:T(8,128)(2,1)S(1)}, bf16[8,32,1024]{2,1,0:T(8,128)(2,1)S(1)}, u32[]{:S(2)}, u32[]{:S(2)}) collective-permute-start(bf16[8,32,1024]{2,1,0:T(8,128)(2,1)S(1)} %collective-permute-done.60), channel_id=1, source_target_pairs={{1,0},{2,1},{5,4},{6,5},{9,8},{10,9},{13,12},{14,13},{17,16},{18,1... | collective-permute-start | bytes 1572872 | tf_op jit(solution)/shard_map/ppermute | solution.py:209
  260.1 25.0 %collective-permute-start.63 = (bf16[8,32,1024]{2,1,0:T(8,128)(2,1)S(1)}, bf16[8,32,1024]{2,1,0:T(8,128)(2,1)S(1)}, u32[]{:S(2)}, u32[]{:S(2)}) collective-permute-start(bf16[8,32,1024]{2,1,0:T(8,128)(2,1)S(1)} %collective-permute-done.62), channel_id=1, source_target_pairs={{2,3},{6,7},{10,11},{14,15},{18,19},{22,23},{26,27},{30,31}} | collective-permute-start | bytes 1572872 | tf_op jit(solution)/shard_map/ppermute | solution.py:207
  281.8 28.3 %collective-permute-start.65 = (bf16[8,32,1024]{2,1,0:T(8,128)(2,1)S(1)}, bf16[8,32,1024]{2,1,0:T(8,128)(2,1)S(1)}, u32[]{:S(2)}, u32[]{:S(2)}) collective-permute-start(bf16[8,32,1024]{2,1,0:T(8,128)(2,1)S(1)} %collective-permute-done.64), channel_id=1, source_target_pairs={{1,0},{5,4},{9,8},{13,12},{17,16},{21,20},{25,24},{29,28}} | collective-permute-start | bytes 1572872 | tf_op jit(solution)/shard_map/ppermute | solution.py:209
  283.1 25.7 %collective-permute-start.40 = (bf16[8,32,1024]{2,1,0:T(8,128)(2,1)S(1)}, bf16[8,32,1024]{2,1,0:T(8,128)(2,1)S(1)}, u32[]{:S(2)}, u32[]{:S(2)}) collective-permute-start(bf16[8,32,1024]{2,1,0:T(8,128)(2,1)S(1)} %multiply_convert_fusion.5), channel_id=1, source_target_pairs={{1,0},{2,1},{3,2},{5,4},{6,5},{7,6},{9,8},{10,9},{11,10},{13,12},{... | collective-permute-start | bytes 1572872 | tf_op jit(solution)/shard_map/ppermute | solution.py:209
  284.5 27.2 %collective-permute-start.42 = (bf16[8,32,1024]{2,1,0:T(8,128)(2,1)S(1)}, bf16[8,32,1024]{2,1,0:T(8,128)(2,1)S(1)}, u32[]{:S(2)}, u32[]{:S(2)}) collective-permute-start(bf16[8,32,1024]{2,1,0:T(8,128)(2,1)S(1)} %collective-permute-done.41), channel_id=1, source_target_pairs={{1,2},{2,3},{5,6},{6,7},{9,10},{10,11},{13,14},{14,15},{17,18},{18... | collective-permute-start | bytes 1572872 | tf_op jit(solution)/shard_map/ppermute | solution.py:207
  361.7 23.4 %collective-permute-start.73 = (bf16[8,32,1024]{2,1,0:T(8,128)(2,1)S(1)}, bf16[8,32,1024]{2,1,0:T(8,128)(2,1)S(1)}, u32[]{:S(2)}, u32[]{:S(2)}) collective-permute-start(bf16[8,32,1024]{2,1,0:T(8,128)(2,1)S(1)} %get-tuple-element.63), channel_id=1, source_target_pairs={{0,1},{4,5},{8,9},{12,13},{16,17},{20,21},{24,25},{28,29}} | collective-permute-start | bytes 1572872 | tf_op jit(solution)/shard_map/ppermute | solution.py:199
  363.3 23.2 %collective-permute-start.76 = (bf16[8,32,1024]{2,1,0:T(8,128)(2,1)S(1)}, bf16[8,32,1024]{2,1,0:T(8,128)(2,1)S(1)}, u32[]{:S(2)}, u32[]{:S(2)}) collective-permute-start(bf16[8,32,1024]{2,1,0:T(8,128)(2,1)S(1)} %get-tuple-element.64), channel_id=1, source_target_pairs={{3,2},{7,6},{11,10},{15,14},{19,18},{23,22},{27,26},{31,30}} | collective-permute-start | bytes 1572872 | tf_op jit(solution)/shard_map/ppermute | solution.py:202
  400.0 43.5 %collective-permute-start.136 = (bf16[128,2048]{1,0:T(8,128)(2,1)S(1)}, bf16[128,2048]{1,0:T(8,128)(2,1)S(1)}, u32[]{:S(2)}, u32[]{:S(2)}) collective-permute-start(bf16[128,2048]{1,0:T(8,128)(2,1)S(1)} %get-tuple-element.40), channel_id=1, source_target_pairs={{0,20},{4,16},{8,28},{12,24},{16,4},{20,0},{24,12},{28,8},{1,21},{... | collective-permute-start | bytes 1572872 | tf_op jit(solution)/shard_map/ppermute | solution.py:193
  418.3 25.2 %collective-permute-start.137 = (bf16[128,2048]{1,0:T(8,128)(2,1)S(1)}, bf16[128,2048]{1,0:T(8,128)(2,1)S(1)}, u32[]{:S(2)}, u32[]{:S(2)}) collective-permute-start(bf16[128,2048]{1,0:T(8,128)(2,1)S(1)} %get-tuple-element.39), channel_id=1, source_target_pairs={{0,24},{4,28},{8,16},{12,20},{16,8},{20,12},{24,0},{28,4},{1,25},{... | collective-permute-start | bytes 1572872 | tf_op jit(solution)/shard_map/ppermute | solution.py:193
  420.1 40.9 %collective-permute-start.138 = (bf16[128,2048]{1,0:T(8,128)(2,1)S(1)}, bf16[128,2048]{1,0:T(8,128)(2,1)S(1)}, u32[]{:S(2)}, u32[]{:S(2)}) collective-permute-start(bf16[128,2048]{1,0:T(8,128)(2,1)S(1)} %get-tuple-element.38), channel_id=1, source_target_pairs={{0,28},{4,24},{8,20},{12,16},{16,12},{20,8},{24,4},{28,0},{1,29},{... | collective-permute-start | bytes 1572872 | tf_op jit(solution)/shard_map/ppermute | solution.py:193
  512.0 96.0 %collective-permute-start.85 = (bf16[8,32,1024]{2,1,0:T(8,128)(2,1)}, bf16[8,32,1024]{2,1,0:T(8,128)(2,1)}, u32[]{:S(2)}, u32[]{:S(2)}) collective-permute-start(bf16[8,32,1024]{2,1,0:T(8,128)(2,1)} %get-tuple-element.57), channel_id=1, source_target_pairs={{0,1},{4,5},{8,9},{12,13},{16,17},{20,21},{24,25},{28,29}} | collective-permute-start | bytes 1572872 | tf_op jit(solution)/shard_map/ppermute | solution.py:199
  516.0 92.3 %collective-permute-start.88 = (bf16[8,32,1024]{2,1,0:T(8,128)(2,1)}, bf16[8,32,1024]{2,1,0:T(8,128)(2,1)}, u32[]{:S(2)}, u32[]{:S(2)}) collective-permute-start(bf16[8,32,1024]{2,1,0:T(8,128)(2,1)} %get-tuple-element.58), channel_id=1, source_target_pairs={{3,2},{7,6},{11,10},{15,14},{19,18},{23,22},{27,26},{31,30}} | collective-permute-start | bytes 1572872 | tf_op jit(solution)/shard_map/ppermute | solution.py:202
  578.2 65.1 %collective-permute-start.112 = (bf16[8,32,1024]{2,1,0:T(8,128)(2,1)}, bf16[8,32,1024]{2,1,0:T(8,128)(2,1)}, u32[]{:S(2)}, u32[]{:S(2)}) collective-permute-start(bf16[8,32,1024]{2,1,0:T(8,128)(2,1)} %get-tuple-element.51), channel_id=1, source_target_pairs={{0,1},{4,5},{8,9},{12,13},{16,17},{20,21},{24,25},{28,29}} | collective-permute-start | bytes 1572872 | tf_op jit(solution)/shard_map/ppermute | solution.py:199
  593.1 50.2 %collective-permute-start.115 = (bf16[8,32,1024]{2,1,0:T(8,128)(2,1)}, bf16[8,32,1024]{2,1,0:T(8,128)(2,1)}, u32[]{:S(2)}, u32[]{:S(2)}) collective-permute-start(bf16[8,32,1024]{2,1,0:T(8,128)(2,1)} %get-tuple-element.52), channel_id=1, source_target_pairs={{3,2},{7,6},{11,10},{15,14},{19,18},{23,22},{27,26},{31,30}} | collective-permute-start | bytes 1572872 | tf_op jit(solution)/shard_map/ppermute | solution.py:202
  620.8 27.6 %collective-permute-start.86 = (bf16[8,32,1024]{2,1,0:T(8,128)(2,1)}, bf16[8,32,1024]{2,1,0:T(8,128)(2,1)}, u32[]{:S(2)}, u32[]{:S(2)}) collective-permute-start(bf16[8,32,1024]{2,1,0:T(8,128)(2,1)} %get-tuple-element.55), channel_id=1, source_target_pairs={{0,1},{1,2},{4,5},{5,6},{8,9},{9,10},{12,13},{13,14},{16,17},{17,1... | collective-permute-start | bytes 1572872 | tf_op jit(solution)/shard_map/ppermute | solution.py:199
  623.2 25.3 %collective-permute-start.89 = (bf16[8,32,1024]{2,1,0:T(8,128)(2,1)}, bf16[8,32,1024]{2,1,0:T(8,128)(2,1)}, u32[]{:S(2)}, u32[]{:S(2)}) collective-permute-start(bf16[8,32,1024]{2,1,0:T(8,128)(2,1)} %get-tuple-element.56), channel_id=1, source_target_pairs={{2,1},{3,2},{6,5},{7,6},{10,9},{11,10},{14,13},{15,14},{18,17},{19... | collective-permute-start | bytes 1572872 | tf_op jit(solution)/shard_map/ppermute | solution.py:202
  685.7 32.9 %collective-permute-start.124 = (bf16[48,1024]{1,0:T(8,128)(2,1)S(1)}, bf16[48,1024]{1,0:T(8,128)(2,1)S(1)}, u32[]{:S(2)}, u32[]{:S(2)}) collective-permute-start(bf16[48,1024]{1,0:T(8,128)(2,1)S(1)} %fusion.54), channel_id=1, source_target_pairs={{0,28},{4,24},{8,20},{12,16},{16,12},{20,8},{24,4},{28,0},{1,29},{... | collective-permute-start | bytes 294920 | tf_op jit(solution)/shard_map/ppermute | solution.py:193
  685.8 33.4 %collective-permute-start.123 = (bf16[48,1024]{1,0:T(8,128)(2,1)S(1)}, bf16[48,1024]{1,0:T(8,128)(2,1)S(1)}, u32[]{:S(2)}, u32[]{:S(2)}) collective-permute-start(bf16[48,1024]{1,0:T(8,128)(2,1)S(1)} %fusion.53), channel_id=1, source_target_pairs={{0,24},{4,28},{8,16},{12,20},{16,8},{20,12},{24,0},{28,4},{1,25},{... | collective-permute-start | bytes 294920 | tf_op jit(solution)/shard_map/ppermute | solution.py:193
  687.3 32.9 %collective-permute-start.122 = (bf16[48,1024]{1,0:T(8,128)(2,1)S(1)}, bf16[48,1024]{1,0:T(8,128)(2,1)S(1)}, u32[]{:S(2)}, u32[]{:S(2)}) collective-permute-start(bf16[48,1024]{1,0:T(8,128)(2,1)S(1)} %fusion.52), channel_id=1, source_target_pairs={{0,20},{4,16},{8,28},{12,24},{16,4},{20,0},{24,12},{28,8},{1,21},{... | collective-permute-start | bytes 294920 | tf_op jit(solution)/shard_map/ppermute | solution.py:193
  689.2 30.9 %collective-permute-start.121 = (bf16[48,1024]{1,0:T(8,128)(2,1)S(1)}, bf16[48,1024]{1,0:T(8,128)(2,1)S(1)}, u32[]{:S(2)}, u32[]{:S(2)}) collective-permute-start(bf16[48,1024]{1,0:T(8,128)(2,1)S(1)} %fusion.51), channel_id=1, source_target_pairs={{0,16},{4,20},{8,24},{12,28},{16,0},{20,4},{24,8},{28,12},{1,17},{... | collective-permute-start | bytes 294920 | tf_op jit(solution)/shard_map/ppermute | solution.py:193
  (179 other events, 2097.3 us)

commit v4 on v3

--- a/solution.py
+++ b/solution.py
@@ -189,35 +189,27 @@
 
 def make_step_shards(count, lanes):
 
-    def swap(block, k):
-        return lax.ppermute(block, "dp", [(i, i ^ k) for i in range(count)])
-
     def exchange(blocks):
-        return [blocks[0]] + [swap(blocks[k], k) for k in range(1, count)]
-
-    def up(block, senders):
-        return lax.ppermute(block, "tensor", [(i, i + 1) for i in range(senders)])
-
-    def down(block, senders):
-        return lax.ppermute(block, "tensor", [(i, i - 1) for i in range(lanes - senders, lanes)])
+        return lax.all_to_all(blocks, "dp", 0, 0, tiled=True)
 
     def collect(rows):
-        below, above = [rows], [rows]
-        for k in range(1, lanes):
-            below.append(lax.ppermute(
-                below[-1], "tensor", [(i, i + 1) for i in range(k - 1, lanes - 1)]))
-            above.append(lax.ppermute(
-                above[-1], "tensor", [(i, i - 1) for i in range(1, lanes - k + 1)]))
-        parts = [rows] + [above[k] + below[lanes - k] for k in range(1, lanes)]
-        return jnp.stack(parts, axis=1).reshape(-1, rows.shape[-1])
+        return lax.all_gather(rows, "tensor", axis=0).reshape(-1, rows.shape[-1])
 
     def deal(partial):
-        slots = partial.reshape(count, lanes, -1, partial.shape[-1])
-        rising, falling = 0.0, 0.0
-        for r in range(1, lanes):
-            rising = up((slots[:, lanes - r] + rising).astype(BF), r).astype(F32)
-            falling = down((slots[:, r] + falling).astype(BF), r).astype(F32)
-        return slots[:, 0] + rising + falling
+        slots = partial.astype(BF).reshape(lanes, count, -1, partial.shape[-1])
+        return lax.psum_scatter(slots, "tensor", scatter_dimension=0).astype(F32)
+
+    def frame_split(array):
+        slots = array.reshape(lanes, count, -1, array.shape[-1])
+        slots = jnp.swapaxes(slots, 0, 1)
+        return exchange(slots.reshape(count, -1, array.shape[-1]))
+
+    def frame_join(array):
+        slots = exchange(array).reshape(count, lanes, -1, array.shape[-1])
+        return jnp.swapaxes(slots, 0, 1).reshape(-1, array.shape[-1])
+
+    def after(value, *waiting):
+        return lax.optimization_barrier((value,) + waiting)
 
     def shards(
         layer_in, text_mask, w_qkv, w_out, w_gate_up, w_down, norm_gains, pad_row, out_grad
@@ -226,56 +218,35 @@
         steps, local, width = layer_in.shape
         block = width // count
 
-        def pick(array, k):
-            return lax.dynamic_index_in_dim(array, me ^ k, 0, keepdims=False)
-
-        def relative(array):
-            return jnp.concatenate(
-                [
-                    lax.dynamic_slice_in_dim(array, (me ^ r) * block, block, array.ndim - 1)
-                    for r in range(count)
-                ],
-                axis=-1,
-            )
-
-        def place(blocks):
-            whole = jnp.zeros((count,) + blocks[0].shape, blocks[0].dtype)
-            for k in range(count):
-                whole = lax.dynamic_update_index_in_dim(whole, blocks[k], me ^ k, 0)
-            return whole
-
-        def tag(rows, *vectors):
-            line = jnp.concatenate([v.astype(rows.dtype) for v in vectors])
-            return jnp.concatenate(
-                [rows, jnp.pad(line[None], ((0, TILE - 1), (0, width - line.shape[0])))]
-            )
+        def tile(line):
+            pads = [(0, 0)] * (line.ndim - 1) + [(0, TILE - 1), (0, width - line.shape[-1])]
+            return jnp.pad(line[..., None, :], pads)
 
         small = jnp.concatenate([norm_gains, pad_row[None]], axis=0).astype(BF).reshape(-1)
-        hello = exchange([tag(pick(layer_in, k), small, text_mask) for k in range(count)])
-        rows_in = relative(jnp.stack([h[:local] for h in hello])).astype(F32)
-        notes = jnp.stack([h[local] for h in hello]).astype(F32)
+        line = jnp.concatenate([small, text_mask.astype(BF)])
+        notes = jnp.broadcast_to(tile(line)[None], (count, TILE, width))
+        hello = exchange(jnp.concatenate([layer_in, notes], axis=1))
+        rows_in = hello[:, :local].astype(F32)
+        notes = hello[:, local].astype(F32)
         small = jnp.swapaxes(notes[:, : 3 * block].reshape(count, 3, block), 0, 1)
         gain_one, gain_two, pad_vec = small.reshape(3, width)
         padded = jnp.where(me == 0, 1.0 - notes[:, 3 * block : 3 * block + local], 0.0)[..., None]
         h0 = rows_in + padded * pad_vec
         r1 = lax.rsqrt(jnp.mean(h0 * h0, axis=-1, keepdims=True) + EPS)
         n1 = (h0 * r1 * gain_one).astype(BF)
+        n1, w_qkv, w_out = after(n1, w_qkv, w_out)
         n1_all = collect(n1)
 
-        def attn_block(k):
-            parts = [pick(w_qkv, k)[j] for j in range(3)] + [pick(w_out, k).T]
-            return jnp.concatenate(parts, axis=1).astype(BF)
-
-        w_attn = jnp.concatenate(exchange([attn_block(k) for k in range(count)]), axis=0)
+        w_attn = jnp.concatenate(
+            [w_qkv[:, 0], w_qkv[:, 1], w_qkv[:, 2], jnp.swapaxes(w_out, 1, 2)], axis=2
+        )
+        w_attn = exchange(w_attn.astype(BF)).reshape(width, -1)
         cols = w_attn.shape[1] // 4
         w_in, wout_t = w_attn[:, : 3 * cols], w_attn[:, 3 * cols :]
+        w_attn, out_grad = after(w_attn, out_grad)
+        grad = exchange(out_grad)
+        grad_all = collect(grad)
         qkv = jnp.dot(n1_all, w_in, preferred_element_type=F32).astype(BF)
-
-        def frame_split(array):
-            return jnp.stack(exchange(list(array.reshape(count, -1, array.shape[-1]))))
-
-        def frame_join(array):
-            return jnp.concatenate(exchange(list(array)), axis=0)
 
         qkv = frame_split(qkv)
         frames = qkv.shape[1]
@@ -284,8 +255,7 @@
         query = qkv[..., :cols].reshape(steps, frames, heads, HEAD)
         keyv = qkv[..., cols : 2 * cols].reshape(steps, frames, heads, HEAD)
         value = qkv[..., 2 * cols :].reshape(steps, frames, heads, HEAD)
-        order = jnp.arange(steps) ^ me
-        causal = order[:, None] >= order[None, :]
+        causal = jnp.arange(steps)[:, None] >= jnp.arange(steps)[None, :]
 
         def score_of(qv, kv):
             raw = jnp.einsum("sfhe,tfhe->fhst", qv, kv, preferred_element_type=F32) * scale
@@ -299,26 +269,20 @@
         probs_low = (expo / total).astype(BF)
         mixed = jnp.einsum("fhst,tfhe->sfhe", probs_low, value, preferred_element_type=F32)
         mixed_all = frame_join(mixed.reshape(steps, frames, cols).astype(BF))
-
-        w_gate_up, w_down, mixed_all = lax.optimization_barrier((w_gate_up, w_down, mixed_all))
-
-        def gu_block(k):
-            pair = pick(w_gate_up, k)
-            return jnp.concatenate([pair[0], pair[1]], axis=1).astype(BF)
-
-        wgu = jnp.concatenate(exchange([gu_block(k) for k in range(count)]), axis=0)
-        wdown = jnp.concatenate(
-            exchange([pick(w_down, k).astype(BF) for k in range(count)]), axis=1
-        )
-        out_grad, _ = lax.optimization_barrier((out_grad, n1_all))
-        grad = relative(jnp.stack(exchange([pick(out_grad, k) for k in range(count)])))
-        grad_all = collect(grad)
-
-        attn = deal(jnp.einsum("fe,de->fd", mixed_all, wout_t, preferred_element_type=F32))
+        attn = jnp.einsum("fe,de->fd", mixed_all, wout_t, preferred_element_type=F32)
+
+        attn, w_down = after(attn.astype(BF), w_down)
+        attn = deal(attn)
+        wdown = exchange(w_down.astype(BF))
+        wdown = jnp.swapaxes(wdown, 0, 1).reshape(-1, width)
         h1 = h0 + attn
         r2 = lax.rsqrt(jnp.mean(h1 * h1, axis=-1, keepdims=True) + EPS)
         n2 = (h1 * r2 * gain_two).astype(BF)
+        n2, w_gate_up = after(n2, w_gate_up)
         n2_all = collect(n2)
+        wgu = jnp.concatenate([w_gate_up[:, 0], w_gate_up[:, 1]], axis=2).astype(BF)
+        wgu = exchange(wgu).reshape(width, -1)
+
         gate_up = jnp.dot(n2_all, wgu, preferred_element_type=F32)
         hid_width = gate_up.shape[1] // 2
         gate, upval = gate_up[:, :hid_width], gate_up[:, hid_width:]
@@ -329,24 +293,29 @@
         d_gate = d_hidden * upval * (sigma * (1.0 + gate * (1.0 - sigma)))
         d_up = d_hidden * silu_val
         d_gu = jnp.concatenate([d_gate, d_up], axis=1).astype(BF)
-        dn2 = deal(jnp.einsum("fk,dk->fd", d_gu, wgu, preferred_element_type=F32))
-
-        d_down = jnp.einsum("fk,fd->kd", hidden, grad_all, preferred_element_type=F32).astype(BF)
-        g_down = exchange([d_down[:, r * block : (r + 1) * block] for r in range(count)])
-        d_gate_up = jnp.einsum("fd,fk->dk", n2_all, d_gu, preferred_element_type=F32).astype(BF)
-        g_gate_up = exchange(list(d_gate_up.reshape(count, block, -1)))
-
+        dn2 = jnp.einsum("fk,dk->fd", d_gu, wgu, preferred_element_type=F32).astype(BF)
+
+        dn2, hidden = after(dn2, hidden)
+        dn2 = deal(dn2)
+        d_down = jnp.einsum(
+            "fk,frd->rkd",
+            hidden,
+            grad_all.reshape(-1, count, block),
+            preferred_element_type=F32,
+        )
+        g_down = exchange(d_down.astype(BF)).astype(F32)
         dh_norm2, dgain_two = norm_back(dn2, h1, r2, gain_two)
         dh1 = grad.astype(F32) + dh_norm2
-        dh1_all = collect(dh1.astype(BF))
+        dh1_low, d_gu, hidden = after(dh1.astype(BF), d_gu, hidden)
+        dh1_all = collect(dh1_low)
+        d_gate_up = jnp.einsum("fd,fk->dk", n2_all, d_gu, preferred_element_type=F32)
+        g_gate_up = exchange(d_gate_up.astype(BF).reshape(count, block, -1))
+        g_gate_up = jnp.stack([g_gate_up[..., :hid_width], g_gate_up[..., hid_width:]], axis=1)
+        g_gate_up = g_gate_up.astype(F32)
+
+        ffout = deal(jnp.dot(hidden, wdown, preferred_element_type=F32))
         d_mixed = jnp.dot(dh1_all, wout_t, preferred_element_type=F32).astype(BF)
         d_mixed = frame_split(d_mixed).reshape(steps, frames, heads, HEAD)
-
-        hidden, _ = lax.optimization_barrier((hidden, dh1_all))
-        ffout = deal(jnp.dot(hidden, wdown, preferred_element_type=F32))
-        layer_out = relative((h1 + ffout).astype(BF))
-        layer_out = place(exchange(list(layer_out)))
-
         probs = jnp.exp(score_of(query, keyv) - lse)
         d_probs = jnp.einsum("sfhe,tfhe->fhst", d_mixed, value, preferred_element_type=F32)
         d_value = jnp.einsum("fhst,sfhe->tfhe", probs_low, d_mixed, preferred_element_type=F32)
@@ -362,7 +331,10 @@
             axis=-1,
         )
         d_qkv = frame_join(d_qkv)
-        dn1 = deal(jnp.einsum("fe,de->fd", d_qkv, w_in, preferred_element_type=F32))
+        dn1 = jnp.einsum("fe,de->fd", d_qkv, w_in, preferred_element_type=F32).astype(BF)
+
+        dn1, d_qkv, ffout = after(dn1, d_qkv, ffout)
+        dn1 = deal(dn1)
         d_attn = jnp.concatenate(
             [
                 jnp.einsum("fd,fe->de", n1_all, d_qkv, preferred_element_type=F32).astype(BF),
@@ -370,44 +342,27 @@
             ],
             axis=1,
         )
-        g_attn = exchange(list(d_attn.reshape(count, block, -1)))
+        g_attn = exchange(d_attn.reshape(count, block, -1)).astype(F32)
+        g_qkv = jnp.stack([g_attn[..., j * cols : (j + 1) * cols] for j in range(3)], axis=1)
+        g_out = jnp.swapaxes(g_attn[..., 3 * cols :], 1, 2)
+        layer_out = exchange((h1 + ffout).astype(BF))
 
         dh_norm1, dgain_one = norm_back(dn1, h0, r1, gain_one)
         dh0 = dh1 + dh_norm1
         d_pad = jnp.sum(dh0 * padded, axis=(0, 1))
         sums = jnp.stack([dgain_one, dgain_two, d_pad]).reshape(3, count, block)
+        sums = jnp.swapaxes(sums, 0, 1).reshape(count, -1)
         high = sums.astype(BF)
         rest = (sums - high.astype(F32)).astype(BF)
-        input_grad = relative(dh0.astype(BF))
-        last = exchange(
-            [
-                tag(input_grad[k], high[:, k].reshape(-1), rest[:, k].reshape(-1))
-                for k in range(count)
-            ]
-        )
-        input_grad = place([h[:local] for h in last])
-        sums = jnp.stack([h[local] for h in last]).astype(F32)
-        sums = jnp.sum(sums, axis=0)[: 6 * block].reshape(2, 3, block)
+        notes = tile(jnp.concatenate([high, rest], axis=1))
+        last = exchange(jnp.concatenate([dh0.astype(BF), notes], axis=1))
+        input_grad = last[:, :local]
+        sums = jnp.sum(last[:, local].astype(F32), axis=0)[: 6 * block].reshape(2, 3, block)
         sums = sums[0] + sums[1]
         g_small = sums
         for k in range(1, lanes):
             around = [(i, (i + k) % lanes) for i in range(lanes)]
             g_small = g_small + lax.ppermute(sums, "tensor", around)
-
-        g_down = place([g.astype(F32) for g in g_down])
-        g_gate_up = place(
-            [
-                jnp.stack([g[:, :hid_width], g[:, hid_width:]]).astype(F32)
-                for g in g_gate_up
-            ]
-        )
-        g_qkv = place(
-            [
-                jnp.stack([g[:, j * cols : (j + 1) * cols] for j in range(3)]).astype(F32)
-                for g in g_attn
-            ]
-        )
-        g_out = place([g[:, 3 * cols :].T.astype(F32) for g in g_attn])
         return (layer_out, input_grad, g_qkv, g_out, g_gate_up, g_down, g_small[0:2], g_small[2])
 
     return shards

time: 743 us -> 631 us (0.85)
  starting transfers between devices: 184 us -> 53.9 us
  blocking collectives: 0 us -> 41.8 us
  local copies, waits for them, and re-layouts: 104 us -> 64.4 us
  matrix products: 49.3 us -> 84.7 us
  waiting for transfers between devices: 353 us -> 318 us
  between operations: 4.21 us -> 15.1 us
    ppermute x146 -> x0, waiting for transfers between devices: 351 us -> none  [the longest x98 210 us: swap(): return lax.ppermute(block, 'dp', [(i, i ^ k) for i in range(count)])]
    all_to_all x0 -> x12, waiting for transfers between devices: none -> 180 us  [exchange(): return lax.all_to_all(blocks, 'dp', 0, 0, tiled=True)]
    ppermute x146 -> x0, starting transfers between devices: 178 us -> none  [the longest x98 89 us: swap(): return lax.ppermute(block, 'dp', [(i, i ^ k) for i in range(count)])]
    reduce_scatter x0 -> x4, waiting for transfers between devices: none -> 77.1 us  [deal(): return lax.psum_scatter(slots, 'tensor', scatter_dimension=0).astype(F32)]
    all_gather x0 -> x4, waiting for transfers between devices: none -> 61 us  [collect(): return lax.all_gather(rows, 'tensor', axis=0).reshape(-1, rows.shape[-1])]
    all_to_all x0 -> x12, starting transfers between devices: none -> 48.5 us  [exchange(): return lax.all_to_all(blocks, 'dp', 0, 0, tiled=True)]
    all_to_all x0 -> x2, blocking collectives: none -> 41.8 us  [exchange(): return lax.all_to_all(blocks, 'dp', 0, 0, tiled=True)]
    another operation x52 -> x1, local copies, waits for them, and re-layouts: 41.9 us -> 2.66 us  [shards(): jnp.stack([g_gate_up[..., :hid_width], g_gate_up[..., hid_width:]], axis=1)]
  transfers between devices with their start and end apart: 149 -> 23, of which waited for: 66 -> 16; matrix products, arithmetic and copies ran while one was open for 18% -> 21% of each run, Pallas kernels for 0% -> 0%
where the time goes in v4:
time: 631 us; the launch traced here: 625 us
  waiting for transfers between devices  318 us (50%)
  matrix products  84.7 us (13%)
  local copies, waits for them, and re-layouts  64.4 us (10%)
  starting transfers between devices  53.9 us (9%)
  other arithmetic  47.2 us (7%)
  blocking collectives  41.8 us (7%)
  between operations  15.1 us (2%)
    all_to_all x12, waiting for transfers between devices, exchange(): return lax.all_to_all(blocks, 'dp', 0, 0, tiled=True)  180 us
    reduce_scatter x4, waiting for transfers between devices, deal(): return lax.psum_scatter(slots, 'tensor', scatter_dimension=0).astype(F32)  77.1 us
    all_gather x4, waiting for transfers between devices, collect(): return lax.all_gather(rows, 'tensor', axis=0).reshape(-1, rows.shape[-1])  61 us
    all_to_all x12, starting transfers between devices, exchange(): return lax.all_to_all(blocks, 'dp', 0, 0, tiled=True)  48.5 us
    all_to_all x2, blocking collectives, exchange(): return lax.all_to_all(blocks, 'dp', 0, 0, tiled=True)  41.8 us
    unnamed x47, local copies, waits for them, and re-layouts  16.9 us
  transfers between devices with their start and end apart: 23, of which 16 were waited for; matrix products, arithmetic and copies ran while one was open for 21% of the time, Pallas kernels for 0%

profile of v4, /device:TPU:0, one launch (start us, length us, event | category | flops | bytes accessed | tf_op | source)
XLA Modules:
  0.0 625.1 jit_solution(9615107412233734935)
XLA Ops:
  11.2 5.3 all-to-all-start
  16.6 12.5 %all-to-all-done = bf16[8,48,1024]{2,1,0:T(8,128)(2,1)S(1)} async-done(((bf16[8,48,1024]{2,1,0:T(8,128)(2,1)}), bf16[8,48,1024]{2,1,0:T(8,128)(2,1)S(1)}, u32[]{:S(2)}, u32[]{:S(2)}) %all-to-all-start) | async-done | bytes 786464 | tf_op jit(solution)/shard_map/all_to_all | solution.py:193
  33.2 29.0 %all_to_all.70 = bf16[8,128,1024]{2,1,0:T(8,128)(2,1)S(1)} all-to-all(bf16[8,128,1024]{2,1,0:T(8,128)(2,1)S(1)} %pad_maximum_fusion.3), channel_id=1, replica_groups=mesh['dp'=8,'tensor'=4] {'dp'}, dimensions={0} | all-to-all | bytes 4194304 | tf_op jit(solution)/shard_map/all_to_all | solution.py:193
  62.2 13.6 %all-gather.9.cloned.1.call-done = bf16[32,32,1024]{2,1,0:T(8,128)(2,1)} async-done(((bf16[8,32,1024]{2,1,0:T(8,128)(2,1)}), bf16[32,32,1024]{2,1,0:T(8,128)(2,1)}) %all-gather.9.cloned.1.call-update) | async-done | bytes 2097168 | tf_op jit(solution)/shard_map/all_gather | solution.py:196
  84.4 20.7 %all-to-all-done.2 = bf16[8,128,768]{2,1,0:T(8,128)(2,1)S(1)} async-done(((bf16[8,128,768]{2,1,0:T(8,128)(2,1)}), bf16[8,128,768]{2,1,0:T(8,128)(2,1)S(1)}, u32[]{:S(2)}, u32[]{:S(2)}) %all-to-all-start.2) | async-done | bytes 1572896 | tf_op jit(solution)/shard_map/all_to_all | solution.py:193
  123.7 12.8 %all_to_all.71 = bf16[8,128,256]{1,2,0:T(8,128)(2,1)} all-to-all(bf16[8,128,256]{1,2,0:T(8,128)(2,1)S(1)} %bitcast.218), channel_id=1, replica_groups=mesh['dp'=8,'tensor'=4] {'dp'}, dimensions={0} | all-to-all | bytes 1048576 | tf_op jit(solution)/shard_map/all_to_all | solution.py:193
  141.2 40.7 %reduce-scatter.5.cloned.1.call-done = bf16[1,8,32,1024]{3,2,1,0:T(8,128)(2,1)} async-done(((bf16[4,8,32,1024]{3,2,1,0:T(8,128)(2,1)}), bf16[1,8,32,1024]{3,2,1,0:T(8,128)(2,1)}) %reduce-scatter.5.cloned.1.call-update) | async-done | bytes 524304 | tf_op jit(solution)/shard_map/reduce_scatter | solution.py:200
  189.2 4.3 convert.45
  199.7 4.5 all-to-all-start.6
  204.9 4.6 copy.178
  209.5 43.9 %all-to-all-done.6 = bf16[8,128,2048]{2,1,0:T(8,128)(2,1)} async-done(((bf16[8,128,2048]{2,1,0:T(8,128)(2,1)}), bf16[8,128,2048]{2,1,0:T(8,128)(2,1)}, u32[]{:S(2)}, u32[]{:S(2)}) %all-to-all-start.6) | async-done | bytes 4194336 | tf_op jit(solution)/shard_map/all_to_all | solution.py:193
  253.4 4.4 all-to-all-start.5
  257.8 10.8 %fusion.45 = f32[1024,2048]{0,1:T(8,128)} fusion(bf16[1024,1024]{1,0:T(8,128)(2,1)} %bitcast.247, bf16[1024,2048]{1,0:T(8,128)(2,1)} %bitcast.35), kind=kOutput, calls=%fused_computation.124 | convolution fusion | flops 4294967296 | bytes 14680064 | tf_op jit(solution)/shard_map/dot_general | solution.py:286
  268.6 8.5 %all-gather.11.cloned.1.call-done = bf16[32,32,1024]{2,1,0:T(8,128)(2,1)} async-done(((bf16[8,32,1024]{2,1,0:T(8,128)(2,1)}), bf16[32,32,1024]{2,1,0:T(8,128)(2,1)}) %all-gather.11.cloned.1.call-update) | async-done | bytes 2097168 | tf_op jit(solution)/shard_map/all_gather | solution.py:196
  277.1 7.3 %all-to-all-done.5 = bf16[8,1024,128]{1,2,0:T(8,128)(2,1)} async-done(((bf16[8,1024,128]{1,2,0:T(8,128)(2,1)}), bf16[8,1024,128]{1,2,0:T(8,128)(2,1)}, u32[]{:S(2)}, u32[]{:S(2)}) %all-to-all-start.5) | async-done | bytes 2097184 | tf_op jit(solution)/shard_map/all_to_all | solution.py:193
  284.4 10.0 %multiply_convert_fusion.2 = (bf16[1024,1024]{0,1:T(8,128)(2,1)S(1)}, bf16[1024,1024]{0,1:T(8,128)(2,1)S(1)}, bf16[1024,1024]{0,1:T(8,128)(2,1)}) fusion(f32[1024,2048]{0,1:T(8,128)} %fusion.45, bf16[1024,1024]{1,0:T(8,128)(2,1)} %bitcast.220, bf16[1024,1024]{0,1:T(8,128)(2,1)} %bitcast.30), kind=kOutput, calls=%fused_computation.5 | convolution fusion | flops 2163212288 | bytes 18874368 | tf_op jit(solution)/shard_map/fd,kd->fk/dot_general | solution.py:292
  294.4 9.5 %convolution_convert_fusion.2 = bf16[1024,1024]{1,0:T(8,128)(2,1)} fusion(bf16[1024,2048]{1,0:T(8,128)(2,1)} %bitcast.35, bf16[1024,1024]{0,1:T(8,128)(2,1)S(1)} %get-tuple-element.87, bf16[1024,1024]{0,1:T(8,128)(2,1)S(1)} %get-tuple-element.86), kind=kOutput, calls=%fused_computation.31 | convolution fusion | flops 4304404480 | bytes 10485760 | tf_op jit(solution)/shard_map/fk,dk->fd/dot_general | solution.py:296
  304.2 4.7 pad_maximum_fusion.1
  308.8 36.3 %reduce-scatter.7.cloned.1.call-done = bf16[1,8,32,1024]{3,2,1,0:T(8,128)(2,1)} async-done(((bf16[4,8,32,1024]{3,2,1,0:T(8,128)(2,1)}), bf16[1,8,32,1024]{3,2,1,0:T(8,128)(2,1)}) %reduce-scatter.7.cloned.1.call-update) | async-done | bytes 524304 | tf_op jit(solution)/shard_map/reduce_scatter | solution.py:200
  349.4 6.0 convolution_convert_fusion.1
  355.4 39.0 %all-gather.15.cloned.1.call-done = bf16[32,32,1024]{2,1,0:T(8,128)(2,1)} async-done(((bf16[8,32,1024]{2,1,0:T(8,128)(2,1)}), bf16[32,32,1024]{2,1,0:T(8,128)(2,1)}) %all-gather.15.cloned.1.call-update) | async-done | bytes 2097168 | tf_op jit(solution)/shard_map/all_gather | solution.py:196
  397.6 4.1 all-to-all-start.7
  403.5 7.9 %all-to-all-done.7 = bf16[8,128,256]{2,1,0:T(8,128)(2,1)} async-done(((bf16[8,128,256]{2,1,0:T(8,128)(2,1)}), bf16[8,128,256]{2,1,0:T(8,128)(2,1)}, u32[]{:S(2)}, u32[]{:S(2)}) %all-to-all-start.7) | async-done | bytes 524320 | tf_op jit(solution)/shard_map/all_to_all | solution.py:193
  427.3 5.1 fusion.15
  453.1 14.8 %all-to-all-done.8 = bf16[8,128,768]{1,2,0:T(8,128)(2,1)S(1)} async-done(((bf16[8,128,768]{1,2,0:T(8,128)(2,1)}), bf16[8,128,768]{1,2,0:T(8,128)(2,1)S(1)}, u32[]{:S(2)}, u32[]{:S(2)}) %all-to-all-start.8) | async-done | bytes 1572896 | tf_op jit(solution)/shard_map/all_to_all | solution.py:193
  482.7 9.4 %convolution_convert_fusion = bf16[1024,2048]{1,0:T(8,128)(2,1)} fusion(bf16[1024,1024]{1,0:T(8,128)(2,1)} %bitcast.248, bf16[1024,2048]{0,1:T(8,128)(2,1)} %pad_maximum_fusion.1), kind=kOutput, calls=%fused_computation.8 | convolution fusion | flops 4297064448 | bytes 10485760 | tf_op jit(solution)/shard_map/fd,fk->dk/dot_general | solution.py:311
  492.1 7.1 %all-to-all-done.13 = bf16[8,1024,128]{1,2,0:T(8,128)(2,1)S(1)} async-done(((bf16[8,1024,128]{1,2,0:T(8,128)(2,1)}), bf16[8,1024,128]{1,2,0:T(8,128)(2,1)S(1)}, u32[]{:S(2)}, u32[]{:S(2)}) %all-to-all-start.13) | async-done | bytes 2097184 | tf_op jit(solution)/shard_map/all_to_all | solution.py:193
  500.6 4.8 all-to-all-start.12
  512.0 42.5 %all-to-all-done.12 = bf16[8,128,2048]{2,1,0:T(8,128)(2,1)} async-done(((bf16[8,128,2048]{2,1,0:T(8,128)(2,1)}), bf16[8,128,2048]{2,1,0:T(8,128)(2,1)}, u32[]{:S(2)}, u32[]{:S(2)}) %all-to-all-start.12) | async-done | bytes 4194336 | tf_op jit(solution)/shard_map/all_to_all | solution.py:193
  558.1 4.1 copy.201
  568.2 16.4 %all-to-all-done.11 = bf16[8,128,1024]{1,2,0:T(8,128)(2,1)S(1)} async-done(((bf16[8,128,1024]{1,2,0:T(8,128)(2,1)}), bf16[8,128,1024]{1,2,0:T(8,128)(2,1)S(1)}, u32[]{:S(2)}, u32[]{:S(2)}) %all-to-all-start.11) | async-done | bytes 2097184 | tf_op jit(solution)/shard_map/all_to_all | solution.py:193
  590.9 3.9 maximum_convert_fusion
  (164 shorter events, 161.2 us)
Async XLA Ops:
  11.2 19.4 %copy-start.18 = (f32[8,256,128]{2,1,0:T(8,128)S(1)}, f32[8,256,128]{2,1,0:T(8,128)}, u32[]{:S(2)}) copy-start(f32[8,256,128]{2,1,0:T(8,128)} %param.12) | copy-start | bytes 3145732
  11.2 17.9 %all-to-all-start = ((bf16[8,48,1024]{2,1,0:T(8,128)(2,1)}), bf16[8,48,1024]{2,1,0:T(8,128)(2,1)S(1)}, u32[]{:S(2)}, u32[]{:S(2)}) async-start(bf16[8,48,1024]{2,1,0:T(8,128)(2,1)} %pad_maximum_fusion.5), calls=%async_computation | async-start | bytes 1572864 | tf_op jit(solution)/shard_map/all_to_all | solution.py:193
  16.6 59.2 %all-gather.9.cloned.1.call-start = ((), (), s32[]{:S(2)}) async-start(), calls=%async_computation.22 | async-start | bytes 2621440 | tf_op jit(solution)/shard_map/all_gather | solution.py:196
  62.2 17.0 %copy-start.8 = (bf16[8,128,1024]{2,1,0:T(8,128)(2,1)}, bf16[8,128,1024]{2,1,0:T(8,128)(2,1)S(1)}, u32[]{:S(2)}) copy-start(bf16[8,128,1024]{2,1,0:T(8,128)(2,1)S(1)} %all_to_all.70) | copy-start | bytes 6291460
  80.4 24.6 %all-to-all-start.2 = ((bf16[8,128,768]{2,1,0:T(8,128)(2,1)}), bf16[8,128,768]{2,1,0:T(8,128)(2,1)S(1)}, u32[]{:S(2)}, u32[]{:S(2)}) async-start(bf16[8,128,768]{2,1,0:T(8,128)(2,1)} %bitcast.204), calls=%async_computation.2 | async-start | bytes 3145728 | tf_op jit(solution)/shard_map/all_to_all | solution.py:193
  84.1 97.8 %reduce-scatter.5.cloned.1.call-start = ((), (), s32[]{:S(2)}) async-start(), calls=%async_computation.18 | async-start | bytes 2621440 | tf_op jit(solution)/shard_map/reduce_scatter | solution.py:200
  137.8 3.3 copy-start.12
  141.1 116.7 %all-gather.13.cloned.1.call-start = ((), (), s32[]{:S(2)}) async-start(), calls=%async_computation.24 | async-start | bytes 2621440 | tf_op jit(solution)/shard_map/all_gather | solution.py:196
  185.6 13.4 %all-to-all-start.4 = ((bf16[8,32,1024]{2,1,0:T(8,128)(2,1)}), bf16[8,32,1024]{2,1,0:T(8,128)(2,1)S(1)}, u32[]{:S(2)}, u32[]{:S(2)}) async-start(bf16[8,32,1024]{2,1,0:T(8,128)(2,1)} %param.17), calls=%async_computation.5 | async-start | bytes 1048576 | tf_op jit(solution)/shard_map/all_to_all | solution.py:193
  199.7 53.6 %all-to-all-start.6 = ((bf16[8,128,2048]{2,1,0:T(8,128)(2,1)}), bf16[8,128,2048]{2,1,0:T(8,128)(2,1)}, u32[]{:S(2)}, u32[]{:S(2)}) async-start(bf16[8,128,2048]{2,1,0:T(8,128)(2,1)} %pad_maximum_fusion), calls=%async_computation.7 | async-start | bytes 8388608 | tf_op jit(solution)/shard_map/all_to_all | solution.py:193
  204.3 72.8 %all-gather.11.cloned.1.call-start = ((), (), s32[]{:S(2)}) async-start(), calls=%async_computation.23 | async-start | bytes 2621440 | tf_op jit(solution)/shard_map/all_gather | solution.py:196
  253.4 31.0 %all-to-all-start.5 = ((bf16[8,1024,128]{1,2,0:T(8,128)(2,1)}), bf16[8,1024,128]{1,2,0:T(8,128)(2,1)}, u32[]{:S(2)}, u32[]{:S(2)}) async-start(bf16[8,1024,128]{1,2,0:T(8,128)(2,1)} %copy.178), calls=%async_computation.6 | async-start | bytes 4194304 | tf_op jit(solution)/shard_map/all_to_all | solution.py:193
  257.7 87.4 %reduce-scatter.7.cloned.1.call-start = ((), (), s32[]{:S(2)}) async-start(), calls=%async_computation.19 | async-start | bytes 2621440 | tf_op jit(solution)/shard_map/reduce_scatter | solution.py:200
  294.4 9.5 %copy-start.13 = (bf16[1024,1024]{0,1:T(8,128)(2,1)}, bf16[1024,1024]{0,1:T(8,128)(2,1)S(1)}, u32[]{:S(2)}) copy-start(bf16[1024,1024]{0,1:T(8,128)(2,1)S(1)} %get-tuple-element.86) | copy-start | bytes 6291460
  294.4 9.5 %copy-start.14 = (bf16[1024,1024]{0,1:T(8,128)(2,1)}, bf16[1024,1024]{0,1:T(8,128)(2,1)S(1)}, u32[]{:S(2)}) copy-start(bf16[1024,1024]{0,1:T(8,128)(2,1)S(1)} %get-tuple-element.87) | copy-start | bytes 6291460
  303.9 41.2 %copy-start.1 = (bf16[1,8,32,1024]{3,2,1,0:T(8,128)(2,1)S(1)}, bf16[1,8,32,1024]{3,2,1,0:T(8,128)(2,1)}, u32[]{:S(2)}) copy-start(bf16[1,8,32,1024]{3,2,1,0:T(8,128)(2,1)} %reduce-scatter.5.cloned.1.call-done) | copy-start | bytes 1572868
  303.9 90.4 %all-gather.15.cloned.1.call-start = ((), (), s32[]{:S(2)}) async-start(), calls=%async_computation.25 | async-start | bytes 2621440 | tf_op jit(solution)/shard_map/all_gather | solution.py:196
  349.4 123.4 %reduce-scatter.9.cloned.1.call-start = ((), (), s32[]{:S(2)}) async-start(), calls=%async_computation.20 | async-start | bytes 2621440 | tf_op jit(solution)/shard_map/reduce_scatter | solution.py:200
  397.6 13.9 %all-to-all-start.7 = ((bf16[8,128,256]{2,1,0:T(8,128)(2,1)}), bf16[8,128,256]{2,1,0:T(8,128)(2,1)}, u32[]{:S(2)}, u32[]{:S(2)}) async-start(bf16[8,128,256]{2,1,0:T(8,128)(2,1)} %bitcast.230), calls=%async_computation.9 | async-start | bytes 1048576 | tf_op jit(solution)/shard_map/all_to_all | solution.py:193
  416.9 4.2 copy-start.2
  416.9 4.2 copy-start.7
  443.2 24.7 %all-to-all-start.8 = ((bf16[8,128,768]{1,2,0:T(8,128)(2,1)}), bf16[8,128,768]{1,2,0:T(8,128)(2,1)S(1)}, u32[]{:S(2)}, u32[]{:S(2)}) async-start(bf16[8,128,768]{1,2,0:T(8,128)(2,1)} %pad_maximum_fusion.4), calls=%async_computation.10 | async-start | bytes 3145728 | tf_op jit(solution)/shard_map/all_to_all | solution.py:193
  469.0 30.2 %all-to-all-start.13 = ((bf16[8,1024,128]{1,2,0:T(8,128)(2,1)}), bf16[8,1024,128]{1,2,0:T(8,128)(2,1)S(1)}, u32[]{:S(2)}, u32[]{:S(2)}) async-start(bf16[8,1024,128]{1,2,0:T(8,128)(2,1)} %convert_bitcast_fusion), calls=%async_computation.17 | async-start | bytes 4194304 | tf_op jit(solution)/shard_map/all_to_all | solution.py:193
  472.7 89.6 %reduce-scatter.11.cloned.1.call-start = ((), (), s32[]{:S(2)}) async-start(), calls=%async_computation.21 | async-start | bytes 2621440 | tf_op jit(solution)/shard_map/reduce_scatter | solution.py:200
  479.1 3.5 copy-start.15
  500.6 53.9 %all-to-all-start.12 = ((bf16[8,128,2048]{2,1,0:T(8,128)(2,1)}), bf16[8,128,2048]{2,1,0:T(8,128)(2,1)}, u32[]{:S(2)}, u32[]{:S(2)}) async-start(bf16[8,128,2048]{2,1,0:T(8,128)(2,1)} %bitcast.206), calls=%async_computation.16 | async-start | bytes 8388608 | tf_op jit(solution)/shard_map/all_to_all | solution.py:193
  554.5 30.2 %all-to-all-start.11 = ((bf16[8,128,1024]{1,2,0:T(8,128)(2,1)}), bf16[8,128,1024]{1,2,0:T(8,128)(2,1)S(1)}, u32[]{:S(2)}, u32[]{:S(2)}) async-start(bf16[8,128,1024]{1,2,0:T(8,128)(2,1)} %copy_bitcast_fusion), calls=%async_computation.15 | async-start | bytes 4194304 | tf_op jit(solution)/shard_map/all_to_all | solution.py:193
  584.7 16.1 %all-to-all-start.10 = ((bf16[8,48,1024]{2,1,0:T(8,128)(2,1)}), bf16[8,48,1024]{2,1,0:T(8,128)(2,1)S(1)}, u32[]{:S(2)}, u32[]{:S(2)}) async-start(bf16[8,48,1024]{2,1,0:T(8,128)(2,1)} %fusion.31), calls=%async_computation.14 | async-start | bytes 1572864 | tf_op jit(solution)/shard_map/all_to_all | solution.py:193
  600.7 14.3 %all-to-all-start.9 = ((bf16[8,32,1024]{2,1,0:T(8,128)(2,1)}), bf16[8,32,1024]{2,1,0:T(8,128)(2,1)S(1)}, u32[]{:S(2)}, u32[]{:S(2)}) async-start(bf16[8,32,1024]{2,1,0:T(8,128)(2,1)} %get-tuple-element.103), calls=%async_computation.12 | async-start | bytes 1048576 | tf_op jit(solution)/shard_map/all_to_all | solution.py:193
  604.3 11.6 %collective-permute-start = (f32[3,128]{1,0:T(4,128)S(1)}, f32[3,128]{1,0:T(4,128)S(1)}, u32[]{:S(2)}, u32[]{:S(2)}) collective-permute-start(f32[3,128]{1,0:T(4,128)S(1)} %add_bitcast_fusion), channel_id=1, source_target_pairs={{0,1},{1,2},{2,3},{3,0},{4,5},{5,6},{6,7},{7,4},{8,9},{9,10},{10,1... | collective-permute-start | bytes 4616 | tf_op jit(solution)/shard_map/ppermute | solution.py:365
  604.5 11.4 %collective-permute-start.1 = (f32[3,128]{1,0:T(4,128)S(1)}, f32[3,128]{1,0:T(4,128)S(1)}, u32[]{:S(2)}, u32[]{:S(2)}) collective-permute-start(f32[3,128]{1,0:T(4,128)S(1)} %add_bitcast_fusion), channel_id=1, source_target_pairs={{0,2},{1,3},{2,0},{3,1},{4,6},{5,7},{6,4},{7,5},{8,10},{9,11},{10,... | collective-permute-start | bytes 4616 | tf_op jit(solution)/shard_map/ppermute | solution.py:365
  606.2 9.7 %collective-permute-start.2 = (f32[3,128]{1,0:T(4,128)S(1)}, f32[3,128]{1,0:T(4,128)S(1)}, u32[]{:S(2)}, u32[]{:S(2)}) collective-permute-start(f32[3,128]{1,0:T(4,128)S(1)} %add_bitcast_fusion), channel_id=1, source_target_pairs={{0,3},{1,0},{2,1},{3,2},{4,7},{5,4},{6,5},{7,6},{8,11},{9,8},{10,9... | collective-permute-start | bytes 4616 | tf_op jit(solution)/shard_map/ppermute | solution.py:365
  (12 other events, 19.2 us)
Sparse Core Ops, SparseCore 0:
  30.7 45.0 all-gather.8
  141.2 40.6 reduce-scatter.4
  185.7 44.8 all-gather.12
  232.6 44.4 all-gather.10
  304.0 41.0 reduce-scatter.6
  349.5 44.8 all-gather.14
  396.7 42.4 reduce-scatter.8
  482.8 42.9 reduce-scatter.10

commit v5 on v4

--- a/solution.py
+++ b/solution.py
@@ -245,6 +245,7 @@
         w_in, wout_t = w_attn[:, : 3 * cols], w_attn[:, 3 * cols :]
         w_attn, out_grad = after(w_attn, out_grad)
         grad = exchange(out_grad)
+        n1_all, grad = after(n1_all, grad)
         grad_all = collect(grad)
         qkv = jnp.dot(n1_all, w_in, preferred_element_type=F32).astype(BF)
 
@@ -271,16 +272,17 @@
         mixed_all = frame_join(mixed.reshape(steps, frames, cols).astype(BF))
         attn = jnp.einsum("fe,de->fd", mixed_all, wout_t, preferred_element_type=F32)
 
-        attn, w_down = after(attn.astype(BF), w_down)
+        attn, w_down, w_gate_up, grad_all = after(attn.astype(BF), w_down, w_gate_up, grad_all)
         attn = deal(attn)
         wdown = exchange(w_down.astype(BF))
+        wgu = jnp.concatenate([w_gate_up[:, 0], w_gate_up[:, 1]], axis=2).astype(BF)
+        attn, wdown, wgu = after(attn, wdown, wgu)
         wdown = jnp.swapaxes(wdown, 0, 1).reshape(-1, width)
         h1 = h0 + attn
         r2 = lax.rsqrt(jnp.mean(h1 * h1, axis=-1, keepdims=True) + EPS)
         n2 = (h1 * r2 * gain_two).astype(BF)
-        n2, w_gate_up = after(n2, w_gate_up)
+        n2, wgu = after(n2, wgu)
         n2_all = collect(n2)
-        wgu = jnp.concatenate([w_gate_up[:, 0], w_gate_up[:, 1]], axis=2).astype(BF)
         wgu = exchange(wgu).reshape(width, -1)
 
         gate_up = jnp.dot(n2_all, wgu, preferred_element_type=F32)
@@ -290,12 +292,13 @@
         silu_val = gate * sigma
         hidden = (silu_val * upval).astype(BF)
         d_hidden = jnp.einsum("fd,kd->fk", grad_all, wdown, preferred_element_type=F32)
-        d_gate = d_hidden * upval * (sigma * (1.0 + gate * (1.0 - sigma)))
-        d_up = d_hidden * silu_val
-        d_gu = jnp.concatenate([d_gate, d_up], axis=1).astype(BF)
-        dn2 = jnp.einsum("fk,dk->fd", d_gu, wgu, preferred_element_type=F32).astype(BF)
-
-        dn2, hidden = after(dn2, hidden)
+        d_gate = (d_hidden * upval * (sigma * (1.0 + gate * (1.0 - sigma)))).astype(BF)
+        d_up = (d_hidden * silu_val).astype(BF)
+        wgate, wup = wgu[:, :hid_width], wgu[:, hid_width:]
+        dn2 = jnp.einsum("fk,dk->fd", d_gate, wgate, preferred_element_type=F32)
+        dn2 = dn2 + jnp.einsum("fk,dk->fd", d_up, wup, preferred_element_type=F32)
+
+        dn2, hidden, d_gate, d_up = after(dn2.astype(BF), hidden, d_gate, d_up)
         dn2 = deal(dn2)
         d_down = jnp.einsum(
             "fk,frd->rkd",
@@ -303,19 +306,22 @@
             grad_all.reshape(-1, count, block),
             preferred_element_type=F32,
         )
-        g_down = exchange(d_down.astype(BF)).astype(F32)
+        g_down = exchange(d_down.astype(BF))
+        g_gate = jnp.einsum("fd,fk->dk", n2_all, d_gate, preferred_element_type=F32).astype(BF)
+        g_up = jnp.einsum("fd,fk->dk", n2_all, d_up, preferred_element_type=F32).astype(BF)
+        dn2, g_down, g_gate, g_up = after(dn2, g_down, g_gate, g_up)
         dh_norm2, dgain_two = norm_back(dn2, h1, r2, gain_two)
         dh1 = grad.astype(F32) + dh_norm2
-        dh1_low, d_gu, hidden = after(dh1.astype(BF), d_gu, hidden)
+        dh1_low, g_gate, hidden = after(dh1.astype(BF), g_gate, hidden)
         dh1_all = collect(dh1_low)
-        d_gate_up = jnp.einsum("fd,fk->dk", n2_all, d_gu, preferred_element_type=F32)
-        g_gate_up = exchange(d_gate_up.astype(BF).reshape(count, block, -1))
-        g_gate_up = jnp.stack([g_gate_up[..., :hid_width], g_gate_up[..., hid_width:]], axis=1)
-        g_gate_up = g_gate_up.astype(F32)
+        g_gate = exchange(g_gate.reshape(count, block, -1))
+        dh1_all, g_gate = after(dh1_all, g_gate)
 
         ffout = deal(jnp.dot(hidden, wdown, preferred_element_type=F32))
         d_mixed = jnp.dot(dh1_all, wout_t, preferred_element_type=F32).astype(BF)
-        d_mixed = frame_split(d_mixed).reshape(steps, frames, heads, HEAD)
+        d_mixed, g_up = after(frame_split(d_mixed), g_up)
+        d_mixed = d_mixed.reshape(steps, frames, heads, HEAD)
+        g_up = exchange(g_up.reshape(count, block, -1))
         probs = jnp.exp(score_of(query, keyv) - lse)
         d_probs = jnp.einsum("sfhe,tfhe->fhst", d_mixed, value, preferred_element_type=F32)
         d_value = jnp.einsum("fhst,sfhe->tfhe", probs_low, d_mixed, preferred_element_type=F32)
@@ -330,6 +336,8 @@
             [a.reshape(steps, frames, cols).astype(BF) for a in (d_query, d_key, d_value)],
             axis=-1,
         )
+        d_qkv, g_up = after(d_qkv, g_up)
+        g_gate_up = jnp.stack([g_gate, g_up], axis=1).astype(F32)
         d_qkv = frame_join(d_qkv)
         dn1 = jnp.einsum("fe,de->fd", d_qkv, w_in, preferred_element_type=F32).astype(BF)
 
@@ -342,10 +350,12 @@
             ],
             axis=1,
         )
-        g_attn = exchange(d_attn.reshape(count, block, -1)).astype(F32)
+        g_attn = exchange(d_attn.reshape(count, block, -1))
+        layer_out = exchange((h1 + ffout).astype(BF))
+        dn1, g_attn, layer_out = after(dn1, g_attn, layer_out)
+        g_down, g_attn = g_down.astype(F32), g_attn.astype(F32)
         g_qkv = jnp.stack([g_attn[..., j * cols : (j + 1) * cols] for j in range(3)], axis=1)
         g_out = jnp.swapaxes(g_attn[..., 3 * cols :], 1, 2)
-        layer_out = exchange((h1 + ffout).astype(BF))
 
         dh_norm1, dgain_one = norm_back(dn1, h0, r1, gain_one)
         dh0 = dh1 + dh_norm1

time: 631 us -> 536 us (0.85)
  waiting for transfers between devices: 318 us -> 208 us
  blocking collectives: 41.8 us -> 67.3 us
  local copies, waits for them, and re-layouts: 64.4 us -> 57.4 us
    all_to_all x12 -> x11, waiting for transfers between devices: 180 us -> 84.2 us  [exchange(): return lax.all_to_all(blocks, 'dp', 0, 0, tiled=True)]
    all_to_all x2 -> x4, blocking collectives: 41.8 us -> 67.3 us  [exchange(): return lax.all_to_all(blocks, 'dp', 0, 0, tiled=True)]
    reduce_scatter x4, waiting for transfers between devices: 77.1 us -> 60.6 us  [deal(): return lax.psum_scatter(slots, 'tensor', scatter_dimension=0).astype(F32)]
    convert_element_type x1 -> x4, other arithmetic: 2.13 us -> 8.54 us  [deal(): return lax.psum_scatter(slots, 'tensor', scatter_dimension=0).astype(F32)]
    unnamed x47 -> x62, local copies, waits for them, and re-layouts: 16.9 us -> 12.8 us
    dot_general x2 -> x4, matrix products: 18.9 us -> 20.7 us  [the longest x1 6.11 us: shards(): jnp.einsum('fd,fk->dk', n2_all, d_up, preferred_element_type=F32).astype(BF)]
    all_to_all x12 -> x11, starting transfers between devices: 48.5 us -> 47 us  [exchange(): return lax.all_to_all(blocks, 'dp', 0, 0, tiled=True)]
  transfers between devices with their start and end apart: 23 -> 22, of which waited for: 16 -> 13; matrix products, arithmetic and copies ran while one was open for 21% -> 25% of each run, Pallas kernels for 0% -> 0%
where the time goes in v5:
time: 536 us; the launch traced here: 531 us
  waiting for transfers between devices  208 us (39%)
  matrix products  83.5 us (16%)
  blocking collectives  67.3 us (13%)
  local copies, waits for them, and re-layouts  57.4 us (11%)
  starting transfers between devices  52.3 us (10%)
  other arithmetic  47 us (9%)
  between operations  15 us (3%)
    all_to_all x11, waiting for transfers between devices, exchange(): return lax.all_to_all(blocks, 'dp', 0, 0, tiled=True)  84.2 us
    all_to_all x4, blocking collectives, exchange(): return lax.all_to_all(blocks, 'dp', 0, 0, tiled=True)  67.3 us
    all_gather x4, waiting for transfers between devices, collect(): return lax.all_gather(rows, 'tensor', axis=0).reshape(-1, rows.shape[-1])  62.1 us
    reduce_scatter x4, waiting for transfers between devices, deal(): return lax.psum_scatter(slots, 'tensor', scatter_dimension=0).astype(F32)  60.6 us
    all_to_all x11, starting transfers between devices, exchange(): return lax.all_to_all(blocks, 'dp', 0, 0, tiled=True)  47 us
    unnamed x62, local copies, waits for them, and re-layouts  12.8 us
  transfers between devices with their start and end apart: 22, of which 13 were waited for; matrix products, arithmetic and copies ran while one was open for 25% of the time, Pallas kernels for 0%

profile of v5, /device:TPU:0, one launch (start us, length us, event | category | flops | bytes accessed | tf_op | source)
XLA Modules:
  0.0 530.7 jit_solution(4563782431991042095)
XLA Ops:
  11.2 5.3 %all-to-all-start = ((bf16[8,48,1024]{2,1,0:T(8,128)(2,1)}), bf16[8,48,1024]{2,1,0:T(8,128)(2,1)S(1)}, u32[]{:S(2)}, u32[]{:S(2)}) async-start(bf16[8,48,1024]{2,1,0:T(8,128)(2,1)} %pad_maximum_fusion.4), calls=%async_computation | async-start | bytes 1572864 | tf_op jit(solution)/shard_map/all_to_all | solution.py:193
  16.6 12.5 %all-to-all-done = bf16[8,48,1024]{2,1,0:T(8,128)(2,1)S(1)} async-done(((bf16[8,48,1024]{2,1,0:T(8,128)(2,1)}), bf16[8,48,1024]{2,1,0:T(8,128)(2,1)S(1)}, u32[]{:S(2)}, u32[]{:S(2)}) %all-to-all-start) | async-done | bytes 786464 | tf_op jit(solution)/shard_map/all_to_all | solution.py:193
  33.2 29.1 %all_to_all.75 = bf16[8,128,1024]{2,1,0:T(8,128)(2,1)S(1)} all-to-all(bf16[8,128,1024]{2,1,0:T(8,128)(2,1)S(1)} %pad_maximum_fusion.2), channel_id=1, replica_groups=mesh['dp'=8,'tensor'=4] {'dp'}, dimensions={0} | all-to-all | bytes 4194304 | tf_op jit(solution)/shard_map/all_to_all | solution.py:193
  62.4 12.8 %all_to_all.76 = bf16[8,32,1024]{2,1,0:T(8,128)(2,1)} all-to-all(bf16[8,32,1024]{2,1,0:T(8,128)(2,1)S(1)} %copy-done.23), channel_id=1, replica_groups=mesh['dp'=8,'tensor'=4] {'dp'}, dimensions={0} | all-to-all | bytes 1048576 | tf_op jit(solution)/shard_map/all_to_all | solution.py:193
  85.1 20.0 %all-to-all-done.3 = bf16[8,128,768]{2,1,0:T(8,128)(2,1)S(1)} async-done(((bf16[8,128,768]{2,1,0:T(8,128)(2,1)}), bf16[8,128,768]{2,1,0:T(8,128)(2,1)S(1)}, u32[]{:S(2)}, u32[]{:S(2)}) %all-to-all-start.3) | async-done | bytes 1572896 | tf_op jit(solution)/shard_map/all_to_all | solution.py:193
  120.7 12.1 %all_to_all.77 = bf16[8,128,256]{1,2,0:T(8,128)(2,1)S(1)} all-to-all(bf16[8,128,256]{1,2,0:T(8,128)(2,1)S(1)} %bitcast.182), channel_id=1, replica_groups=mesh['dp'=8,'tensor'=4] {'dp'}, dimensions={0} | all-to-all | bytes 1048576 | tf_op jit(solution)/shard_map/all_to_all | solution.py:193
  136.4 4.6 copy.156
  141.0 4.4 all-to-all-start.5
  152.5 26.3 %reduce-scatter.5.cloned.1.call-done = bf16[1,8,32,1024]{3,2,1,0:T(8,128)(2,1)} async-done(((bf16[4,8,32,1024]{3,2,1,0:T(8,128)(2,1)}), bf16[1,8,32,1024]{3,2,1,0:T(8,128)(2,1)}) %reduce-scatter.5.cloned.1.call-update) | async-done | bytes 524304 | tf_op jit(solution)/shard_map/reduce_scatter | solution.py:200
  183.6 4.8 all-to-all-start.6
  189.0 47.5 %all-gather.13.cloned.1.call-done = bf16[32,32,1024]{2,1,0:T(8,128)(2,1)} async-done(((bf16[8,32,1024]{2,1,0:T(8,128)(2,1)}), bf16[32,32,1024]{2,1,0:T(8,128)(2,1)}) %all-gather.13.cloned.1.call-update) | async-done | bytes 2097168 | tf_op jit(solution)/shard_map/all_gather | solution.py:196
  237.5 7.1 %fusion.32 = f32[1024,2048]{1,0:T(8,128)S(1)} fusion(bf16[1024,1024]{1,0:T(8,128)(2,1)} %bitcast.215, bf16[1024,2048]{1,0:T(8,128)(2,1)} %bitcast.35), kind=kOutput, calls=%fused_computation.113 | convolution fusion | flops 4294967296 | bytes 14680064 | tf_op jit(solution)/shard_map/dot_general | solution.py:288
  244.6 6.6 %multiply_convert_fusion.2 = (bf16[1024,1024]{1,0:T(8,128)(2,1)S(1)}, bf16[1024,1024]{1,0:T(8,128)(2,1)S(1)}, bf16[1024,1024]{1,0:T(8,128)(2,1)}) fusion(f32[1024,2048]{1,0:T(8,128)S(1)} %fusion.32, bf16[1024,1024]{1,0:T(8,128)(2,1)S(1)} %bitcast.185, bf16[1024,1024]{0,1:T(8,128)(2,1)} %bitcast.32), kind=kOutput, calls=%fused_computation.5 | convolution fusion | flops 2163212288 | bytes 18874368 | tf_op jit(solution)/shard_map/fd,kd->fk/dot_general | solution.py:294
  251.2 5.5 %fusion.1 = f32[1024,1024]{1,0:T(8,128)S(1)} fusion(bf16[1024,1024]{1,0:T(8,128)(2,1)S(1)} %get-tuple-element.64, bf16[1024,2048]{1,0:T(8,128)(2,1)} %bitcast.35), kind=kOutput, calls=%fused_computation.11 | convolution fusion | flops 2147483648 | bytes 8388608 | tf_op jit(solution)/shard_map/fk,dk->fd/dot_general | solution.py:299
  256.7 5.3 %add_convert_fusion = bf16[1024,1024]{1,0:T(8,128)(2,1)} fusion(f32[1024,1024]{1,0:T(8,128)S(1)} %fusion.1, bf16[1024,1024]{1,0:T(8,128)(2,1)S(1)} %get-tuple-element.63, bf16[1024,2048]{1,0:T(8,128)(2,1)} %bitcast.35), kind=kOutput, calls=%fused_computation.3 | convolution fusion | flops 2149580800 | bytes 10485760 | tf_op jit(solution)/shard_map/fk,dk->fd/dot_general | solution.py:298
  266.0 5.9 %convert_bitcast_fusion = bf16[8,1024,128]{1,2,0:T(8,128)(2,1)} fusion(bf16[1024,8,128]{0,2,1:T(8,128)(2,1)} %bitcast.191, bf16[1024,1024]{1,0:T(8,128)(2,1)} %get-tuple-element.74), kind=kOutput, calls=%fused_computation.25 | convolution fusion | flops 2148532224 | bytes 6291456 | tf_op jit(solution)/shard_map/fk,frd->rkd/dot_general | solution.py:303
  271.9 4.4 all-to-all-start.7
  276.8 6.1 %convolution_convert_fusion.1 = bf16[1024,1024]{1,0:T(8,128)(2,1)} fusion(bf16[1024,1024]{1,0:T(8,128)(2,1)} %bitcast.216, bf16[1024,1024]{1,0:T(8,128)(2,1)} %copy-done.26), kind=kOutput, calls=%fused_computation.31 | convolution fusion | flops 2148532224 | bytes 6291456 | tf_op jit(solution)/shard_map/fd,fk->dk/dot_general | solution.py:311
  286.6 17.0 %reduce-scatter.7.cloned.1.call-done = bf16[1,8,32,1024]{3,2,1,0:T(8,128)(2,1)} async-done(((bf16[4,8,32,1024]{3,2,1,0:T(8,128)(2,1)}), bf16[1,8,32,1024]{3,2,1,0:T(8,128)(2,1)}) %reduce-scatter.7.cloned.1.call-update) | async-done | bytes 524304 | tf_op jit(solution)/shard_map/reduce_scatter | solution.py:200
  308.7 4.4 all-to-all-start.8
  313.1 6.1 %convolution_convert_fusion = bf16[1024,1024]{1,0:T(8,128)(2,1)} fusion(bf16[1024,1024]{1,0:T(8,128)(2,1)} %get-tuple-element.74, bf16[1024,1024]{0,1:T(8,128)(2,1)} %bitcast.32), kind=kOutput, calls=%fused_computation.30 | convolution fusion | flops 2148532224 | bytes 6291456 | tf_op jit(solution)/shard_map/dot_general | solution.py:320
  319.2 20.4 %all-to-all-done.8 = bf16[8,128,1024]{2,1,0:T(8,128)(2,1)} async-done(((bf16[8,128,1024]{2,1,0:T(8,128)(2,1)}), bf16[8,128,1024]{2,1,0:T(8,128)(2,1)}, u32[]{:S(2)}, u32[]{:S(2)}) %all-to-all-start.8) | async-done | bytes 2097184 | tf_op jit(solution)/shard_map/all_to_all | solution.py:193
  339.7 14.0 %all-gather.15.cloned.1.call-done = bf16[32,32,1024]{2,1,0:T(8,128)(2,1)} async-done(((bf16[8,32,1024]{2,1,0:T(8,128)(2,1)}), bf16[32,32,1024]{2,1,0:T(8,128)(2,1)}) %all-gather.15.cloned.1.call-update) | async-done | bytes 2097168 | tf_op jit(solution)/shard_map/all_gather | solution.py:196
  356.1 13.3 %all_to_all.78 = bf16[8,128,256]{2,1,0:T(8,128)(2,1)} all-to-all(bf16[8,128,256]{2,1,0:T(8,128)(2,1)S(1)} %bitcast.196), channel_id=1, replica_groups=mesh['dp'=8,'tensor'=4] {'dp'}, dimensions={0} | all-to-all | bytes 1048576 | tf_op jit(solution)/shard_map/all_to_all | solution.py:193
  369.3 4.5 all-to-all-start.10
  390.7 5.1 fusion.18
  413.0 18.6 %all-to-all-done.11 = bf16[8,128,768]{1,2,0:T(8,128)(2,1)S(1)} async-done(((bf16[8,128,768]{1,2,0:T(8,128)(2,1)}), bf16[8,128,768]{1,2,0:T(8,128)(2,1)S(1)}, u32[]{:S(2)}, u32[]{:S(2)}) %all-to-all-start.11) | async-done | bytes 1572896 | tf_op jit(solution)/shard_map/all_to_all | solution.py:193
  452.3 4.4 all-to-all-done.13
  457.6 4.4 all-to-all-start.12
  462.0 17.3 %reduce-scatter.11.cloned.1.call-done = bf16[1,8,32,1024]{3,2,1,0:T(8,128)(2,1)} async-done(((bf16[4,8,32,1024]{3,2,1,0:T(8,128)(2,1)}), bf16[1,8,32,1024]{3,2,1,0:T(8,128)(2,1)}) %reduce-scatter.11.cloned.1.call-update) | async-done | bytes 524304 | tf_op jit(solution)/shard_map/reduce_scatter | solution.py:200
  481.4 7.2 %all-to-all-done.12 = bf16[8,128,1024]{1,2,0:T(8,128)(2,1)} async-done(((bf16[8,128,1024]{1,2,0:T(8,128)(2,1)}), bf16[8,128,1024]{1,2,0:T(8,128)(2,1)}, u32[]{:S(2)}, u32[]{:S(2)}) %all-to-all-start.12) | async-done | bytes 2097184 | tf_op jit(solution)/shard_map/all_to_all | solution.py:193
  499.9 6.2 %maximum_convert_fusion = f32[8,2,128,1024]{3,2,1,0:T(8,128)} fusion(bf16[8,1,128,1024]{3,2,1,0:T(8,128)(2,1)} %bitcast.74, bf16[8,1,128,1024]{3,2,1,0:T(8,128)(2,1)} %bitcast.73), kind=kLoop, calls=%fused_computation.1 | loop fusion | flops 4194304 | bytes 12582912 | tf_op jit(solution)/shard_map/convert_element_type | solution.py:340
  (184 shorter events, 152.5 us)
Async XLA Ops:
  11.2 19.4 %copy-start.22 = (f32[8,256,128]{2,1,0:T(8,128)S(1)}, f32[8,256,128]{2,1,0:T(8,128)}, u32[]{:S(2)}) copy-start(f32[8,256,128]{2,1,0:T(8,128)} %param.12) | copy-start | bytes 3145732
  11.2 17.9 %all-to-all-start = ((bf16[8,48,1024]{2,1,0:T(8,128)(2,1)}), bf16[8,48,1024]{2,1,0:T(8,128)(2,1)S(1)}, u32[]{:S(2)}, u32[]{:S(2)}) async-start(bf16[8,48,1024]{2,1,0:T(8,128)(2,1)} %pad_maximum_fusion.4), calls=%async_computation | async-start | bytes 1572864 | tf_op jit(solution)/shard_map/all_to_all | solution.py:193
  16.6 59.2 %all-gather.9.cloned.1.call-start = ((), (), s32[]{:S(2)}) async-start(), calls=%async_computation.23 | async-start | bytes 2621440 | tf_op jit(solution)/shard_map/all_gather | solution.py:196
  33.2 29.2 %copy-start.23 = (bf16[8,32,1024]{2,1,0:T(8,128)(2,1)S(1)}, bf16[8,32,1024]{2,1,0:T(8,128)(2,1)}, u32[]{:S(2)}) copy-start(bf16[8,32,1024]{2,1,0:T(8,128)(2,1)} %param.17) | copy-start | bytes 1572868
  62.4 16.8 %copy-start.12 = (bf16[8,128,1024]{2,1,0:T(8,128)(2,1)}, bf16[8,128,1024]{2,1,0:T(8,128)(2,1)S(1)}, u32[]{:S(2)}) copy-start(bf16[8,128,1024]{2,1,0:T(8,128)(2,1)S(1)} %all_to_all.75) | copy-start | bytes 6291460
  80.4 24.6 %all-to-all-start.3 = ((bf16[8,128,768]{2,1,0:T(8,128)(2,1)}), bf16[8,128,768]{2,1,0:T(8,128)(2,1)S(1)}, u32[]{:S(2)}, u32[]{:S(2)}) async-start(bf16[8,128,768]{2,1,0:T(8,128)(2,1)} %bitcast.17), calls=%async_computation.3 | async-start | bytes 3145728 | tf_op jit(solution)/shard_map/all_to_all | solution.py:193
  84.1 52.3 %all-gather.11.cloned.1.call-start = ((), (), s32[]{:S(2)}) async-start(), calls=%async_computation.24 | async-start | bytes 2621440 | tf_op jit(solution)/shard_map/all_gather | solution.py:196
  84.8 94.0 %reduce-scatter.5.cloned.1.call-start = ((), (), s32[]{:S(2)}) async-start(), calls=%async_computation.19 | async-start | bytes 2621440 | tf_op jit(solution)/shard_map/reduce_scatter | solution.py:200
  107.2 5.6 %copy-start.5 = (bf16[8,128,4,64]{3,0,2,1:T(8,128)(2,1)}, bf16[8,128,4,64]{3,0,2,1:T(8,128)(2,1)S(1)}, u32[]{:S(2)}) copy-start(bf16[8,128,4,64]{3,0,2,1:T(8,128)(2,1)S(1)} %copy.148) | copy-start | bytes 1572868
  141.0 39.9 %all-to-all-start.5 = ((bf16[8,1024,128]{1,2,0:T(8,128)(2,1)}), bf16[8,1024,128]{1,2,0:T(8,128)(2,1)}, u32[]{:S(2)}, u32[]{:S(2)}) async-start(bf16[8,1024,128]{1,2,0:T(8,128)(2,1)} %copy.156), calls=%async_computation.6 | async-start | bytes 4194304 | tf_op jit(solution)/shard_map/all_to_all | solution.py:193
  183.6 53.9 %all-to-all-start.6 = ((bf16[8,128,2048]{2,1,0:T(8,128)(2,1)}), bf16[8,128,2048]{2,1,0:T(8,128)(2,1)}, u32[]{:S(2)}, u32[]{:S(2)}) async-start(bf16[8,128,2048]{2,1,0:T(8,128)(2,1)} %pad_maximum_fusion), calls=%async_computation.7 | async-start | bytes 8388608 | tf_op jit(solution)/shard_map/all_to_all | solution.py:193
  188.4 48.1 %all-gather.13.cloned.1.call-start = ((), (), s32[]{:S(2)}) async-start(), calls=%async_computation.25 | async-start | bytes 2621440 | tf_op jit(solution)/shard_map/all_gather | solution.py:196
  189.0 114.7 %reduce-scatter.7.cloned.1.call-start = ((), (), s32[]{:S(2)}) async-start(), calls=%async_computation.20 | async-start | bytes 2621440 | tf_op jit(solution)/shard_map/reduce_scatter | solution.py:200
  237.5 7.1 %copy-start.17 = (bf16[32,32,1024]{2,1,0:T(8,128)(2,1)S(1)}, bf16[32,32,1024]{2,1,0:T(8,128)(2,1)}, u32[]{:S(2)}) copy-start(bf16[32,32,1024]{2,1,0:T(8,128)(2,1)} %all-gather.11.cloned.1.call-done) | copy-start | bytes 6291460
  271.9 33.9 %all-to-all-start.7 = ((bf16[8,1024,128]{1,2,0:T(8,128)(2,1)}), bf16[8,1024,128]{1,2,0:T(8,128)(2,1)}, u32[]{:S(2)}, u32[]{:S(2)}) async-start(bf16[8,1024,128]{1,2,0:T(8,128)(2,1)} %convert_bitcast_fusion), calls=%async_computation.9 | async-start | bytes 4194304 | tf_op jit(solution)/shard_map/all_to_all | solution.py:193
  276.3 77.4 %all-gather.15.cloned.1.call-start = ((), (), s32[]{:S(2)}) async-start(), calls=%async_computation.26 | async-start | bytes 2621440 | tf_op jit(solution)/shard_map/all_gather | solution.py:196
  276.7 6.1 %copy-start.25 = (bf16[32,32,1024]{2,1,0:T(8,128)(2,1)S(1)}, bf16[32,32,1024]{2,1,0:T(8,128)(2,1)}, u32[]{:S(2)}) copy-start(bf16[32,32,1024]{2,1,0:T(8,128)(2,1)} %all-gather.13.cloned.1.call-done) | copy-start | bytes 6291460
  276.8 6.1 %copy-start.28 = (bf16[1024,1024]{1,0:T(8,128)(2,1)S(1)}, bf16[1024,1024]{1,0:T(8,128)(2,1)}, u32[]{:S(2)}) copy-start(bf16[1024,1024]{1,0:T(8,128)(2,1)} %copy-done.27) | copy-start | bytes 6291460
  308.7 31.0 %all-to-all-start.8 = ((bf16[8,128,1024]{2,1,0:T(8,128)(2,1)}), bf16[8,128,1024]{2,1,0:T(8,128)(2,1)}, u32[]{:S(2)}, u32[]{:S(2)}) async-start(bf16[8,128,1024]{2,1,0:T(8,128)(2,1)} %bitcast.188), calls=%async_computation.10 | async-start | bytes 4194304 | tf_op jit(solution)/shard_map/all_to_all | solution.py:193
  313.0 97.9 %reduce-scatter.9.cloned.1.call-start = ((), (), s32[]{:S(2)}) async-start(), calls=%async_computation.21 | async-start | bytes 2621440 | tf_op jit(solution)/shard_map/reduce_scatter | solution.py:200
  369.3 37.1 %all-to-all-start.10 = ((bf16[8,128,1024]{2,1,0:T(8,128)(2,1)}), bf16[8,128,1024]{2,1,0:T(8,128)(2,1)}, u32[]{:S(2)}, u32[]{:S(2)}) async-start(bf16[8,128,1024]{2,1,0:T(8,128)(2,1)} %bitcast.186), calls=%async_computation.12 | async-start | bytes 4194304 | tf_op jit(solution)/shard_map/all_to_all | solution.py:193
  406.5 25.2 %all-to-all-start.11 = ((bf16[8,128,768]{1,2,0:T(8,128)(2,1)}), bf16[8,128,768]{1,2,0:T(8,128)(2,1)S(1)}, u32[]{:S(2)}, u32[]{:S(2)}) async-start(bf16[8,128,768]{1,2,0:T(8,128)(2,1)} %pad_maximum_fusion.3), calls=%async_computation.13 | async-start | bytes 3145728 | tf_op jit(solution)/shard_map/all_to_all | solution.py:193
  410.6 68.6 %reduce-scatter.11.cloned.1.call-start = ((), (), s32[]{:S(2)}) async-start(), calls=%async_computation.22 | async-start | bytes 2621440 | tf_op jit(solution)/shard_map/reduce_scatter | solution.py:200
  443.6 13.2 %all-to-all-start.13 = ((bf16[8,32,1024]{2,1,0:T(8,128)(2,1)}), bf16[8,32,1024]{2,1,0:T(8,128)(2,1)S(1)}, u32[]{:S(2)}, u32[]{:S(2)}) async-start(bf16[8,32,1024]{2,1,0:T(8,128)(2,1)} %add_convert_fusion.1), calls=%async_computation.17 | async-start | bytes 1048576 | tf_op jit(solution)/shard_map/all_to_all | solution.py:193
  452.3 36.3 %copy-start.4 = (bf16[8,48,1024]{2,1,0:T(8,128)(2,1)S(1)}, bf16[8,48,1024]{2,1,0:T(8,128)(2,1)}, u32[]{:S(2)}) copy-start(bf16[8,48,1024]{2,1,0:T(8,128)(2,1)} %copy-done.3) | copy-start | bytes 2359300
  457.6 31.0 %all-to-all-start.12 = ((bf16[8,128,1024]{1,2,0:T(8,128)(2,1)}), bf16[8,128,1024]{1,2,0:T(8,128)(2,1)}, u32[]{:S(2)}, u32[]{:S(2)}) async-start(bf16[8,128,1024]{1,2,0:T(8,128)(2,1)} %copy_bitcast_fusion), calls=%async_computation.16 | async-start | bytes 4194304 | tf_op jit(solution)/shard_map/all_to_all | solution.py:193
  462.0 28.4 %copy-start.2 = (f32[8,32,1024]{2,1,0:T(8,128)S(1)}, f32[8,32,1024]{2,1,0:T(8,128)}, u32[]{:S(2)}) copy-start(f32[8,32,1024]{2,1,0:T(8,128)} %bitcast_convert_fusion.2) | copy-start | bytes 3145732
  462.0 28.4 %copy-start.9 = (bf16[8,32,1024]{2,1,0:T(8,128)(2,1)S(1)}, bf16[8,32,1024]{2,1,0:T(8,128)(2,1)}, u32[]{:S(2)}) copy-start(bf16[8,32,1024]{2,1,0:T(8,128)(2,1)} %all_to_all.76) | copy-start | bytes 1572868
  492.3 17.8 %all-to-all-start.14 = ((bf16[8,48,1024]{2,1,0:T(8,128)(2,1)}), bf16[8,48,1024]{2,1,0:T(8,128)(2,1)S(1)}, u32[]{:S(2)}, u32[]{:S(2)}) async-start(bf16[8,48,1024]{2,1,0:T(8,128)(2,1)} %fusion.20), calls=%async_computation.18 | async-start | bytes 1572864 | tf_op jit(solution)/shard_map/all_to_all | solution.py:193
  510.1 10.5 %collective-permute-start = (f32[3,128]{1,0:T(4,128)S(1)}, f32[3,128]{1,0:T(4,128)S(1)}, u32[]{:S(2)}, u32[]{:S(2)}) collective-permute-start(f32[3,128]{1,0:T(4,128)S(1)} %add_bitcast_fusion), channel_id=1, source_target_pairs={{0,1},{1,2},{2,3},{3,0},{4,5},{5,6},{6,7},{7,4},{8,9},{9,10},{10,1... | collective-permute-start | bytes 4616 | tf_op jit(solution)/shard_map/ppermute | solution.py:375
  510.4 10.3 %collective-permute-start.1 = (f32[3,128]{1,0:T(4,128)S(1)}, f32[3,128]{1,0:T(4,128)S(1)}, u32[]{:S(2)}, u32[]{:S(2)}) collective-permute-start(f32[3,128]{1,0:T(4,128)S(1)} %add_bitcast_fusion), channel_id=1, source_target_pairs={{0,2},{1,3},{2,0},{3,1},{4,6},{5,7},{6,4},{7,5},{8,10},{9,11},{10,... | collective-permute-start | bytes 4616 | tf_op jit(solution)/shard_map/ppermute | solution.py:375
  512.0 8.7 %collective-permute-start.2 = (f32[3,128]{1,0:T(4,128)S(1)}, f32[3,128]{1,0:T(4,128)S(1)}, u32[]{:S(2)}, u32[]{:S(2)}) collective-permute-start(f32[3,128]{1,0:T(4,128)S(1)} %add_bitcast_fusion), channel_id=1, source_target_pairs={{0,3},{1,0},{2,1},{3,2},{4,7},{5,4},{6,5},{7,6},{8,11},{9,8},{10,9... | collective-permute-start | bytes 4616 | tf_op jit(solution)/shard_map/ppermute | solution.py:375
  (19 other events, 50.8 us)
Sparse Core Ops, SparseCore 0:
  30.7 45.0 all-gather.8
  86.5 46.5 all-gather.10
  136.5 42.2 reduce-scatter.4
  191.0 45.4 all-gather.12
  262.1 41.4 reduce-scatter.6
  308.8 44.8 all-gather.14
  356.5 42.4 reduce-scatter.8
  438.5 40.6 reduce-scatter.10

commit v6 on v5

--- a/solution.py
+++ b/solution.py
@@ -222,34 +222,48 @@
             pads = [(0, 0)] * (line.ndim - 1) + [(0, TILE - 1), (0, width - line.shape[-1])]
             return jnp.pad(line[..., None, :], pads)
 
+        here = lax.axis_index("tensor")
+
+        def own(array):
+            return lax.dynamic_index_in_dim(array, here, 0, keepdims=False)
+
         small = jnp.concatenate([norm_gains, pad_row[None]], axis=0).astype(BF).reshape(-1)
         line = jnp.concatenate([small, text_mask.astype(BF)])
-        notes = jnp.broadcast_to(tile(line)[None], (count, TILE, width))
-        hello = exchange(jnp.concatenate([layer_in, notes], axis=1))
-        rows_in = hello[:, :local].astype(F32)
-        notes = hello[:, local].astype(F32)
-        small = jnp.swapaxes(notes[:, : 3 * block].reshape(count, 3, block), 0, 1)
-        gain_one, gain_two, pad_vec = small.reshape(3, width)
-        padded = jnp.where(me == 0, 1.0 - notes[:, 3 * block : 3 * block + local], 0.0)[..., None]
-        h0 = rows_in + padded * pad_vec
-        r1 = lax.rsqrt(jnp.mean(h0 * h0, axis=-1, keepdims=True) + EPS)
-        n1 = (h0 * r1 * gain_one).astype(BF)
-        n1, w_qkv, w_out = after(n1, w_qkv, w_out)
-        n1_all = collect(n1)
+        hello = jnp.concatenate([layer_in.reshape(-1, width), tile(line)])
+        hello = lax.all_gather(hello, "tensor", axis=0)
 
         w_attn = jnp.concatenate(
             [w_qkv[:, 0], w_qkv[:, 1], w_qkv[:, 2], jnp.swapaxes(w_out, 1, 2)], axis=2
         )
         w_attn = exchange(w_attn.astype(BF)).reshape(width, -1)
         cols = w_attn.shape[1] // 4
+        hello, w_attn = after(hello, w_attn)
         w_in, wout_t = w_attn[:, : 3 * cols], w_attn[:, 3 * cols :]
-        w_attn, out_grad = after(w_attn, out_grad)
+        wout_all = lax.all_gather(wout_t, "tensor", axis=0)
+
+        rows_in = hello[:, : steps * local].reshape(lanes, steps, local, width)
+        rows_in = jnp.swapaxes(rows_in, 0, 1).reshape(steps, -1, width)
+        notes = jnp.pad(hello[:, steps * local], ((0, TILE - lanes), (0, 0)))
+        notes = jnp.broadcast_to(notes[None], (count, TILE, width))
+        hello = exchange(jnp.concatenate([rows_in, notes], axis=1))
+        rows_in = jnp.swapaxes(hello[:, : lanes * local].reshape(count, lanes, local, width), 0, 1)
+        notes = hello[:, lanes * local : lanes * local + lanes].astype(F32)
+        small = jnp.swapaxes(notes[:, 0, : 3 * block].reshape(count, 3, block), 0, 1)
+        gain_one, gain_two, pad_vec = small.reshape(3, width)
+        mask = jnp.swapaxes(notes[..., 3 * block : 3 * block + local], 0, 1)
+        padded = jnp.where(me == 0, 1.0 - mask, 0.0)[..., None]
+        h0 = rows_in.astype(F32) + padded * pad_vec
+        r1 = lax.rsqrt(jnp.mean(h0 * h0, axis=-1, keepdims=True) + EPS)
+        n1_all = (h0 * r1 * gain_one).astype(BF).reshape(-1, width)
+        rows_in, out_grad = after(rows_in, out_grad)
         grad = exchange(out_grad)
-        n1_all, grad = after(n1_all, grad)
+        qkv = jnp.dot(n1_all, w_in, preferred_element_type=F32).astype(BF)
+        qkv, grad, w_gate_up, w_down = after(qkv, grad, w_gate_up, w_down)
         grad_all = collect(grad)
-        qkv = jnp.dot(n1_all, w_in, preferred_element_type=F32).astype(BF)
-
-        qkv = frame_split(qkv)
+        wgu = jnp.concatenate([w_gate_up[:, 0], w_gate_up[:, 1]], axis=2).astype(BF)
+        wdown = w_down.astype(BF)
+
+        qkv, wgu, wdown = after(frame_split(qkv), wgu, wdown)
         frames = qkv.shape[1]
         heads = cols // HEAD
         scale = 1.0 / math.sqrt(HEAD)
@@ -270,20 +284,20 @@
         probs_low = (expo / total).astype(BF)
         mixed = jnp.einsum("fhst,tfhe->sfhe", probs_low, value, preferred_element_type=F32)
         mixed_all = frame_join(mixed.reshape(steps, frames, cols).astype(BF))
-        attn = jnp.einsum("fe,de->fd", mixed_all, wout_t, preferred_element_type=F32)
-
-        attn, w_down, w_gate_up, grad_all = after(attn.astype(BF), w_down, w_gate_up, grad_all)
-        attn = deal(attn)
-        wdown = exchange(w_down.astype(BF))
-        wgu = jnp.concatenate([w_gate_up[:, 0], w_gate_up[:, 1]], axis=2).astype(BF)
-        attn, wdown, wgu = after(attn, wdown, wgu)
-        wdown = jnp.swapaxes(wdown, 0, 1).reshape(-1, width)
-        h1 = h0 + attn
+
+        mixed_all, wout_all, grad_all, wgu, wdown = after(
+            mixed_all, wout_all, grad_all, wgu, wdown
+        )
+        mixed_full = lax.all_gather(mixed_all, "tensor", axis=0)
+        mixed_full = jnp.concatenate([mixed_full[k] for k in range(lanes)], axis=1)
+        wout_full = jnp.concatenate([wout_all[k] for k in range(lanes)], axis=1)
+        wgu, wdown = after(exchange(wgu).reshape(width, -1), wdown)
+        wdown = jnp.swapaxes(exchange(wdown), 0, 1).reshape(-1, width)
+        attn = jnp.einsum("fe,de->fd", mixed_full, wout_full, preferred_element_type=F32)
+        h1 = h0 + attn.reshape(h0.shape)
         r2 = lax.rsqrt(jnp.mean(h1 * h1, axis=-1, keepdims=True) + EPS)
-        n2 = (h1 * r2 * gain_two).astype(BF)
-        n2, wgu = after(n2, wgu)
-        n2_all = collect(n2)
-        wgu = exchange(wgu).reshape(width, -1)
+        n2_all = (h1 * r2 * gain_two).astype(BF).reshape(-1, width)
+        h0, r1, h1, r2, padded = own(h0), own(r1), own(h1), own(r2), own(padded)
 
         gate_up = jnp.dot(n2_all, wgu, preferred_element_type=F32)
         hid_width = gate_up.shape[1] // 2

time: 536 us -> 560 us (1.045)
  local copies, waits for them, and re-layouts: 57.4 us -> 79 us
  other arithmetic: 47 us -> 58.9 us
  blocking collectives: 67.3 us -> 57.1 us
  waiting for transfers between devices: 208 us -> 199 us
    all_gather x0 -> x3, waiting for transfers between devices: none -> 52 us  [the longest x1 35.5 us: shards(): mixed_full = lax.all_gather(mixed_all, 'tensor', axis=0)]
    all_gather x4 -> x2, waiting for transfers between devices: 62.1 us -> 14 us  [collect(): return lax.all_gather(rows, 'tensor', axis=0).reshape(-1, rows.shape[-1])]
    reduce_scatter x4 -> x3, waiting for transfers between devices: 60.6 us -> 31.3 us  [deal(): return lax.psum_scatter(slots, 'tensor', scatter_dimension=0).astype(F32)]
    all_to_all x11 -> x12, waiting for transfers between devices: 84.2 us -> 102 us  [exchange(): return lax.all_to_all(blocks, 'dp', 0, 0, tiled=True)]
    all_to_all x4 -> x3, blocking collectives: 67.3 us -> 57.1 us  [exchange(): return lax.all_to_all(blocks, 'dp', 0, 0, tiled=True)]
    slice x1 -> x7, local copies, waits for them, and re-layouts: 0.02 us -> 6.41 us  [the longest x1 1.87 us: shards(): w_in, wout_t = (w_attn[:, :3 * cols], w_attn[:, 3 * cols:])]
    unnamed x62 -> x88, local copies, waits for them, and re-layouts: 12.8 us -> 16.6 us
    all_to_all x11 -> x12, starting transfers between devices: 47 us -> 49.5 us  [exchange(): return lax.all_to_all(blocks, 'dp', 0, 0, tiled=True)]
  transfers between devices with their start and end apart: 22 -> 23, of which waited for: 13 -> 14; matrix products, arithmetic and copies ran while one was open for 25% -> 31% of each run, Pallas kernels for 0% -> 0%
where the time goes in v6:
time: 560 us; the launch traced here: 553 us
  waiting for transfers between devices  199 us (36%)
  matrix products  88.5 us (16%)
  local copies, waits for them, and re-layouts  79 us (14%)
  other arithmetic  58.9 us (11%)
  blocking collectives  57.1 us (10%)
  starting transfers between devices  54.7 us (10%)
  between operations  15.2 us (3%)
    all_to_all x12, waiting for transfers between devices, exchange(): return lax.all_to_all(blocks, 'dp', 0, 0, tiled=True)  102 us
    all_to_all x3, blocking collectives, exchange(): return lax.all_to_all(blocks, 'dp', 0, 0, tiled=True)  57.1 us
    all_to_all x12, starting transfers between devices, exchange(): return lax.all_to_all(blocks, 'dp', 0, 0, tiled=True)  49.5 us
    all_gather x1, waiting for transfers between devices, shards(): mixed_full = lax.all_gather(mixed_all, 'tensor', axis=0)  35.5 us
    reduce_scatter x3, waiting for transfers between devices, deal(): return lax.psum_scatter(slots, 'tensor', scatter_dimension=0).astype(F32)  31.3 us
    unnamed x88, local copies, waits for them, and re-layouts  16.6 us
    all_gather x1, waiting for transfers between devices, shards(): hello = lax.all_gather(hello, 'tensor', axis=0)  16.5 us
    all_gather x2, waiting for transfers between devices, collect(): return lax.all_gather(rows, 'tensor', axis=0).reshape(-1, rows.shape[-1])  14 us
  transfers between devices with their start and end apart: 23, of which 14 were waited for; matrix products, arithmetic and copies ran while one was open for 31% of the time, Pallas kernels for 0%

profile of v6, /device:TPU:0, one launch (start us, length us, event | category | flops | bytes accessed | tf_op | source)
XLA Modules:
  0.0 552.5 jit_solution(13847504880652454059)
XLA Ops:
  13.8 31.7 %all_to_all.75 = bf16[8,128,1024]{2,1,0:T(8,128)(2,1)} all-to-all(bf16[8,128,1024]{2,1,0:T(8,128)(2,1)S(1)} %pad_maximum_fusion.3), channel_id=1, replica_groups=mesh['dp'=8,'tensor'=4] {'dp'}, dimensions={0} | all-to-all | bytes 4194304 | tf_op jit(solution)/shard_map/all_to_all | solution.py:193
  45.5 16.5 %all-gather.11.cloned.1.call-done = bf16[1088,1024]{1,0:T(8,128)(2,1)} async-done(((bf16[272,1024]{1,0:T(8,128)(2,1)}), bf16[1088,1024]{1,0:T(8,128)(2,1)}) %all-gather.11.cloned.1.call-update) | async-done | bytes 2228240 | tf_op jit(solution)/shard_map/all_gather | solution.py:233
  72.0 27.5 %all-to-all-done.1 = bf16[8,144,1024]{2,1,0:T(8,128)(2,1)S(1)} async-done(((bf16[8,144,1024]{2,1,0:T(8,128)(2,1)}), bf16[8,144,1024]{2,1,0:T(8,128)(2,1)S(1)}, u32[]{:S(2)}, u32[]{:S(2)}) %all-to-all-start.1) | async-done | bytes 2359328 | tf_op jit(solution)/shard_map/all_to_all | solution.py:193
  109.0 4.5 convolution_convert_fusion.5
  113.5 5.1 all-to-all-done.2
  126.5 6.2 %convert.37 = bf16[8,2,128,1024]{3,2,1,0:T(8,128)(2,1)} convert(f32[8,2,128,1024]{3,2,1,0:T(8,128)} %param.13) | non-fusion elementwise | flops 2097152 | bytes 12582912 | tf_op jit(solution)/shard_map/convert.8 | solution.py:430
  132.7 4.6 copy.104
  163.0 12.1 %all_to_all.76 = bf16[8,128,256]{1,2,0:T(8,128)(2,1)S(1)} all-to-all(bf16[8,128,256]{1,2,0:T(8,128)(2,1)S(1)} %bitcast.250), channel_id=1, replica_groups=mesh['dp'=8,'tensor'=4] {'dp'}, dimensions={0} | all-to-all | bytes 1048576 | tf_op jit(solution)/shard_map/all_to_all | solution.py:193
  176.2 4.6 all-to-all-start.5
  183.5 35.5 %all-gather.17.cloned.1.call-done = bf16[4096,256]{1,0:T(8,128)(2,1)} async-done(((bf16[1024,256]{1,0:T(8,128)(2,1)}), bf16[4096,256]{1,0:T(8,128)(2,1)}) %all-gather.17.cloned.1.call-update) | async-done | bytes 2097168 | tf_op jit(solution)/shard_map/all_gather | solution.py:291
  229.9 4.3 all-to-all-start.6
  241.9 8.9 %fusion.61 = f32[1024,2048]{1,0:T(8,128)} fusion(bf16[1024,1024]{1,0:T(8,128)(2,1)S(1)} %bitcast.259, bf16[1024,2048]{1,0:T(8,128)(2,1)} %bitcast.43), kind=kOutput, calls=%fused_computation.150 | convolution fusion | flops 4294967296 | bytes 14680064 | tf_op jit(solution)/shard_map/dot_general | solution.py:302
  250.8 10.1 %all-to-all-done.6 = bf16[8,1024,128]{1,2,0:T(8,128)(2,1)} async-done(((bf16[8,1024,128]{1,2,0:T(8,128)(2,1)}), bf16[8,1024,128]{1,2,0:T(8,128)(2,1)}, u32[]{:S(2)}, u32[]{:S(2)}) %all-to-all-start.6) | async-done | bytes 2097184 | tf_op jit(solution)/shard_map/all_to_all | solution.py:193
  260.9 9.7 %multiply_convert_fusion.2 = (bf16[1024,1024]{1,0:T(8,128)(2,1)S(1)}, bf16[1024,1024]{1,0:T(8,128)(2,1)S(1)}, bf16[1024,1024]{1,0:T(8,128)(2,1)}) fusion(f32[1024,2048]{1,0:T(8,128)} %fusion.61, bf16[1024,1024]{1,0:T(8,128)(2,1)} %bitcast.254, bf16[1024,1024]{0,1:T(8,128)(2,1)} %bitcast.45), kind=kOutput, calls=%fused_computation.6 | convolution fusion | flops 2163212288 | bytes 18874368 | tf_op jit(solution)/shard_map/fd,kd->fk/dot_general | solution.py:308
  270.5 5.5 fusion.18
  276.0 5.3 add_convert_fusion
  285.3 5.9 %convert_bitcast_fusion = bf16[8,1024,128]{1,2,0:T(8,128)(2,1)} fusion(bf16[1024,8,128]{0,2,1:T(8,128)(2,1)} %bitcast.265, bf16[1024,1024]{1,0:T(8,128)(2,1)} %get-tuple-element.78), kind=kOutput, calls=%fused_computation.43 | convolution fusion | flops 2148532224 | bytes 6291456 | tf_op jit(solution)/shard_map/fk,frd->rkd/dot_general | solution.py:317
  291.2 4.8 all-to-all-start.7
  296.1 6.2 %convolution_convert_fusion.1 = bf16[1024,1024]{1,0:T(8,128)(2,1)} fusion(bf16[1024,1024]{1,0:T(8,128)(2,1)} %bitcast.260, bf16[1024,1024]{1,0:T(8,128)(2,1)} %copy-done.38), kind=kOutput, calls=%fused_computation.53 | convolution fusion | flops 2148532224 | bytes 6291456 | tf_op jit(solution)/shard_map/fd,fk->dk/dot_general | solution.py:325
  306.1 16.1 %reduce-scatter.4.cloned.1.call-done = bf16[1,8,32,1024]{3,2,1,0:T(8,128)(2,1)} async-done(((bf16[4,8,32,1024]{3,2,1,0:T(8,128)(2,1)}), bf16[1,8,32,1024]{3,2,1,0:T(8,128)(2,1)}) %reduce-scatter.4.cloned.1.call-update) | async-done | bytes 524304 | tf_op jit(solution)/shard_map/reduce_scatter | solution.py:200
  328.0 4.4 all-to-all-start.8
  332.4 6.1 %convolution_convert_fusion = bf16[1024,1024]{1,0:T(8,128)(2,1)} fusion(bf16[1024,1024]{1,0:T(8,128)(2,1)} %get-tuple-element.78, bf16[1024,1024]{0,1:T(8,128)(2,1)} %bitcast.45), kind=kOutput, calls=%fused_computation.52 | convolution fusion | flops 2148532224 | bytes 6291456 | tf_op jit(solution)/shard_map/dot_general | solution.py:334
  338.5 20.4 %all-to-all-done.8 = bf16[8,128,1024]{2,1,0:T(8,128)(2,1)} async-done(((bf16[8,128,1024]{2,1,0:T(8,128)(2,1)}), bf16[8,128,1024]{2,1,0:T(8,128)(2,1)}, u32[]{:S(2)}, u32[]{:S(2)}) %all-to-all-start.8) | async-done | bytes 2097184 | tf_op jit(solution)/shard_map/all_to_all | solution.py:193
  358.9 14.0 %all-gather.19.cloned.1.call-done = bf16[32,32,1024]{2,1,0:T(8,128)(2,1)} async-done(((bf16[8,32,1024]{2,1,0:T(8,128)(2,1)}), bf16[32,32,1024]{2,1,0:T(8,128)(2,1)}) %all-gather.19.cloned.1.call-update) | async-done | bytes 2097168 | tf_op jit(solution)/shard_map/all_gather | solution.py:196
  375.4 13.3 %all_to_all.77 = bf16[8,128,256]{2,1,0:T(8,128)(2,1)} all-to-all(bf16[8,128,256]{2,1,0:T(8,128)(2,1)S(1)} %bitcast.272), channel_id=1, replica_groups=mesh['dp'=8,'tensor'=4] {'dp'}, dimensions={0} | all-to-all | bytes 1048576 | tf_op jit(solution)/shard_map/all_to_all | solution.py:193
  388.6 4.5 all-to-all-start.10
  410.1 5.1 fusion.33
  432.4 18.6 %all-to-all-done.11 = bf16[8,128,768]{1,2,0:T(8,128)(2,1)S(1)} async-done(((bf16[8,128,768]{1,2,0:T(8,128)(2,1)}), bf16[8,128,768]{1,2,0:T(8,128)(2,1)S(1)}, u32[]{:S(2)}, u32[]{:S(2)}) %all-to-all-start.11) | async-done | bytes 1572896 | tf_op jit(solution)/shard_map/all_to_all | solution.py:193
  473.5 4.7 all-to-all-done.13
  483.4 15.2 %reduce-scatter.8.cloned.1.call-done = bf16[1,8,32,1024]{3,2,1,0:T(8,128)(2,1)} async-done(((bf16[4,8,32,1024]{3,2,1,0:T(8,128)(2,1)}), bf16[1,8,32,1024]{3,2,1,0:T(8,128)(2,1)}) %reduce-scatter.8.cloned.1.call-update) | async-done | bytes 524304 | tf_op jit(solution)/shard_map/reduce_scatter | solution.py:200
  499.7 9.4 %all-to-all-done.12 = bf16[8,128,1024]{1,2,0:T(8,128)(2,1)} async-done(((bf16[8,128,1024]{1,2,0:T(8,128)(2,1)}), bf16[8,128,1024]{1,2,0:T(8,128)(2,1)}, u32[]{:S(2)}, u32[]{:S(2)}) %all-to-all-start.12) | async-done | bytes 2097184 | tf_op jit(solution)/shard_map/all_to_all | solution.py:193
  521.7 6.2 %maximum_convert_fusion = f32[8,2,128,1024]{3,2,1,0:T(8,128)} fusion(bf16[8,1,128,1024]{3,2,1,0:T(8,128)(2,1)} %bitcast.90, bf16[8,1,128,1024]{3,2,1,0:T(8,128)(2,1)} %bitcast.89), kind=kLoop, calls=%fused_computation.1 | loop fusion | flops 4194304 | bytes 12582912 | tf_op jit(solution)/shard_map/convert_element_type | solution.py:354
  (225 shorter events, 190.5 us)
Async XLA Ops:
  7.2 54.8 %all-gather.11.cloned.1.call-start = ((), (), s32[]{:S(2)}) async-start(), calls=%async_computation.21 | async-start | bytes 2785280 | tf_op jit(solution)/shard_map/all_gather | solution.py:233
  66.4 33.1 %all-to-all-start.1 = ((bf16[8,144,1024]{2,1,0:T(8,128)(2,1)}), bf16[8,144,1024]{2,1,0:T(8,128)(2,1)S(1)}, u32[]{:S(2)}, u32[]{:S(2)}) async-start(bf16[8,144,1024]{2,1,0:T(8,128)(2,1)} %pad_maximum_fusion.2), calls=%async_computation.1 | async-start | bytes 4718592 | tf_op jit(solution)/shard_map/all_to_all | solution.py:193
  70.1 106.1 %all-gather.13.cloned.1.call-start = ((), (), s32[]{:S(2)}) async-start(), calls=%async_computation.22 | async-start | bytes 2621440 | tf_op jit(solution)/shard_map/all_gather | solution.py:242
  105.4 13.2 %all-to-all-start.2 = ((bf16[8,32,1024]{2,1,0:T(8,128)(2,1)}), bf16[8,32,1024]{2,1,0:T(8,128)(2,1)S(1)}, u32[]{:S(2)}, u32[]{:S(2)}) async-start(bf16[8,32,1024]{2,1,0:T(8,128)(2,1)} %param.17), calls=%async_computation.2 | async-start | bytes 1048576 | tf_op jit(solution)/shard_map/all_to_all | solution.py:193
  108.9 67.2 %all-gather.15.cloned.1.call-start = ((), (), s32[]{:S(2)}) async-start(), calls=%async_computation.23 | async-start | bytes 2621440 | tf_op jit(solution)/shard_map/all_gather | solution.py:196
  122.1 24.5 %all-to-all-start.3 = ((bf16[8,128,768]{2,1,0:T(8,128)(2,1)}), bf16[8,128,768]{2,1,0:T(8,128)(2,1)S(1)}, u32[]{:S(2)}, u32[]{:S(2)}) async-start(bf16[8,128,768]{2,1,0:T(8,128)(2,1)} %bitcast.24), calls=%async_computation.3 | async-start | bytes 3145728 | tf_op jit(solution)/shard_map/all_to_all | solution.py:193
  125.7 93.3 %all-gather.17.cloned.1.call-start = ((), (), s32[]{:S(2)}) async-start(), calls=%async_computation.24 | async-start | bytes 2621440 | tf_op jit(solution)/shard_map/all_gather | solution.py:291
  149.5 5.6 %copy-start.5 = (bf16[8,128,4,64]{3,0,2,1:T(8,128)(2,1)}, bf16[8,128,4,64]{3,0,2,1:T(8,128)(2,1)S(1)}, u32[]{:S(2)}) copy-start(bf16[8,128,4,64]{3,0,2,1:T(8,128)(2,1)S(1)} %copy.107) | copy-start | bytes 1572868
  176.2 53.7 %all-to-all-start.5 = ((bf16[8,128,2048]{2,1,0:T(8,128)(2,1)}), bf16[8,128,2048]{2,1,0:T(8,128)(2,1)}, u32[]{:S(2)}, u32[]{:S(2)}) async-start(bf16[8,128,2048]{2,1,0:T(8,128)(2,1)} %pad_maximum_fusion), calls=%async_computation.5 | async-start | bytes 8388608 | tf_op jit(solution)/shard_map/all_to_all | solution.py:193
  229.9 31.0 %all-to-all-start.6 = ((bf16[8,1024,128]{1,2,0:T(8,128)(2,1)}), bf16[8,1024,128]{1,2,0:T(8,128)(2,1)}, u32[]{:S(2)}, u32[]{:S(2)}) async-start(bf16[8,1024,128]{1,2,0:T(8,128)(2,1)} %copy.104), calls=%async_computation.6 | async-start | bytes 4194304 | tf_op jit(solution)/shard_map/all_to_all | solution.py:193
  234.2 88.0 %reduce-scatter.4.cloned.1.call-start = ((), (), s32[]{:S(2)}) async-start(), calls=%async_computation.18 | async-start | bytes 2621440 | tf_op jit(solution)/shard_map/reduce_scatter | solution.py:200
  270.5 5.5 copy-start.39
  291.2 32.1 %all-to-all-start.7 = ((bf16[8,1024,128]{1,2,0:T(8,128)(2,1)}), bf16[8,1024,128]{1,2,0:T(8,128)(2,1)}, u32[]{:S(2)}, u32[]{:S(2)}) async-start(bf16[8,1024,128]{1,2,0:T(8,128)(2,1)} %convert_bitcast_fusion), calls=%async_computation.8 | async-start | bytes 4194304 | tf_op jit(solution)/shard_map/all_to_all | solution.py:193
  296.0 77.0 %all-gather.19.cloned.1.call-start = ((), (), s32[]{:S(2)}) async-start(), calls=%async_computation.25 | async-start | bytes 2621440 | tf_op jit(solution)/shard_map/all_gather | solution.py:196
  296.1 6.2 %copy-start.19 = (bf16[4,8,32,1024]{3,2,1,0:T(8,128)(2,1)S(1)}, bf16[4,8,32,1024]{3,2,1,0:T(8,128)(2,1)}, u32[]{:S(2)}) copy-start(bf16[4,8,32,1024]{3,2,1,0:T(8,128)(2,1)} %copy-done.18) | copy-start | bytes 6291460
  296.1 6.2 %copy-start.40 = (bf16[1024,1024]{1,0:T(8,128)(2,1)S(1)}, bf16[1024,1024]{1,0:T(8,128)(2,1)}, u32[]{:S(2)}) copy-start(bf16[1024,1024]{1,0:T(8,128)(2,1)} %copy-done.39) | copy-start | bytes 6291460
  328.0 31.0 %all-to-all-start.8 = ((bf16[8,128,1024]{2,1,0:T(8,128)(2,1)}), bf16[8,128,1024]{2,1,0:T(8,128)(2,1)}, u32[]{:S(2)}, u32[]{:S(2)}) async-start(bf16[8,128,1024]{2,1,0:T(8,128)(2,1)} %bitcast.262), calls=%async_computation.9 | async-start | bytes 4194304 | tf_op jit(solution)/shard_map/all_to_all | solution.py:193
  332.3 97.9 %reduce-scatter.6.cloned.1.call-start = ((), (), s32[]{:S(2)}) async-start(), calls=%async_computation.19 | async-start | bytes 2621440 | tf_op jit(solution)/shard_map/reduce_scatter | solution.py:200
  388.6 37.1 %all-to-all-start.10 = ((bf16[8,128,1024]{2,1,0:T(8,128)(2,1)}), bf16[8,128,1024]{2,1,0:T(8,128)(2,1)}, u32[]{:S(2)}, u32[]{:S(2)}) async-start(bf16[8,128,1024]{2,1,0:T(8,128)(2,1)} %bitcast.257), calls=%async_computation.11 | async-start | bytes 4194304 | tf_op jit(solution)/shard_map/all_to_all | solution.py:193
  425.8 25.2 %all-to-all-start.11 = ((bf16[8,128,768]{1,2,0:T(8,128)(2,1)}), bf16[8,128,768]{1,2,0:T(8,128)(2,1)S(1)}, u32[]{:S(2)}, u32[]{:S(2)}) async-start(bf16[8,128,768]{1,2,0:T(8,128)(2,1)} %pad_maximum_fusion.4), calls=%async_computation.12 | async-start | bytes 3145728 | tf_op jit(solution)/shard_map/all_to_all | solution.py:193
  430.0 68.6 %reduce-scatter.8.cloned.1.call-start = ((), (), s32[]{:S(2)}) async-start(), calls=%async_computation.20 | async-start | bytes 2621440 | tf_op jit(solution)/shard_map/reduce_scatter | solution.py:200
  462.0 6.5 %copy-start.17 = (bf16[4,8,32,1024]{3,2,1,0:T(8,128)(2,1)S(1)}, bf16[4,8,32,1024]{3,2,1,0:T(8,128)(2,1)}, u32[]{:S(2)}) copy-start(bf16[4,8,32,1024]{3,2,1,0:T(8,128)(2,1)} %copy.101) | copy-start | bytes 6291460
  464.3 13.9 %all-to-all-start.13 = ((bf16[8,32,1024]{2,1,0:T(8,128)(2,1)}), bf16[8,32,1024]{2,1,0:T(8,128)(2,1)}, u32[]{:S(2)}, u32[]{:S(2)}) async-start(bf16[8,32,1024]{2,1,0:T(8,128)(2,1)} %fusion.45), calls=%async_computation.16 | async-start | bytes 1048576 | tf_op jit(solution)/shard_map/all_to_all | solution.py:193
  473.5 35.7 %copy-start.34 = (f32[1024]{0:T(1024)S(1)}, f32[1024]{0:T(1024)}, u32[]{:S(2)}) copy-start(f32[1024]{0:T(1024)} %copy-done.33) | copy-start | bytes 12292
  478.2 31.0 %all-to-all-start.12 = ((bf16[8,128,1024]{1,2,0:T(8,128)(2,1)}), bf16[8,128,1024]{1,2,0:T(8,128)(2,1)}, u32[]{:S(2)}, u32[]{:S(2)}) async-start(bf16[8,128,1024]{1,2,0:T(8,128)(2,1)} %copy_bitcast_fusion), calls=%async_computation.15 | async-start | bytes 4194304 | tf_op jit(solution)/shard_map/all_to_all | solution.py:193
  482.5 28.2 %copy-start.9 = (bf16[8,32,1024]{2,1,0:T(8,128)(2,1)S(1)}, bf16[8,32,1024]{2,1,0:T(8,128)(2,1)}, u32[]{:S(2)}) copy-start(bf16[8,32,1024]{2,1,0:T(8,128)(2,1)} %copy-done.7) | copy-start | bytes 1572868
  482.5 28.1 %copy-start.31 = (f32[1024]{0:T(1024)S(1)}, f32[1024]{0:T(1024)}, u32[]{:S(2)}) copy-start(f32[1024]{0:T(1024)} %get-tuple-element.151) | copy-start | bytes 12292
  482.5 28.1 %copy-start.36 = (f32[8,32]{1,0:T(8,128)S(1)}, f32[8,32]{1,0:T(8,128)}, u32[]{:S(2)}) copy-start(f32[8,32]{1,0:T(8,128)} %copy-done.35) | copy-start | bytes 3076
  514.0 17.8 %all-to-all-start.14 = ((bf16[8,48,1024]{2,1,0:T(8,128)(2,1)}), bf16[8,48,1024]{2,1,0:T(8,128)(2,1)S(1)}, u32[]{:S(2)}, u32[]{:S(2)}) async-start(bf16[8,48,1024]{2,1,0:T(8,128)(2,1)} %fusion.48), calls=%async_computation.17 | async-start | bytes 1572864 | tf_op jit(solution)/shard_map/all_to_all | solution.py:193
  531.9 10.6 %collective-permute-start = (f32[3,128]{1,0:T(4,128)S(1)}, f32[3,128]{1,0:T(4,128)S(1)}, u32[]{:S(2)}, u32[]{:S(2)}) collective-permute-start(f32[3,128]{1,0:T(4,128)S(1)} %add_bitcast_fusion), channel_id=1, source_target_pairs={{0,1},{1,2},{2,3},{3,0},{4,5},{5,6},{6,7},{7,4},{8,9},{9,10},{10,1... | collective-permute-start | bytes 4616 | tf_op jit(solution)/shard_map/ppermute | solution.py:389
  532.3 10.2 %collective-permute-start.1 = (f32[3,128]{1,0:T(4,128)S(1)}, f32[3,128]{1,0:T(4,128)S(1)}, u32[]{:S(2)}, u32[]{:S(2)}) collective-permute-start(f32[3,128]{1,0:T(4,128)S(1)} %add_bitcast_fusion), channel_id=1, source_target_pairs={{0,2},{1,3},{2,0},{3,1},{4,6},{5,7},{6,4},{7,5},{8,10},{9,11},{10,... | collective-permute-start | bytes 4616 | tf_op jit(solution)/shard_map/ppermute | solution.py:389
  533.7 8.8 %collective-permute-start.2 = (f32[3,128]{1,0:T(4,128)S(1)}, f32[3,128]{1,0:T(4,128)S(1)}, u32[]{:S(2)}, u32[]{:S(2)}) collective-permute-start(f32[3,128]{1,0:T(4,128)S(1)} %add_bitcast_fusion), channel_id=1, source_target_pairs={{0,3},{1,0},{2,1},{3,2},{4,7},{5,4},{6,5},{7,6},{8,11},{9,8},{10,9... | collective-permute-start | bytes 4616 | tf_op jit(solution)/shard_map/ppermute | solution.py:389
  (32 other events, 87.3 us)
Sparse Core Ops, SparseCore 0:
  11.4 50.5 all-gather.10
  73.0 45.0 all-gather.12
  119.7 44.4 all-gather.14
  176.3 42.6 all-gather.16
  281.5 40.6 reduce-scatter.3
  328.1 44.8 all-gather.18
  375.8 42.4 reduce-scatter.5
  457.9 40.6 reduce-scatter.7

commit v7 on v5

--- a/solution.py
+++ b/solution.py
@@ -4,6 +4,7 @@
 import jax.numpy as jnp
 import numpy as np
 from jax import lax
+from jax.experimental import pallas as pl
 from jax.sharding import Mesh
 from jax.sharding import PartitionSpec as P
 
@@ -187,6 +188,94 @@
     return shards
 
 
+def attention_masks(steps):
+    size = steps * TILE
+    row = lax.broadcasted_iota(jnp.int32, (size, size), 0)
+    col = lax.broadcasted_iota(jnp.int32, (size, size), 1)
+    keep = (row % TILE == col % TILE) & (row >= col)
+    lane = lax.broadcasted_iota(jnp.int32, (size, 2 * HEAD), 1)
+    return keep, lane < HEAD
+
+
+def times(left, right, left_axis, right_axis):
+    return lax.dot_general(
+        left, right, (((left_axis,), (right_axis,)), ((), ())), preferred_element_type=F32
+    )
+
+
+def attention_probs(query, keyv, keep):
+    scores = jnp.where(keep, times(query, keyv, 1, 1) * (1.0 / math.sqrt(HEAD)), -1e30)
+    expo = jnp.exp(scores - jnp.max(scores, axis=-1, keepdims=True))
+    return expo / jnp.sum(expo, axis=-1, keepdims=True)
+
+
+def attention_tile(ref, tile, start):
+    part = ref[:, tile * TILE : (tile + 1) * TILE, start : start + 2 * HEAD]
+    return part.reshape(-1, 2 * HEAD)
+
+
+def attention_forward_body(qkv_ref, out_ref):
+    steps, frames, cols = out_ref.shape
+    keep, is_first = attention_masks(steps)
+    for tile in range(frames // TILE):
+        for pair in range(0, cols, 2 * HEAD):
+            query, keyv, value = [
+                attention_tile(qkv_ref, tile, j * cols + pair) for j in range(3)
+            ]
+            mixed = []
+            for mine in (is_first, ~is_first):
+                probs = attention_probs(jnp.where(mine, query, 0), keyv, keep)
+                mixed.append(times(probs.astype(BF), value, 1, 0))
+            mixed = jnp.where(is_first, mixed[0], mixed[1]).astype(BF)
+            out_ref[:, tile * TILE : (tile + 1) * TILE, pair : pair + 2 * HEAD] = mixed.reshape(
+                steps, TILE, 2 * HEAD
+            )
+
+
+def attention_backward_body(qkv_ref, grad_ref, out_ref):
+    steps, frames, cols = grad_ref.shape
+    keep, is_first = attention_masks(steps)
+    scale = 1.0 / math.sqrt(HEAD)
+    for tile in range(frames // TILE):
+        for pair in range(0, cols, 2 * HEAD):
+            query, keyv, value = [
+                attention_tile(qkv_ref, tile, j * cols + pair) for j in range(3)
+            ]
+            grad = attention_tile(grad_ref, tile, pair)
+            found = []
+            for mine in (is_first, ~is_first):
+                probs = attention_probs(jnp.where(mine, query, 0), keyv, keep)
+                d_probs = times(jnp.where(mine, grad, 0), value, 1, 1)
+                d_value = times(probs.astype(BF), grad, 0, 0)
+                d_scores = probs * (d_probs - jnp.sum(probs * d_probs, axis=-1, keepdims=True))
+                high = d_scores.astype(BF)
+                rest = (d_scores - high.astype(F32)).astype(BF)
+                d_query = (times(high, keyv, 1, 0) + times(rest, keyv, 1, 0)) * scale
+                d_key = (times(high, query, 0, 0) + times(rest, query, 0, 0)) * scale
+                found.append((d_query, d_key, d_value))
+            for j in range(3):
+                part = jnp.where(is_first, found[0][j], found[1][j]).astype(BF)
+                start = j * cols + pair
+                out_ref[:, tile * TILE : (tile + 1) * TILE, start : start + 2 * HEAD] = (
+                    part.reshape(steps, TILE, 2 * HEAD)
+                )
+
+
+def attention_call(body, arrays, cols, span):
+    steps, frames = arrays[0].shape[:2]
+
+    def spec(width):
+        return pl.BlockSpec((steps, span, width), lambda i: (0, i, 0))
+
+    return pl.pallas_call(
+        body,
+        grid=(frames // span,),
+        in_specs=[spec(a.shape[2]) for a in arrays],
+        out_specs=spec(cols),
+        out_shape=jax.ShapeDtypeStruct((steps, frames, cols), BF),
+    )(*arrays)
+
+
 def make_step_shards(count, lanes):
 
     def exchange(blocks):
@@ -250,26 +339,7 @@
         qkv = jnp.dot(n1_all, w_in, preferred_element_type=F32).astype(BF)
 
         qkv = frame_split(qkv)
-        frames = qkv.shape[1]
-        heads = cols // HEAD
-        scale = 1.0 / math.sqrt(HEAD)
-        query = qkv[..., :cols].reshape(steps, frames, heads, HEAD)
-        keyv = qkv[..., cols : 2 * cols].reshape(steps, frames, heads, HEAD)
-        value = qkv[..., 2 * cols :].reshape(steps, frames, heads, HEAD)
-        causal = jnp.arange(steps)[:, None] >= jnp.arange(steps)[None, :]
-
-        def score_of(qv, kv):
-            raw = jnp.einsum("sfhe,tfhe->fhst", qv, kv, preferred_element_type=F32) * scale
-            return jnp.where(causal, raw, -1e30)
-
-        scores = score_of(query, keyv)
-        top = jnp.max(scores, axis=-1, keepdims=True)
-        expo = jnp.exp(scores - top)
-        total = jnp.sum(expo, axis=-1, keepdims=True)
-        lse = top + jnp.log(total)
-        probs_low = (expo / total).astype(BF)
-        mixed = jnp.einsum("fhst,tfhe->sfhe", probs_low, value, preferred_element_type=F32)
-        mixed_all = frame_join(mixed.reshape(steps, frames, cols).astype(BF))
+        mixed_all = frame_join(attention_call(attention_forward_body, (qkv,), cols, 2 * TILE))
         attn = jnp.einsum("fe,de->fd", mixed_all, wout_t, preferred_element_type=F32)
 
         attn, w_down, w_gate_up, grad_all = after(attn.astype(BF), w_down, w_gate_up, grad_all)
@@ -309,35 +379,25 @@
         g_down = exchange(d_down.astype(BF))
         g_gate = jnp.einsum("fd,fk->dk", n2_all, d_gate, preferred_element_type=F32).astype(BF)
         g_up = jnp.einsum("fd,fk->dk", n2_all, d_up, preferred_element_type=F32).astype(BF)
+        part = hid_width // 2
+        g_gate = jnp.concatenate([g_gate, g_up[:, :part]], axis=1).reshape(count, block, -1)
+        g_up = g_up[:, part:].reshape(count, block, -1)
         dn2, g_down, g_gate, g_up = after(dn2, g_down, g_gate, g_up)
         dh_norm2, dgain_two = norm_back(dn2, h1, r2, gain_two)
         dh1 = grad.astype(F32) + dh_norm2
         dh1_low, g_gate, hidden = after(dh1.astype(BF), g_gate, hidden)
         dh1_all = collect(dh1_low)
-        g_gate = exchange(g_gate.reshape(count, block, -1))
+        g_gate = exchange(g_gate)
         dh1_all, g_gate = after(dh1_all, g_gate)
 
         ffout = deal(jnp.dot(hidden, wdown, preferred_element_type=F32))
         d_mixed = jnp.dot(dh1_all, wout_t, preferred_element_type=F32).astype(BF)
         d_mixed, g_up = after(frame_split(d_mixed), g_up)
-        d_mixed = d_mixed.reshape(steps, frames, heads, HEAD)
-        g_up = exchange(g_up.reshape(count, block, -1))
-        probs = jnp.exp(score_of(query, keyv) - lse)
-        d_probs = jnp.einsum("sfhe,tfhe->fhst", d_mixed, value, preferred_element_type=F32)
-        d_value = jnp.einsum("fhst,sfhe->tfhe", probs_low, d_mixed, preferred_element_type=F32)
-        d_scores = probs * (d_probs - jnp.sum(probs * d_probs, axis=-1, keepdims=True))
-        d_query = (
-            jnp.einsum("fhst,tfhe->sfhe", d_scores, keyv.astype(F32), precision=HIGH) * scale
-        )
-        d_key = (
-            jnp.einsum("fhst,sfhe->tfhe", d_scores, query.astype(F32), precision=HIGH) * scale
-        )
-        d_qkv = jnp.concatenate(
-            [a.reshape(steps, frames, cols).astype(BF) for a in (d_query, d_key, d_value)],
-            axis=-1,
-        )
+        g_up = exchange(g_up)
+        d_qkv = attention_call(attention_backward_body, (qkv, d_mixed), 3 * cols, 2 * TILE)
         d_qkv, g_up = after(d_qkv, g_up)
-        g_gate_up = jnp.stack([g_gate, g_up], axis=1).astype(F32)
+        g_up = jnp.concatenate([g_gate[..., hid_width:], g_up], axis=2)
+        g_gate_up = jnp.stack([g_gate[..., :hid_width], g_up], axis=1).astype(F32)
         d_qkv = frame_join(d_qkv)
         dn1 = jnp.einsum("fe,de->fd", d_qkv, w_in, preferred_element_type=F32).astype(BF)
 

time: 536 us -> 515 us (0.961)
  waiting for transfers between devices: 208 us -> 174 us
  Pallas kernels: 0 us -> 29 us
  blocking collectives: 67.3 us -> 92.3 us
  matrix products: 83.5 us -> 61.7 us
  local copies, waits for them, and re-layouts: 57.4 us -> 46.6 us
  other arithmetic: 47 us -> 39 us
    pallas_call x0 -> x2, Pallas kernels: none -> 29 us  [attention_call(): pl.pallas_call(body, grid=(frames // span,), in_specs=[spec(a.shape[2]) f...]
    all_to_all x4 -> x5, blocking collectives: 67.3 us -> 92.3 us  [exchange(): return lax.all_to_all(blocks, 'dp', 0, 0, tiled=True)]
    dot_general x6 -> x0, matrix products: 18.2 us -> none  [the longest x1 5.07 us: shards(): jnp.einsum('fhst,sfhe->tfhe', d_scores, query.astype(F32), precision=HIGH)]
    all_gather x4, waiting for transfers between devices: 62.1 us -> 47.9 us  [collect(): return lax.all_gather(rows, 'tensor', axis=0).reshape(-1, rows.shape[-1])]
    reduce_scatter x4, waiting for transfers between devices: 60.6 us -> 48.8 us  [deal(): return lax.psum_scatter(slots, 'tensor', scatter_dimension=0).astype(F32)]
    convert_element_type x4 -> x0, local copies, waits for them, and re-layouts: 10.3 us -> none  [the longest x3 8.14 us: shards(): a.reshape(steps, frames, cols).astype(BF)]
    reshape x4 -> x2, local copies, waits for them, and re-layouts: 10 us -> 1.7 us  [frame_join(): slots = exchange(array).reshape(count, lanes, -1, array.shape[-1])]
    all_to_all x11 -> x10, waiting for transfers between devices: 84.2 us -> 76.9 us  [exchange(): return lax.all_to_all(blocks, 'dp', 0, 0, tiled=True)]
  transfers between devices with their start and end apart: 22 -> 21, of which waited for: 13 -> 12; matrix products, arithmetic and copies ran while one was open for 25% -> 20% of each run, Pallas kernels for 0% -> 6%
where the time goes in v7:
time: 515 us; the launch traced here: 507 us
  waiting for transfers between devices  174 us (34%)
  blocking collectives  92.3 us (18%)
  matrix products  61.7 us (12%)
  starting transfers between devices  49.2 us (10%)
  local copies, waits for them, and re-layouts  46.6 us (9%)
  other arithmetic  39 us (8%)
  Pallas kernels  29 us (6%)
  between operations  15.1 us (3%)
    all_to_all x5, blocking collectives, exchange(): return lax.all_to_all(blocks, 'dp', 0, 0, tiled=True)  92.3 us
    all_to_all x10, waiting for transfers between devices, exchange(): return lax.all_to_all(blocks, 'dp', 0, 0, tiled=True)  76.9 us
    reduce_scatter x4, waiting for transfers between devices, deal(): return lax.psum_scatter(slots, 'tensor', scatter_dimension=0).astype(F32)  48.8 us
    all_gather x4, waiting for transfers between devices, collect(): return lax.all_gather(rows, 'tensor', axis=0).reshape(-1, rows.shape[-1])  47.9 us
    all_to_all x10, starting transfers between devices, exchange(): return lax.all_to_all(blocks, 'dp', 0, 0, tiled=True)  43.9 us
    pallas_call x2, Pallas kernels, attention_call(): pl.pallas_call(body, grid=(frames // span,), in_specs=[spec(a.shape[2]) f...  29 us
    unnamed x41, local copies, waits for them, and re-layouts  17 us
    optimization_barrier x4, local copies, waits for them, and re-layouts, after(): return lax.optimization_barrier((value,) + waiting)  12.1 us
  transfers between devices with their start and end apart: 21, of which 12 were waited for; matrix products, arithmetic and copies ran while one was open for 20% of the time, Pallas kernels for 6%

profile of v7, /device:TPU:0, one launch (start us, length us, event | category | flops | bytes accessed | tf_op | source)
XLA Modules:
  0.0 507.2 jit_solution(14357505750518836287)
XLA Ops:
  11.2 5.3 %all-to-all-start = ((bf16[8,48,1024]{2,1,0:T(8,128)(2,1)}), bf16[8,48,1024]{2,1,0:T(8,128)(2,1)S(1)}, u32[]{:S(2)}, u32[]{:S(2)}) async-start(bf16[8,48,1024]{2,1,0:T(8,128)(2,1)} %pad_maximum_fusion.3), calls=%async_computation | async-start | bytes 1572864 | tf_op jit(solution)/shard_map/all_to_all | solution.py:282
  16.6 12.5 %all-to-all-done = bf16[8,48,1024]{2,1,0:T(8,128)(2,1)S(1)} async-done(((bf16[8,48,1024]{2,1,0:T(8,128)(2,1)}), bf16[8,48,1024]{2,1,0:T(8,128)(2,1)S(1)}, u32[]{:S(2)}, u32[]{:S(2)}) %all-to-all-start) | async-done | bytes 786464 | tf_op jit(solution)/shard_map/all_to_all | solution.py:282
  33.3 29.1 %all_to_all.75 = bf16[8,128,1024]{2,1,0:T(8,128)(2,1)S(1)} all-to-all(bf16[8,128,1024]{2,1,0:T(8,128)(2,1)S(1)} %pad_maximum_fusion.2), channel_id=1, replica_groups=mesh['dp'=8,'tensor'=4] {'dp'}, dimensions={0} | all-to-all | bytes 4194304 | tf_op jit(solution)/shard_map/all_to_all | solution.py:282
  62.4 12.8 %all_to_all.76 = bf16[8,32,1024]{2,1,0:T(8,128)(2,1)} all-to-all(bf16[8,32,1024]{2,1,0:T(8,128)(2,1)S(1)} %copy-done.11), channel_id=1, replica_groups=mesh['dp'=8,'tensor'=4] {'dp'}, dimensions={0} | all-to-all | bytes 1048576 | tf_op jit(solution)/shard_map/all_to_all | solution.py:282
  79.4 24.5 %all_to_all.77.qkv_ref = bf16[8,128,768]{2,1,0:T(8,128)(2,1)} all-to-all(bf16[8,128,768]{2,1,0:T(8,128)(2,1)S(1)} %bitcast.156), channel_id=1, replica_groups=mesh['dp'=8,'tensor'=4] {'dp'}, dimensions={0} | all-to-all | bytes 3145728 | tf_op jit(solution)/shard_map/all_to_all | solution.py:282
  103.9 12.5 %shard_map.152 = bf16[8,128,256]{2,1,0:T(8,128)(2,1)} custom-call(bf16[8,128,768]{2,1,0:T(8,128)(2,1)} %all_to_all.77.qkv_ref), custom_call_target="tpu_custom_call" | custom-call | tf_op jit(solution)/shard_map/pallas_call | solution.py:270
  116.3 13.1 %all_to_all.78 = bf16[8,128,256]{2,1,0:T(8,128)(2,1)S(1)} all-to-all(bf16[8,128,256]{2,1,0:T(8,128)(2,1)} %shard_map.152), channel_id=1, replica_groups=mesh['dp'=8,'tensor'=4] {'dp'}, dimensions={0} | all-to-all | bytes 1048576 | tf_op jit(solution)/shard_map/all_to_all | solution.py:282
  132.4 4.6 copy.105
  137.0 4.4 all-to-all-start.5
  148.4 26.1 %reduce-scatter.5.cloned.1.call-done = bf16[1,8,32,1024]{3,2,1,0:T(8,128)(2,1)} async-done(((bf16[4,8,32,1024]{3,2,1,0:T(8,128)(2,1)}), bf16[1,8,32,1024]{3,2,1,0:T(8,128)(2,1)}) %reduce-scatter.5.cloned.1.call-update) | async-done | bytes 524304 | tf_op jit(solution)/shard_map/reduce_scatter | solution.py:289
  177.0 4.6 all-to-all-start.6
  182.4 47.3 %all-gather.13.cloned.1.call-done = bf16[32,32,1024]{2,1,0:T(8,128)(2,1)} async-done(((bf16[8,32,1024]{2,1,0:T(8,128)(2,1)}), bf16[32,32,1024]{2,1,0:T(8,128)(2,1)}) %all-gather.13.cloned.1.call-update) | async-done | bytes 2097168 | tf_op jit(solution)/shard_map/all_gather | solution.py:285
  230.7 7.1 %fusion.25 = f32[1024,2048]{1,0:T(8,128)S(1)} fusion(bf16[1024,1024]{1,0:T(8,128)(2,1)} %bitcast.187, bf16[1024,2048]{1,0:T(8,128)(2,1)} %bitcast.30), kind=kOutput, calls=%fused_computation.97 | convolution fusion | flops 4294967296 | bytes 14680064 | tf_op jit(solution)/shard_map/dot_general | solution.py:358
  237.8 6.6 %multiply_convert_fusion.2 = (bf16[1024,1024]{1,0:T(8,128)(2,1)S(1)}, bf16[1024,1024]{1,0:T(8,128)(2,1)S(1)}, bf16[1024,1024]{1,0:T(8,128)(2,1)}) fusion(f32[1024,2048]{1,0:T(8,128)S(1)} %fusion.25, bf16[1024,1024]{1,0:T(8,128)(2,1)S(1)} %bitcast.163, bf16[1024,1024]{0,1:T(8,128)(2,1)} %bitcast.27), kind=kOutput, calls=%fused_computation.5 | convolution fusion | flops 2163212288 | bytes 18874368 | tf_op jit(solution)/shard_map/fd,kd->fk/dot_general | solution.py:364
  244.4 5.5 %fusion.1 = f32[1024,1024]{1,0:T(8,128)S(1)} fusion(bf16[1024,1024]{1,0:T(8,128)(2,1)S(1)} %get-tuple-element.64, bf16[1024,2048]{1,0:T(8,128)(2,1)} %bitcast.30), kind=kOutput, calls=%fused_computation.12 | convolution fusion | flops 2147483648 | bytes 8388608 | tf_op jit(solution)/shard_map/fk,dk->fd/dot_general | solution.py:369
  249.9 5.3 %add_convert_fusion = bf16[1024,1024]{1,0:T(8,128)(2,1)} fusion(f32[1024,1024]{1,0:T(8,128)S(1)} %fusion.1, bf16[1024,1024]{1,0:T(8,128)(2,1)S(1)} %get-tuple-element.63, bf16[1024,2048]{1,0:T(8,128)(2,1)} %bitcast.30), kind=kOutput, calls=%fused_computation.3 | convolution fusion | flops 2149580800 | bytes 10485760 | tf_op jit(solution)/shard_map/fk,dk->fd/dot_general | solution.py:368
  259.2 6.0 %convert_bitcast_fusion = bf16[8,1024,128]{1,2,0:T(8,128)(2,1)} fusion(bf16[1024,8,128]{0,2,1:T(8,128)(2,1)} %bitcast.167, bf16[1024,1024]{1,0:T(8,128)(2,1)} %get-tuple-element.74), kind=kOutput, calls=%fused_computation.24 | convolution fusion | flops 2148532224 | bytes 6291456 | tf_op jit(solution)/shard_map/fk,frd->rkd/dot_general | solution.py:373
  265.1 4.4 all-to-all-start.7
  269.8 4.6 convolution_convert_fusion.1
  283.6 13.3 %reduce-scatter.7.cloned.1.call-done = bf16[1,8,32,1024]{3,2,1,0:T(8,128)(2,1)} async-done(((bf16[4,8,32,1024]{3,2,1,0:T(8,128)(2,1)}), bf16[1,8,32,1024]{3,2,1,0:T(8,128)(2,1)}) %reduce-scatter.7.cloned.1.call-update) | async-done | bytes 524304 | tf_op jit(solution)/shard_map/reduce_scatter | solution.py:289
  299.5 4.9 copy.109
  304.4 4.5 all-to-all-start.8
  308.9 5.9 %convolution_convert_fusion = bf16[1024,1024]{1,0:T(8,128)(2,1)} fusion(bf16[1024,1024]{1,0:T(8,128)(2,1)} %get-tuple-element.74, bf16[1024,1024]{0,1:T(8,128)(2,1)} %bitcast.27), kind=kOutput, calls=%fused_computation.25 | convolution fusion | flops 2148532224 | bytes 6291456 | tf_op jit(solution)/shard_map/dot_general | solution.py:393
  314.8 31.9 %all-to-all-done.8 = bf16[8,128,1536]{2,1,0:T(8,128)(2,1)} async-done(((bf16[8,128,1536]{2,1,0:T(8,128)(2,1)}), bf16[8,128,1536]{2,1,0:T(8,128)(2,1)}, u32[]{:S(2)}, u32[]{:S(2)}) %all-to-all-start.8) | async-done | bytes 3145760 | tf_op jit(solution)/shard_map/all_to_all | solution.py:282
  349.1 12.8 %all_to_all.79.grad_ref = bf16[8,128,256]{2,1,0:T(8,128)(2,1)} all-to-all(bf16[8,128,256]{2,1,0:T(8,128)(2,1)S(1)} %bitcast.169), channel_id=1, replica_groups=mesh['dp'=8,'tensor'=4] {'dp'}, dimensions={0} | all-to-all | bytes 1048576 | tf_op jit(solution)/shard_map/all_to_all | solution.py:282
  364.3 4.5 all-to-all-start.10
  368.9 16.5 %shard_map.153 = bf16[8,128,768]{2,1,0:T(8,128)(2,1)} custom-call(bf16[8,128,768]{2,1,0:T(8,128)(2,1)} %all_to_all.77.qkv_ref, bf16[8,128,256]{2,1,0:T(8,128)(2,1)} %all_to_all.79.grad_ref), custom_call_target="tpu_custom_call" | custom-call | tf_op jit(solution)/shard_map/pallas_call | solution.py:270
  385.4 4.3 all-to-all-start.11
  391.9 18.8 %all-to-all-done.11 = bf16[8,128,768]{2,1,0:T(8,128)(2,1)} async-done(((bf16[8,128,768]{2,1,0:T(8,128)(2,1)}), bf16[8,128,768]{2,1,0:T(8,128)(2,1)}, u32[]{:S(2)}, u32[]{:S(2)}) %all-to-all-start.11) | async-done | bytes 1572896 | tf_op jit(solution)/shard_map/all_to_all | solution.py:282
  434.1 4.3 all-to-all-start.12
  448.0 9.3 %reduce-scatter.11.cloned.1.call-done = bf16[1,8,32,1024]{3,2,1,0:T(8,128)(2,1)} async-done(((bf16[4,8,32,1024]{3,2,1,0:T(8,128)(2,1)}), bf16[1,8,32,1024]{3,2,1,0:T(8,128)(2,1)}) %reduce-scatter.11.cloned.1.call-update) | async-done | bytes 524304 | tf_op jit(solution)/shard_map/reduce_scatter | solution.py:289
  459.5 5.6 %all-to-all-done.12 = bf16[8,128,1024]{1,2,0:T(8,128)(2,1)} async-done(((bf16[8,128,1024]{1,2,0:T(8,128)(2,1)}), bf16[8,128,1024]{1,2,0:T(8,128)(2,1)}, u32[]{:S(2)}, u32[]{:S(2)}) %all-to-all-start.12) | async-done | bytes 2097184 | tf_op jit(solution)/shard_map/all_to_all | solution.py:282
  (145 shorter events, 119.2 us)
Async XLA Ops:
  11.2 19.4 %copy-start.10 = (f32[8,256,128]{2,1,0:T(8,128)S(1)}, f32[8,256,128]{2,1,0:T(8,128)}, u32[]{:S(2)}) copy-start(f32[8,256,128]{2,1,0:T(8,128)} %param.12) | copy-start | bytes 3145732
  11.2 17.9 %all-to-all-start = ((bf16[8,48,1024]{2,1,0:T(8,128)(2,1)}), bf16[8,48,1024]{2,1,0:T(8,128)(2,1)S(1)}, u32[]{:S(2)}, u32[]{:S(2)}) async-start(bf16[8,48,1024]{2,1,0:T(8,128)(2,1)} %pad_maximum_fusion.3), calls=%async_computation | async-start | bytes 1572864 | tf_op jit(solution)/shard_map/all_to_all | solution.py:282
  16.6 59.2 %all-gather.9.cloned.1.call-start = ((), (), s32[]{:S(2)}) async-start(), calls=%async_computation.23 | async-start | bytes 2621440 | tf_op jit(solution)/shard_map/all_gather | solution.py:285
  30.6 101.8 %all-gather.11.cloned.1.call-start = ((), (), s32[]{:S(2)}) async-start(), calls=%async_computation.24 | async-start | bytes 2621440 | tf_op jit(solution)/shard_map/all_gather | solution.py:285
  33.2 29.2 %copy-start.11 = (bf16[8,32,1024]{2,1,0:T(8,128)(2,1)S(1)}, bf16[8,32,1024]{2,1,0:T(8,128)(2,1)}, u32[]{:S(2)}) copy-start(bf16[8,32,1024]{2,1,0:T(8,128)(2,1)} %param.17) | copy-start | bytes 1572868
  62.4 67.1 %copy-start.5 = (bf16[8,128,1024]{2,1,0:T(8,128)(2,1)}, bf16[8,128,1024]{2,1,0:T(8,128)(2,1)S(1)}, u32[]{:S(2)}) copy-start(bf16[8,128,1024]{2,1,0:T(8,128)(2,1)S(1)} %all_to_all.75) | copy-start | bytes 6291460
  75.8 98.7 %reduce-scatter.5.cloned.1.call-start = ((), (), s32[]{:S(2)}) async-start(), calls=%async_computation.19 | async-start | bytes 2621440 | tf_op jit(solution)/shard_map/reduce_scatter | solution.py:289
  137.0 38.7 %all-to-all-start.5 = ((bf16[8,1024,128]{1,2,0:T(8,128)(2,1)}), bf16[8,1024,128]{1,2,0:T(8,128)(2,1)}, u32[]{:S(2)}, u32[]{:S(2)}) async-start(bf16[8,1024,128]{1,2,0:T(8,128)(2,1)} %copy.105), calls=%async_computation.6 | async-start | bytes 4194304 | tf_op jit(solution)/shard_map/all_to_all | solution.py:282
  177.0 53.7 %all-to-all-start.6 = ((bf16[8,128,2048]{2,1,0:T(8,128)(2,1)}), bf16[8,128,2048]{2,1,0:T(8,128)(2,1)}, u32[]{:S(2)}, u32[]{:S(2)}) async-start(bf16[8,128,2048]{2,1,0:T(8,128)(2,1)} %pad_maximum_fusion), calls=%async_computation.7 | async-start | bytes 8388608 | tf_op jit(solution)/shard_map/all_to_all | solution.py:282
  181.6 48.1 %all-gather.13.cloned.1.call-start = ((), (), s32[]{:S(2)}) async-start(), calls=%async_computation.25 | async-start | bytes 2621440 | tf_op jit(solution)/shard_map/all_gather | solution.py:285
  182.2 114.7 %reduce-scatter.7.cloned.1.call-start = ((), (), s32[]{:S(2)}) async-start(), calls=%async_computation.20 | async-start | bytes 2621440 | tf_op jit(solution)/shard_map/reduce_scatter | solution.py:289
  230.7 7.1 %copy-start.7 = (bf16[32,32,1024]{2,1,0:T(8,128)(2,1)S(1)}, bf16[32,32,1024]{2,1,0:T(8,128)(2,1)}, u32[]{:S(2)}) copy-start(bf16[32,32,1024]{2,1,0:T(8,128)(2,1)} %all-gather.11.cloned.1.call-done) | copy-start | bytes 6291460
  244.4 5.5 %copy-start.14 = (bf16[1024,1024]{1,0:T(8,128)(2,1)}, bf16[1024,1024]{1,0:T(8,128)(2,1)S(1)}, u32[]{:S(2)}) copy-start(bf16[1024,1024]{1,0:T(8,128)(2,1)S(1)} %get-tuple-element.64) | copy-start | bytes 6291460
  244.4 5.5 %copy-start.15 = (bf16[1024,1024]{1,0:T(8,128)(2,1)}, bf16[1024,1024]{1,0:T(8,128)(2,1)S(1)}, u32[]{:S(2)}) copy-start(bf16[1024,1024]{1,0:T(8,128)(2,1)S(1)} %get-tuple-element.63) | copy-start | bytes 6291460
  265.1 32.9 %all-to-all-start.7 = ((bf16[8,1024,128]{1,2,0:T(8,128)(2,1)}), bf16[8,1024,128]{1,2,0:T(8,128)(2,1)}, u32[]{:S(2)}, u32[]{:S(2)}) async-start(bf16[8,1024,128]{1,2,0:T(8,128)(2,1)} %convert_bitcast_fusion), calls=%async_computation.9 | async-start | bytes 4194304 | tf_op jit(solution)/shard_map/all_to_all | solution.py:282
  269.5 77.2 %all-gather.15.cloned.1.call-start = ((), (), s32[]{:S(2)}) async-start(), calls=%async_computation.26 | async-start | bytes 2621440 | tf_op jit(solution)/shard_map/all_gather | solution.py:285
  283.6 14.8 %copy-start.2 = (bf16[8,32,1024]{2,1,0:T(8,128)(2,1)S(1)}, bf16[8,32,1024]{2,1,0:T(8,128)(2,1)}, u32[]{:S(2)}) copy-start(bf16[8,32,1024]{2,1,0:T(8,128)(2,1)} %all_to_all.76) | copy-start | bytes 1572868
  304.4 42.3 %all-to-all-start.8 = ((bf16[8,128,1536]{2,1,0:T(8,128)(2,1)}), bf16[8,128,1536]{2,1,0:T(8,128)(2,1)}, u32[]{:S(2)}, u32[]{:S(2)}) async-start(bf16[8,128,1536]{2,1,0:T(8,128)(2,1)} %copy.109), calls=%async_computation.10 | async-start | bytes 6291456 | tf_op jit(solution)/shard_map/all_to_all | solution.py:282
  308.8 81.0 %reduce-scatter.9.cloned.1.call-start = ((), (), s32[]{:S(2)}) async-start(), calls=%async_computation.21 | async-start | bytes 2621440 | tf_op jit(solution)/shard_map/reduce_scatter | solution.py:289
  364.3 21.1 %all-to-all-start.10 = ((bf16[8,128,512]{2,1,0:T(8,128)(2,1)}), bf16[8,128,512]{2,1,0:T(8,128)(2,1)}, u32[]{:S(2)}, u32[]{:S(2)}) async-start(bf16[8,128,512]{2,1,0:T(8,128)(2,1)} %copy.111), calls=%async_computation.12 | async-start | bytes 2097152 | tf_op jit(solution)/shard_map/all_to_all | solution.py:282
  385.4 25.3 %all-to-all-start.11 = ((bf16[8,128,768]{2,1,0:T(8,128)(2,1)}), bf16[8,128,768]{2,1,0:T(8,128)(2,1)}, u32[]{:S(2)}, u32[]{:S(2)}) async-start(bf16[8,128,768]{2,1,0:T(8,128)(2,1)} %shard_map.153), calls=%async_computation.13 | async-start | bytes 3145728 | tf_op jit(solution)/shard_map/all_to_all | solution.py:282
  389.7 67.6 %reduce-scatter.11.cloned.1.call-start = ((), (), s32[]{:S(2)}) async-start(), calls=%async_computation.22 | async-start | bytes 2621440 | tf_op jit(solution)/shard_map/reduce_scatter | solution.py:289
  412.4 3.5 copy-start.9
  416.0 3.3 copy-start.3
  420.2 13.9 %all-to-all-start.13 = ((bf16[8,32,1024]{2,1,0:T(8,128)(2,1)}), bf16[8,32,1024]{2,1,0:T(8,128)(2,1)}, u32[]{:S(2)}, u32[]{:S(2)}) async-start(bf16[8,32,1024]{2,1,0:T(8,128)(2,1)} %add_convert_fusion.1), calls=%async_computation.17 | async-start | bytes 1048576 | tf_op jit(solution)/shard_map/all_to_all | solution.py:282
  424.4 4.0 copy-start.12
  434.1 31.0 %all-to-all-start.12 = ((bf16[8,128,1024]{1,2,0:T(8,128)(2,1)}), bf16[8,128,1024]{1,2,0:T(8,128)(2,1)}, u32[]{:S(2)}, u32[]{:S(2)}) async-start(bf16[8,128,1024]{1,2,0:T(8,128)(2,1)} %copy_bitcast_fusion), calls=%async_computation.16 | async-start | bytes 4194304 | tf_op jit(solution)/shard_map/all_to_all | solution.py:282
  467.6 4.8 copy-start.4
  468.8 16.1 %all-to-all-start.14 = ((bf16[8,48,1024]{2,1,0:T(8,128)(2,1)}), bf16[8,48,1024]{2,1,0:T(8,128)(2,1)S(1)}, u32[]{:S(2)}, u32[]{:S(2)}) async-start(bf16[8,48,1024]{2,1,0:T(8,128)(2,1)} %fusion.15), calls=%async_computation.18 | async-start | bytes 1572864 | tf_op jit(solution)/shard_map/all_to_all | solution.py:282
  484.9 12.0 %collective-permute-start = (f32[3,128]{1,0:T(4,128)S(1)}, f32[3,128]{1,0:T(4,128)S(1)}, u32[]{:S(2)}, u32[]{:S(2)}) collective-permute-start(f32[3,128]{1,0:T(4,128)S(1)} %add_bitcast_fusion), channel_id=1, source_target_pairs={{0,1},{1,2},{2,3},{3,0},{4,5},{5,6},{6,7},{7,4},{8,9},{9,10},{10,1... | collective-permute-start | bytes 4616 | tf_op jit(solution)/shard_map/ppermute | solution.py:435
  485.6 11.3 %collective-permute-start.1 = (f32[3,128]{1,0:T(4,128)S(1)}, f32[3,128]{1,0:T(4,128)S(1)}, u32[]{:S(2)}, u32[]{:S(2)}) collective-permute-start(f32[3,128]{1,0:T(4,128)S(1)} %add_bitcast_fusion), channel_id=1, source_target_pairs={{0,2},{1,3},{2,0},{3,1},{4,6},{5,7},{6,4},{7,5},{8,10},{9,11},{10,... | collective-permute-start | bytes 4616 | tf_op jit(solution)/shard_map/ppermute | solution.py:435
  487.3 9.6 %collective-permute-start.2 = (f32[3,128]{1,0:T(4,128)S(1)}, f32[3,128]{1,0:T(4,128)S(1)}, u32[]{:S(2)}, u32[]{:S(2)}) collective-permute-start(f32[3,128]{1,0:T(4,128)S(1)} %add_bitcast_fusion), channel_id=1, source_target_pairs={{0,3},{1,0},{2,1},{3,2},{4,7},{5,4},{6,5},{7,6},{8,11},{9,8},{10,9... | collective-permute-start | bytes 4616 | tf_op jit(solution)/shard_map/ppermute | solution.py:435
  (6 other events, 10.4 us)
Sparse Core Ops, SparseCore 0:
  30.7 45.0 all-gather.8
  77.4 44.4 all-gather.10
  132.5 41.9 reduce-scatter.4
  184.2 45.4 all-gather.12
  255.3 41.4 reduce-scatter.6
  299.6 44.8 all-gather.14
  347.3 42.4 reduce-scatter.8
  416.1 41.2 reduce-scatter.10

commit v8 on v7

--- a/solution.py
+++ b/solution.py
@@ -5,6 +5,8 @@
 import numpy as np
 from jax import lax
 from jax.experimental import pallas as pl
+from jax.experimental.layout import Layout, with_layout_constraint
+from jax.experimental.pallas import tpu as pltpu
 from jax.sharding import Mesh
 from jax.sharding import PartitionSpec as P
 
@@ -192,7 +194,7 @@
     size = steps * TILE
     row = lax.broadcasted_iota(jnp.int32, (size, size), 0)
     col = lax.broadcasted_iota(jnp.int32, (size, size), 1)
-    keep = (row % TILE == col % TILE) & (row >= col)
+    keep = (row % TILE == col % TILE) & (row <= col)
     lane = lax.broadcasted_iota(jnp.int32, (size, 2 * HEAD), 1)
     return keep, lane < HEAD
 
@@ -204,9 +206,9 @@
 
 
 def attention_probs(query, keyv, keep):
-    scores = jnp.where(keep, times(query, keyv, 1, 1) * (1.0 / math.sqrt(HEAD)), -1e30)
-    expo = jnp.exp(scores - jnp.max(scores, axis=-1, keepdims=True))
-    return expo / jnp.sum(expo, axis=-1, keepdims=True)
+    scores = jnp.where(keep, times(keyv, query, 1, 1) * (1.0 / math.sqrt(HEAD)), -1e30)
+    expo = jnp.exp(scores - jnp.max(scores, axis=0, keepdims=True))
+    return expo * (1.0 / jnp.sum(expo, axis=0, keepdims=True))
 
 
 def attention_tile(ref, tile, start):
@@ -225,7 +227,7 @@
             mixed = []
             for mine in (is_first, ~is_first):
                 probs = attention_probs(jnp.where(mine, query, 0), keyv, keep)
-                mixed.append(times(probs.astype(BF), value, 1, 0))
+                mixed.append(times(probs.astype(BF), value, 0, 0))
             mixed = jnp.where(is_first, mixed[0], mixed[1]).astype(BF)
             out_ref[:, tile * TILE : (tile + 1) * TILE, pair : pair + 2 * HEAD] = mixed.reshape(
                 steps, TILE, 2 * HEAD
@@ -245,13 +247,13 @@
             found = []
             for mine in (is_first, ~is_first):
                 probs = attention_probs(jnp.where(mine, query, 0), keyv, keep)
-                d_probs = times(jnp.where(mine, grad, 0), value, 1, 1)
-                d_value = times(probs.astype(BF), grad, 0, 0)
-                d_scores = probs * (d_probs - jnp.sum(probs * d_probs, axis=-1, keepdims=True))
+                d_probs = times(value, jnp.where(mine, grad, 0), 1, 1)
+                d_value = times(probs.astype(BF), grad, 1, 0)
+                d_scores = probs * (d_probs - jnp.sum(probs * d_probs, axis=0, keepdims=True))
                 high = d_scores.astype(BF)
                 rest = (d_scores - high.astype(F32)).astype(BF)
-                d_query = (times(high, keyv, 1, 0) + times(rest, keyv, 1, 0)) * scale
-                d_key = (times(high, query, 0, 0) + times(rest, query, 0, 0)) * scale
+                d_query = (times(high, keyv, 0, 0) + times(rest, keyv, 0, 0)) * scale
+                d_key = (times(high, query, 1, 0) + times(rest, query, 1, 0)) * scale
                 found.append((d_query, d_key, d_value))
             for j in range(3):
                 part = jnp.where(is_first, found[0][j], found[1][j]).astype(BF)
@@ -276,6 +278,65 @@
     )(*arrays)
 
 
+def feed_body(
+    n2_ref, grad_ref, wgate_ref, wup_ref, wdown_ref, hid_ref, d_gate_ref, d_up_ref, dn2_ref, sum_ref
+):
+    step = pl.program_id(0)
+    wgate, wup = wgate_ref[...], wup_ref[...]
+    wdown = jnp.concatenate([wdown_ref[r] for r in range(wdown_ref.shape[0])], axis=1)
+    span = min(256, n2_ref.shape[0])
+    for start in range(0, n2_ref.shape[0], span):
+        rows = slice(start, start + span)
+        n2 = n2_ref[rows]
+        gate = times(n2, wgate, 1, 0)
+        upval = times(n2, wup, 1, 0)
+        d_hidden = times(grad_ref[rows], wdown, 1, 1)
+        sigma = 1.0 / (1.0 + jnp.exp(-gate))
+        silu_val = gate * sigma
+        hid_ref[rows] = (silu_val * upval).astype(BF)
+        d_gate = (d_hidden * upval * (sigma * (1.0 + gate * (1.0 - sigma)))).astype(BF)
+        d_up = (d_hidden * silu_val).astype(BF)
+        d_gate_ref[rows] = d_gate
+        d_up_ref[rows] = d_up
+        part = times(d_gate, wgate, 1, 1) + times(d_up, wup, 1, 1)
+
+        @pl.when(step == 0)
+        def _():
+            sum_ref[rows] = part
+
+        @pl.when(step > 0)
+        def _():
+            sum_ref[rows] += part
+
+    @pl.when(step == pl.num_programs(0) - 1)
+    def _():
+        dn2_ref[...] = sum_ref[...].astype(BF)
+
+
+def feed_call(n2, grad, wgu, wdown):
+    frames, width = n2.shape
+    parts, hidden, block = wdown.shape
+    span = min(256, hidden)
+    count = hidden // span
+    whole = pl.BlockSpec((frames, width), lambda i: (0, 0))
+    piece = pl.BlockSpec((frames, span), lambda i: (0, i))
+    return pl.pallas_call(
+        feed_body,
+        grid=(count,),
+        in_specs=[
+            whole,
+            whole,
+            pl.BlockSpec((width, span), lambda i: (0, i)),
+            pl.BlockSpec((width, span), lambda i: (0, i + count)),
+            pl.BlockSpec((parts, span, block), lambda i: (0, i, 0)),
+        ],
+        out_specs=[piece, piece, piece, whole],
+        out_shape=[jax.ShapeDtypeStruct((frames, hidden), BF)] * 3
+        + [jax.ShapeDtypeStruct((frames, width), BF)],
+        scratch_shapes=[pltpu.VMEM((frames, width), F32)],
+    )(n2, grad, wgu, wgu, wdown)
+
+
 def make_step_shards(count, lanes):
 
     def exchange(blocks):
@@ -296,6 +357,9 @@
     def frame_join(array):
         slots = exchange(array).reshape(count, lanes, -1, array.shape[-1])
         return jnp.swapaxes(slots, 0, 1).reshape(-1, array.shape[-1])
+
+    def rowwise(array):
+        return with_layout_constraint(array, Layout(tuple(range(array.ndim))))
 
     def after(value, *waiting):
         return lax.optimization_barrier((value,) + waiting)
@@ -347,7 +411,6 @@
         wdown = exchange(w_down.astype(BF))
         wgu = jnp.concatenate([w_gate_up[:, 0], w_gate_up[:, 1]], axis=2).astype(BF)
         attn, wdown, wgu = after(attn, wdown, wgu)
-        wdown = jnp.swapaxes(wdown, 0, 1).reshape(-1, width)
         h1 = h0 + attn
         r2 = lax.rsqrt(jnp.mean(h1 * h1, axis=-1, keepdims=True) + EPS)
         n2 = (h1 * r2 * gain_two).astype(BF)
@@ -355,20 +418,9 @@
         n2_all = collect(n2)
         wgu = exchange(wgu).reshape(width, -1)
 
-        gate_up = jnp.dot(n2_all, wgu, preferred_element_type=F32)
-        hid_width = gate_up.shape[1] // 2
-        gate, upval = gate_up[:, :hid_width], gate_up[:, hid_width:]
-        sigma = jax.nn.sigmoid(gate)
-        silu_val = gate * sigma
-        hidden = (silu_val * upval).astype(BF)
-        d_hidden = jnp.einsum("fd,kd->fk", grad_all, wdown, preferred_element_type=F32)
-        d_gate = (d_hidden * upval * (sigma * (1.0 + gate * (1.0 - sigma)))).astype(BF)
-        d_up = (d_hidden * silu_val).astype(BF)
-        wgate, wup = wgu[:, :hid_width], wgu[:, hid_width:]
-        dn2 = jnp.einsum("fk,dk->fd", d_gate, wgate, preferred_element_type=F32)
-        dn2 = dn2 + jnp.einsum("fk,dk->fd", d_up, wup, preferred_element_type=F32)
-
-        dn2, hidden, d_gate, d_up = after(dn2.astype(BF), hidden, d_gate, d_up)
+        hidden, d_gate, d_up, dn2 = feed_call(n2_all, grad_all, wgu, wdown)
+        hid_width = hidden.shape[1]
+        dn2, hidden, d_gate, d_up = after(dn2, hidden, d_gate, d_up)
         dn2 = deal(dn2)
         d_down = jnp.einsum(
             "fk,frd->rkd",
@@ -376,7 +428,7 @@
             grad_all.reshape(-1, count, block),
             preferred_element_type=F32,
         )
-        g_down = exchange(d_down.astype(BF))
+        g_down = exchange(rowwise(d_down.astype(BF)))
         g_gate = jnp.einsum("fd,fk->dk", n2_all, d_gate, preferred_element_type=F32).astype(BF)
         g_up = jnp.einsum("fd,fk->dk", n2_all, d_up, preferred_element_type=F32).astype(BF)
         part = hid_width // 2
@@ -390,6 +442,7 @@
         g_gate = exchange(g_gate)
         dh1_all, g_gate = after(dh1_all, g_gate)
 
+        wdown = jnp.swapaxes(wdown, 0, 1).reshape(-1, width)
         ffout = deal(jnp.dot(hidden, wdown, preferred_element_type=F32))
         d_mixed = jnp.dot(dh1_all, wout_t, preferred_element_type=F32).astype(BF)
         d_mixed, g_up = after(frame_split(d_mixed), g_up)
@@ -410,8 +463,8 @@
             ],
             axis=1,
         )
-        g_attn = exchange(d_attn.reshape(count, block, -1))
-        layer_out = exchange((h1 + ffout).astype(BF))
+        g_attn = exchange(rowwise(d_attn.reshape(count, block, -1)))
+        layer_out = (h1 + ffout).astype(BF)
         dn1, g_attn, layer_out = after(dn1, g_attn, layer_out)
         g_down, g_attn = g_down.astype(F32), g_attn.astype(F32)
         g_qkv = jnp.stack([g_attn[..., j * cols : (j + 1) * cols] for j in range(3)], axis=1)
@@ -425,9 +478,11 @@
         high = sums.astype(BF)
         rest = (sums - high.astype(F32)).astype(BF)
         notes = tile(jnp.concatenate([high, rest], axis=1))
-        last = exchange(jnp.concatenate([dh0.astype(BF), notes], axis=1))
-        input_grad = last[:, :local]
-        sums = jnp.sum(last[:, local].astype(F32), axis=0)[: 6 * block].reshape(2, 3, block)
+        last = exchange(jnp.concatenate([dh0.astype(BF), layer_out, notes], axis=1))
+        g_qkv, g_out = rowwise(g_qkv), rowwise(g_out)
+        last, g_gate_up, g_qkv, g_out, g_down = after(last, g_gate_up, g_qkv, g_out, g_down)
+        input_grad, layer_out = last[:, :local], last[:, local : 2 * local]
+        sums = jnp.sum(last[:, 2 * local].astype(F32), axis=0)[: 6 * block].reshape(2, 3, block)
         sums = sums[0] + sums[1]
         g_small = sums
         for k in range(1, lanes):

time: 515 us -> 510 us (level)
  matrix products: 61.7 us -> 33 us
  Pallas kernels: 29 us -> 48.5 us
  waiting for transfers between devices: 174 us -> 181 us
  other arithmetic: 39 us -> 45.3 us
  starting transfers between devices: 49.2 us -> 43.9 us
    pallas_call x0 -> x1, Pallas kernels: none -> 24.8 us  [feed_call(): pl.pallas_call(feed_body, grid=(count,), in_specs=[whole, whole, pl.Block...]
    dot_general x4 -> x0, matrix products: 24.5 us -> none  [the longest x1 7.06 us: shards(): gate_up = jnp.dot(n2_all, wgu, preferred_element_type=F32)]
    reduce_scatter x4, waiting for transfers between devices: 48.8 us -> 65 us  [deal(): return lax.psum_scatter(slots, 'tensor', scatter_dimension=0).astype(F32)]
    all_to_all x10 -> x9, waiting for transfers between devices: 76.9 us -> 67.4 us  [exchange(): return lax.all_to_all(blocks, 'dp', 0, 0, tiled=True)]
    another operation x0 -> x2, local copies, waits for them, and re-layouts: none -> 6.27 us  [the longest x1 3.91 us: rowwise(): return with_layout_constraint(array, Layout(tuple(range(array.ndim))))]
    optimization_barrier x4 -> x3, local copies, waits for them, and re-layouts: 12.1 us -> 6.55 us  [after(): return lax.optimization_barrier((value,) + waiting)]
    all_to_all x10 -> x9, starting transfers between devices: 43.9 us -> 38.6 us  [exchange(): return lax.all_to_all(blocks, 'dp', 0, 0, tiled=True)]
    pallas_call x2, Pallas kernels: 29 us -> 23.7 us  [attention_call(): pl.pallas_call(body, grid=(frames // span,), in_specs=[spec(a.shape[2]) f...]
  transfers between devices with their start and end apart: 21 -> 20, of which waited for: 12 -> 12; matrix products, arithmetic and copies ran while one was open for 20% -> 18% of each run, Pallas kernels for 6% -> 5%
where the time goes in v8:
time: 510 us; the launch traced here: 502 us
  waiting for transfers between devices  181 us (35%)
  blocking collectives  92.5 us (18%)
  Pallas kernels  48.5 us (10%)
  other arithmetic  45.3 us (9%)
  starting transfers between devices  43.9 us (9%)
  local copies, waits for them, and re-layouts  42.4 us (8%)
  matrix products  33 us (6%)
  between operations  15.1 us (3%)
    all_to_all x5, blocking collectives, exchange(): return lax.all_to_all(blocks, 'dp', 0, 0, tiled=True)  92.5 us
    all_to_all x9, waiting for transfers between devices, exchange(): return lax.all_to_all(blocks, 'dp', 0, 0, tiled=True)  67.4 us
    reduce_scatter x4, waiting for transfers between devices, deal(): return lax.psum_scatter(slots, 'tensor', scatter_dimension=0).astype(F32)  65 us
    all_gather x4, waiting for transfers between devices, collect(): return lax.all_gather(rows, 'tensor', axis=0).reshape(-1, rows.shape[-1])  47.9 us
    all_to_all x9, starting transfers between devices, exchange(): return lax.all_to_all(blocks, 'dp', 0, 0, tiled=True)  38.6 us
    pallas_call x1, Pallas kernels, feed_call(): pl.pallas_call(feed_body, grid=(count,), in_specs=[whole, whole, pl.Block...  24.8 us
    pallas_call x2, Pallas kernels, attention_call(): pl.pallas_call(body, grid=(frames // span,), in_specs=[spec(a.shape[2]) f...  23.7 us
    unnamed x58, local copies, waits for them, and re-layouts  12.4 us
  transfers between devices with their start and end apart: 20, of which 12 were waited for; matrix products, arithmetic and copies ran while one was open for 18% of the time, Pallas kernels for 5%

profile of v8, /device:TPU:0, one launch (start us, length us, event | category | flops | bytes accessed | tf_op | source)
XLA Modules:
  0.0 501.7 jit_solution(18135244599455871967)
XLA Ops:
  11.2 5.3 %all-to-all-start = ((bf16[8,48,1024]{2,1,0:T(8,128)(2,1)}), bf16[8,48,1024]{2,1,0:T(8,128)(2,1)S(1)}, u32[]{:S(2)}, u32[]{:S(2)}) async-start(bf16[8,48,1024]{2,1,0:T(8,128)(2,1)} %pad_maximum_fusion.4), calls=%async_computation | async-start | bytes 1572864 | tf_op jit(solution)/shard_map/all_to_all | solution.py:343
  16.6 12.5 %all-to-all-done = bf16[8,48,1024]{2,1,0:T(8,128)(2,1)S(1)} async-done(((bf16[8,48,1024]{2,1,0:T(8,128)(2,1)}), bf16[8,48,1024]{2,1,0:T(8,128)(2,1)S(1)}, u32[]{:S(2)}, u32[]{:S(2)}) %all-to-all-start) | async-done | bytes 786464 | tf_op jit(solution)/shard_map/all_to_all | solution.py:343
  33.3 29.1 %all_to_all.70 = bf16[8,128,1024]{2,1,0:T(8,128)(2,1)S(1)} all-to-all(bf16[8,128,1024]{2,1,0:T(8,128)(2,1)S(1)} %pad_maximum_fusion.2), channel_id=1, replica_groups=mesh['dp'=8,'tensor'=4] {'dp'}, dimensions={0} | all-to-all | bytes 4194304 | tf_op jit(solution)/shard_map/all_to_all | solution.py:343
  62.4 12.8 %all_to_all.71 = bf16[8,32,1024]{2,1,0:T(8,128)(2,1)} all-to-all(bf16[8,32,1024]{2,1,0:T(8,128)(2,1)S(1)} %copy-done.24), channel_id=1, replica_groups=mesh['dp'=8,'tensor'=4] {'dp'}, dimensions={0} | all-to-all | bytes 1048576 | tf_op jit(solution)/shard_map/all_to_all | solution.py:343
  79.4 24.5 %all_to_all.72.qkv_ref = bf16[8,128,768]{2,1,0:T(8,128)(2,1)} all-to-all(bf16[8,128,768]{2,1,0:T(8,128)(2,1)S(1)} %bitcast.155), channel_id=1, replica_groups=mesh['dp'=8,'tensor'=4] {'dp'}, dimensions={0} | all-to-all | bytes 3145728 | tf_op jit(solution)/shard_map/all_to_all | solution.py:343
  103.9 10.9 %shard_map.152 = bf16[8,128,256]{2,1,0:T(8,128)(2,1)} custom-call(bf16[8,128,768]{2,1,0:T(8,128)(2,1)} %all_to_all.72.qkv_ref), custom_call_target="tpu_custom_call" | custom-call | tf_op jit(solution)/shard_map/pallas_call | solution.py:272
  114.8 13.1 %all_to_all.73 = bf16[8,128,256]{2,1,0:T(8,128)(2,1)S(1)} all-to-all(bf16[8,128,256]{2,1,0:T(8,128)(2,1)} %shard_map.152), channel_id=1, replica_groups=mesh['dp'=8,'tensor'=4] {'dp'}, dimensions={0} | all-to-all | bytes 1048576 | tf_op jit(solution)/shard_map/all_to_all | solution.py:343
  130.8 3.8 convert_element_type.134
  138.3 4.0 convert.39
  145.3 27.7 %reduce-scatter.5.cloned.1.call-done = bf16[1,8,32,1024]{3,2,1,0:T(8,128)(2,1)} async-done(((bf16[4,8,32,1024]{3,2,1,0:T(8,128)(2,1)}), bf16[1,8,32,1024]{3,2,1,0:T(8,128)(2,1)}) %reduce-scatter.5.cloned.1.call-update) | async-done | bytes 524304 | tf_op jit(solution)/shard_map/reduce_scatter | solution.py:350
  178.5 4.6 all-to-all-start.6
  183.9 47.3 %all-gather.13.cloned.1.call-done = bf16[32,32,1024]{2,1,0:T(8,128)(2,1)} async-done(((bf16[8,32,1024]{2,1,0:T(8,128)(2,1)}), bf16[32,32,1024]{2,1,0:T(8,128)(2,1)}) %all-gather.13.cloned.1.call-update) | async-done | bytes 2097168 | tf_op jit(solution)/shard_map/all_gather | solution.py:346
  232.2 24.8 %shard_map.153 = (bf16[1024,1024]{1,0:T(8,128)(2,1)}, bf16[1024,1024]{1,0:T(8,128)(2,1)}, bf16[1024,1024]{1,0:T(8,128)(2,1)}, bf16[1024,1024]{1,0:T(8,128)(2,1)}) custom-call(bf16[1024,1024]{1,0:T(8,128)(2,1)} %bitcast.163, bf16[1024,1024]{1,0:T(8,128)(2,1)} %bitcast.161, bf16[1024,2048]{1,0:T(8,128)(2,1)} %bitcast.28.wgate_ref.wup_ref, ...), custom_call_target="tpu_custom_call" | custom-call | tf_op jit(solution)/shard_map/pallas_call | solution.py:323
  258.6 5.3 %convert_bitcast_fusion = bf16[8,1024,128]{2,1,0:T(8,128)(2,1)} fusion(bf16[1024,1024]{1,0:T(8,128)(2,1)} %get-tuple-element.87, bf16[1024,1024]{1,0:T(8,128)(2,1)S(1)} %bitcast.162), kind=kOutput, calls=%fused_computation.17 | convolution fusion | flops 2148532224 | bytes 6291456 | tf_op jit(solution)/shard_map/fk,frd->rkd/dot_general | solution.py:425
  263.9 4.5 all-to-all-start.7
  268.7 4.0 convolution_convert_fusion.1
  281.2 17.5 %reduce-scatter.7.cloned.1.call-done = bf16[1,8,32,1024]{3,2,1,0:T(8,128)(2,1)} async-done(((bf16[4,8,32,1024]{3,2,1,0:T(8,128)(2,1)}), bf16[1,8,32,1024]{3,2,1,0:T(8,128)(2,1)}) %reduce-scatter.7.cloned.1.call-update) | async-done | bytes 524304 | tf_op jit(solution)/shard_map/reduce_scatter | solution.py:350
  301.3 4.9 copy.116
  306.2 4.6 all-to-all-start.8
  313.4 5.9 %convolution_convert_fusion = bf16[1024,1024]{1,0:T(8,128)(2,1)} fusion(bf16[1024,1024]{1,0:T(8,128)(2,1)} %get-tuple-element.87, bf16[1024,1024]{0,1:T(8,128)(2,1)} %bitcast.169), kind=kOutput, calls=%fused_computation.18 | convolution fusion | flops 2148532224 | bytes 6291456 | tf_op jit(solution)/shard_map/dot_general | solution.py:446
  319.4 29.2 %all-to-all-done.8 = bf16[8,128,1536]{2,1,0:T(8,128)(2,1)} async-done(((bf16[8,128,1536]{2,1,0:T(8,128)(2,1)}), bf16[8,128,1536]{2,1,0:T(8,128)(2,1)}, u32[]{:S(2)}, u32[]{:S(2)}) %all-to-all-start.8) | async-done | bytes 3145760 | tf_op jit(solution)/shard_map/all_to_all | solution.py:343
  351.1 12.9 %all_to_all.74.grad_ref = bf16[8,128,256]{2,1,0:T(8,128)(2,1)} all-to-all(bf16[8,128,256]{2,1,0:T(8,128)(2,1)S(1)} %bitcast.171), channel_id=1, replica_groups=mesh['dp'=8,'tensor'=4] {'dp'}, dimensions={0} | all-to-all | bytes 1048576 | tf_op jit(solution)/shard_map/all_to_all | solution.py:343
  365.5 3.8 all-to-all-start.10
  369.3 12.8 %shard_map.154 = bf16[8,128,768]{2,1,0:T(8,128)(2,1)} custom-call(bf16[8,128,768]{2,1,0:T(8,128)(2,1)} %all_to_all.72.qkv_ref, bf16[8,128,256]{2,1,0:T(8,128)(2,1)} %all_to_all.74.grad_ref), custom_call_target="tpu_custom_call" | custom-call | tf_op jit(solution)/shard_map/pallas_call | solution.py:272
  393.8 16.3 %all-to-all-done.11 = bf16[8,128,768]{2,1,0:T(8,128)(2,1)S(1)} async-done(((bf16[8,128,768]{2,1,0:T(8,128)(2,1)}), bf16[8,128,768]{2,1,0:T(8,128)(2,1)S(1)}, u32[]{:S(2)}, u32[]{:S(2)}) %all-to-all-start.11) | async-done | bytes 1572896 | tf_op jit(solution)/shard_map/all_to_all | solution.py:343
  423.8 3.9 copy.122
  427.7 4.3 all-to-all-start.12
  432.1 3.9 convert_element_type.159
  439.3 17.5 %reduce-scatter.11.cloned.1.call-done = bf16[1,8,32,1024]{3,2,1,0:T(8,128)(2,1)} async-done(((bf16[4,8,32,1024]{3,2,1,0:T(8,128)(2,1)}), bf16[1,8,32,1024]{3,2,1,0:T(8,128)(2,1)}) %reduce-scatter.11.cloned.1.call-update) | async-done | bytes 524304 | tf_op jit(solution)/shard_map/reduce_scatter | solution.py:350
  463.0 4.3 all-to-all-start.13
  469.8 3.9 maximum_convert_fusion
  479.6 5.9 %all-to-all-done.13 = bf16[8,80,1024]{2,1,0:T(8,128)(2,1)} async-done(((bf16[8,80,1024]{2,1,0:T(8,128)(2,1)}), bf16[8,80,1024]{2,1,0:T(8,128)(2,1)}, u32[]{:S(2)}, u32[]{:S(2)}) %all-to-all-start.13) | async-done | bytes 1310752 | tf_op jit(solution)/shard_map/all_to_all | solution.py:343
  (161 shorter events, 100.6 us)
Async XLA Ops:
  11.2 19.4 %copy-start.23 = (f32[8,256,128]{2,1,0:T(8,128)S(1)}, f32[8,256,128]{2,1,0:T(8,128)}, u32[]{:S(2)}) copy-start(f32[8,256,128]{2,1,0:T(8,128)} %param.12) | copy-start | bytes 3145732
  11.2 17.9 %all-to-all-start = ((bf16[8,48,1024]{2,1,0:T(8,128)(2,1)}), bf16[8,48,1024]{2,1,0:T(8,128)(2,1)S(1)}, u32[]{:S(2)}, u32[]{:S(2)}) async-start(bf16[8,48,1024]{2,1,0:T(8,128)(2,1)} %pad_maximum_fusion.4), calls=%async_computation | async-start | bytes 1572864 | tf_op jit(solution)/shard_map/all_to_all | solution.py:343
  16.6 59.2 %all-gather.9.cloned.1.call-start = ((), (), s32[]{:S(2)}) async-start(), calls=%async_computation.22 | async-start | bytes 2621440 | tf_op jit(solution)/shard_map/all_gather | solution.py:346
  29.1 3.9 copy-start.4
  30.6 100.2 %all-gather.11.cloned.1.call-start = ((), (), s32[]{:S(2)}) async-start(), calls=%async_computation.23 | async-start | bytes 2621440 | tf_op jit(solution)/shard_map/all_gather | solution.py:346
  33.3 29.2 %copy-start.24 = (bf16[8,32,1024]{2,1,0:T(8,128)(2,1)S(1)}, bf16[8,32,1024]{2,1,0:T(8,128)(2,1)}, u32[]{:S(2)}) copy-start(bf16[8,32,1024]{2,1,0:T(8,128)(2,1)} %param.17) | copy-start | bytes 1572868
  62.4 65.5 %copy-start.14 = (bf16[8,128,1024]{2,1,0:T(8,128)(2,1)}, bf16[8,128,1024]{2,1,0:T(8,128)(2,1)S(1)}, u32[]{:S(2)}) copy-start(bf16[8,128,1024]{2,1,0:T(8,128)(2,1)S(1)} %all_to_all.70) | copy-start | bytes 6291460
  75.8 97.1 %reduce-scatter.5.cloned.1.call-start = ((), (), s32[]{:S(2)}) async-start(), calls=%async_computation.18 | async-start | bytes 2621440 | tf_op jit(solution)/shard_map/reduce_scatter | solution.py:350
  134.7 40.4 %all-to-all-start.5 = ((bf16[8,1024,128]{2,1,0:T(8,128)(2,1)}), bf16[8,1024,128]{2,1,0:T(8,128)(2,1)S(1)}, u32[]{:S(2)}, u32[]{:S(2)}) async-start(bf16[8,1024,128]{2,1,0:T(8,128)(2,1)} %convert_element_type.134), calls=%async_computation.6 | async-start | bytes 4194304 | tf_op jit(solution)/shard_map/all_to_all | solution.py:343
  178.5 53.7 %all-to-all-start.6 = ((bf16[8,128,2048]{2,1,0:T(8,128)(2,1)}), bf16[8,128,2048]{2,1,0:T(8,128)(2,1)}, u32[]{:S(2)}, u32[]{:S(2)}) async-start(bf16[8,128,2048]{2,1,0:T(8,128)(2,1)} %pad_maximum_fusion), calls=%async_computation.7 | async-start | bytes 8388608 | tf_op jit(solution)/shard_map/all_to_all | solution.py:343
  183.1 48.1 %all-gather.13.cloned.1.call-start = ((), (), s32[]{:S(2)}) async-start(), calls=%async_computation.24 | async-start | bytes 2621440 | tf_op jit(solution)/shard_map/all_gather | solution.py:346
  183.7 115.0 %reduce-scatter.7.cloned.1.call-start = ((), (), s32[]{:S(2)}) async-start(), calls=%async_computation.19 | async-start | bytes 2621440 | tf_op jit(solution)/shard_map/reduce_scatter | solution.py:350
  263.9 4.8 copy-start.17
  263.9 35.9 %all-to-all-start.7 = ((bf16[8,1024,128]{2,1,0:T(8,128)(2,1)}), bf16[8,1024,128]{2,1,0:T(8,128)(2,1)}, u32[]{:S(2)}, u32[]{:S(2)}) async-start(bf16[8,1024,128]{2,1,0:T(8,128)(2,1)} %convert_bitcast_fusion), calls=%async_computation.9 | async-start | bytes 4194304 | tf_op jit(solution)/shard_map/all_to_all | solution.py:343
  268.4 80.2 %all-gather.15.cloned.1.call-start = ((), (), s32[]{:S(2)}) async-start(), calls=%async_computation.25 | async-start | bytes 2621440 | tf_op jit(solution)/shard_map/all_gather | solution.py:346
  281.2 19.0 %copy-start.7 = (bf16[8,32,1024]{2,1,0:T(8,128)(2,1)S(1)}, bf16[8,32,1024]{2,1,0:T(8,128)(2,1)}, u32[]{:S(2)}) copy-start(bf16[8,32,1024]{2,1,0:T(8,128)(2,1)} %all_to_all.71) | copy-start | bytes 1572868
  306.2 4.6 copy-start.1
  306.2 42.4 %all-to-all-start.8 = ((bf16[8,128,1536]{2,1,0:T(8,128)(2,1)}), bf16[8,128,1536]{2,1,0:T(8,128)(2,1)}, u32[]{:S(2)}, u32[]{:S(2)}) async-start(bf16[8,128,1536]{2,1,0:T(8,128)(2,1)} %copy.116), calls=%async_computation.10 | async-start | bytes 6291456 | tf_op jit(solution)/shard_map/all_to_all | solution.py:343
  310.8 80.9 %reduce-scatter.9.cloned.1.call-start = ((), (), s32[]{:S(2)}) async-start(), calls=%async_computation.20 | async-start | bytes 2621440 | tf_op jit(solution)/shard_map/reduce_scatter | solution.py:350
  351.0 13.0 %copy-start.9 = (bf16[64,8,8,128]{3,2,1,0:T(8,128)(2,1)S(1)}, bf16[64,8,8,128]{3,2,1,0:T(8,128)(2,1)}, u32[]{:S(2)}) copy-start(bf16[64,8,8,128]{3,2,1,0:T(8,128)(2,1)} %copy.134) | copy-start | bytes 3145732
  365.5 19.1 %all-to-all-start.10 = ((bf16[8,128,512]{2,1,0:T(8,128)(2,1)}), bf16[8,128,512]{2,1,0:T(8,128)(2,1)S(1)}, u32[]{:S(2)}, u32[]{:S(2)}) async-start(bf16[8,128,512]{2,1,0:T(8,128)(2,1)} %copy.118), calls=%async_computation.12 | async-start | bytes 2097152 | tf_op jit(solution)/shard_map/all_to_all | solution.py:343
  385.6 24.5 %all-to-all-start.11 = ((bf16[8,128,768]{2,1,0:T(8,128)(2,1)}), bf16[8,128,768]{2,1,0:T(8,128)(2,1)S(1)}, u32[]{:S(2)}, u32[]{:S(2)}) async-start(bf16[8,128,768]{2,1,0:T(8,128)(2,1)} %shard_map.154), calls=%async_computation.13 | async-start | bytes 3145728 | tf_op jit(solution)/shard_map/all_to_all | solution.py:343
  389.1 67.6 %reduce-scatter.11.cloned.1.call-start = ((), (), s32[]{:S(2)}) async-start(), calls=%async_computation.21 | async-start | bytes 2621440 | tf_op jit(solution)/shard_map/reduce_scatter | solution.py:350
  410.2 5.2 %copy-start.21 = (bf16[8,4,32,768]{3,2,0,1:T(8,128)(2,1)}, bf16[8,4,32,768]{3,2,0,1:T(8,128)(2,1)S(1)}, u32[]{:S(2)}) copy-start(bf16[8,4,32,768]{3,2,0,1:T(8,128)(2,1)S(1)} %copy.119) | copy-start | bytes 4718596
  427.7 31.2 %all-to-all-start.12 = ((bf16[8,128,1024]{1,2,0:T(8,128)(2,1)}), bf16[8,128,1024]{1,2,0:T(8,128)(2,1)}, u32[]{:S(2)}, u32[]{:S(2)}) async-start(bf16[8,128,1024]{1,2,0:T(8,128)(2,1)} %copy.122), calls=%async_computation.16 | async-start | bytes 4194304 | tf_op jit(solution)/shard_map/all_to_all | solution.py:343
  438.4 20.5 %copy-start.5 = (bf16[8,48,1024]{2,1,0:T(8,128)(2,1)S(1)}, bf16[8,48,1024]{2,1,0:T(8,128)(2,1)}, u32[]{:S(2)}) copy-start(bf16[8,48,1024]{2,1,0:T(8,128)(2,1)} %copy-done.4) | copy-start | bytes 2359300
  439.3 21.4 %copy-start.3 = (f32[8,32,1024]{2,1,0:T(8,128)S(1)}, f32[8,32,1024]{2,1,0:T(8,128)}, u32[]{:S(2)}) copy-start(f32[8,32,1024]{2,1,0:T(8,128)} %copy-done.2) | copy-start | bytes 3145732
  439.3 21.4 %copy-start.8 = (bf16[8,32,1024]{2,1,0:T(8,128)(2,1)S(1)}, bf16[8,32,1024]{2,1,0:T(8,128)(2,1)}, u32[]{:S(2)}) copy-start(bf16[8,32,1024]{2,1,0:T(8,128)(2,1)} %all_to_all.71) | copy-start | bytes 1572868
  463.0 22.5 %all-to-all-start.13 = ((bf16[8,80,1024]{2,1,0:T(8,128)(2,1)}), bf16[8,80,1024]{2,1,0:T(8,128)(2,1)}, u32[]{:S(2)}, u32[]{:S(2)}) async-start(bf16[8,80,1024]{2,1,0:T(8,128)(2,1)} %fusion.11), calls=%async_computation.17 | async-start | bytes 2621440 | tf_op jit(solution)/shard_map/all_to_all | solution.py:343
  486.5 6.9 %collective-permute-start = (f32[3,128]{1,0:T(4,128)S(1)}, f32[3,128]{1,0:T(4,128)S(1)}, u32[]{:S(2)}, u32[]{:S(2)}) collective-permute-start(f32[3,128]{1,0:T(4,128)S(1)} %add_bitcast_fusion), channel_id=1, source_target_pairs={{0,1},{1,2},{2,3},{3,0},{4,5},{5,6},{6,7},{7,4},{8,9},{9,10},{10,1... | collective-permute-start | bytes 4616 | tf_op jit(solution)/shard_map/ppermute | solution.py:490
  487.2 6.2 %collective-permute-start.1 = (f32[3,128]{1,0:T(4,128)S(1)}, f32[3,128]{1,0:T(4,128)S(1)}, u32[]{:S(2)}, u32[]{:S(2)}) collective-permute-start(f32[3,128]{1,0:T(4,128)S(1)} %add_bitcast_fusion), channel_id=1, source_target_pairs={{0,2},{1,3},{2,0},{3,1},{4,6},{5,7},{6,4},{7,5},{8,10},{9,11},{10,... | collective-permute-start | bytes 4616 | tf_op jit(solution)/shard_map/ppermute | solution.py:490
  488.9 4.5 collective-permute-start.2
  (15 other events, 27.7 us)
Sparse Core Ops, SparseCore 0:
  30.7 45.0 all-gather.8
  77.4 44.4 all-gather.10
  131.0 41.9 reduce-scatter.4
  185.8 45.4 all-gather.12
  257.1 41.4 reduce-scatter.6
  301.4 44.8 all-gather.14
  349.2 42.4 reduce-scatter.8
  415.5 41.2 reduce-scatter.10

commit v9 on v8

--- a/solution.py
+++ b/solution.py
@@ -279,62 +279,64 @@
 
 
 def feed_body(
-    n2_ref, grad_ref, wgate_ref, wup_ref, wdown_ref, hid_ref, d_gate_ref, d_up_ref, dn2_ref, sum_ref
+    n2_ref, grad_ref, wgate_ref, wup_ref, wdown_ref, wrow_ref,
+    hid_ref, d_gate_ref, d_up_ref, dn2_ref, kept_ref,
 ):
     step = pl.program_id(0)
-    wgate, wup = wgate_ref[...], wup_ref[...]
-    wdown = jnp.concatenate([wdown_ref[r] for r in range(wdown_ref.shape[0])], axis=1)
-    span = min(256, n2_ref.shape[0])
-    for start in range(0, n2_ref.shape[0], span):
-        rows = slice(start, start + span)
-        n2 = n2_ref[rows]
-        gate = times(n2, wgate, 1, 0)
-        upval = times(n2, wup, 1, 0)
-        d_hidden = times(grad_ref[rows], wdown, 1, 1)
+    count = kept_ref.shape[0]
+
+    @pl.when(step < count)
+    def _():
+        wdown = jnp.concatenate([wdown_ref[r] for r in range(wdown_ref.shape[0])], axis=1)
+        gate = times(n2_ref[...], wgate_ref[...], 1, 0)
+        upval = times(n2_ref[...], wup_ref[...], 1, 0)
+        d_hidden = times(grad_ref[...], wdown, 1, 1)
         sigma = 1.0 / (1.0 + jnp.exp(-gate))
         silu_val = gate * sigma
-        hid_ref[rows] = (silu_val * upval).astype(BF)
+        hid_ref[...] = (silu_val * upval).astype(BF)
         d_gate = (d_hidden * upval * (sigma * (1.0 + gate * (1.0 - sigma)))).astype(BF)
         d_up = (d_hidden * silu_val).astype(BF)
-        d_gate_ref[rows] = d_gate
-        d_up_ref[rows] = d_up
-        part = times(d_gate, wgate, 1, 1) + times(d_up, wup, 1, 1)
-
-        @pl.when(step == 0)
-        def _():
-            sum_ref[rows] = part
-
-        @pl.when(step > 0)
-        def _():
-            sum_ref[rows] += part
-
-    @pl.when(step == pl.num_programs(0) - 1)
+        d_gate_ref[...] = d_gate
+        d_up_ref[...] = d_up
+        kept_ref[step, 0] = d_gate
+        kept_ref[step, 1] = d_up
+
+    @pl.when(step >= count)
     def _():
-        dn2_ref[...] = sum_ref[...].astype(BF)
+        kept = [kept_ref[k, half] for half in range(2) for k in range(count)]
+        dn2_ref[...] = times(jnp.concatenate(kept, axis=1), wrow_ref[...], 1, 1).astype(BF)
 
 
 def feed_call(n2, grad, wgu, wdown):
     frames, width = n2.shape
     parts, hidden, block = wdown.shape
-    span = min(256, hidden)
+    span, part = min(256, hidden), min(512, width)
     count = hidden // span
+
+    def hid_block(i):
+        return jnp.minimum(i, count - 1)
+
+    def out_block(i):
+        return jnp.maximum(i - count, 0)
+
     whole = pl.BlockSpec((frames, width), lambda i: (0, 0))
-    piece = pl.BlockSpec((frames, span), lambda i: (0, i))
+    piece = pl.BlockSpec((frames, span), lambda i: (0, hid_block(i)))
     return pl.pallas_call(
         feed_body,
-        grid=(count,),
+        grid=(count + width // part,),
         in_specs=[
             whole,
             whole,
-            pl.BlockSpec((width, span), lambda i: (0, i)),
-            pl.BlockSpec((width, span), lambda i: (0, i + count)),
-            pl.BlockSpec((parts, span, block), lambda i: (0, i, 0)),
+            pl.BlockSpec((width, span), lambda i: (0, hid_block(i))),
+            pl.BlockSpec((width, span), lambda i: (0, hid_block(i) + count)),
+            pl.BlockSpec((parts, span, block), lambda i: (0, hid_block(i), 0)),
+            pl.BlockSpec((part, 2 * hidden), lambda i: (out_block(i), 0)),
         ],
-        out_specs=[piece, piece, piece, whole],
+        out_specs=[piece, piece, piece, pl.BlockSpec((frames, part), lambda i: (0, out_block(i)))],
         out_shape=[jax.ShapeDtypeStruct((frames, hidden), BF)] * 3
         + [jax.ShapeDtypeStruct((frames, width), BF)],
-        scratch_shapes=[pltpu.VMEM((frames, width), F32)],
-    )(n2, grad, wgu, wgu, wdown)
+        scratch_shapes=[pltpu.VMEM((count, 2, frames, span), BF)],
+    )(n2, grad, wgu, wgu, wdown, wgu)
 
 
 def make_step_shards(count, lanes):
@@ -347,7 +349,7 @@
 
     def deal(partial):
         slots = partial.astype(BF).reshape(lanes, count, -1, partial.shape[-1])
-        return lax.psum_scatter(slots, "tensor", scatter_dimension=0).astype(F32)
+        return lax.psum_scatter(slots, "tensor", scatter_dimension=0)
 
     def frame_split(array):
         slots = array.reshape(lanes, count, -1, array.shape[-1])
@@ -410,13 +412,13 @@
         attn = deal(attn)
         wdown = exchange(w_down.astype(BF))
         wgu = jnp.concatenate([w_gate_up[:, 0], w_gate_up[:, 1]], axis=2).astype(BF)
-        attn, wdown, wgu = after(attn, wdown, wgu)
-        h1 = h0 + attn
+        wdown, wgu = after(wdown, wgu)
+        attn, wdown = after(attn, wdown)
+        wgu = exchange(wgu).reshape(width, -1)
+        h1 = h0 + attn.astype(F32)
         r2 = lax.rsqrt(jnp.mean(h1 * h1, axis=-1, keepdims=True) + EPS)
         n2 = (h1 * r2 * gain_two).astype(BF)
-        n2, wgu = after(n2, wgu)
         n2_all = collect(n2)
-        wgu = exchange(wgu).reshape(width, -1)
 
         hidden, d_gate, d_up, dn2 = feed_call(n2_all, grad_all, wgu, wdown)
         hid_width = hidden.shape[1]
@@ -435,7 +437,7 @@
         g_gate = jnp.concatenate([g_gate, g_up[:, :part]], axis=1).reshape(count, block, -1)
         g_up = g_up[:, part:].reshape(count, block, -1)
         dn2, g_down, g_gate, g_up = after(dn2, g_down, g_gate, g_up)
-        dh_norm2, dgain_two = norm_back(dn2, h1, r2, gain_two)
+        dh_norm2, dgain_two = norm_back(dn2.astype(F32), h1, r2, gain_two)
         dh1 = grad.astype(F32) + dh_norm2
         dh1_low, g_gate, hidden = after(dh1.astype(BF), g_gate, hidden)
         dh1_all = collect(dh1_low)
@@ -464,30 +466,33 @@
             axis=1,
         )
         g_attn = exchange(rowwise(d_attn.reshape(count, block, -1)))
-        layer_out = (h1 + ffout).astype(BF)
+        layer_out = (h1 + ffout.astype(F32)).astype(BF)
         dn1, g_attn, layer_out = after(dn1, g_attn, layer_out)
         g_down, g_attn = g_down.astype(F32), g_attn.astype(F32)
         g_qkv = jnp.stack([g_attn[..., j * cols : (j + 1) * cols] for j in range(3)], axis=1)
         g_out = jnp.swapaxes(g_attn[..., 3 * cols :], 1, 2)
 
-        dh_norm1, dgain_one = norm_back(dn1, h0, r1, gain_one)
+        dh_norm1, dgain_one = norm_back(dn1.astype(F32), h0, r1, gain_one)
         dh0 = dh1 + dh_norm1
         d_pad = jnp.sum(dh0 * padded, axis=(0, 1))
-        sums = jnp.stack([dgain_one, dgain_two, d_pad]).reshape(3, count, block)
-        sums = jnp.swapaxes(sums, 0, 1).reshape(count, -1)
-        high = sums.astype(BF)
-        rest = (sums - high.astype(F32)).astype(BF)
-        notes = tile(jnp.concatenate([high, rest], axis=1))
-        last = exchange(jnp.concatenate([dh0.astype(BF), layer_out, notes], axis=1))
-        g_qkv, g_out = rowwise(g_qkv), rowwise(g_out)
-        last, g_gate_up, g_qkv, g_out, g_down = after(last, g_gate_up, g_qkv, g_out, g_down)
-        input_grad, layer_out = last[:, :local], last[:, local : 2 * local]
-        sums = jnp.sum(last[:, 2 * local].astype(F32), axis=0)[: 6 * block].reshape(2, 3, block)
-        sums = sums[0] + sums[1]
-        g_small = sums
+        sums = jnp.stack([dgain_one, dgain_two, d_pad])
+        last = exchange(jnp.concatenate([dh0.astype(BF), layer_out], axis=1))
+
+        total = sums
         for k in range(1, lanes):
             around = [(i, (i + k) % lanes) for i in range(lanes)]
-            g_small = g_small + lax.ppermute(sums, "tensor", around)
+            total = total + lax.ppermute(sums, "tensor", around)
+        total = jnp.swapaxes(total.reshape(3, count, block), 0, 1)
+        g_small = lax.dynamic_index_in_dim(total, me, 0, keepdims=False)
+        for k in range(1, count):
+            theirs = lax.dynamic_index_in_dim(total, me ^ k, 0, keepdims=False)
+            g_small = g_small + lax.ppermute(theirs, "dp", [(i, i ^ k) for i in range(count)])
+
+        g_qkv, g_out = rowwise(g_qkv), rowwise(g_out)
+        last, g_small, g_gate_up, g_qkv, g_out, g_down = after(
+            last, g_small, g_gate_up, g_qkv, g_out, g_down
+        )
+        input_grad, layer_out = last[:, :local], last[:, local:]
         return (layer_out, input_grad, g_qkv, g_out, g_gate_up, g_down, g_small[0:2], g_small[2])
 
     return shards
@@ -519,7 +524,7 @@
         steps, frames, width = layer_in.shape
         local = frames // (dp_size * tensor_size)
         block = width // dp_size
-        fits = 6 * block <= width and 3 * block + local <= width
+        fits = 3 * block + local <= width
         if steps == dp_size and dp_size & (dp_size - 1) == 0 and fits:
             body, over, dp = make_step_shards(dp_size, tensor_size), mesh, ("dp",)
         else:

time: 510 us -> 497 us (0.975)
  waiting for transfers between devices: 181 us -> 150 us
  blocking collectives: 92.5 us -> 117 us
  Pallas kernels: 48.5 us -> 41.1 us
    all_to_all x9 -> x8, waiting for transfers between devices: 67.4 us -> 136 us  [exchange(): return lax.all_to_all(blocks, 'dp', 0, 0, tiled=True)]
    reduce_scatter x4, waiting for transfers between devices: 65 us -> 7.67 us  [deal(): return lax.psum_scatter(slots, 'tensor', scatter_dimension=0)]
    all_gather x4, waiting for transfers between devices: 47.9 us -> 2.43 us  [collect(): return lax.all_gather(rows, 'tensor', axis=0).reshape(-1, rows.shape[-1])]
    all_to_all x5 -> x6, blocking collectives: 92.5 us -> 117 us  [exchange(): return lax.all_to_all(blocks, 'dp', 0, 0, tiled=True)]
    convert_element_type x8 -> x1, other arithmetic: 9.17 us -> 0.33 us  [shards(): layer_out = (h1 + ffout.astype(F32)).astype(BF)]
    pallas_call x1, Pallas kernels: 24.8 us -> 17.4 us  [feed_call(): pl.pallas_call(feed_body, grid=(count + width // part,), in_specs=[whole,...]
    ppermute x3 -> x10, starting transfers between devices: 4.61 us -> 11.7 us  [the longest x7 7.14 us: shards(): lax.ppermute(theirs, 'dp', [(i, i ^ k) for i in range(count)])]
    all_to_all x9 -> x8, starting transfers between devices: 38.6 us -> 33.3 us  [exchange(): return lax.all_to_all(blocks, 'dp', 0, 0, tiled=True)]
  transfers between devices with their start and end apart: 20 -> 26, of which waited for: 12 -> 12; matrix products, arithmetic and copies ran while one was open for 18% -> 19% of each run, Pallas kernels for 5% -> 5%
where the time goes in v9:
time: 497 us; the launch traced here: 489 us
  waiting for transfers between devices  150 us (30%)
  blocking collectives  117 us (24%)
  starting transfers between devices  46 us (9%)
  local copies, waits for them, and re-layouts  43.9 us (9%)
  other arithmetic  41.8 us (8%)
  Pallas kernels  41.1 us (8%)
  matrix products  33.7 us (7%)
  between operations  15.1 us (3%)
    all_to_all x8, waiting for transfers between devices, exchange(): return lax.all_to_all(blocks, 'dp', 0, 0, tiled=True)  136 us
    all_to_all x6, blocking collectives, exchange(): return lax.all_to_all(blocks, 'dp', 0, 0, tiled=True)  117 us
    all_to_all x8, starting transfers between devices, exchange(): return lax.all_to_all(blocks, 'dp', 0, 0, tiled=True)  33.3 us
    pallas_call x2, Pallas kernels, attention_call(): pl.pallas_call(body, grid=(frames // span,), in_specs=[spec(a.shape[2]) f...  23.7 us
    pallas_call x1, Pallas kernels, feed_call(): pl.pallas_call(feed_body, grid=(count + width // part,), in_specs=[whole,...  17.4 us
    unnamed x49, local copies, waits for them, and re-layouts  12.9 us
  transfers between devices with their start and end apart: 26, of which 12 were waited for; matrix products, arithmetic and copies ran while one was open for 19% of the time, Pallas kernels for 5%

profile of v9, /device:TPU:0, one launch (start us, length us, event | category | flops | bytes accessed | tf_op | source)
XLA Modules:
  0.0 488.7 jit_solution(13448442026507493185)
XLA Ops:
  11.2 5.3 %all-to-all-start = ((bf16[8,48,1024]{2,1,0:T(8,128)(2,1)}), bf16[8,48,1024]{2,1,0:T(8,128)(2,1)S(1)}, u32[]{:S(2)}, u32[]{:S(2)}) async-start(bf16[8,48,1024]{2,1,0:T(8,128)(2,1)} %pad_maximum_fusion.5), calls=%async_computation | async-start | bytes 1572864 | tf_op jit(solution)/shard_map/all_to_all | solution.py:345
  16.6 12.5 %all-to-all-done = bf16[8,48,1024]{2,1,0:T(8,128)(2,1)S(1)} async-done(((bf16[8,48,1024]{2,1,0:T(8,128)(2,1)}), bf16[8,48,1024]{2,1,0:T(8,128)(2,1)S(1)}, u32[]{:S(2)}, u32[]{:S(2)}) %all-to-all-start) | async-done | bytes 786464 | tf_op jit(solution)/shard_map/all_to_all | solution.py:345
  33.2 29.1 %all_to_all.70 = bf16[8,128,1024]{2,1,0:T(8,128)(2,1)S(1)} all-to-all(bf16[8,128,1024]{2,1,0:T(8,128)(2,1)S(1)} %pad_maximum_fusion.2), channel_id=1, replica_groups=mesh['dp'=8,'tensor'=4] {'dp'}, dimensions={0} | all-to-all | bytes 4194304 | tf_op jit(solution)/shard_map/all_to_all | solution.py:345
  62.4 12.8 %all_to_all.71 = bf16[8,32,1024]{2,1,0:T(8,128)(2,1)} all-to-all(bf16[8,32,1024]{2,1,0:T(8,128)(2,1)S(1)} %copy-done.19), channel_id=1, replica_groups=mesh['dp'=8,'tensor'=4] {'dp'}, dimensions={0} | all-to-all | bytes 1048576 | tf_op jit(solution)/shard_map/all_to_all | solution.py:345
  79.4 24.5 %all_to_all.72.qkv_ref = bf16[8,128,768]{2,1,0:T(8,128)(2,1)} all-to-all(bf16[8,128,768]{2,1,0:T(8,128)(2,1)S(1)} %bitcast.166), channel_id=1, replica_groups=mesh['dp'=8,'tensor'=4] {'dp'}, dimensions={0} | all-to-all | bytes 3145728 | tf_op jit(solution)/shard_map/all_to_all | solution.py:345
  103.9 10.9 %shard_map.152 = bf16[8,128,256]{2,1,0:T(8,128)(2,1)} custom-call(bf16[8,128,768]{2,1,0:T(8,128)(2,1)} %all_to_all.72.qkv_ref), custom_call_target="tpu_custom_call" | custom-call | tf_op jit(solution)/shard_map/pallas_call | solution.py:272
  114.8 13.1 %all_to_all.73 = bf16[8,128,256]{2,1,0:T(8,128)(2,1)S(1)} all-to-all(bf16[8,128,256]{2,1,0:T(8,128)(2,1)} %shard_map.152), channel_id=1, replica_groups=mesh['dp'=8,'tensor'=4] {'dp'}, dimensions={0} | all-to-all | bytes 1048576 | tf_op jit(solution)/shard_map/all_to_all | solution.py:345
  130.8 3.8 convert_element_type.105
  134.7 3.6 all-to-all-start.5
  138.3 4.0 convert.35
  145.3 19.5 %all-to-all-done.5.wdown_ref = bf16[8,1024,128]{2,1,0:T(8,128)(2,1)S(1)} async-done(((bf16[8,1024,128]{2,1,0:T(8,128)(2,1)}), bf16[8,1024,128]{2,1,0:T(8,128)(2,1)S(1)}, u32[]{:S(2)}, u32[]{:S(2)}) %all-to-all-start.5) | async-done | bytes 2097184 | tf_op jit(solution)/shard_map/all_to_all | solution.py:345
  166.1 4.5 all-to-all-start.6
  176.8 43.0 %all-to-all-done.6 = bf16[8,128,2048]{2,1,0:T(8,128)(2,1)} async-done(((bf16[8,128,2048]{2,1,0:T(8,128)(2,1)}), bf16[8,128,2048]{2,1,0:T(8,128)(2,1)}, u32[]{:S(2)}, u32[]{:S(2)}) %all-to-all-start.6) | async-done | bytes 4194336 | tf_op jit(solution)/shard_map/all_to_all | solution.py:345
  221.6 17.4 %shard_map.153 = (bf16[1024,1024]{1,0:T(8,128)(2,1)}, bf16[1024,1024]{1,0:T(8,128)(2,1)}, bf16[1024,1024]{1,0:T(8,128)(2,1)}, bf16[1024,1024]{1,0:T(8,128)(2,1)}) custom-call(bf16[1024,1024]{1,0:T(8,128)(2,1)} %bitcast.178, bf16[1024,1024]{1,0:T(8,128)(2,1)} %bitcast.176, bf16[1024,2048]{1,0:T(8,128)(2,1)} %bitcast.28.wgate_ref.wup_ref.wrow_ref, ...), custom_call_target="tpu_custom_call" | custom-call | tf_op jit(solution)/shard_map/pallas_call | solution.py:324
  240.6 5.3 %convert_bitcast_fusion = bf16[8,1024,128]{2,1,0:T(8,128)(2,1)} fusion(bf16[1024,1024]{1,0:T(8,128)(2,1)} %get-tuple-element.86, bf16[1024,1024]{1,0:T(8,128)(2,1)S(1)} %bitcast.177), kind=kOutput, calls=%fused_computation.15 | convolution fusion | flops 2148532224 | bytes 6291456 | tf_op jit(solution)/shard_map/fk,frd->rkd/dot_general | solution.py:427
  245.9 3.6 all-to-all-start.7
  249.8 4.7 convolution_convert_fusion.1
  263.6 12.6 %all-to-all-done.7 = bf16[8,1024,128]{2,1,0:T(8,128)(2,1)S(1)} async-done(((bf16[8,1024,128]{2,1,0:T(8,128)(2,1)}), bf16[8,1024,128]{2,1,0:T(8,128)(2,1)S(1)}, u32[]{:S(2)}, u32[]{:S(2)}) %all-to-all-start.7) | async-done | bytes 2097184 | tf_op jit(solution)/shard_map/all_to_all | solution.py:345
  276.2 5.5 %reduce-scatter.7.cloned.1.call-done = bf16[1,8,32,1024]{3,2,1,0:T(8,128)(2,1)} async-done(((bf16[4,8,32,1024]{3,2,1,0:T(8,128)(2,1)}), bf16[1,8,32,1024]{3,2,1,0:T(8,128)(2,1)}) %reduce-scatter.7.cloned.1.call-update) | async-done | bytes 524304 | tf_op jit(solution)/shard_map/reduce_scatter | solution.py:352
  285.8 4.9 %copy.115 = bf16[8,128,1536]{2,1,0:T(8,128)(2,1)} copy(bf16[8,128,1536]{1,0,2:T(8,128)(2,1)} %bitcast.163) | data formatting | bytes 6291456 | tf_op jit(solution)/shard_map/optimization_barrier | solution.py:367
  290.7 4.6 all-to-all-start.8
  298.0 5.9 %convolution_convert_fusion = bf16[1024,1024]{1,0:T(8,128)(2,1)} fusion(bf16[1024,1024]{1,0:T(8,128)(2,1)} %get-tuple-element.86, bf16[1024,1024]{0,1:T(8,128)(2,1)} %bitcast.186), kind=kOutput, calls=%fused_computation.16 | convolution fusion | flops 2148532224 | bytes 6291456 | tf_op jit(solution)/shard_map/dot_general | solution.py:448
  304.0 29.2 %all-to-all-done.8 = bf16[8,128,1536]{2,1,0:T(8,128)(2,1)} async-done(((bf16[8,128,1536]{2,1,0:T(8,128)(2,1)}), bf16[8,128,1536]{2,1,0:T(8,128)(2,1)}, u32[]{:S(2)}, u32[]{:S(2)}) %all-to-all-start.8) | async-done | bytes 3145760 | tf_op jit(solution)/shard_map/all_to_all | solution.py:345
  335.6 12.9 %all_to_all.74.grad_ref = bf16[8,128,256]{2,1,0:T(8,128)(2,1)} all-to-all(bf16[8,128,256]{2,1,0:T(8,128)(2,1)S(1)} %bitcast.188), channel_id=1, replica_groups=mesh['dp'=8,'tensor'=4] {'dp'}, dimensions={0} | all-to-all | bytes 1048576 | tf_op jit(solution)/shard_map/all_to_all | solution.py:345
  353.9 12.8 %shard_map.154 = bf16[8,128,768]{2,1,0:T(8,128)(2,1)} custom-call(bf16[8,128,768]{2,1,0:T(8,128)(2,1)} %all_to_all.72.qkv_ref, bf16[8,128,256]{2,1,0:T(8,128)(2,1)} %all_to_all.74.grad_ref), custom_call_target="tpu_custom_call" | custom-call | tf_op jit(solution)/shard_map/pallas_call | solution.py:272
  368.9 24.4 %all_to_all.75 = bf16[8,128,768]{2,1,0:T(8,128)(2,1)S(1)} all-to-all(bf16[8,128,768]{2,1,0:T(8,128)(2,1)} %shard_map.154), channel_id=1, replica_groups=mesh['dp'=8,'tensor'=4] {'dp'}, dimensions={0} | all-to-all | bytes 3145728 | tf_op jit(solution)/shard_map/all_to_all | solution.py:345
  407.1 4.0 copy.121
  411.0 4.5 all-to-all-start.12
  421.3 3.9 maximum_convert_fusion
  425.6 16.5 %all-to-all-done.12 = bf16[8,128,1024]{1,2,0:T(8,128)(2,1)} async-done(((bf16[8,128,1024]{1,2,0:T(8,128)(2,1)}), bf16[8,128,1024]{1,2,0:T(8,128)(2,1)}, u32[]{:S(2)}, u32[]{:S(2)}) %all-to-all-start.12) | async-done | bytes 2097184 | tf_op jit(solution)/shard_map/all_to_all | solution.py:345
  451.4 3.8 convert_element_type.124
  468.9 4.4 collective-permute-done.4
  (158 shorter events, 105.8 us)
Async XLA Ops:
  11.2 19.4 %copy-start.18 = (f32[8,256,128]{2,1,0:T(8,128)S(1)}, f32[8,256,128]{2,1,0:T(8,128)}, u32[]{:S(2)}) copy-start(f32[8,256,128]{2,1,0:T(8,128)} %param.12) | copy-start | bytes 3145732
  11.2 17.9 %all-to-all-start = ((bf16[8,48,1024]{2,1,0:T(8,128)(2,1)}), bf16[8,48,1024]{2,1,0:T(8,128)(2,1)S(1)}, u32[]{:S(2)}, u32[]{:S(2)}) async-start(bf16[8,48,1024]{2,1,0:T(8,128)(2,1)} %pad_maximum_fusion.5), calls=%async_computation | async-start | bytes 1572864 | tf_op jit(solution)/shard_map/all_to_all | solution.py:345
  16.6 59.2 %all-gather.9.cloned.1.call-start = ((), (), s32[]{:S(2)}) async-start(), calls=%async_computation.22 | async-start | bytes 2621440 | tf_op jit(solution)/shard_map/all_gather | solution.py:348
  30.6 100.2 %all-gather.11.cloned.1.call-start = ((), (), s32[]{:S(2)}) async-start(), calls=%async_computation.23 | async-start | bytes 2621440 | tf_op jit(solution)/shard_map/all_gather | solution.py:348
  33.2 29.2 %copy-start.19 = (bf16[8,32,1024]{2,1,0:T(8,128)(2,1)S(1)}, bf16[8,32,1024]{2,1,0:T(8,128)(2,1)}, u32[]{:S(2)}) copy-start(bf16[8,32,1024]{2,1,0:T(8,128)(2,1)} %param.17) | copy-start | bytes 1572868
  62.4 65.5 %copy-start.10 = (bf16[8,128,1024]{2,1,0:T(8,128)(2,1)}, bf16[8,128,1024]{2,1,0:T(8,128)(2,1)S(1)}, u32[]{:S(2)}) copy-start(bf16[8,128,1024]{2,1,0:T(8,128)(2,1)S(1)} %all_to_all.70) | copy-start | bytes 6291460
  75.8 97.1 %reduce-scatter.5.cloned.1.call-start = ((), (), s32[]{:S(2)}) async-start(), calls=%async_computation.18 | async-start | bytes 2621440 | tf_op jit(solution)/shard_map/reduce_scatter | solution.py:352
  134.7 30.2 %all-to-all-start.5 = ((bf16[8,1024,128]{2,1,0:T(8,128)(2,1)}), bf16[8,1024,128]{2,1,0:T(8,128)(2,1)S(1)}, u32[]{:S(2)}, u32[]{:S(2)}) async-start(bf16[8,1024,128]{2,1,0:T(8,128)(2,1)} %convert_element_type.105), calls=%async_computation.6 | async-start | bytes 4194304 | tf_op jit(solution)/shard_map/all_to_all | solution.py:345
  166.1 53.6 %all-to-all-start.6 = ((bf16[8,128,2048]{2,1,0:T(8,128)(2,1)}), bf16[8,128,2048]{2,1,0:T(8,128)(2,1)}, u32[]{:S(2)}, u32[]{:S(2)}) async-start(bf16[8,128,2048]{2,1,0:T(8,128)(2,1)} %pad_maximum_fusion), calls=%async_computation.7 | async-start | bytes 8388608 | tf_op jit(solution)/shard_map/all_to_all | solution.py:345
  170.7 50.9 %all-gather.13.cloned.1.call-start = ((), (), s32[]{:S(2)}) async-start(), calls=%async_computation.24 | async-start | bytes 2621440 | tf_op jit(solution)/shard_map/all_gather | solution.py:348
  176.6 105.0 %reduce-scatter.7.cloned.1.call-start = ((), (), s32[]{:S(2)}) async-start(), calls=%async_computation.19 | async-start | bytes 2621440 | tf_op jit(solution)/shard_map/reduce_scatter | solution.py:352
  245.9 30.3 %all-to-all-start.7 = ((bf16[8,1024,128]{2,1,0:T(8,128)(2,1)}), bf16[8,1024,128]{2,1,0:T(8,128)(2,1)S(1)}, u32[]{:S(2)}, u32[]{:S(2)}) async-start(bf16[8,1024,128]{2,1,0:T(8,128)(2,1)} %convert_bitcast_fusion), calls=%async_computation.9 | async-start | bytes 4194304 | tf_op jit(solution)/shard_map/all_to_all | solution.py:345
  249.5 83.7 %all-gather.15.cloned.1.call-start = ((), (), s32[]{:S(2)}) async-start(), calls=%async_computation.25 | async-start | bytes 2621440 | tf_op jit(solution)/shard_map/all_gather | solution.py:348
  262.3 19.3 %copy-start.2 = (bf16[1,8,32,1024]{3,2,1,0:T(8,128)(2,1)S(1)}, bf16[1,8,32,1024]{3,2,1,0:T(8,128)(2,1)}, u32[]{:S(2)}) copy-start(bf16[1,8,32,1024]{3,2,1,0:T(8,128)(2,1)} %reduce-scatter.5.cloned.1.call-done) | copy-start | bytes 1572868
  290.7 42.5 %all-to-all-start.8 = ((bf16[8,128,1536]{2,1,0:T(8,128)(2,1)}), bf16[8,128,1536]{2,1,0:T(8,128)(2,1)}, u32[]{:S(2)}, u32[]{:S(2)}) async-start(bf16[8,128,1536]{2,1,0:T(8,128)(2,1)} %copy.115), calls=%async_computation.10 | async-start | bytes 6291456 | tf_op jit(solution)/shard_map/all_to_all | solution.py:345
  295.3 103.3 %reduce-scatter.9.cloned.1.call-start = ((), (), s32[]{:S(2)}) async-start(), calls=%async_computation.20 | async-start | bytes 2621440 | tf_op jit(solution)/shard_map/reduce_scatter | solution.py:352
  350.0 18.9 %all-to-all-start.10 = ((bf16[8,128,512]{2,1,0:T(8,128)(2,1)}), bf16[8,128,512]{2,1,0:T(8,128)(2,1)S(1)}, u32[]{:S(2)}, u32[]{:S(2)}) async-start(bf16[8,128,512]{2,1,0:T(8,128)(2,1)} %copy.117), calls=%async_computation.12 | async-start | bytes 2097152 | tf_op jit(solution)/shard_map/all_to_all | solution.py:345
  353.6 88.6 %reduce-scatter.11.cloned.1.call-start = ((), (), s32[]{:S(2)}) async-start(), calls=%async_computation.21 | async-start | bytes 2621440 | tf_op jit(solution)/shard_map/reduce_scatter | solution.py:352
  368.9 24.5 %copy-start.8 = (bf16[8,128,512]{2,1,0:T(8,128)(2,1)}, bf16[8,128,512]{2,1,0:T(8,128)(2,1)S(1)}, u32[]{:S(2)}) copy-start(bf16[8,128,512]{2,1,0:T(8,128)(2,1)S(1)} %all-to-all-done.10) | copy-start | bytes 3145732
  411.0 31.1 %all-to-all-start.12 = ((bf16[8,128,1024]{1,2,0:T(8,128)(2,1)}), bf16[8,128,1024]{1,2,0:T(8,128)(2,1)}, u32[]{:S(2)}, u32[]{:S(2)}) async-start(bf16[8,128,1024]{1,2,0:T(8,128)(2,1)} %copy.121), calls=%async_computation.16 | async-start | bytes 4194304 | tf_op jit(solution)/shard_map/all_to_all | solution.py:345
  425.3 18.5 %copy-start.6 = (bf16[1,8,32,1024]{3,2,1,0:T(8,128)(2,1)S(1)}, bf16[1,8,32,1024]{3,2,1,0:T(8,128)(2,1)}, u32[]{:S(2)}) copy-start(bf16[1,8,32,1024]{3,2,1,0:T(8,128)(2,1)} %reduce-scatter.7.cloned.1.call-done) | copy-start | bytes 1572868
  445.7 13.1 %collective-permute-start = (f32[3,1024]{1,0:T(4,128)S(1)}, f32[3,1024]{1,0:T(4,128)S(1)}, u32[]{:S(2)}, u32[]{:S(2)}) collective-permute-start(f32[3,1024]{1,0:T(4,128)S(1)} %pad_maximum_fusion.6), channel_id=1, source_target_pairs={{0,1},{1,2},{2,3},{3,0},{4,5},{5,6},{6,7},{7,4},{8,9},{9,10},{10,1... | collective-permute-start | bytes 36872 | tf_op jit(solution)/shard_map/ppermute | solution.py:484
  446.4 12.4 %collective-permute-start.1 = (f32[3,1024]{1,0:T(4,128)S(1)}, f32[3,1024]{1,0:T(4,128)S(1)}, u32[]{:S(2)}, u32[]{:S(2)}) collective-permute-start(f32[3,1024]{1,0:T(4,128)S(1)} %pad_maximum_fusion.6), channel_id=1, source_target_pairs={{0,2},{1,3},{2,0},{3,1},{4,6},{5,7},{6,4},{7,5},{8,10},{9,11},{10,... | collective-permute-start | bytes 36872 | tf_op jit(solution)/shard_map/ppermute | solution.py:484
  448.1 10.7 %collective-permute-start.2 = (f32[3,1024]{1,0:T(4,128)S(1)}, f32[3,1024]{1,0:T(4,128)S(1)}, u32[]{:S(2)}, u32[]{:S(2)}) collective-permute-start(f32[3,1024]{1,0:T(4,128)S(1)} %pad_maximum_fusion.6), channel_id=1, source_target_pairs={{0,3},{1,0},{2,1},{3,2},{4,7},{5,4},{6,5},{7,6},{8,11},{9,8},{10,9... | collective-permute-start | bytes 36872 | tf_op jit(solution)/shard_map/ppermute | solution.py:484
  455.2 24.1 %all-to-all-start.13 = ((bf16[8,64,1024]{2,1,0:T(8,128)(2,1)}), bf16[8,64,1024]{2,1,0:T(8,128)(2,1)S(1)}, u32[]{:S(2)}, u32[]{:S(2)}) async-start(bf16[8,64,1024]{2,1,0:T(8,128)(2,1)} %pad_maximum_fusion.4), calls=%async_computation.17 | async-start | bytes 2097152 | tf_op jit(solution)/shard_map/all_to_all | solution.py:345
  458.9 7.5 %collective-permute-start.3 = (f32[3,128]{1,0:T(4,128)S(1)}, f32[3,128]{1,0:T(4,128)S(1)}, u32[]{:S(2)}, u32[]{:S(2)}) collective-permute-start(f32[3,128]{1,0:T(4,128)S(1)} %get-tuple-element.137), channel_id=1, source_target_pairs={{0,4},{4,0},{8,12},{12,8},{16,20},{20,16},{24,28},{28,24},{1,5},{5... | collective-permute-start | bytes 4616 | tf_op jit(solution)/shard_map/ppermute | solution.py:489
  459.3 13.9 %collective-permute-start.4 = (f32[3,128]{1,0:T(4,128)S(1)}, f32[3,128]{1,0:T(4,128)S(1)}, u32[]{:S(2)}, u32[]{:S(2)}) collective-permute-start(f32[3,128]{1,0:T(4,128)S(1)} %get-tuple-element.143), channel_id=1, source_target_pairs={{0,8},{4,12},{8,0},{12,4},{16,24},{20,28},{24,16},{28,20},{1,9},{5... | collective-permute-start | bytes 4616 | tf_op jit(solution)/shard_map/ppermute | solution.py:489
  464.5 14.8 %collective-permute-start.5 = (f32[3,128]{1,0:T(4,128)S(1)}, f32[3,128]{1,0:T(4,128)S(1)}, u32[]{:S(2)}, u32[]{:S(2)}) collective-permute-start(f32[3,128]{1,0:T(4,128)S(1)} %get-tuple-element.142), channel_id=1, source_target_pairs={{0,12},{4,8},{8,4},{12,0},{16,28},{20,24},{24,20},{28,16},{1,13},{... | collective-permute-start | bytes 4616 | tf_op jit(solution)/shard_map/ppermute | solution.py:489
  464.5 14.8 %collective-permute-start.6 = (f32[3,128]{1,0:T(4,128)S(1)}, f32[3,128]{1,0:T(4,128)S(1)}, u32[]{:S(2)}, u32[]{:S(2)}) collective-permute-start(f32[3,128]{1,0:T(4,128)S(1)} %get-tuple-element.141), channel_id=1, source_target_pairs={{0,16},{4,20},{8,24},{12,28},{16,0},{20,4},{24,8},{28,12},{1,17},{... | collective-permute-start | bytes 4616 | tf_op jit(solution)/shard_map/ppermute | solution.py:489
  466.2 13.0 %collective-permute-start.7 = (f32[3,128]{1,0:T(4,128)S(1)}, f32[3,128]{1,0:T(4,128)S(1)}, u32[]{:S(2)}, u32[]{:S(2)}) collective-permute-start(f32[3,128]{1,0:T(4,128)S(1)} %get-tuple-element.140), channel_id=1, source_target_pairs={{0,20},{4,16},{8,28},{12,24},{16,4},{20,0},{24,12},{28,8},{1,21},{... | collective-permute-start | bytes 4616 | tf_op jit(solution)/shard_map/ppermute | solution.py:489
  466.3 12.9 %collective-permute-start.8 = (f32[3,128]{1,0:T(4,128)S(1)}, f32[3,128]{1,0:T(4,128)S(1)}, u32[]{:S(2)}, u32[]{:S(2)}) collective-permute-start(f32[3,128]{1,0:T(4,128)S(1)} %get-tuple-element.139), channel_id=1, source_target_pairs={{0,24},{4,28},{8,16},{12,20},{16,8},{20,12},{24,0},{28,4},{1,25},{... | collective-permute-start | bytes 4616 | tf_op jit(solution)/shard_map/ppermute | solution.py:489
  473.2 6.0 %collective-permute-start.9 = (f32[3,128]{1,0:T(4,128)S(1)}, f32[3,128]{1,0:T(4,128)S(1)}, u32[]{:S(2)}, u32[]{:S(2)}) collective-permute-start(f32[3,128]{1,0:T(4,128)S(1)} %get-tuple-element.138), channel_id=1, source_target_pairs={{0,28},{4,24},{8,20},{12,16},{16,12},{20,8},{24,4},{28,0},{1,29},{... | collective-permute-start | bytes 4616 | tf_op jit(solution)/shard_map/ppermute | solution.py:489
  (17 other events, 73.2 us)
Sparse Core Ops, SparseCore 0:
  30.7 45.0 all-gather.8
  77.3 44.4 all-gather.10
  130.9 41.9 reduce-scatter.4
  176.7 44.8 all-gather.12
  239.1 42.4 reduce-scatter.6
  286.0 44.8 all-gather.14
  333.7 42.4 reduce-scatter.8
  398.8 41.1 reduce-scatter.10

commit v10 on v9

--- a/solution.py
+++ b/solution.py
@@ -373,19 +373,17 @@
         steps, local, width = layer_in.shape
         block = width // count
 
-        def tile(line):
-            pads = [(0, 0)] * (line.ndim - 1) + [(0, TILE - 1), (0, width - line.shape[-1])]
-            return jnp.pad(line[..., None, :], pads)
-
-        small = jnp.concatenate([norm_gains, pad_row[None]], axis=0).astype(BF).reshape(-1)
-        line = jnp.concatenate([small, text_mask.astype(BF)])
-        notes = jnp.broadcast_to(tile(line)[None], (count, TILE, width))
-        hello = exchange(jnp.concatenate([layer_in, notes], axis=1))
-        rows_in = hello[:, :local].astype(F32)
-        notes = hello[:, local].astype(F32)
-        small = jnp.swapaxes(notes[:, : 3 * block].reshape(count, 3, block), 0, 1)
+        small = jnp.concatenate([norm_gains, pad_row[None]], axis=0).astype(BF)
+        mask = jnp.pad(text_mask.astype(BF)[None], ((0, 0), (0, block - local)))
+        notes = jnp.concatenate([small, mask])
+        notes = jnp.pad(notes, ((0, local - notes.shape[0]), (0, 0)))
+        notes = jnp.broadcast_to(notes[None], (count, local, block))
+        hello = exchange(jnp.concatenate([layer_in, notes], axis=2))
+        rows_in = hello[..., :width].astype(F32)
+        notes = hello[:, :4, width:].astype(F32)
+        small = jnp.swapaxes(notes[:, :3], 0, 1)
         gain_one, gain_two, pad_vec = small.reshape(3, width)
-        padded = jnp.where(me == 0, 1.0 - notes[:, 3 * block : 3 * block + local], 0.0)[..., None]
+        padded = jnp.where(me == 0, 1.0 - notes[:, 3, :local], 0.0)[..., None]
         h0 = rows_in + padded * pad_vec
         r1 = lax.rsqrt(jnp.mean(h0 * h0, axis=-1, keepdims=True) + EPS)
         n1 = (h0 * r1 * gain_one).astype(BF)
@@ -465,23 +463,29 @@
             ],
             axis=1,
         )
-        g_attn = exchange(rowwise(d_attn.reshape(count, block, -1)))
+        g_attn = exchange(d_attn.reshape(count, block, -1))
         layer_out = (h1 + ffout.astype(F32)).astype(BF)
-        dn1, g_attn, layer_out = after(dn1, g_attn, layer_out)
-        g_down, g_attn = g_down.astype(F32), g_attn.astype(F32)
-        g_qkv = jnp.stack([g_attn[..., j * cols : (j + 1) * cols] for j in range(3)], axis=1)
-        g_out = jnp.swapaxes(g_attn[..., 3 * cols :], 1, 2)
-
-        dh_norm1, dgain_one = norm_back(dn1.astype(F32), h0, r1, gain_one)
+        g_down = g_down.astype(F32)
+        dn1, g_attn, layer_out, g_gate_up, g_down = after(
+            dn1, g_attn, layer_out, g_gate_up, g_down
+        )
+
+        dh_norm1, _ = norm_back(dn1.astype(F32), h0, r1, gain_one)
         dh0 = dh1 + dh_norm1
+        last = jnp.concatenate([dh0.astype(BF), layer_out], axis=1)
+        last, dn1, dh0, g_attn = after(last, dn1, dh0, g_attn)
+        last = exchange(last)
+        dgain_one = jnp.sum(dn1.astype(F32) * h0 * r1, axis=(0, 1))
         d_pad = jnp.sum(dh0 * padded, axis=(0, 1))
         sums = jnp.stack([dgain_one, dgain_two, d_pad])
-        last = exchange(jnp.concatenate([dh0.astype(BF), layer_out], axis=1))
-
         total = sums
         for k in range(1, lanes):
             around = [(i, (i + k) % lanes) for i in range(lanes)]
             total = total + lax.ppermute(sums, "tensor", around)
+        total, g_attn = after(total, g_attn)
+        g_attn = g_attn.astype(F32)
+        g_qkv = jnp.stack([g_attn[..., j * cols : (j + 1) * cols] for j in range(3)], axis=1)
+        g_out = jnp.swapaxes(g_attn[..., 3 * cols :], 1, 2)
         total = jnp.swapaxes(total.reshape(3, count, block), 0, 1)
         g_small = lax.dynamic_index_in_dim(total, me, 0, keepdims=False)
         for k in range(1, count):
@@ -524,7 +528,7 @@
         steps, frames, width = layer_in.shape
         local = frames // (dp_size * tensor_size)
         block = width // dp_size
-        fits = 3 * block + local <= width
+        fits = 4 <= local <= block
         if steps == dp_size and dp_size & (dp_size - 1) == 0 and fits:
             body, over, dp = make_step_shards(dp_size, tensor_size), mesh, ("dp",)
         else:

time: 497 us -> 489 us (0.984)
    unnamed x49 -> x47, local copies, waits for them, and re-layouts: 12.9 us -> 12.9 us
  transfers between devices with their start and end apart: 26 -> 26, of which waited for: 12 -> 14; matrix products, arithmetic and copies ran while one was open for 19% -> 18% of each run, Pallas kernels for 5% -> 5%
where the time goes in v10:
time: 489 us; the launch traced here: 481 us
  waiting for transfers between devices  148 us (30%)
  blocking collectives  117 us (24%)
  starting transfers between devices  44.4 us (9%)
  local copies, waits for them, and re-layouts  41.8 us (9%)
  Pallas kernels  41.1 us (8%)
  other arithmetic  39.7 us (8%)
  matrix products  33.7 us (7%)
  between operations  15.1 us (3%)
    all_to_all x8, waiting for transfers between devices, exchange(): return lax.all_to_all(blocks, 'dp', 0, 0, tiled=True)  131 us
    all_to_all x6, blocking collectives, exchange(): return lax.all_to_all(blocks, 'dp', 0, 0, tiled=True)  117 us
    all_to_all x8, starting transfers between devices, exchange(): return lax.all_to_all(blocks, 'dp', 0, 0, tiled=True)  33 us
    pallas_call x2, Pallas kernels, attention_call(): pl.pallas_call(body, grid=(frames // span,), in_specs=[spec(a.shape[2]) f...  23.7 us
    pallas_call x1, Pallas kernels, feed_call(): pl.pallas_call(feed_body, grid=(count + width // part,), in_specs=[whole,...  17.4 us
    unnamed x47, local copies, waits for them, and re-layouts  12.9 us
  transfers between devices with their start and end apart: 26, of which 14 were waited for; matrix products, arithmetic and copies ran while one was open for 18% of the time, Pallas kernels for 5%

profile of v10, /device:TPU:0, one launch (start us, length us, event | category | flops | bytes accessed | tf_op | source)
XLA Modules:
  0.0 481.1 jit_solution(1015615113762158412)
XLA Ops:
  11.2 5.2 %all-to-all-start = ((bf16[8,32,1152]{2,1,0:T(8,128)(2,1)}), bf16[8,32,1152]{2,1,0:T(8,128)(2,1)S(1)}, u32[]{:S(2)}, u32[]{:S(2)}) async-start(bf16[8,32,1152]{2,1,0:T(8,128)(2,1)} %pad_maximum_fusion.5), calls=%async_computation | async-start | bytes 1179648 | tf_op jit(solution)/shard_map/all_to_all | solution.py:345
  16.5 10.4 %all-to-all-done = bf16[8,32,1152]{2,1,0:T(8,128)(2,1)S(1)} async-done(((bf16[8,32,1152]{2,1,0:T(8,128)(2,1)}), bf16[8,32,1152]{2,1,0:T(8,128)(2,1)S(1)}, u32[]{:S(2)}, u32[]{:S(2)}) %all-to-all-start) | async-done | bytes 589856 | tf_op jit(solution)/shard_map/all_to_all | solution.py:345
  30.9 29.1 %all_to_all.70 = bf16[8,128,1024]{2,1,0:T(8,128)(2,1)S(1)} all-to-all(bf16[8,128,1024]{2,1,0:T(8,128)(2,1)S(1)} %pad_maximum_fusion.2), channel_id=1, replica_groups=mesh['dp'=8,'tensor'=4] {'dp'}, dimensions={0} | all-to-all | bytes 4194304 | tf_op jit(solution)/shard_map/all_to_all | solution.py:345
  60.1 12.8 %all_to_all.71 = bf16[8,32,1024]{2,1,0:T(8,128)(2,1)} all-to-all(bf16[8,32,1024]{2,1,0:T(8,128)(2,1)S(1)} %copy-done.18), channel_id=1, replica_groups=mesh['dp'=8,'tensor'=4] {'dp'}, dimensions={0} | all-to-all | bytes 1048576 | tf_op jit(solution)/shard_map/all_to_all | solution.py:345
  77.1 24.5 %all_to_all.72.qkv_ref = bf16[8,128,768]{2,1,0:T(8,128)(2,1)} all-to-all(bf16[8,128,768]{2,1,0:T(8,128)(2,1)S(1)} %bitcast.156), channel_id=1, replica_groups=mesh['dp'=8,'tensor'=4] {'dp'}, dimensions={0} | all-to-all | bytes 3145728 | tf_op jit(solution)/shard_map/all_to_all | solution.py:345
  101.6 10.9 %shard_map.152 = bf16[8,128,256]{2,1,0:T(8,128)(2,1)} custom-call(bf16[8,128,768]{2,1,0:T(8,128)(2,1)} %all_to_all.72.qkv_ref), custom_call_target="tpu_custom_call" | custom-call | tf_op jit(solution)/shard_map/pallas_call | solution.py:272
  112.4 13.1 %all_to_all.73 = bf16[8,128,256]{2,1,0:T(8,128)(2,1)S(1)} all-to-all(bf16[8,128,256]{2,1,0:T(8,128)(2,1)} %shard_map.152), channel_id=1, replica_groups=mesh['dp'=8,'tensor'=4] {'dp'}, dimensions={0} | all-to-all | bytes 1048576 | tf_op jit(solution)/shard_map/all_to_all | solution.py:345
  128.5 3.8 convert_element_type.101
  132.3 3.6 all-to-all-start.5
  136.0 4.0 convert.34
  143.0 19.5 %all-to-all-done.5.wdown_ref = bf16[8,1024,128]{2,1,0:T(8,128)(2,1)S(1)} async-done(((bf16[8,1024,128]{2,1,0:T(8,128)(2,1)}), bf16[8,1024,128]{2,1,0:T(8,128)(2,1)S(1)}, u32[]{:S(2)}, u32[]{:S(2)}) %all-to-all-start.5) | async-done | bytes 2097184 | tf_op jit(solution)/shard_map/all_to_all | solution.py:345
  163.8 4.6 all-to-all-start.6
  174.5 43.0 %all-to-all-done.6 = bf16[8,128,2048]{2,1,0:T(8,128)(2,1)} async-done(((bf16[8,128,2048]{2,1,0:T(8,128)(2,1)}), bf16[8,128,2048]{2,1,0:T(8,128)(2,1)}, u32[]{:S(2)}, u32[]{:S(2)}) %all-to-all-start.6) | async-done | bytes 4194336 | tf_op jit(solution)/shard_map/all_to_all | solution.py:345
  219.3 17.4 %shard_map.153 = (bf16[1024,1024]{1,0:T(8,128)(2,1)}, bf16[1024,1024]{1,0:T(8,128)(2,1)}, bf16[1024,1024]{1,0:T(8,128)(2,1)}, bf16[1024,1024]{1,0:T(8,128)(2,1)}) custom-call(bf16[1024,1024]{1,0:T(8,128)(2,1)} %bitcast.171, bf16[1024,1024]{1,0:T(8,128)(2,1)} %bitcast.169, bf16[1024,2048]{1,0:T(8,128)(2,1)} %bitcast.25.wgate_ref.wup_ref.wrow_ref, ...), custom_call_target="tpu_custom_call" | custom-call | tf_op jit(solution)/shard_map/pallas_call | solution.py:324
  238.3 5.3 %convert_bitcast_fusion = bf16[8,1024,128]{2,1,0:T(8,128)(2,1)} fusion(bf16[1024,1024]{1,0:T(8,128)(2,1)} %get-tuple-element.94, bf16[1024,1024]{1,0:T(8,128)(2,1)S(1)} %bitcast.170), kind=kOutput, calls=%fused_computation.15 | convolution fusion | flops 2148532224 | bytes 6291456 | tf_op jit(solution)/shard_map/fk,frd->rkd/dot_general | solution.py:425
  243.6 3.6 all-to-all-start.7
  247.5 4.7 convolution_convert_fusion.1
  261.3 12.6 %all-to-all-done.7 = bf16[8,1024,128]{2,1,0:T(8,128)(2,1)S(1)} async-done(((bf16[8,1024,128]{2,1,0:T(8,128)(2,1)}), bf16[8,1024,128]{2,1,0:T(8,128)(2,1)S(1)}, u32[]{:S(2)}, u32[]{:S(2)}) %all-to-all-start.7) | async-done | bytes 2097184 | tf_op jit(solution)/shard_map/all_to_all | solution.py:345
  273.8 5.5 %reduce-scatter.7.cloned.1.call-done = bf16[1,8,32,1024]{3,2,1,0:T(8,128)(2,1)} async-done(((bf16[4,8,32,1024]{3,2,1,0:T(8,128)(2,1)}), bf16[1,8,32,1024]{3,2,1,0:T(8,128)(2,1)}) %reduce-scatter.7.cloned.1.call-update) | async-done | bytes 524304 | tf_op jit(solution)/shard_map/reduce_scatter | solution.py:352
  283.5 4.9 %copy.53 = bf16[8,128,1536]{2,1,0:T(8,128)(2,1)} copy(bf16[8,128,1536]{1,0,2:T(8,128)(2,1)} %bitcast.153) | data formatting | bytes 6291456 | tf_op jit(solution)/shard_map/optimization_barrier | solution.py:367
  288.4 4.6 all-to-all-start.8
  295.7 5.9 %convolution_convert_fusion = bf16[1024,1024]{1,0:T(8,128)(2,1)} fusion(bf16[1024,1024]{1,0:T(8,128)(2,1)} %get-tuple-element.94, bf16[1024,1024]{0,1:T(8,128)(2,1)} %bitcast.177), kind=kOutput, calls=%fused_computation.16 | convolution fusion | flops 2148532224 | bytes 6291456 | tf_op jit(solution)/shard_map/dot_general | solution.py:446
  301.7 29.2 %all-to-all-done.8 = bf16[8,128,1536]{2,1,0:T(8,128)(2,1)} async-done(((bf16[8,128,1536]{2,1,0:T(8,128)(2,1)}), bf16[8,128,1536]{2,1,0:T(8,128)(2,1)}, u32[]{:S(2)}, u32[]{:S(2)}) %all-to-all-start.8) | async-done | bytes 3145760 | tf_op jit(solution)/shard_map/all_to_all | solution.py:345
  333.3 12.9 %all_to_all.74.grad_ref = bf16[8,128,256]{2,1,0:T(8,128)(2,1)} all-to-all(bf16[8,128,256]{2,1,0:T(8,128)(2,1)S(1)} %bitcast.179), channel_id=1, replica_groups=mesh['dp'=8,'tensor'=4] {'dp'}, dimensions={0} | all-to-all | bytes 1048576 | tf_op jit(solution)/shard_map/all_to_all | solution.py:345
  351.6 12.8 %shard_map.154 = bf16[8,128,768]{2,1,0:T(8,128)(2,1)} custom-call(bf16[8,128,768]{2,1,0:T(8,128)(2,1)} %all_to_all.72.qkv_ref, bf16[8,128,256]{2,1,0:T(8,128)(2,1)} %all_to_all.74.grad_ref), custom_call_target="tpu_custom_call" | custom-call | tf_op jit(solution)/shard_map/pallas_call | solution.py:272
  366.6 24.4 %all_to_all.75 = bf16[8,128,768]{2,1,0:T(8,128)(2,1)S(1)} all-to-all(bf16[8,128,768]{2,1,0:T(8,128)(2,1)} %shard_map.154), channel_id=1, replica_groups=mesh['dp'=8,'tensor'=4] {'dp'}, dimensions={0} | all-to-all | bytes 3145728 | tf_op jit(solution)/shard_map/all_to_all | solution.py:345
  404.8 3.9 copy.59
  412.3 3.9 convert_element_type.118
  419.7 3.9 maximum_convert_fusion
  424.8 14.1 %all-to-all-done.12 = bf16[8,128,1024]{1,2,0:T(8,128)(2,1)S(1)} async-done(((bf16[8,128,1024]{1,2,0:T(8,128)(2,1)}), bf16[8,128,1024]{1,2,0:T(8,128)(2,1)S(1)}, u32[]{:S(2)}, u32[]{:S(2)}) %all-to-all-start.12) | async-done | bytes 2097184 | tf_op jit(solution)/shard_map/all_to_all | solution.py:345
  447.8 4.3 all-to-all-start.13
  459.9 7.0 %collective-permute-done.9 = f32[3,128]{1,0:T(4,128)S(1)} collective-permute-done((f32[3,128]{1,0:T(4,128)S(1)}, f32[3,128]{1,0:T(4,128)S(1)}, u32[]{:S(2)}, u32[]{:S(2)}) %collective-permute-start.9) | collective-permute-done | bytes 1568 | tf_op jit(solution)/shard_map/ppermute | solution.py:493
  (154 shorter events, 100.4 us)
Async XLA Ops:
  9.2 19.1 %copy-start.17 = (f32[8,256,128]{2,1,0:T(8,128)S(1)}, f32[8,256,128]{2,1,0:T(8,128)}, u32[]{:S(2)}) copy-start(f32[8,256,128]{2,1,0:T(8,128)} %param.12) | copy-start | bytes 3145732
  11.2 15.6 %all-to-all-start = ((bf16[8,32,1152]{2,1,0:T(8,128)(2,1)}), bf16[8,32,1152]{2,1,0:T(8,128)(2,1)S(1)}, u32[]{:S(2)}, u32[]{:S(2)}) async-start(bf16[8,32,1152]{2,1,0:T(8,128)(2,1)} %pad_maximum_fusion.5), calls=%async_computation | async-start | bytes 1179648 | tf_op jit(solution)/shard_map/all_to_all | solution.py:345
  16.4 57.1 %all-gather.9.cloned.1.call-start = ((), (), s32[]{:S(2)}) async-start(), calls=%async_computation.22 | async-start | bytes 2621440 | tf_op jit(solution)/shard_map/all_gather | solution.py:348
  28.3 100.2 %all-gather.11.cloned.1.call-start = ((), (), s32[]{:S(2)}) async-start(), calls=%async_computation.23 | async-start | bytes 2621440 | tf_op jit(solution)/shard_map/all_gather | solution.py:348
  30.9 29.2 %copy-start.18 = (bf16[8,32,1024]{2,1,0:T(8,128)(2,1)S(1)}, bf16[8,32,1024]{2,1,0:T(8,128)(2,1)}, u32[]{:S(2)}) copy-start(bf16[8,32,1024]{2,1,0:T(8,128)(2,1)} %param.17) | copy-start | bytes 1572868
  60.1 65.5 %copy-start.8 = (bf16[8,128,1024]{2,1,0:T(8,128)(2,1)}, bf16[8,128,1024]{2,1,0:T(8,128)(2,1)S(1)}, u32[]{:S(2)}) copy-start(bf16[8,128,1024]{2,1,0:T(8,128)(2,1)S(1)} %all_to_all.70) | copy-start | bytes 6291460
  73.5 97.1 %reduce-scatter.5.cloned.1.call-start = ((), (), s32[]{:S(2)}) async-start(), calls=%async_computation.18 | async-start | bytes 2621440 | tf_op jit(solution)/shard_map/reduce_scatter | solution.py:352
  132.3 30.2 %all-to-all-start.5 = ((bf16[8,1024,128]{2,1,0:T(8,128)(2,1)}), bf16[8,1024,128]{2,1,0:T(8,128)(2,1)S(1)}, u32[]{:S(2)}, u32[]{:S(2)}) async-start(bf16[8,1024,128]{2,1,0:T(8,128)(2,1)} %convert_element_type.101), calls=%async_computation.6 | async-start | bytes 4194304 | tf_op jit(solution)/shard_map/all_to_all | solution.py:345
  163.8 53.7 %all-to-all-start.6 = ((bf16[8,128,2048]{2,1,0:T(8,128)(2,1)}), bf16[8,128,2048]{2,1,0:T(8,128)(2,1)}, u32[]{:S(2)}, u32[]{:S(2)}) async-start(bf16[8,128,2048]{2,1,0:T(8,128)(2,1)} %pad_maximum_fusion), calls=%async_computation.7 | async-start | bytes 8388608 | tf_op jit(solution)/shard_map/all_to_all | solution.py:345
  168.4 50.9 %all-gather.13.cloned.1.call-start = ((), (), s32[]{:S(2)}) async-start(), calls=%async_computation.24 | async-start | bytes 2621440 | tf_op jit(solution)/shard_map/all_gather | solution.py:348
  174.3 105.0 %reduce-scatter.7.cloned.1.call-start = ((), (), s32[]{:S(2)}) async-start(), calls=%async_computation.19 | async-start | bytes 2621440 | tf_op jit(solution)/shard_map/reduce_scatter | solution.py:352
  243.6 30.3 %all-to-all-start.7 = ((bf16[8,1024,128]{2,1,0:T(8,128)(2,1)}), bf16[8,1024,128]{2,1,0:T(8,128)(2,1)S(1)}, u32[]{:S(2)}, u32[]{:S(2)}) async-start(bf16[8,1024,128]{2,1,0:T(8,128)(2,1)} %convert_bitcast_fusion), calls=%async_computation.9 | async-start | bytes 4194304 | tf_op jit(solution)/shard_map/all_to_all | solution.py:345
  247.2 83.7 %all-gather.15.cloned.1.call-start = ((), (), s32[]{:S(2)}) async-start(), calls=%async_computation.25 | async-start | bytes 2621440 | tf_op jit(solution)/shard_map/all_gather | solution.py:348
  260.0 19.3 %copy-start.2 = (bf16[1,8,32,1024]{3,2,1,0:T(8,128)(2,1)S(1)}, bf16[1,8,32,1024]{3,2,1,0:T(8,128)(2,1)}, u32[]{:S(2)}) copy-start(bf16[1,8,32,1024]{3,2,1,0:T(8,128)(2,1)} %reduce-scatter.5.cloned.1.call-done) | copy-start | bytes 1572868
  288.4 42.5 %all-to-all-start.8 = ((bf16[8,128,1536]{2,1,0:T(8,128)(2,1)}), bf16[8,128,1536]{2,1,0:T(8,128)(2,1)}, u32[]{:S(2)}, u32[]{:S(2)}) async-start(bf16[8,128,1536]{2,1,0:T(8,128)(2,1)} %copy.53), calls=%async_computation.10 | async-start | bytes 6291456 | tf_op jit(solution)/shard_map/all_to_all | solution.py:345
  293.0 103.3 %reduce-scatter.9.cloned.1.call-start = ((), (), s32[]{:S(2)}) async-start(), calls=%async_computation.20 | async-start | bytes 2621440 | tf_op jit(solution)/shard_map/reduce_scatter | solution.py:352
  333.3 13.0 %copy-start.5 = (bf16[64,8,8,128]{3,2,1,0:T(8,128)(2,1)S(1)}, bf16[64,8,8,128]{3,2,1,0:T(8,128)(2,1)}, u32[]{:S(2)}) copy-start(bf16[64,8,8,128]{3,2,1,0:T(8,128)(2,1)} %copy.68) | copy-start | bytes 3145732
  347.7 18.9 %all-to-all-start.10 = ((bf16[8,128,512]{2,1,0:T(8,128)(2,1)}), bf16[8,128,512]{2,1,0:T(8,128)(2,1)S(1)}, u32[]{:S(2)}, u32[]{:S(2)}) async-start(bf16[8,128,512]{2,1,0:T(8,128)(2,1)} %copy.55), calls=%async_computation.12 | async-start | bytes 2097152 | tf_op jit(solution)/shard_map/all_to_all | solution.py:345
  351.3 87.6 %reduce-scatter.11.cloned.1.call-start = ((), (), s32[]{:S(2)}) async-start(), calls=%async_computation.21 | async-start | bytes 2621440 | tf_op jit(solution)/shard_map/reduce_scatter | solution.py:352
  366.6 24.5 %copy-start.6 = (bf16[8,128,512]{2,1,0:T(8,128)(2,1)}, bf16[8,128,512]{2,1,0:T(8,128)(2,1)S(1)}, u32[]{:S(2)}) copy-start(bf16[8,128,512]{2,1,0:T(8,128)(2,1)S(1)} %all-to-all-done.10) | copy-start | bytes 3145732
  408.7 30.2 %all-to-all-start.12 = ((bf16[8,128,1024]{1,2,0:T(8,128)(2,1)}), bf16[8,128,1024]{1,2,0:T(8,128)(2,1)S(1)}, u32[]{:S(2)}, u32[]{:S(2)}) async-start(bf16[8,128,1024]{1,2,0:T(8,128)(2,1)} %copy.59), calls=%async_computation.16 | async-start | bytes 4194304 | tf_op jit(solution)/shard_map/all_to_all | solution.py:345
  444.1 7.9 %collective-permute-start.2 = (f32[3,1024]{1,0:T(4,128)S(1)}, f32[3,1024]{1,0:T(4,128)S(1)}, u32[]{:S(2)}, u32[]{:S(2)}) collective-permute-start(f32[3,1024]{1,0:T(4,128)S(1)} %pad_maximum_fusion.6), channel_id=1, source_target_pairs={{0,3},{1,0},{2,1},{3,2},{4,7},{5,4},{6,5},{7,6},{8,11},{9,8},{10,9... | collective-permute-start | bytes 36872 | tf_op jit(solution)/shard_map/ppermute | solution.py:484
  445.9 6.1 %collective-permute-start.1 = (f32[3,1024]{1,0:T(4,128)S(1)}, f32[3,1024]{1,0:T(4,128)S(1)}, u32[]{:S(2)}, u32[]{:S(2)}) collective-permute-start(f32[3,1024]{1,0:T(4,128)S(1)} %pad_maximum_fusion.6), channel_id=1, source_target_pairs={{0,2},{1,3},{2,0},{3,1},{4,6},{5,7},{6,4},{7,5},{8,10},{9,11},{10,... | collective-permute-start | bytes 36872 | tf_op jit(solution)/shard_map/ppermute | solution.py:484
  446.2 5.8 %collective-permute-start = (f32[3,1024]{1,0:T(4,128)S(1)}, f32[3,1024]{1,0:T(4,128)S(1)}, u32[]{:S(2)}, u32[]{:S(2)}) collective-permute-start(f32[3,1024]{1,0:T(4,128)S(1)} %pad_maximum_fusion.6), channel_id=1, source_target_pairs={{0,1},{1,2},{2,3},{3,0},{4,5},{5,6},{6,7},{7,4},{8,9},{9,10},{10,1... | collective-permute-start | bytes 36872 | tf_op jit(solution)/shard_map/ppermute | solution.py:484
  447.8 22.7 %all-to-all-start.13 = ((bf16[8,64,1024]{2,1,0:T(8,128)(2,1)}), bf16[8,64,1024]{2,1,0:T(8,128)(2,1)}, u32[]{:S(2)}, u32[]{:S(2)}) async-start(bf16[8,64,1024]{2,1,0:T(8,128)(2,1)} %pad_maximum_fusion.4), calls=%async_computation.17 | async-start | bytes 2097152 | tf_op jit(solution)/shard_map/all_to_all | solution.py:345
  452.1 14.7 %collective-permute-start.9 = (f32[3,128]{1,0:T(4,128)S(1)}, f32[3,128]{1,0:T(4,128)S(1)}, u32[]{:S(2)}, u32[]{:S(2)}) collective-permute-start(f32[3,128]{1,0:T(4,128)S(1)} %get-tuple-element.138), channel_id=1, source_target_pairs={{0,28},{4,24},{8,20},{12,16},{16,12},{20,8},{24,4},{28,0},{1,29},{... | collective-permute-start | bytes 4616 | tf_op jit(solution)/shard_map/ppermute | solution.py:493
  454.7 12.8 %collective-permute-start.8 = (f32[3,128]{1,0:T(4,128)S(1)}, f32[3,128]{1,0:T(4,128)S(1)}, u32[]{:S(2)}, u32[]{:S(2)}) collective-permute-start(f32[3,128]{1,0:T(4,128)S(1)} %get-tuple-element.139), channel_id=1, source_target_pairs={{0,24},{4,28},{8,16},{12,20},{16,8},{20,12},{24,0},{28,4},{1,25},{... | collective-permute-start | bytes 4616 | tf_op jit(solution)/shard_map/ppermute | solution.py:493
  455.1 15.2 %collective-permute-start.7 = (f32[3,128]{1,0:T(4,128)S(1)}, f32[3,128]{1,0:T(4,128)S(1)}, u32[]{:S(2)}, u32[]{:S(2)}) collective-permute-start(f32[3,128]{1,0:T(4,128)S(1)} %get-tuple-element.140), channel_id=1, source_target_pairs={{0,20},{4,16},{8,28},{12,24},{16,4},{20,0},{24,12},{28,8},{1,21},{... | collective-permute-start | bytes 4616 | tf_op jit(solution)/shard_map/ppermute | solution.py:493
  456.5 13.8 %collective-permute-start.6 = (f32[3,128]{1,0:T(4,128)S(1)}, f32[3,128]{1,0:T(4,128)S(1)}, u32[]{:S(2)}, u32[]{:S(2)}) collective-permute-start(f32[3,128]{1,0:T(4,128)S(1)} %get-tuple-element.141), channel_id=1, source_target_pairs={{0,16},{4,20},{8,24},{12,28},{16,0},{20,4},{24,8},{28,12},{1,17},{... | collective-permute-start | bytes 4616 | tf_op jit(solution)/shard_map/ppermute | solution.py:493
  456.8 13.5 %collective-permute-start.5 = (f32[3,128]{1,0:T(4,128)S(1)}, f32[3,128]{1,0:T(4,128)S(1)}, u32[]{:S(2)}, u32[]{:S(2)}) collective-permute-start(f32[3,128]{1,0:T(4,128)S(1)} %get-tuple-element.142), channel_id=1, source_target_pairs={{0,12},{4,8},{8,4},{12,0},{16,28},{20,24},{24,20},{28,16},{1,13},{... | collective-permute-start | bytes 4616 | tf_op jit(solution)/shard_map/ppermute | solution.py:493
  466.8 3.6 collective-permute-start.4
  467.5 3.0 collective-permute-start.3
  (16 other events, 40.7 us)
Sparse Core Ops, SparseCore 0:
  28.4 45.0 all-gather.8
  75.0 44.4 all-gather.10
  128.6 41.9 reduce-scatter.4
  174.4 44.8 all-gather.12
  236.8 42.4 reduce-scatter.6
  283.7 44.8 all-gather.14
  331.4 42.4 reduce-scatter.8
  396.5 41.1 reduce-scatter.10

commit v11 on v10

--- a/solution.py
+++ b/solution.py
@@ -431,26 +431,22 @@
         g_down = exchange(rowwise(d_down.astype(BF)))
         g_gate = jnp.einsum("fd,fk->dk", n2_all, d_gate, preferred_element_type=F32).astype(BF)
         g_up = jnp.einsum("fd,fk->dk", n2_all, d_up, preferred_element_type=F32).astype(BF)
-        part = hid_width // 2
-        g_gate = jnp.concatenate([g_gate, g_up[:, :part]], axis=1).reshape(count, block, -1)
-        g_up = g_up[:, part:].reshape(count, block, -1)
-        dn2, g_down, g_gate, g_up = after(dn2, g_down, g_gate, g_up)
+        g_gate_up = rowwise(jnp.concatenate([g_gate, g_up], axis=1))
+        g_down, g_gate_up = after(g_down, g_gate_up)
+        wdown = jnp.swapaxes(wdown, 0, 1).reshape(-1, width)
+        ffout = jnp.dot(hidden, wdown, preferred_element_type=F32).astype(BF)
+        dn2, g_down, ffout = after(dn2, g_down, ffout)
+        g_gate_up = exchange(g_gate_up.reshape(count, block, -1))
         dh_norm2, dgain_two = norm_back(dn2.astype(F32), h1, r2, gain_two)
         dh1 = grad.astype(F32) + dh_norm2
-        dh1_low, g_gate, hidden = after(dh1.astype(BF), g_gate, hidden)
-        dh1_all = collect(dh1_low)
-        g_gate = exchange(g_gate)
-        dh1_all, g_gate = after(dh1_all, g_gate)
-
-        wdown = jnp.swapaxes(wdown, 0, 1).reshape(-1, width)
-        ffout = deal(jnp.dot(hidden, wdown, preferred_element_type=F32))
+        dh1_all = collect(dh1.astype(BF))
+        dh1_all, g_gate_up, ffout = after(dh1_all, g_gate_up, ffout)
+        ffout = deal(ffout)
         d_mixed = jnp.dot(dh1_all, wout_t, preferred_element_type=F32).astype(BF)
-        d_mixed, g_up = after(frame_split(d_mixed), g_up)
-        g_up = exchange(g_up)
+        d_mixed = frame_split(d_mixed)
         d_qkv = attention_call(attention_backward_body, (qkv, d_mixed), 3 * cols, 2 * TILE)
-        d_qkv, g_up = after(d_qkv, g_up)
-        g_up = jnp.concatenate([g_gate[..., hid_width:], g_up], axis=2)
-        g_gate_up = jnp.stack([g_gate[..., :hid_width], g_up], axis=1).astype(F32)
+        g_gate_up = jnp.stack([g_gate_up[..., :hid_width], g_gate_up[..., hid_width:]], axis=1)
+        g_gate_up = g_gate_up.astype(F32)
         d_qkv = frame_join(d_qkv)
         dn1 = jnp.einsum("fe,de->fd", d_qkv, w_in, preferred_element_type=F32).astype(BF)
 

time: 489 us -> 485 us (level)
  local copies, waits for them, and re-layouts: 41.8 us -> 32 us
  waiting for transfers between devices: 148 us -> 156 us
    all_to_all x8 -> x7, waiting for transfers between devices: 131 us -> 145 us  [exchange(): return lax.all_to_all(blocks, 'dp', 0, 0, tiled=True)]
    optimization_barrier x3 -> x1, local copies, waits for them, and re-layouts: 6.55 us -> 0.2 us  [after(): return lax.optimization_barrier((value,) + waiting)]
    reduce_scatter x4, waiting for transfers between devices: 7.67 us -> 2.21 us  [deal(): return lax.psum_scatter(slots, 'tensor', scatter_dimension=0)]
    unnamed x47 -> x42, local copies, waits for them, and re-layouts: 12.9 us -> 8.88 us
    all_to_all x8 -> x7, starting transfers between devices: 33 us -> 29.9 us  [exchange(): return lax.all_to_all(blocks, 'dp', 0, 0, tiled=True)]
  transfers between devices with their start and end apart: 26 -> 25, of which waited for: 14 -> 11; matrix products, arithmetic and copies ran while one was open for 18% -> 18% of each run, Pallas kernels for 5% -> 5%
where the time goes in v11:
time: 485 us; the launch traced here: 477 us
  waiting for transfers between devices  156 us (32%)
  blocking collectives  117 us (24%)
  other arithmetic  42.7 us (9%)
  Pallas kernels  41 us (8%)
  starting transfers between devices  40 us (8%)
  matrix products  32.6 us (7%)
  local copies, waits for them, and re-layouts  32 us (7%)
  between operations  15.1 us (3%)
    all_to_all x7, waiting for transfers between devices, exchange(): return lax.all_to_all(blocks, 'dp', 0, 0, tiled=True)  145 us
    all_to_all x6, blocking collectives, exchange(): return lax.all_to_all(blocks, 'dp', 0, 0, tiled=True)  117 us
    all_to_all x7, starting transfers between devices, exchange(): return lax.all_to_all(blocks, 'dp', 0, 0, tiled=True)  29.9 us
    pallas_call x2, Pallas kernels, attention_call(): pl.pallas_call(body, grid=(frames // span,), in_specs=[spec(a.shape[2]) f...  23.7 us
    pallas_call x1, Pallas kernels, feed_call(): pl.pallas_call(feed_body, grid=(count + width // part,), in_specs=[whole,...  17.4 us
  transfers between devices with their start and end apart: 25, of which 11 were waited for; matrix products, arithmetic and copies ran while one was open for 18% of the time, Pallas kernels for 5%

profile of v11, /device:TPU:0, one launch (start us, length us, event | category | flops | bytes accessed | tf_op | source)
XLA Modules:
  0.0 477.0 jit_solution(15166215980263308861)
XLA Ops:
  11.2 5.2 %all-to-all-start = ((bf16[8,32,1152]{2,1,0:T(8,128)(2,1)}), bf16[8,32,1152]{2,1,0:T(8,128)(2,1)S(1)}, u32[]{:S(2)}, u32[]{:S(2)}) async-start(bf16[8,32,1152]{2,1,0:T(8,128)(2,1)} %pad_maximum_fusion.6), calls=%async_computation | async-start | bytes 1179648 | tf_op jit(solution)/shard_map/all_to_all | solution.py:345
  16.5 10.4 %all-to-all-done = bf16[8,32,1152]{2,1,0:T(8,128)(2,1)S(1)} async-done(((bf16[8,32,1152]{2,1,0:T(8,128)(2,1)}), bf16[8,32,1152]{2,1,0:T(8,128)(2,1)S(1)}, u32[]{:S(2)}, u32[]{:S(2)}) %all-to-all-start) | async-done | bytes 589856 | tf_op jit(solution)/shard_map/all_to_all | solution.py:345
  30.9 29.1 %all_to_all.65 = bf16[8,128,1024]{2,1,0:T(8,128)(2,1)S(1)} all-to-all(bf16[8,128,1024]{2,1,0:T(8,128)(2,1)S(1)} %pad_maximum_fusion.3), channel_id=1, replica_groups=mesh['dp'=8,'tensor'=4] {'dp'}, dimensions={0} | all-to-all | bytes 4194304 | tf_op jit(solution)/shard_map/all_to_all | solution.py:345
  60.1 12.8 %all_to_all.66 = bf16[8,32,1024]{2,1,0:T(8,128)(2,1)} all-to-all(bf16[8,32,1024]{2,1,0:T(8,128)(2,1)S(1)} %copy-done.16), channel_id=1, replica_groups=mesh['dp'=8,'tensor'=4] {'dp'}, dimensions={0} | all-to-all | bytes 1048576 | tf_op jit(solution)/shard_map/all_to_all | solution.py:345
  77.1 24.5 %all_to_all.67.qkv_ref = bf16[8,128,768]{2,1,0:T(8,128)(2,1)} all-to-all(bf16[8,128,768]{2,1,0:T(8,128)(2,1)S(1)} %bitcast.147), channel_id=1, replica_groups=mesh['dp'=8,'tensor'=4] {'dp'}, dimensions={0} | all-to-all | bytes 3145728 | tf_op jit(solution)/shard_map/all_to_all | solution.py:345
  101.6 10.9 %shard_map.152 = bf16[8,128,256]{2,1,0:T(8,128)(2,1)} custom-call(bf16[8,128,768]{2,1,0:T(8,128)(2,1)} %all_to_all.67.qkv_ref), custom_call_target="tpu_custom_call" | custom-call | tf_op jit(solution)/shard_map/pallas_call | solution.py:272
  112.4 13.1 %all_to_all.68 = bf16[8,128,256]{2,1,0:T(8,128)(2,1)S(1)} all-to-all(bf16[8,128,256]{2,1,0:T(8,128)(2,1)} %shard_map.152), channel_id=1, replica_groups=mesh['dp'=8,'tensor'=4] {'dp'}, dimensions={0} | all-to-all | bytes 1048576 | tf_op jit(solution)/shard_map/all_to_all | solution.py:345
  128.5 3.8 convert_element_type.101
  132.3 3.6 all-to-all-start.5
  136.0 4.0 convert.34
  143.0 19.5 %all-to-all-done.5.wdown_ref = bf16[8,1024,128]{2,1,0:T(8,128)(2,1)S(1)} async-done(((bf16[8,1024,128]{2,1,0:T(8,128)(2,1)}), bf16[8,1024,128]{2,1,0:T(8,128)(2,1)S(1)}, u32[]{:S(2)}, u32[]{:S(2)}) %all-to-all-start.5) | async-done | bytes 2097184 | tf_op jit(solution)/shard_map/all_to_all | solution.py:345
  163.8 4.6 all-to-all-start.6
  174.5 43.0 %all-to-all-done.6 = bf16[8,128,2048]{2,1,0:T(8,128)(2,1)} async-done(((bf16[8,128,2048]{2,1,0:T(8,128)(2,1)}), bf16[8,128,2048]{2,1,0:T(8,128)(2,1)}, u32[]{:S(2)}, u32[]{:S(2)}) %all-to-all-start.6) | async-done | bytes 4194336 | tf_op jit(solution)/shard_map/all_to_all | solution.py:345
  219.3 17.4 %shard_map.153 = (bf16[1024,1024]{1,0:T(8,128)(2,1)}, bf16[1024,1024]{1,0:T(8,128)(2,1)}, bf16[1024,1024]{1,0:T(8,128)(2,1)}, bf16[1024,1024]{1,0:T(8,128)(2,1)}) custom-call(bf16[1024,1024]{1,0:T(8,128)(2,1)} %bitcast.161, bf16[1024,1024]{1,0:T(8,128)(2,1)} %bitcast.159, bf16[1024,2048]{1,0:T(8,128)(2,1)} %bitcast.25.wgate_ref.wup_ref.wrow_ref, ...), custom_call_target="tpu_custom_call" | custom-call | tf_op jit(solution)/shard_map/pallas_call | solution.py:324
  240.8 6.3 %convert_bitcast_fusion = bf16[8,1024,128]{2,1,0:T(8,128)(2,1)} fusion(bf16[1024,1024]{1,0:T(8,128)(2,1)} %get-tuple-element.77, bf16[1024,1024]{1,0:T(8,128)(2,1)} %bitcast.160), kind=kOutput, calls=%fused_computation.15 | convolution fusion | flops 2148532224 | bytes 6291456 | tf_op jit(solution)/shard_map/fk,frd->rkd/dot_general | solution.py:425
  247.1 4.0 all-to-all-start.7
  251.1 4.8 convolution_convert_fusion.1
  262.1 3.7 convolution_convert_fusion
  265.8 11.9 %all-to-all-done.7 = bf16[8,1024,128]{2,1,0:T(8,128)(2,1)S(1)} async-done(((bf16[8,1024,128]{2,1,0:T(8,128)(2,1)}), bf16[8,1024,128]{2,1,0:T(8,128)(2,1)S(1)}, u32[]{:S(2)}, u32[]{:S(2)}) %all-to-all-start.7) | async-done | bytes 2097184 | tf_op jit(solution)/shard_map/all_to_all | solution.py:345
  279.0 4.7 all-to-all-start.8
  287.9 44.9 %all-to-all-done.8 = bf16[8,128,2048]{2,1,0:T(8,128)(2,1)} async-done(((bf16[8,128,2048]{2,1,0:T(8,128)(2,1)}), bf16[8,128,2048]{2,1,0:T(8,128)(2,1)}, u32[]{:S(2)}, u32[]{:S(2)}) %all-to-all-start.8) | async-done | bytes 4194336 | tf_op jit(solution)/shard_map/all_to_all | solution.py:345
  335.2 13.0 %all_to_all.69.grad_ref = bf16[8,128,256]{2,1,0:T(8,128)(2,1)} all-to-all(bf16[8,128,256]{2,1,0:T(8,128)(2,1)S(1)} %bitcast.169), channel_id=1, replica_groups=mesh['dp'=8,'tensor'=4] {'dp'}, dimensions={0} | all-to-all | bytes 1048576 | tf_op jit(solution)/shard_map/all_to_all | solution.py:345
  348.2 12.8 %shard_map.154 = bf16[8,128,768]{2,1,0:T(8,128)(2,1)} custom-call(bf16[8,128,768]{2,1,0:T(8,128)(2,1)} %all_to_all.67.qkv_ref, bf16[8,128,256]{2,1,0:T(8,128)(2,1)} %all_to_all.69.grad_ref), custom_call_target="tpu_custom_call" | custom-call | tf_op jit(solution)/shard_map/pallas_call | solution.py:272
  361.0 24.7 %all_to_all.70 = bf16[8,128,768]{2,1,0:T(8,128)(2,1)S(1)} all-to-all(bf16[8,128,768]{2,1,0:T(8,128)(2,1)} %shard_map.154), channel_id=1, replica_groups=mesh['dp'=8,'tensor'=4] {'dp'}, dimensions={0} | all-to-all | bytes 3145728 | tf_op jit(solution)/shard_map/all_to_all | solution.py:345
  398.9 3.9 copy.56
  402.8 3.6 all-to-all-start.11
  406.4 3.9 convert_element_type.118
  413.0 3.9 maximum_convert_fusion
  418.1 14.9 %all-to-all-done.11 = bf16[8,128,1024]{1,2,0:T(8,128)(2,1)S(1)} async-done(((bf16[8,128,1024]{1,2,0:T(8,128)(2,1)}), bf16[8,128,1024]{1,2,0:T(8,128)(2,1)S(1)}, u32[]{:S(2)}, u32[]{:S(2)}) %all-to-all-start.11) | async-done | bytes 2097184 | tf_op jit(solution)/shard_map/all_to_all | solution.py:345
  441.1 4.2 all-to-all-start.12
  453.2 7.0 %collective-permute-done.9 = f32[3,128]{1,0:T(4,128)S(1)} collective-permute-done((f32[3,128]{1,0:T(4,128)S(1)}, f32[3,128]{1,0:T(4,128)S(1)}, u32[]{:S(2)}, u32[]{:S(2)}) %collective-permute-start.9) | collective-permute-done | bytes 1568 | tf_op jit(solution)/shard_map/ppermute | solution.py:489
  462.8 3.5 copy.58
  (143 shorter events, 84.4 us)
Async XLA Ops:
  9.2 19.1 %copy-start.15 = (f32[8,256,128]{2,1,0:T(8,128)S(1)}, f32[8,256,128]{2,1,0:T(8,128)}, u32[]{:S(2)}) copy-start(f32[8,256,128]{2,1,0:T(8,128)} %param.12) | copy-start | bytes 3145732
  11.2 15.6 %all-to-all-start = ((bf16[8,32,1152]{2,1,0:T(8,128)(2,1)}), bf16[8,32,1152]{2,1,0:T(8,128)(2,1)S(1)}, u32[]{:S(2)}, u32[]{:S(2)}) async-start(bf16[8,32,1152]{2,1,0:T(8,128)(2,1)} %pad_maximum_fusion.6), calls=%async_computation | async-start | bytes 1179648 | tf_op jit(solution)/shard_map/all_to_all | solution.py:345
  16.4 57.1 %all-gather.9.cloned.1.call-start = ((), (), s32[]{:S(2)}) async-start(), calls=%async_computation.21 | async-start | bytes 2621440 | tf_op jit(solution)/shard_map/all_gather | solution.py:348
  28.3 100.2 %all-gather.11.cloned.1.call-start = ((), (), s32[]{:S(2)}) async-start(), calls=%async_computation.22 | async-start | bytes 2621440 | tf_op jit(solution)/shard_map/all_gather | solution.py:348
  30.9 29.2 %copy-start.16 = (bf16[8,32,1024]{2,1,0:T(8,128)(2,1)S(1)}, bf16[8,32,1024]{2,1,0:T(8,128)(2,1)}, u32[]{:S(2)}) copy-start(bf16[8,32,1024]{2,1,0:T(8,128)(2,1)} %param.17) | copy-start | bytes 1572868
  60.1 65.5 %copy-start.6 = (bf16[8,128,1024]{2,1,0:T(8,128)(2,1)}, bf16[8,128,1024]{2,1,0:T(8,128)(2,1)S(1)}, u32[]{:S(2)}) copy-start(bf16[8,128,1024]{2,1,0:T(8,128)(2,1)S(1)} %all_to_all.65) | copy-start | bytes 6291460
  73.5 97.1 %reduce-scatter.5.cloned.1.call-start = ((), (), s32[]{:S(2)}) async-start(), calls=%async_computation.17 | async-start | bytes 2621440 | tf_op jit(solution)/shard_map/reduce_scatter | solution.py:352
  132.3 30.2 %all-to-all-start.5 = ((bf16[8,1024,128]{2,1,0:T(8,128)(2,1)}), bf16[8,1024,128]{2,1,0:T(8,128)(2,1)S(1)}, u32[]{:S(2)}, u32[]{:S(2)}) async-start(bf16[8,1024,128]{2,1,0:T(8,128)(2,1)} %convert_element_type.101), calls=%async_computation.6 | async-start | bytes 4194304 | tf_op jit(solution)/shard_map/all_to_all | solution.py:345
  163.8 53.7 %all-to-all-start.6 = ((bf16[8,128,2048]{2,1,0:T(8,128)(2,1)}), bf16[8,128,2048]{2,1,0:T(8,128)(2,1)}, u32[]{:S(2)}, u32[]{:S(2)}) async-start(bf16[8,128,2048]{2,1,0:T(8,128)(2,1)} %pad_maximum_fusion), calls=%async_computation.7 | async-start | bytes 8388608 | tf_op jit(solution)/shard_map/all_to_all | solution.py:345
  168.4 50.9 %all-gather.13.cloned.1.call-start = ((), (), s32[]{:S(2)}) async-start(), calls=%async_computation.23 | async-start | bytes 2621440 | tf_op jit(solution)/shard_map/all_gather | solution.py:348
  174.3 109.5 %reduce-scatter.7.cloned.1.call-start = ((), (), s32[]{:S(2)}) async-start(), calls=%async_computation.18 | async-start | bytes 2621440 | tf_op jit(solution)/shard_map/reduce_scatter | solution.py:352
  247.1 30.5 %all-to-all-start.7 = ((bf16[8,1024,128]{2,1,0:T(8,128)(2,1)}), bf16[8,1024,128]{2,1,0:T(8,128)(2,1)S(1)}, u32[]{:S(2)}, u32[]{:S(2)}) async-start(bf16[8,1024,128]{2,1,0:T(8,128)(2,1)} %convert_bitcast_fusion), calls=%async_computation.9 | async-start | bytes 4194304 | tf_op jit(solution)/shard_map/all_to_all | solution.py:345
  251.1 4.8 %copy-start.8 = (bf16[32,32,1024]{2,1,0:T(8,128)(2,1)S(1)}, bf16[32,32,1024]{2,1,0:T(8,128)(2,1)}, u32[]{:S(2)}) copy-start(bf16[32,32,1024]{2,1,0:T(8,128)(2,1)} %all-gather.13.cloned.1.call-done) | copy-start | bytes 6291460
  251.1 4.8 %copy-start.20 = (bf16[1024,1024]{1,0:T(8,128)(2,1)S(1)}, bf16[1024,1024]{1,0:T(8,128)(2,1)}, u32[]{:S(2)}) copy-start(bf16[1024,1024]{1,0:T(8,128)(2,1)} %get-tuple-element.78) | copy-start | bytes 6291460
  279.0 6.4 %copy-start.4 = (bf16[8,32,1024]{2,1,0:T(8,128)(2,1)S(1)}, bf16[8,32,1024]{2,1,0:T(8,128)(2,1)}, u32[]{:S(2)}) copy-start(bf16[8,32,1024]{2,1,0:T(8,128)(2,1)} %all_to_all.66) | copy-start | bytes 1572868
  279.0 53.8 %all-to-all-start.8 = ((bf16[8,128,2048]{2,1,0:T(8,128)(2,1)}), bf16[8,128,2048]{2,1,0:T(8,128)(2,1)}, u32[]{:S(2)}, u32[]{:S(2)}) async-start(bf16[8,128,2048]{2,1,0:T(8,128)(2,1)} %bitcast.144), calls=%async_computation.10 | async-start | bytes 8388608 | tf_op jit(solution)/shard_map/all_to_all | solution.py:345
  283.7 49.1 %all-gather.15.cloned.1.call-start = ((), (), s32[]{:S(2)}) async-start(), calls=%async_computation.24 | async-start | bytes 2621440 | tf_op jit(solution)/shard_map/all_gather | solution.py:348
  287.8 45.0 %copy-start.7 = (bf16[8,128,1024]{2,1,0:T(8,128)(2,1)S(1)}, bf16[8,128,1024]{2,1,0:T(8,128)(2,1)}, u32[]{:S(2)}) copy-start(bf16[8,128,1024]{2,1,0:T(8,128)(2,1)} %copy-done.6) | copy-start | bytes 6291460
  287.8 102.3 %reduce-scatter.9.cloned.1.call-start = ((), (), s32[]{:S(2)}) async-start(), calls=%async_computation.19 | async-start | bytes 2621440 | tf_op jit(solution)/shard_map/reduce_scatter | solution.py:352
  332.8 100.2 %reduce-scatter.11.cloned.1.call-start = ((), (), s32[]{:S(2)}) async-start(), calls=%async_computation.20 | async-start | bytes 2621440 | tf_op jit(solution)/shard_map/reduce_scatter | solution.py:352
  402.8 30.2 %all-to-all-start.11 = ((bf16[8,128,1024]{1,2,0:T(8,128)(2,1)}), bf16[8,128,1024]{1,2,0:T(8,128)(2,1)S(1)}, u32[]{:S(2)}, u32[]{:S(2)}) async-start(bf16[8,128,1024]{1,2,0:T(8,128)(2,1)} %copy.56), calls=%async_computation.15 | async-start | bytes 4194304 | tf_op jit(solution)/shard_map/all_to_all | solution.py:345
  438.2 7.2 %collective-permute-start.2 = (f32[3,1024]{1,0:T(4,128)S(1)}, f32[3,1024]{1,0:T(4,128)S(1)}, u32[]{:S(2)}, u32[]{:S(2)}) collective-permute-start(f32[3,1024]{1,0:T(4,128)S(1)} %pad_maximum_fusion.7), channel_id=1, source_target_pairs={{0,3},{1,0},{2,1},{3,2},{4,7},{5,4},{6,5},{7,6},{8,11},{9,8},{10,9... | collective-permute-start | bytes 36872 | tf_op jit(solution)/shard_map/ppermute | solution.py:480
  439.0 6.3 %collective-permute-start.1 = (f32[3,1024]{1,0:T(4,128)S(1)}, f32[3,1024]{1,0:T(4,128)S(1)}, u32[]{:S(2)}, u32[]{:S(2)}) collective-permute-start(f32[3,1024]{1,0:T(4,128)S(1)} %pad_maximum_fusion.7), channel_id=1, source_target_pairs={{0,2},{1,3},{2,0},{3,1},{4,6},{5,7},{6,4},{7,5},{8,10},{9,11},{10,... | collective-permute-start | bytes 36872 | tf_op jit(solution)/shard_map/ppermute | solution.py:480
  439.5 5.9 %collective-permute-start = (f32[3,1024]{1,0:T(4,128)S(1)}, f32[3,1024]{1,0:T(4,128)S(1)}, u32[]{:S(2)}, u32[]{:S(2)}) collective-permute-start(f32[3,1024]{1,0:T(4,128)S(1)} %pad_maximum_fusion.7), channel_id=1, source_target_pairs={{0,1},{1,2},{2,3},{3,0},{4,5},{5,6},{6,7},{7,4},{8,9},{9,10},{10,1... | collective-permute-start | bytes 36872 | tf_op jit(solution)/shard_map/ppermute | solution.py:480
  441.1 25.3 %all-to-all-start.12 = ((bf16[8,64,1024]{2,1,0:T(8,128)(2,1)}), bf16[8,64,1024]{2,1,0:T(8,128)(2,1)}, u32[]{:S(2)}, u32[]{:S(2)}) async-start(bf16[8,64,1024]{2,1,0:T(8,128)(2,1)} %pad_maximum_fusion.5), calls=%async_computation.16 | async-start | bytes 2097152 | tf_op jit(solution)/shard_map/all_to_all | solution.py:345
  445.5 14.7 %collective-permute-start.9 = (f32[3,128]{1,0:T(4,128)S(1)}, f32[3,128]{1,0:T(4,128)S(1)}, u32[]{:S(2)}, u32[]{:S(2)}) collective-permute-start(f32[3,128]{1,0:T(4,128)S(1)} %get-tuple-element.128), channel_id=1, source_target_pairs={{0,28},{4,24},{8,20},{12,16},{16,12},{20,8},{24,4},{28,0},{1,29},{... | collective-permute-start | bytes 4616 | tf_op jit(solution)/shard_map/ppermute | solution.py:489
  448.1 12.8 %collective-permute-start.8 = (f32[3,128]{1,0:T(4,128)S(1)}, f32[3,128]{1,0:T(4,128)S(1)}, u32[]{:S(2)}, u32[]{:S(2)}) collective-permute-start(f32[3,128]{1,0:T(4,128)S(1)} %get-tuple-element.129), channel_id=1, source_target_pairs={{0,24},{4,28},{8,16},{12,20},{16,8},{20,12},{24,0},{28,4},{1,25},{... | collective-permute-start | bytes 4616 | tf_op jit(solution)/shard_map/ppermute | solution.py:489
  448.4 17.9 %collective-permute-start.7 = (f32[3,128]{1,0:T(4,128)S(1)}, f32[3,128]{1,0:T(4,128)S(1)}, u32[]{:S(2)}, u32[]{:S(2)}) collective-permute-start(f32[3,128]{1,0:T(4,128)S(1)} %get-tuple-element.130), channel_id=1, source_target_pairs={{0,20},{4,16},{8,28},{12,24},{16,4},{20,0},{24,12},{28,8},{1,21},{... | collective-permute-start | bytes 4616 | tf_op jit(solution)/shard_map/ppermute | solution.py:489
  449.8 16.5 %collective-permute-start.6 = (f32[3,128]{1,0:T(4,128)S(1)}, f32[3,128]{1,0:T(4,128)S(1)}, u32[]{:S(2)}, u32[]{:S(2)}) collective-permute-start(f32[3,128]{1,0:T(4,128)S(1)} %get-tuple-element.131), channel_id=1, source_target_pairs={{0,16},{4,20},{8,24},{12,28},{16,0},{20,4},{24,8},{28,12},{1,17},{... | collective-permute-start | bytes 4616 | tf_op jit(solution)/shard_map/ppermute | solution.py:489
  450.1 16.2 %collective-permute-start.5 = (f32[3,128]{1,0:T(4,128)S(1)}, f32[3,128]{1,0:T(4,128)S(1)}, u32[]{:S(2)}, u32[]{:S(2)}) collective-permute-start(f32[3,128]{1,0:T(4,128)S(1)} %get-tuple-element.132), channel_id=1, source_target_pairs={{0,12},{4,8},{8,4},{12,0},{16,28},{20,24},{24,20},{28,16},{1,13},{... | collective-permute-start | bytes 4616 | tf_op jit(solution)/shard_map/ppermute | solution.py:489
  460.2 6.2 %collective-permute-start.4 = (f32[3,128]{1,0:T(4,128)S(1)}, f32[3,128]{1,0:T(4,128)S(1)}, u32[]{:S(2)}, u32[]{:S(2)}) collective-permute-start(f32[3,128]{1,0:T(4,128)S(1)} %get-tuple-element.133), channel_id=1, source_target_pairs={{0,8},{4,12},{8,0},{12,4},{16,24},{20,28},{24,16},{28,20},{1,9},{5... | collective-permute-start | bytes 4616 | tf_op jit(solution)/shard_map/ppermute | solution.py:489
  460.8 5.5 %collective-permute-start.3 = (f32[3,128]{1,0:T(4,128)S(1)}, f32[3,128]{1,0:T(4,128)S(1)}, u32[]{:S(2)}, u32[]{:S(2)}) collective-permute-start(f32[3,128]{1,0:T(4,128)S(1)} %get-tuple-element.127), channel_id=1, source_target_pairs={{0,4},{4,0},{8,12},{12,8},{16,20},{20,16},{24,28},{28,24},{1,5},{5... | collective-permute-start | bytes 4616 | tf_op jit(solution)/shard_map/ppermute | solution.py:489
  (14 other events, 31.2 us)
Sparse Core Ops, SparseCore 0:
  28.4 45.0 all-gather.8
  75.0 44.4 all-gather.10
  128.6 41.9 reduce-scatter.4
  174.4 44.8 all-gather.12
  236.8 42.4 reduce-scatter.6
  288.0 44.4 all-gather.14
  335.3 42.4 reduce-scatter.8
  390.3 40.5 reduce-scatter.10

commit v12 on v11

--- a/solution.py
+++ b/solution.py
@@ -430,6 +430,7 @@
         )
         g_down = exchange(rowwise(d_down.astype(BF)))
         g_gate = jnp.einsum("fd,fk->dk", n2_all, d_gate, preferred_element_type=F32).astype(BF)
+        g_gate, wdown = after(g_gate, wdown)
         g_up = jnp.einsum("fd,fk->dk", n2_all, d_up, preferred_element_type=F32).astype(BF)
         g_gate_up = rowwise(jnp.concatenate([g_gate, g_up], axis=1))
         g_down, g_gate_up = after(g_down, g_gate_up)
@@ -459,7 +460,7 @@
             ],
             axis=1,
         )
-        g_attn = exchange(d_attn.reshape(count, block, -1))
+        g_attn = rowwise(exchange(rowwise(d_attn).reshape(count, block, -1)))
         layer_out = (h1 + ffout.astype(F32)).astype(BF)
         g_down = g_down.astype(F32)
         dn1, g_attn, layer_out, g_gate_up, g_down = after(
@@ -479,7 +480,7 @@
             around = [(i, (i + k) % lanes) for i in range(lanes)]
             total = total + lax.ppermute(sums, "tensor", around)
         total, g_attn = after(total, g_attn)
-        g_attn = g_attn.astype(F32)
+        g_attn = rowwise(g_attn.astype(F32))
         g_qkv = jnp.stack([g_attn[..., j * cols : (j + 1) * cols] for j in range(3)], axis=1)
         g_out = jnp.swapaxes(g_attn[..., 3 * cols :], 1, 2)
         total = jnp.swapaxes(total.reshape(3, count, block), 0, 1)

time: 485 us -> 473 us (0.975); the launches traced: 477 us -> 471 us
  local copies, waits for them, and re-layouts: 32 us -> 23.3 us
    all_to_all x7, waiting for transfers between devices: 145 us -> 138 us  [exchange(): return lax.all_to_all(blocks, 'dp', 0, 0, tiled=True)]
    unnamed x42 -> x41, local copies, waits for them, and re-layouts: 8.88 us -> 10.1 us
  transfers between devices with their start and end apart: 25 -> 25, of which waited for: 11 -> 13; matrix products, arithmetic and copies ran while one was open for 18% -> 17% of each run, Pallas kernels for 5% -> 5%
where the time goes in v12:
time: 473 us; the launch traced here: 471 us
  waiting for transfers between devices  154 us (33%)
  blocking collectives  117 us (25%)
  other arithmetic  44.5 us (9%)
  starting transfers between devices  41.4 us (9%)
  Pallas kernels  41.1 us (9%)
  matrix products  35.3 us (7%)
  local copies, waits for them, and re-layouts  23.3 us (5%)
  between operations  14.6 us (3%)
    all_to_all x7, waiting for transfers between devices, exchange(): return lax.all_to_all(blocks, 'dp', 0, 0, tiled=True)  138 us
    all_to_all x6, blocking collectives, exchange(): return lax.all_to_all(blocks, 'dp', 0, 0, tiled=True)  117 us
    all_to_all x7, starting transfers between devices, exchange(): return lax.all_to_all(blocks, 'dp', 0, 0, tiled=True)  30.5 us
    pallas_call x2, Pallas kernels, attention_call(): pl.pallas_call(body, grid=(frames // span,), in_specs=[spec(a.shape[2]) f...  23.7 us
    pallas_call x1, Pallas kernels, feed_call(): pl.pallas_call(feed_body, grid=(count + width // part,), in_specs=[whole,...  17.4 us
    unnamed x41, local copies, waits for them, and re-layouts  10.1 us
  transfers between devices with their start and end apart: 25, of which 13 were waited for; matrix products, arithmetic and copies ran while one was open for 17% of the time, Pallas kernels for 5%

profile of v12, /device:TPU:0, one launch (start us, length us, event | category | flops | bytes accessed | tf_op | source)
XLA Modules:
  0.0 471.4 jit_solution(14971083997646809859)
XLA Ops:
  11.2 5.2 %all-to-all-start = ((bf16[8,32,1152]{2,1,0:T(8,128)(2,1)}), bf16[8,32,1152]{2,1,0:T(8,128)(2,1)S(1)}, u32[]{:S(2)}, u32[]{:S(2)}) async-start(bf16[8,32,1152]{2,1,0:T(8,128)(2,1)} %pad_maximum_fusion.6), calls=%async_computation | async-start | bytes 1179648 | tf_op jit(solution)/shard_map/all_to_all | solution.py:345
  16.5 10.4 %all-to-all-done = bf16[8,32,1152]{2,1,0:T(8,128)(2,1)S(1)} async-done(((bf16[8,32,1152]{2,1,0:T(8,128)(2,1)}), bf16[8,32,1152]{2,1,0:T(8,128)(2,1)S(1)}, u32[]{:S(2)}, u32[]{:S(2)}) %all-to-all-start) | async-done | bytes 589856 | tf_op jit(solution)/shard_map/all_to_all | solution.py:345
  30.9 29.1 %all_to_all.65 = bf16[8,128,1024]{2,1,0:T(8,128)(2,1)S(1)} all-to-all(bf16[8,128,1024]{2,1,0:T(8,128)(2,1)S(1)} %pad_maximum_fusion.3), channel_id=1, replica_groups=mesh['dp'=8,'tensor'=4] {'dp'}, dimensions={0} | all-to-all | bytes 4194304 | tf_op jit(solution)/shard_map/all_to_all | solution.py:345
  60.1 12.8 %all_to_all.66 = bf16[8,32,1024]{2,1,0:T(8,128)(2,1)} all-to-all(bf16[8,32,1024]{2,1,0:T(8,128)(2,1)S(1)} %copy-done.16), channel_id=1, replica_groups=mesh['dp'=8,'tensor'=4] {'dp'}, dimensions={0} | all-to-all | bytes 1048576 | tf_op jit(solution)/shard_map/all_to_all | solution.py:345
  73.5 3.4 convolution_convert_fusion.6
  77.1 24.5 %all_to_all.67.qkv_ref = bf16[8,128,768]{2,1,0:T(8,128)(2,1)} all-to-all(bf16[8,128,768]{2,1,0:T(8,128)(2,1)S(1)} %bitcast.146), channel_id=1, replica_groups=mesh['dp'=8,'tensor'=4] {'dp'}, dimensions={0} | all-to-all | bytes 3145728 | tf_op jit(solution)/shard_map/all_to_all | solution.py:345
  101.6 10.9 %shard_map.152 = bf16[8,128,256]{2,1,0:T(8,128)(2,1)} custom-call(bf16[8,128,768]{2,1,0:T(8,128)(2,1)} %all_to_all.67.qkv_ref), custom_call_target="tpu_custom_call" | custom-call | tf_op jit(solution)/shard_map/pallas_call | solution.py:272
  112.4 13.1 %all_to_all.68 = bf16[8,128,256]{2,1,0:T(8,128)(2,1)S(1)} all-to-all(bf16[8,128,256]{2,1,0:T(8,128)(2,1)} %shard_map.152), channel_id=1, replica_groups=mesh['dp'=8,'tensor'=4] {'dp'}, dimensions={0} | all-to-all | bytes 1048576 | tf_op jit(solution)/shard_map/all_to_all | solution.py:345
  128.5 3.8 convert_element_type.101
  132.3 3.6 all-to-all-start.5
  136.0 4.0 convert.34
  143.0 19.5 %all-to-all-done.5.wdown_ref = bf16[8,1024,128]{2,1,0:T(8,128)(2,1)S(1)} async-done(((bf16[8,1024,128]{2,1,0:T(8,128)(2,1)}), bf16[8,1024,128]{2,1,0:T(8,128)(2,1)S(1)}, u32[]{:S(2)}, u32[]{:S(2)}) %all-to-all-start.5) | async-done | bytes 2097184 | tf_op jit(solution)/shard_map/all_to_all | solution.py:345
  163.8 4.6 all-to-all-start.6
  174.5 43.0 %all-to-all-done.6 = bf16[8,128,2048]{2,1,0:T(8,128)(2,1)} async-done(((bf16[8,128,2048]{2,1,0:T(8,128)(2,1)}), bf16[8,128,2048]{2,1,0:T(8,128)(2,1)}, u32[]{:S(2)}, u32[]{:S(2)}) %all-to-all-start.6) | async-done | bytes 4194336 | tf_op jit(solution)/shard_map/all_to_all | solution.py:345
  219.3 17.4 %shard_map.153 = (bf16[1024,1024]{1,0:T(8,128)(2,1)}, bf16[1024,1024]{1,0:T(8,128)(2,1)}, bf16[1024,1024]{1,0:T(8,128)(2,1)}, bf16[1024,1024]{1,0:T(8,128)(2,1)}) custom-call(bf16[1024,1024]{1,0:T(8,128)(2,1)} %bitcast.160, bf16[1024,1024]{1,0:T(8,128)(2,1)} %bitcast.158, bf16[1024,2048]{1,0:T(8,128)(2,1)} %bitcast.25.wgate_ref.wup_ref.wrow_ref, ...), custom_call_target="tpu_custom_call" | custom-call | tf_op jit(solution)/shard_map/pallas_call | solution.py:324
  238.3 5.3 %convert_bitcast_fusion = bf16[8,1024,128]{2,1,0:T(8,128)(2,1)} fusion(bf16[1024,1024]{1,0:T(8,128)(2,1)} %get-tuple-element.79, bf16[1024,1024]{1,0:T(8,128)(2,1)S(1)} %bitcast.159), kind=kOutput, calls=%fused_computation.15 | convolution fusion | flops 2148532224 | bytes 6291456 | tf_op jit(solution)/shard_map/fk,frd->rkd/dot_general | solution.py:425
  243.6 4.6 all-to-all-start.7
  248.2 6.1 %convolution_convert_fusion.2 = bf16[1024,1024]{1,0:T(8,128)(2,1)} fusion(bf16[1024,1024]{1,0:T(8,128)(2,1)} %bitcast.161, bf16[1024,1024]{1,0:T(8,128)(2,1)} %get-tuple-element.80), kind=kOutput, calls=%fused_computation.18 | convolution fusion | flops 2148532224 | bytes 6291456 | tf_op jit(solution)/shard_map/fd,fk->dk/dot_general | solution.py:432
  256.9 4.8 %convolution_convert_fusion.1 = bf16[1024,1024]{1,0:T(8,128)(2,1)S(1)} fusion(bf16[1024,1024]{1,0:T(8,128)(2,1)} %bitcast.162, bf16[1024,1024]{1,0:T(8,128)(2,1)} %get-tuple-element.82), kind=kOutput, calls=%fused_computation.17 | convolution fusion | flops 2148532224 | bytes 6291456 | tf_op jit(solution)/shard_map/fd,fk->dk/dot_general | solution.py:434
  265.4 3.7 convolution_convert_fusion
  269.1 5.5 %all-to-all-done.7 = bf16[8,1024,128]{2,1,0:T(8,128)(2,1)} async-done(((bf16[8,1024,128]{2,1,0:T(8,128)(2,1)}), bf16[8,1024,128]{2,1,0:T(8,128)(2,1)}, u32[]{:S(2)}, u32[]{:S(2)}) %all-to-all-start.7) | async-done | bytes 2097184 | tf_op jit(solution)/shard_map/all_to_all | solution.py:345
  274.6 4.7 all-to-all-start.8
  283.5 44.9 %all-to-all-done.8 = bf16[8,128,2048]{2,1,0:T(8,128)(2,1)} async-done(((bf16[8,128,2048]{2,1,0:T(8,128)(2,1)}), bf16[8,128,2048]{2,1,0:T(8,128)(2,1)}, u32[]{:S(2)}, u32[]{:S(2)}) %all-to-all-start.8) | async-done | bytes 4194336 | tf_op jit(solution)/shard_map/all_to_all | solution.py:345
  331.0 13.3 %all_to_all.69.grad_ref = bf16[8,128,256]{2,1,0:T(8,128)(2,1)} all-to-all(bf16[8,128,256]{2,1,0:T(8,128)(2,1)S(1)} %bitcast.168), channel_id=1, replica_groups=mesh['dp'=8,'tensor'=4] {'dp'}, dimensions={0} | all-to-all | bytes 1048576 | tf_op jit(solution)/shard_map/all_to_all | solution.py:345
  344.3 12.8 %shard_map.154 = bf16[8,128,768]{2,1,0:T(8,128)(2,1)} custom-call(bf16[8,128,768]{2,1,0:T(8,128)(2,1)} %all_to_all.67.qkv_ref, bf16[8,128,256]{2,1,0:T(8,128)(2,1)} %all_to_all.69.grad_ref), custom_call_target="tpu_custom_call" | custom-call | tf_op jit(solution)/shard_map/pallas_call | solution.py:272
  357.1 24.4 %all_to_all.70 = bf16[8,128,768]{2,1,0:T(8,128)(2,1)S(1)} all-to-all(bf16[8,128,768]{2,1,0:T(8,128)(2,1)} %shard_map.154), channel_id=1, replica_groups=mesh['dp'=8,'tensor'=4] {'dp'}, dimensions={0} | all-to-all | bytes 3145728 | tf_op jit(solution)/shard_map/all_to_all | solution.py:345
  393.6 3.6 all-to-all-start.11
  397.3 3.9 convert_element_type.118
  403.9 3.9 maximum_convert_fusion
  408.9 14.9 %all-to-all-done.11 = bf16[8,128,1024]{2,1,0:T(8,128)(2,1)S(1)} async-done(((bf16[8,128,1024]{2,1,0:T(8,128)(2,1)}), bf16[8,128,1024]{2,1,0:T(8,128)(2,1)S(1)}, u32[]{:S(2)}, u32[]{:S(2)}) %all-to-all-start.11) | async-done | bytes 2097184 | tf_op jit(solution)/shard_map/all_to_all | solution.py:345
  435.8 4.2 all-to-all-start.12
  447.0 7.9 %collective-permute-done.9 = f32[3,128]{1,0:T(4,128)S(1)} collective-permute-done((f32[3,128]{1,0:T(4,128)S(1)}, f32[3,128]{1,0:T(4,128)S(1)}, u32[]{:S(2)}, u32[]{:S(2)}) %collective-permute-start.9) | collective-permute-done | bytes 1568 | tf_op jit(solution)/shard_map/ppermute | solution.py:490
  (140 shorter events, 83.1 us)
Async XLA Ops:
  9.2 19.1 %copy-start.15 = (f32[8,256,128]{2,1,0:T(8,128)S(1)}, f32[8,256,128]{2,1,0:T(8,128)}, u32[]{:S(2)}) copy-start(f32[8,256,128]{2,1,0:T(8,128)} %param.12) | copy-start | bytes 3145732
  11.2 15.6 %all-to-all-start = ((bf16[8,32,1152]{2,1,0:T(8,128)(2,1)}), bf16[8,32,1152]{2,1,0:T(8,128)(2,1)S(1)}, u32[]{:S(2)}, u32[]{:S(2)}) async-start(bf16[8,32,1152]{2,1,0:T(8,128)(2,1)} %pad_maximum_fusion.6), calls=%async_computation | async-start | bytes 1179648 | tf_op jit(solution)/shard_map/all_to_all | solution.py:345
  16.4 57.1 %all-gather.9.cloned.1.call-start = ((), (), s32[]{:S(2)}) async-start(), calls=%async_computation.21 | async-start | bytes 2621440 | tf_op jit(solution)/shard_map/all_gather | solution.py:348
  28.3 100.2 %all-gather.11.cloned.1.call-start = ((), (), s32[]{:S(2)}) async-start(), calls=%async_computation.22 | async-start | bytes 2621440 | tf_op jit(solution)/shard_map/all_gather | solution.py:348
  30.9 29.2 %copy-start.16 = (bf16[8,32,1024]{2,1,0:T(8,128)(2,1)S(1)}, bf16[8,32,1024]{2,1,0:T(8,128)(2,1)}, u32[]{:S(2)}) copy-start(bf16[8,32,1024]{2,1,0:T(8,128)(2,1)} %param.17) | copy-start | bytes 1572868
  60.1 65.5 %copy-start.5 = (bf16[8,128,1024]{2,1,0:T(8,128)(2,1)}, bf16[8,128,1024]{2,1,0:T(8,128)(2,1)S(1)}, u32[]{:S(2)}) copy-start(bf16[8,128,1024]{2,1,0:T(8,128)(2,1)S(1)} %all_to_all.65) | copy-start | bytes 6291460
  73.5 97.1 %reduce-scatter.5.cloned.1.call-start = ((), (), s32[]{:S(2)}) async-start(), calls=%async_computation.17 | async-start | bytes 2621440 | tf_op jit(solution)/shard_map/reduce_scatter | solution.py:352
  132.3 30.2 %all-to-all-start.5 = ((bf16[8,1024,128]{2,1,0:T(8,128)(2,1)}), bf16[8,1024,128]{2,1,0:T(8,128)(2,1)S(1)}, u32[]{:S(2)}, u32[]{:S(2)}) async-start(bf16[8,1024,128]{2,1,0:T(8,128)(2,1)} %convert_element_type.101), calls=%async_computation.6 | async-start | bytes 4194304 | tf_op jit(solution)/shard_map/all_to_all | solution.py:345
  163.8 53.7 %all-to-all-start.6 = ((bf16[8,128,2048]{2,1,0:T(8,128)(2,1)}), bf16[8,128,2048]{2,1,0:T(8,128)(2,1)}, u32[]{:S(2)}, u32[]{:S(2)}) async-start(bf16[8,128,2048]{2,1,0:T(8,128)(2,1)} %pad_maximum_fusion), calls=%async_computation.7 | async-start | bytes 8388608 | tf_op jit(solution)/shard_map/all_to_all | solution.py:345
  168.4 50.9 %all-gather.13.cloned.1.call-start = ((), (), s32[]{:S(2)}) async-start(), calls=%async_computation.23 | async-start | bytes 2621440 | tf_op jit(solution)/shard_map/all_gather | solution.py:348
  174.3 105.1 %reduce-scatter.7.cloned.1.call-start = ((), (), s32[]{:S(2)}) async-start(), calls=%async_computation.18 | async-start | bytes 2621440 | tf_op jit(solution)/shard_map/reduce_scatter | solution.py:352
  243.6 31.0 %all-to-all-start.7 = ((bf16[8,1024,128]{2,1,0:T(8,128)(2,1)}), bf16[8,1024,128]{2,1,0:T(8,128)(2,1)}, u32[]{:S(2)}, u32[]{:S(2)}) async-start(bf16[8,1024,128]{2,1,0:T(8,128)(2,1)} %convert_bitcast_fusion), calls=%async_computation.9 | async-start | bytes 4194304 | tf_op jit(solution)/shard_map/all_to_all | solution.py:345
  248.2 6.1 %copy-start.1 = (bf16[8,1024,128]{2,1,0:T(8,128)(2,1)S(1)}, bf16[8,1024,128]{2,1,0:T(8,128)(2,1)}, u32[]{:S(2)}) copy-start(bf16[8,1024,128]{2,1,0:T(8,128)(2,1)} %copy-done) | copy-start | bytes 6291460
  274.6 4.8 %copy-start.2 = (bf16[1,8,32,1024]{3,2,1,0:T(8,128)(2,1)S(1)}, bf16[1,8,32,1024]{3,2,1,0:T(8,128)(2,1)}, u32[]{:S(2)}) copy-start(bf16[1,8,32,1024]{3,2,1,0:T(8,128)(2,1)} %reduce-scatter.5.cloned.1.call-done) | copy-start | bytes 1572868
  274.6 6.4 %copy-start.3 = (bf16[8,32,1024]{2,1,0:T(8,128)(2,1)S(1)}, bf16[8,32,1024]{2,1,0:T(8,128)(2,1)}, u32[]{:S(2)}) copy-start(bf16[8,32,1024]{2,1,0:T(8,128)(2,1)} %all_to_all.66) | copy-start | bytes 1572868
  274.6 53.8 %all-to-all-start.8 = ((bf16[8,128,2048]{2,1,0:T(8,128)(2,1)}), bf16[8,128,2048]{2,1,0:T(8,128)(2,1)}, u32[]{:S(2)}, u32[]{:S(2)}) async-start(bf16[8,128,2048]{2,1,0:T(8,128)(2,1)} %bitcast.143), calls=%async_computation.10 | async-start | bytes 8388608 | tf_op jit(solution)/shard_map/all_to_all | solution.py:345
  279.3 49.3 %all-gather.15.cloned.1.call-start = ((), (), s32[]{:S(2)}) async-start(), calls=%async_computation.24 | async-start | bytes 2621440 | tf_op jit(solution)/shard_map/all_gather | solution.py:348
  283.4 45.3 %copy-start.6 = (bf16[8,128,1024]{2,1,0:T(8,128)(2,1)S(1)}, bf16[8,128,1024]{2,1,0:T(8,128)(2,1)}, u32[]{:S(2)}) copy-start(bf16[8,128,1024]{2,1,0:T(8,128)(2,1)} %copy-done.5) | copy-start | bytes 6291460
  283.4 102.6 %reduce-scatter.9.cloned.1.call-start = ((), (), s32[]{:S(2)}) async-start(), calls=%async_computation.19 | async-start | bytes 2621440 | tf_op jit(solution)/shard_map/reduce_scatter | solution.py:352
  328.6 98.2 %reduce-scatter.11.cloned.1.call-start = ((), (), s32[]{:S(2)}) async-start(), calls=%async_computation.20 | async-start | bytes 2621440 | tf_op jit(solution)/shard_map/reduce_scatter | solution.py:352
  393.6 30.2 %all-to-all-start.11 = ((bf16[8,128,1024]{2,1,0:T(8,128)(2,1)}), bf16[8,128,1024]{2,1,0:T(8,128)(2,1)S(1)}, u32[]{:S(2)}, u32[]{:S(2)}) async-start(bf16[8,128,1024]{2,1,0:T(8,128)(2,1)} %bitcast.145), calls=%async_computation.15 | async-start | bytes 4194304 | tf_op jit(solution)/shard_map/all_to_all | solution.py:345
  432.0 8.0 %collective-permute-start.2 = (f32[3,1024]{1,0:T(4,128)S(1)}, f32[3,1024]{1,0:T(4,128)S(1)}, u32[]{:S(2)}, u32[]{:S(2)}) collective-permute-start(f32[3,1024]{1,0:T(4,128)S(1)} %pad_maximum_fusion.7), channel_id=1, source_target_pairs={{0,3},{1,0},{2,1},{3,2},{4,7},{5,4},{6,5},{7,6},{8,11},{9,8},{10,9... | collective-permute-start | bytes 36872 | tf_op jit(solution)/shard_map/ppermute | solution.py:481
  433.9 6.1 %collective-permute-start.1 = (f32[3,1024]{1,0:T(4,128)S(1)}, f32[3,1024]{1,0:T(4,128)S(1)}, u32[]{:S(2)}, u32[]{:S(2)}) collective-permute-start(f32[3,1024]{1,0:T(4,128)S(1)} %pad_maximum_fusion.7), channel_id=1, source_target_pairs={{0,2},{1,3},{2,0},{3,1},{4,6},{5,7},{6,4},{7,5},{8,10},{9,11},{10,... | collective-permute-start | bytes 36872 | tf_op jit(solution)/shard_map/ppermute | solution.py:481
  434.2 5.8 %collective-permute-start = (f32[3,1024]{1,0:T(4,128)S(1)}, f32[3,1024]{1,0:T(4,128)S(1)}, u32[]{:S(2)}, u32[]{:S(2)}) collective-permute-start(f32[3,1024]{1,0:T(4,128)S(1)} %pad_maximum_fusion.7), channel_id=1, source_target_pairs={{0,1},{1,2},{2,3},{3,0},{4,5},{5,6},{6,7},{7,4},{8,9},{9,10},{10,1... | collective-permute-start | bytes 36872 | tf_op jit(solution)/shard_map/ppermute | solution.py:481
  435.8 25.5 %all-to-all-start.12 = ((bf16[8,64,1024]{2,1,0:T(8,128)(2,1)}), bf16[8,64,1024]{2,1,0:T(8,128)(2,1)}, u32[]{:S(2)}, u32[]{:S(2)}) async-start(bf16[8,64,1024]{2,1,0:T(8,128)(2,1)} %pad_maximum_fusion.5), calls=%async_computation.16 | async-start | bytes 2097152 | tf_op jit(solution)/shard_map/all_to_all | solution.py:345
  440.1 14.7 %collective-permute-start.9 = (f32[3,128]{1,0:T(4,128)S(1)}, f32[3,128]{1,0:T(4,128)S(1)}, u32[]{:S(2)}, u32[]{:S(2)}) collective-permute-start(f32[3,128]{1,0:T(4,128)S(1)} %get-tuple-element.131), channel_id=1, source_target_pairs={{0,28},{4,24},{8,20},{12,16},{16,12},{20,8},{24,4},{28,0},{1,29},{... | collective-permute-start | bytes 4616 | tf_op jit(solution)/shard_map/ppermute | solution.py:490
  442.7 12.8 %collective-permute-start.8 = (f32[3,128]{1,0:T(4,128)S(1)}, f32[3,128]{1,0:T(4,128)S(1)}, u32[]{:S(2)}, u32[]{:S(2)}) collective-permute-start(f32[3,128]{1,0:T(4,128)S(1)} %get-tuple-element.132), channel_id=1, source_target_pairs={{0,24},{4,28},{8,16},{12,20},{16,8},{20,12},{24,0},{28,4},{1,25},{... | collective-permute-start | bytes 4616 | tf_op jit(solution)/shard_map/ppermute | solution.py:490
  443.1 18.1 %collective-permute-start.7 = (f32[3,128]{1,0:T(4,128)S(1)}, f32[3,128]{1,0:T(4,128)S(1)}, u32[]{:S(2)}, u32[]{:S(2)}) collective-permute-start(f32[3,128]{1,0:T(4,128)S(1)} %get-tuple-element.133), channel_id=1, source_target_pairs={{0,20},{4,16},{8,28},{12,24},{16,4},{20,0},{24,12},{28,8},{1,21},{... | collective-permute-start | bytes 4616 | tf_op jit(solution)/shard_map/ppermute | solution.py:490
  444.4 16.7 %collective-permute-start.6 = (f32[3,128]{1,0:T(4,128)S(1)}, f32[3,128]{1,0:T(4,128)S(1)}, u32[]{:S(2)}, u32[]{:S(2)}) collective-permute-start(f32[3,128]{1,0:T(4,128)S(1)} %get-tuple-element.134), channel_id=1, source_target_pairs={{0,16},{4,20},{8,24},{12,28},{16,0},{20,4},{24,8},{28,12},{1,17},{... | collective-permute-start | bytes 4616 | tf_op jit(solution)/shard_map/ppermute | solution.py:490
  444.7 16.5 %collective-permute-start.5 = (f32[3,128]{1,0:T(4,128)S(1)}, f32[3,128]{1,0:T(4,128)S(1)}, u32[]{:S(2)}, u32[]{:S(2)}) collective-permute-start(f32[3,128]{1,0:T(4,128)S(1)} %get-tuple-element.135), channel_id=1, source_target_pairs={{0,12},{4,8},{8,4},{12,0},{16,28},{20,24},{24,20},{28,16},{1,13},{... | collective-permute-start | bytes 4616 | tf_op jit(solution)/shard_map/ppermute | solution.py:490
  454.8 6.4 %collective-permute-start.4 = (f32[3,128]{1,0:T(4,128)S(1)}, f32[3,128]{1,0:T(4,128)S(1)}, u32[]{:S(2)}, u32[]{:S(2)}) collective-permute-start(f32[3,128]{1,0:T(4,128)S(1)} %get-tuple-element.136), channel_id=1, source_target_pairs={{0,8},{4,12},{8,0},{12,4},{16,24},{20,28},{24,16},{28,20},{1,9},{5... | collective-permute-start | bytes 4616 | tf_op jit(solution)/shard_map/ppermute | solution.py:490
  455.5 5.7 %collective-permute-start.3 = (f32[3,128]{1,0:T(4,128)S(1)}, f32[3,128]{1,0:T(4,128)S(1)}, u32[]{:S(2)}, u32[]{:S(2)}) collective-permute-start(f32[3,128]{1,0:T(4,128)S(1)} %get-tuple-element.130), channel_id=1, source_target_pairs={{0,4},{4,0},{8,12},{12,8},{16,20},{20,16},{24,28},{28,24},{1,5},{5... | collective-permute-start | bytes 4616 | tf_op jit(solution)/shard_map/ppermute | solution.py:490
  (13 other events, 29.9 us)
Sparse Core Ops, SparseCore 0:
  28.4 45.0 all-gather.8
  75.0 44.4 all-gather.10
  128.6 41.9 reduce-scatter.4
  174.4 44.8 all-gather.12
  236.8 42.4 reduce-scatter.6
  283.6 44.9 all-gather.14
  331.5 42.4 reduce-scatter.8
  386.2 40.5 reduce-scatter.10
